TPU v7x, 128 devices: a whole 4x4x4 slice. The times are simulated.
128 devices in a mesh: dp: 128 (over x, z, y, core).
Axes of the slice: x: 4, y: 4, z: 4, core: 2. Of those that a mesh axis runs over, the one named last changes fastest.
Arguments:
- query_features: bfloat16 [32768, 768], P('dp'), may hold values from -24 to 24
- passage_features: bfloat16 [32768, 768], P('dp'), may hold values from -24 to 24
- counts: int32 [128], replicated, may hold values from 128 to 256, as said below
- positives: int32 [32768], P('dp'), may hold values from 0 to 17407
- w_first: bfloat16 [768, 1536], replicated, may hold values from -0.21875 to 0.21875
- w_second: bfloat16 [1536, 384], replicated, may hold values from -0.15625 to 0.15625
Outputs:
- mean_loss: float32 [], replicated
- grad_first: float32 [768, 1536], P(None, 'dp')
- grad_second: float32 [1536, 384], P('dp')
Inputs may be any that keep to these rules, and one draw needn't show every extreme that they name: Device i holds counts[i] pairs in the first slots of its 256 slots. Each entry is 128 or 256; among the 16 devices whose indices agree modulo 128 // 16 exactly one entry is 256, so the entries sum to 17408. `positives`: only entries of occupied slots are used; an entry is the index of a passage in the order of occupied slots, device by device.
All inputs are finite; a program needn't handle non-finite values.
Results may differ from a plain program's by a relative error of at most 0.0043.
The roundings to bfloat16 on the way count: a program that leaves them out, or rounds other values in their place, can miss the bound.
Values may be sent and summed in bfloat16 or wider, within the bound.
No kernel may reach another device: no remote copies, remote signals or barrier semaphores. Data moves between devices by JAX's collectives and lax.ppermute only.
A program may use at most 128 MiB of HBM per device.

v0:
```python
import jax
import jax.numpy as jnp
from jax import lax
from jax.sharding import Mesh
from jax.sharding import PartitionSpec as P

DP = ("dp_0", "dp_1", "dp_2", "dp_3")


def from_partner(block, axis, apart):
    count = lax.axis_size(axis)
    route = []
    for low in range(count):
        high = low | 1 << apart
        if high != low and high < count:
            route += [(low, high), (high, low)]
    return lax.ppermute(block, axis, route)


def in_order(tiles, dim):
    dims = list(tiles.shape[1:])
    dims[dim] *= tiles.shape[0]
    return jnp.moveaxis(tiles, 0, dim).reshape(dims)


def stacked_from(x, axes, order):
    tiles = x[None]
    for k in order:
        tiles = lax.all_gather(tiles, axes[k], axis=0, tiled=True)
    carried = [lax.axis_size(axes[k]) for k in reversed(order)]
    tiles = tiles.reshape(*carried, *x.shape)
    turned = sorted(range(len(order)), key=lambda place: order[len(order) - 1 - place])
    return tiles.transpose(*turned, *range(len(order), tiles.ndim)).reshape(-1, *x.shape)


def whole_of(x, axes, order, dim):
    return in_order(stacked_from(x, axes, order), dim)


def sent_together(arrays, axis, dim, along):
    widths = [a.shape[along] for a in arrays]
    both = jnp.concatenate(arrays, axis=along)
    out = lax.all_gather(both, axis, axis=dim, tiled=True)
    return tuple(jnp.split(out, [sum(widths[:k]) for k in range(1, len(widths))], axis=along))


def gather_together(arrays, axis, dims):
    flat = jnp.concatenate([a.reshape(-1) for a in arrays])
    lines, at, gathered = (lax.all_gather(flat, axis), 0, [])
    for a, dim in zip(arrays, dims):
        tiles = lines[:, at : at + a.size].reshape(-1, *a.shape)
        gathered.append(in_order(tiles, dim))
        at += a.size
    return tuple(gathered)


def in_blocks(x, dim, devices):
    before, after = (x.shape[:dim], x.shape[dim + 1 :])
    return jnp.moveaxis(x.reshape(*before, devices, -1, *after), dim, 0)


def summed_rows(x, chips, core, dim):
    sizes = (lax.axis_size(chips), lax.axis_size(core))
    tiles = in_blocks(x, dim, sizes[0] * sizes[1])
    inside = tiles.shape[1:]
    tiles = tiles.reshape(*sizes, *inside).swapaxes(0, 1).reshape(-1, *inside)
    tiles = lax.psum_scatter(tiles, core, scatter_dimension=0, tiled=True)
    return lax.psum_scatter(tiles, chips, scatter_dimension=0, tiled=True)[0]


def gelu_tanh(values):
    return jax.nn.gelu(values, approximate=True)


def tower_pass(features, w_first, w_second):
    pre_act = jnp.dot(features, w_first, preferred_element_type=jnp.float32)
    hidden = gelu_tanh(pre_act).astype(jnp.bfloat16)
    embedded = jnp.dot(hidden, w_second, preferred_element_type=jnp.float32).astype(jnp.bfloat16)
    return (pre_act, hidden, embedded)


def weight_terms(features, pre_act, hidden, grads, w_second):
    grad_second = lax.dot_general(
        hidden, grads, (((0,), (0,)), ((), ())), preferred_element_type=jnp.float32
    )
    back_act = lax.dot_general(
        grads, w_second, (((1,), (1,)), ((), ())), preferred_element_type=jnp.float32
    )
    pull_back = jax.vjp(gelu_tanh, pre_act)[1]
    pre_grad = pull_back(back_act)[0].astype(jnp.bfloat16)
    grad_first = lax.dot_general(
        features, pre_grad, (((0,), (0,)), ((), ())), preferred_element_type=jnp.float32
    )
    return (grad_first, grad_second)


def body(query_features, passage_features, counts, positives, w_first, w_second):
    device_count = lax.axis_size(DP)
    my_index = lax.axis_index(DP)
    stride = device_count // 16
    high_bits = stride.bit_length() - 1
    capacity = query_features.shape[0]
    base_rows = capacity // 2
    unit_rows = base_rows // 16
    block_rows = base_rows + unit_rows
    spare_units = 15
    pair_count = block_rows * device_count
    score_scale = 2.5 * w_second.shape[1] ** (-0.5)
    devices = jnp.arange(device_count, dtype=jnp.int32)
    group_of = devices % stride
    group_place = devices // stride
    heavy_dev = (counts > base_rows).astype(jnp.int32)
    light_dev = 1 - heavy_dev
    same_mat = group_of[:, None] == group_of[None, :]
    earlier = same_mat & (group_place[None, :] < group_place[:, None]) & (light_dev[None, :] == 1)
    piece_slot = jnp.sum(earlier.astype(jnp.int32), axis=1)
    source = jnp.sum(jnp.where(same_mat & (heavy_dev[None, :] == 1), devices[None, :], 0), axis=1)
    my_heavy = jnp.sum(jnp.where(devices == my_index, heavy_dev, 0))
    my_group = my_index % stride
    group_pos = my_index // stride
    same_group = group_of == my_group
    heavy_pos = jnp.sum(jnp.where(same_group & (heavy_dev == 1), group_place, 0))
    relative = jnp.bitwise_xor(group_pos, heavy_pos)
    slot_ids = jnp.arange(16, dtype=jnp.int32)
    slot_dest = my_group + jnp.bitwise_xor(heavy_pos, slot_ids) * stride
    slot_piece = jnp.take(piece_slot, slot_dest)

    def keep_tail(row_data, arrived):
        tail_rows = jnp.where(my_heavy == 1, row_data[base_rows:block_rows], arrived)
        return jnp.concatenate([row_data[:base_rows], tail_rows], axis=0)

    all_pos = whole_of(positives, DP, (0, 1, 2, 3), 0)
    within = jnp.arange(block_rows, dtype=jnp.int32)
    moved_rows = (within[None, :] >= base_rows) & (heavy_dev[:, None] == 0)
    slot_grid = jnp.where(
        moved_rows,
        source[:, None] * capacity
        + block_rows
        + piece_slot[:, None] * unit_rows
        + (within[None, :] - base_rows),
        devices[:, None] * capacity + within[None, :],
    ).reshape(-1)
    anchor = jnp.take(all_pos, slot_grid)
    offsets = jnp.cumsum(counts) - counts
    inside = (offsets[None, :] <= anchor[:, None]) & (anchor[:, None] < (offsets + counts)[None, :])
    owner_dev = jnp.sum(jnp.where(inside, devices[None, :], 0), axis=1)
    owner_start = jnp.sum(jnp.where(inside, offsets[None, :], 0), axis=1)
    owner_group = owner_dev % stride
    offset_row = anchor - owner_start
    beyond = jnp.maximum(offset_row - block_rows, 0)
    unit_ids = beyond // unit_rows
    target_hit = (
        (light_dev[None, :] == 1)
        & (group_of[None, :] == owner_group[:, None])
        & (piece_slot[None, :] == unit_ids[:, None])
    )
    target = jnp.sum(jnp.where(target_hit, devices[None, :], 0), axis=1)
    new_pos = jnp.where(
        offset_row < block_rows,
        owner_dev * block_rows + offset_row,
        target * block_rows + base_rows + beyond % unit_rows,
    )
    stacked = jnp.stack((query_features, passage_features))
    width = stacked.shape[2]
    overflow = stacked[:, block_rows:].reshape(2, spare_units, unit_rows, width)
    held = jnp.take(overflow, slot_piece, axis=1)
    held = jnp.where((slot_ids > 0)[None, :, None, None], held, jnp.zeros((), held.dtype))
    for bit in range(4):
        halves = held.reshape(2, held.shape[1] // 2, 2, unit_rows, width)
        arrived = from_partner(halves[:, :, 1], DP, high_bits + bit)
        taker = jnp.bitwise_and(jnp.right_shift(relative, bit), 1) == 1
        held = jnp.where(taker, arrived, halves[:, :, 0])
    arrived_rows = held[:, 0]
    rows_query = keep_tail(query_features, arrived_rows[0])
    rows_passage = keep_tail(passage_features, arrived_rows[1])
    pre_query, hidden_query, emb_query = tower_pass(rows_query, w_first, w_second)
    pre_passage, hidden_passage, emb_passage = tower_pass(rows_passage, w_first, w_second)
    all_queries, all_passages = sent_together((emb_query, emb_passage), DP, 0, 1)
    columns = jnp.arange(pair_count, dtype=jnp.int32)
    own_pos = lax.dynamic_slice_in_dim(new_pos, my_index * block_rows, block_rows, 0)
    scores = (
        lax.dot_general(
            emb_query, all_passages, (((1,), (1,)), ((), ())), preferred_element_type=jnp.float32
        )
        * score_scale
    )
    row_top = jnp.max(scores, axis=1)
    log_norm = row_top + jnp.log(jnp.sum(jnp.exp(scores - row_top[:, None]), axis=1))
    is_positive = own_pos[:, None] == columns[None, :]
    pos_score = jnp.sum(jnp.where(is_positive, scores, jnp.zeros_like(scores)), axis=1)
    weights = (jnp.exp(scores - log_norm[:, None]) - is_positive.astype(jnp.float32)).astype(
        jnp.bfloat16
    )
    query_grads = (
        score_scale * jnp.dot(weights, all_passages, preferred_element_type=jnp.float32)
    ).astype(jnp.bfloat16)
    all_norm, all_score = gather_together((log_norm, pos_score), DP, (0, 0))
    mean_loss = jnp.sum(all_norm - all_score) / pair_count
    own_columns = my_index * block_rows + within
    scores_back = (
        lax.dot_general(
            emb_passage, all_queries, (((1,), (1,)), ((), ())), preferred_element_type=jnp.float32
        )
        * score_scale
    )
    is_target = new_pos[None, :] == own_columns[:, None]
    weights_back = (
        jnp.exp(scores_back - all_norm[None, :]) - is_target.astype(jnp.float32)
    ).astype(jnp.bfloat16)
    passage_grads = (
        score_scale * jnp.dot(weights_back, all_queries, preferred_element_type=jnp.float32)
    ).astype(jnp.bfloat16)
    act_query, hid_query, unused_query = tower_pass(rows_query, w_first, w_second)
    act_passage, hid_passage, unused_passage = tower_pass(rows_passage, w_first, w_second)
    first_query, second_query = weight_terms(
        rows_query, act_query, hid_query, query_grads, w_second
    )
    first_passage, second_passage = weight_terms(
        rows_passage, act_passage, hid_passage, passage_grads, w_second
    )
    grad_first, grad_second = (
        summed_rows(first_query + first_passage, ("dp_0", "dp_1", "dp_2"), "dp_3", 1),
        summed_rows(second_query + second_passage, ("dp_0", "dp_1", "dp_2"), "dp_3", 0),
    )
    return (mean_loss, grad_first, grad_second)


def solution(mesh):
    finer = Mesh(mesh.devices.reshape(4, 4, 4, 2), ("dp_0", "dp_1", "dp_2", "dp_3"))
    placed = (P(DP, None), P(DP, None), P(), P(DP), P(), P())
    return jax.shard_map(
        body,
        mesh=finer,
        in_specs=placed,
        out_specs=(P(), P(None, DP), P(DP, None)),
        check_vma=False,
    )
```

profile of v0, /device:TPU:0, one launch (start us, length us, event | category | flops | bytes accessed | tf_op | source)
XLA Modules:
  0.0 809.6 jit_solution(3271207705943306324)
XLA Ops:
  19.0 4.2 collective-permute-done
  23.3 3.8 collective-permute-start.1
  33.9 3.1 collective-permute-start.3
  48.8 8.7 %all-gather.2 = s32[4,1,256]{2,1,0:T(1,128)S(1)} all-gather(s32[1,1,256]{2,1,0:T(1,128)S(1)} %bitcast.114), channel_id=2, replica_groups=mesh['dp_0'=4,'dp_1'=4,'dp_2'=4,'dp_3'=2] {'dp_0'}, dimensions={0}, use_global_device_ids=true | all-gather | bytes 5120 | tf_op jit(solution)/shard_map/all_gather | solution.py:29
  57.5 12.9 %all-gather.3 = s32[4,4,256]{2,1,0:T(4,128)S(1)} all-gather(s32[1,4,256]{2,1,0:T(4,128)S(1)} %copy.73), channel_id=1, replica_groups=mesh['dp_0'=4,'dp_1'=4,'dp_2'=4,'dp_3'=2] {'dp_1'}, dimensions={0}, use_global_device_ids=true | all-gather | bytes 20480 | tf_op jit(solution)/shard_map/all_gather | solution.py:29
  70.4 12.4 %all_gather.24 = s32[64,256]{1,0:T(8,128)S(1)} all-gather(s32[16,256]{1,0:T(8,128)S(1)} %reshape.489), channel_id=1, replica_groups=mesh['dp_0'=4,'dp_1'=4,'dp_2'=4,'dp_3'=2] {'dp_2'}, dimensions={0}, use_global_device_ids=true | all-gather | bytes 81920 | tf_op jit(solution)/shard_map/all_gather | solution.py:29
  85.2 96.2 %gather_fusion.2 = s32[17408]{0:T(1024)S(1)} fusion(s32[32768]{0:T(1024)S(1)} %bitcast.95, s32[17408]{0:T(1024)S(1)} %broadcast_clamp_fusion), kind=kCustom, calls=%fused_computation.2 | custom fusion | bytes 208896 | tf_op jit(solution)/shard_map/jit(_take)/gather | solution.py:143
  181.4 12.8 %select_reduce_fusion.2 = (s32[17408]{0:T(1024)S(1)}, s32[17408]{0:T(1024)S(1)}) fusion(s32[128]{0:T(128)S(1)} %reduce.1, s32[128]{0:T(128)S(1)} %copy-done.15, s32[17408]{0:T(1024)S(1)} %and_select_fusion), kind=kLoop, calls=%fused_computation.22 | loop fusion | flops 15562752 | bytes 209920 | tf_op jit(solution)/shard_map/reduce_sum | solution.py:146
  194.3 8.6 %select_reduce_fusion.1 = s32[17408]{0:T(1024)S(1)} fusion(s32[128]{0:T(128)S(1)} %get-tuple-element.8, s32[128]{0:T(128)S(1)} %get-tuple-element.20, s32[17408]{0:T(1024)S(1)} %add_select_fusion.2, s32[17408]{0:T(1024)S(1)} %add_select_fusion.3, pred[128]{0:T(512)(128)(4,1)S(1)} %get-tuple-element.16), kind=kLoop, calls=%fused_computation.21 | loop fusion | flops 13351936 | bytes 210048 | tf_op jit(solution)/shard_map/reduce_sum | solution.py:157
  203.0 14.5 %fusion.108 = (f32[136]{0:T(256)S(1)}, f32[136,17408]{1,0:T(8,128)}) fusion(bf16[136,384]{1,0:T(8,128)(2,1)S(1)} %convolution_convert_fusion.1, bf16[17408,768]{1,0:T(8,128)(2,1)} %all-gather.6.cloned.1.call-done), kind=kOutput, calls=%fused_computation.177 | convolution fusion | flops 1822965632 | bytes 22944288 | tf_op jit(solution)/shard_map/dot_general | solution.py:182
  217.5 6.4 exponential_reduce_fusion
  225.0 11.0 %fusion.33 = bf16[136,384]{1,0:T(8,128)(2,1)S(1)} fusion(bf16[17408,768]{1,0:T(8,128)(2,1)} %all-gather.6.cloned.1.call-done, f32[136,17408]{1,0:T(8,128)} %get-tuple-element.18, f32[136]{0:T(256)S(1)} %log_add_fusion, s32[136]{0:T(256)S(1)} %dynamic_slice.3), kind=kOutput, calls=%fused_computation.40 | convolution fusion | flops 1830172672 | bytes 22944832 | tf_op jit(solution)/shard_map/dot_general | solution.py:195
  237.4 128.4 %all-reduce.5.cloned.1.call-done = f32[34816]{0:T(1024)} async-done(((f32[34816]{0:T(1024)}), f32[34816]{0:T(1024)}) %all-reduce.5.cloned.1.call-update) | async-done | bytes 139280
  369.9 13.9 %fusion.28 = bf16[136,384]{1,0:T(8,128)(2,1)S(1)} fusion(bf16[17408,768]{1,0:T(8,128)(2,1)} %all-gather.6.cloned.1.call-done, bf16[136,384]{1,0:T(8,128)(2,1)} %copy-done.13, s32[17408]{0:T(1024)} %copy-done.14, f32[17408]{0:T(1024)} %sub.98, s32[136]{0:T(256)S(1)} %iota_add_fusion), kind=kOutput, calls=%fused_computation.39 | convolution fusion | flops 3650770944 | bytes 27087392 | tf_op jit(solution)/shard_map/dot_general | solution.py:211
  386.0 3.8 reshape_reshape.7
  389.8 4.7 copy.78
  394.9 3.6 fusion.51
  398.5 6.5 convolution_add_fusion
  405.0 6.0 copy.76
  411.0 6.4 reshape.454
  417.4 6.1 copy.77
  424.2 13.9 %reduce-scatter.5.cloned.1.call-done = f32[64,768,12]{1,2,0:T(8,128)} async-done(((f32[128,768,12]{1,2,0:T(8,128)}), f32[64,768,12]{1,2,0:T(8,128)}) %reduce-scatter.5.cloned.1.call-update) | async-done | bytes 2359312 | tf_op jit(solution)/shard_map/reduce_scatter | solution.py:67
  439.4 136.0 %all-reduce.7.cloned.1.call-done = f32[64,12,384]{2,0,1:T(8,128)} async-done(((f32[64,12,384]{2,0,1:T(8,128)}), f32[64,12,384]{2,0,1:T(8,128)}) %all-reduce.7.cloned.1.call-update) | async-done | bytes 1179664
  577.6 224.0 %reduce-scatter.7.cloned.1.call-done = f32[1,768,12]{1,2,0:T(8,128)} async-done(((f32[64,768,12]{1,2,0:T(8,128)}), f32[1,768,12]{1,2,0:T(8,128)}) %reduce-scatter.7.cloned.1.call-update) | async-done | bytes 36880 | tf_op jit(solution)/shard_map/reduce_scatter | solution.py:68
  (123 shorter events, 44.0 us)
Async XLA Ops:
  7.2 34.6 %copy-start = (bf16[768,1536]{1,0:T(8,128)(2,1)S(1)}, bf16[768,1536]{1,0:T(8,128)(2,1)}, u32[]{:S(2)}) copy-start(bf16[768,1536]{1,0:T(8,128)(2,1)} %param.10) | copy-start | bytes 7077892
  7.2 195.8 %all-gather.6.cloned.1.call-start = ((), (), s32[]{:S(2)}) async-start(), calls=%async_computation.3 | async-start | bytes 26947584 | tf_op jit(solution)/shard_map/all_gather | solution.py:43
  16.1 32.7 %copy-start.16 = (s32[256]{0:T(256)S(1)}, s32[256]{0:T(256)}, u32[]{:S(2)}) copy-start(s32[256]{0:T(256)} %param.9) | copy-start | bytes 3076
  16.2 7.0 collective-permute-start
  23.3 6.4 collective-permute-start.1
  29.7 4.2 collective-permute-start.2
  33.9 6.3 collective-permute-start.3
  41.7 139.6 %copy-start.11 = (bf16[8,768]{1,0:T(8,128)(2,1)}, bf16[8,768]{1,0:T(8,128)(2,1)S(1)}, u32[]{:S(2)}) copy-start(bf16[8,768]{1,0:T(8,128)(2,1)S(1)} %fusion.80) | copy-start | bytes 36868
  44.0 137.4 %copy-start.13 = (bf16[136,384]{1,0:T(8,128)(2,1)}, bf16[136,384]{1,0:T(8,128)(2,1)S(1)}, u32[]{:S(2)}) copy-start(bf16[136,384]{1,0:T(8,128)(2,1)S(1)} %convolution_convert_fusion) | copy-start | bytes 313348
  47.6 318.2 %all-reduce.5.cloned.1.call-start = ((), (), s32[]{:S(2)}) async-start(), calls=%async_computation.7 | async-start | bytes 278528
  85.2 96.2 %copy-start.15 = (s32[128]{0:T(128)S(1)}, s32[128]{0:T(128)}, u32[]{:S(2)}) copy-start(s32[128]{0:T(128)} %get-tuple-element.13) | copy-start | bytes 1540
  202.9 14.6 %copy-start.14 = (s32[17408]{0:T(1024)}, s32[17408]{0:T(1024)S(1)}, u32[]{:S(2)}) copy-start(s32[17408]{0:T(1024)S(1)} %fusion.73) | copy-start | bytes 208900
  224.7 198.9 %reduce-scatter.9.cloned.1.call-start = ((), (), s32[]{:S(2)}) async-start(), calls=%async_computation.6 | async-start | bytes 3538944 | tf_op jit(solution)/shard_map/reduce_scatter | solution.py:67
  225.0 11.7 %copy-start.3 = (f32[136,1536]{1,0:T(8,128)S(1)}, f32[136,1536]{1,0:T(8,128)}, u32[]{:S(2)}) copy-start(f32[136,1536]{1,0:T(8,128)} %copy-done.2) | copy-start | bytes 2506756
  383.8 11.0 %copy-start.12 = (bf16[8,768]{1,0:T(8,128)(2,1)S(1)}, bf16[8,768]{1,0:T(8,128)(2,1)}, u32[]{:S(2)}) copy-start(bf16[8,768]{1,0:T(8,128)(2,1)} %copy-done.11) | copy-start | bytes 36868
  386.0 8.9 %copy-start.4 = (f32[136,1536]{1,0:T(8,128)S(1)}, f32[136,1536]{1,0:T(8,128)}, u32[]{:S(2)}) copy-start(f32[136,1536]{1,0:T(8,128)} %copy-done.2) | copy-start | bytes 2506756
  386.0 8.9 %copy-start.6 = (bf16[1536,384]{1,0:T(8,128)(2,1)S(1)}, bf16[1536,384]{1,0:T(8,128)(2,1)}, u32[]{:S(2)}) copy-start(bf16[1536,384]{1,0:T(8,128)(2,1)} %param.11) | copy-start | bytes 3538948
  386.0 8.9 %copy-start.7 = (bf16[128,768]{1,0:T(8,128)(2,1)S(1)}, bf16[128,768]{1,0:T(8,128)(2,1)}, u32[]{:S(2)}) copy-start(bf16[128,768]{1,0:T(8,128)(2,1)} %slice.53) | copy-start | bytes 589828
  386.0 8.9 %copy-start.10 = (bf16[136,384]{1,0:T(8,128)(2,1)S(1)}, bf16[136,384]{1,0:T(8,128)(2,1)}, u32[]{:S(2)}) copy-start(bf16[136,384]{1,0:T(8,128)(2,1)} %copy-done.9) | copy-start | bytes 313348
  394.5 43.6 %reduce-scatter.5.cloned.1.call-start = ((), (), s32[]{:S(2)}) async-start(), calls=%async_computation.4 | async-start | bytes 9437184 | tf_op jit(solution)/shard_map/reduce_scatter | solution.py:67
  417.4 384.2 %copy-start.1 = (bf16[768,1536]{1,0:T(8,128)(2,1)S(1)}, bf16[768,1536]{1,0:T(8,128)(2,1)}, u32[]{:S(2)}) copy-start(bf16[768,1536]{1,0:T(8,128)(2,1)} %param.10) | copy-start | bytes 7077892
  417.4 20.8 %copy-start.17 = (u32[128]{0:T(128)S(1)}, u32[128]{0:T(128)}, u32[]{:S(2)}) copy-start(u32[128]{0:T(128)} %constant.209) | copy-start | bytes 1540
  423.6 151.8 %all-reduce.7.cloned.1.call-start = ((), (), s32[]{:S(2)}) async-start(), calls=%async_computation.8 | async-start | bytes 2359296
  424.2 377.5 %reduce-scatter.7.cloned.1.call-start = ((), (), s32[]{:S(2)}) async-start(), calls=%async_computation.5 | async-start | bytes 3194880 | tf_op jit(solution)/shard_map/reduce_scatter | solution.py:68
  (4 other events, 8.4 us)
Sparse Core Ops, SparseCore 0:
  47.7 96.5 all-gather.5
  224.8 140.8 all-reduce.4
  394.7 9.7 reduce-scatter.8
  423.7 14.3 reduce-scatter.4
  442.7 132.6 all-reduce.6
  580.3 221.3 reduce-scatter.6
where the time goes:
time: 811 us; the launch traced here: 810 us
  waiting for transfers between devices  512 us (63%)
  local copies, waits for them, and re-layouts  136 us (17%)
  matrix products  56.5 us (7%)
  other arithmetic  39.7 us (5%)
  blocking collectives  36.1 us (4%)
  between operations  17.7 us (2%)
  starting transfers between devices  11.3 us (1%)
    unnamed x8, waiting for transfers between devices  265 us
    reduce_scatter x1, waiting for transfers between devices, summed_rows(): return lax.psum_scatter(tiles, chips, scatter_dimension=0, tiled=True)[0]  224 us
    gather x1, local copies, waits for them, and re-layouts, body(): anchor = jnp.take(all_pos, slot_grid)  96.2 us
    all_gather x4, blocking collectives, stacked_from(): tiles = lax.all_gather(tiles, axes[k], axis=0, tiled=True)  36.1 us
  transfers between devices with their start and end apart: 10, of which 7 were waited for; matrix products, arithmetic and copies ran while one was open for 20% of the time, Pallas kernels for 0%

commit v1 on v0

v1 whole, which is shorter than its diff:
```python
import functools

import jax
import jax.numpy as jnp
from jax import lax
from jax.experimental import pallas as pl
from jax.experimental.pallas import tpu as pltpu
from jax.sharding import Mesh
from jax.sharding import PartitionSpec as P

DP = ("dp_0", "dp_1", "dp_2", "dp_3")
PLANE = ("dp_0", "dp_1")
LINE = "dp_2"
CORE = "dp_3"
F32 = jnp.float32
BF16 = jnp.bfloat16

LOW = 128
UNIT = 8
BLOCK = LOW + UNIT
CHUNK = 144
TILE = 256
LOG2E = 1.4426950408889634


def gelu_tanh(values):
    return jax.nn.gelu(values, approximate=True)


def swap_core(x):
    return lax.ppermute(x, CORE, [(0, 1), (1, 0)])


def plane_exchange(x):
    return lax.all_to_all(x, PLANE, 0, 0, tiled=True)


def line_exchange(x):
    return lax.all_to_all(x, (LINE, CORE), 0, 0, tiled=True)


def chip_exchange(x):
    return lax.all_to_all(x, (*PLANE, LINE), 0, 0, tiled=True)


def place_of(pos, sc):
    over = pos - sc[17]
    slot = jnp.bitwise_and(lax.shift_right_logical(over, 3) + sc[16], 15)
    place = jnp.where(
        (over >= 0) & (over < LOW), 16 * LOW + slot * UNIT + jnp.bitwise_and(over, 7), -1
    )
    for s in range(16):
        at = pos - sc[s]
        place = jnp.where((at >= 0) & (at < LOW), at + s * LOW, place)
    return place


def nt_dot(a, b):
    return lax.dot_general(a, b, (((1,), (1,)), ((), ())), preferred_element_type=F32)


def row_tiles(base, tail):
    tiles = [(base, k * TILE, TILE) for k in range(base.shape[0] // TILE)]
    return tiles + [(tail, 0, tail.shape[0])]


def stats_kernel(sc, qb, qt, pb, pt, q_out, turned_out, place_out, stats_out, *, scale):
    blocks = qb.shape[0] // LOW
    codes = []
    spread = None
    for b in range(blocks):
        q_out[b * LOW : (b + 1) * LOW] = qb[b * LOW : (b + 1) * LOW]
        q_out[blocks * LOW + b * UNIT : blocks * LOW + (b + 1) * UNIT] = qt[
            2 * b * UNIT : (2 * b + 1) * UNIT
        ]
        code = qt[(2 * b + 1) * UNIT : (2 * b + 2) * UNIT, :LOW].astype(F32)
        codes.append(code[0:1] * 128.0 + code[1:2])
        part = code[2:3] * 128.0 + code[3:4]
        spread = part if spread is None else spread + part
    codes.append(spread[:, : blocks * UNIT])
    place_out[...] = place_of(jnp.concatenate(codes, axis=1).astype(jnp.int32), sc)
    rows = q_out.shape[0]
    pull = scale * LOG2E
    top = jnp.full((1, rows), -1e30, F32)
    total = jnp.zeros((1, rows), F32)
    found = jnp.zeros((1, rows), F32)
    at = 0
    for ref, first, size in row_tiles(pb, pt):
        tile = ref[first : first + size]
        turned_out[:, at : at + size] = tile.T
        s = nt_dot(tile, q_out[...])
        row = lax.broadcasted_iota(jnp.int32, s.shape, 0)
        found += jnp.sum(jnp.where(row == place_out[...] - at, s, 0.0), axis=0, keepdims=True)
        new_top = jnp.maximum(top, jnp.max(s, axis=0, keepdims=True))
        total = total * jnp.exp2((top - new_top) * pull) + jnp.sum(
            jnp.exp2(s * pull - new_top * pull), axis=0, keepdims=True
        )
        top = new_top
        at += size
    line = lax.broadcasted_iota(jnp.int32, (8, rows), 0)
    stats = jnp.where(line == 0, top, jnp.where(line == 1, total, jnp.where(line == 2, found, 0.0)))
    for b in range(blocks):
        stats_out[b * 8 : (b + 1) * 8] = stats


def grads_kernel(stats, q, pb, pt, turned, place, dp_out, dq_out, g_ref, *, scale):
    blocks = dq_out.shape[0] // CHUNK
    units = dp_out.shape[0] // CHUNK
    rows = q.shape[0]
    width = q.shape[1]
    pull = scale * LOG2E
    tops = [stats[b * 8 : b * 8 + 1] for b in range(blocks)]
    top = functools.reduce(jnp.maximum, tops)
    total = jnp.zeros((1, rows), F32)
    found = jnp.zeros((1, rows), F32)
    for b in range(blocks):
        total += stats[b * 8 + 1 : b * 8 + 2] * jnp.exp2((tops[b] - top) * pull)
        found += stats[b * 8 + 2 : b * 8 + 3]
    norm = top * scale + jnp.log(total)
    loss = jnp.sum(norm - found * scale, axis=1, keepdims=True)
    norm = norm * LOG2E
    loss_high = loss.astype(BF16).astype(F32)
    loss_mid = (loss - loss_high).astype(BF16).astype(F32)
    loss_low = loss - loss_high - loss_mid
    line = lax.broadcasted_iota(jnp.int32, (UNIT, width), 0)
    loss_tile = jnp.where(
        line == 0,
        loss_high,
        jnp.where(line == 1, loss_mid, jnp.where(line == 2, loss_low, 0.0)),
    ).astype(BF16)
    at = 0
    for ref, first, size in row_tiles(pb, pt):
        s = nt_dot(ref[first : first + size], q[...])
        row = lax.broadcasted_iota(jnp.int32, s.shape, 0)
        e = jnp.exp2(s * pull - norm)
        g_ref[at : at + size] = jnp.where(row == place[...] - at, e - 1.0, e).astype(BF16)
        at += size
    for k in range(units * LOW // TILE):
        dp = scale * jnp.dot(g_ref[k * TILE : (k + 1) * TILE], q[...], preferred_element_type=F32)
        dp = dp.astype(BF16)
        for half in range(TILE // LOW):
            to = (k * (TILE // LOW) + half) * CHUNK
            dp_out[to : to + LOW] = dp[half * LOW : (half + 1) * LOW]
    dp = scale * jnp.dot(g_ref[units * LOW :], q[...], preferred_element_type=F32)
    dp = dp.astype(BF16)
    for k in range(units):
        dp_out[k * CHUNK + LOW : k * CHUNK + BLOCK] = dp[k * UNIT : (k + 1) * UNIT]
        dp_out[k * CHUNK + BLOCK : (k + 1) * CHUNK] = loss_tile
    for k in range(blocks * LOW // TILE):
        dq = jnp.dot(
            turned[...], g_ref[:, k * TILE : (k + 1) * TILE], preferred_element_type=F32
        )
        dq = (scale * dq).T.astype(BF16)
        for half in range(TILE // LOW):
            to = (k * (TILE // LOW) + half) * CHUNK
            dq_out[to : to + LOW] = dq[half * LOW : (half + 1) * LOW]
    dq = jnp.dot(turned[...], g_ref[:, blocks * LOW :], preferred_element_type=F32)
    dq = (scale * dq).T.astype(BF16)
    for k in range(blocks):
        dq_out[k * CHUNK + LOW : k * CHUNK + BLOCK] = dq[k * UNIT : (k + 1) * UNIT]
        dq_out[k * CHUNK + BLOCK : (k + 1) * CHUNK] = jnp.zeros((CHUNK - BLOCK, width), BF16)


def weights_kernel(de_q, de_q_other, de_p, de_p_other, rows, hidden, slope, second, out, de):
    for k, part in enumerate((de_q, de_q_other, de_p, de_p_other)):
        de[k * BLOCK : (k + 1) * BLOCK] = part[...]
    many = out.shape[0]
    wide = rows.shape[1] + de.shape[1]
    for first in range(0, hidden.shape[0], TILE):
        span = slice(first, first + TILE)
        grad_second = jnp.dot(hidden[span], de[...], preferred_element_type=F32)
        back = nt_dot(second[span], de[...])
        dpre = (slope[span] * back).astype(BF16)
        grad_first = jnp.dot(dpre, rows[...], preferred_element_type=F32)
        if first < many:
            out[span, : rows.shape[1]] = grad_first.astype(BF16)
            out[span, rows.shape[1] : wide] = grad_second.astype(BF16)
        else:
            x = jnp.concatenate(
                [grad_first, grad_second, jnp.zeros((TILE, 128), F32)], axis=1
            )
            near, far = x[:, :640], x[:, 640:]
            line = jnp.bitwise_and(lax.broadcasted_iota(jnp.int32, near.shape, 0), 7)
            even = jnp.where(line < 4, near, pltpu.roll(far, 4, 0)).astype(BF16)
            odd = jnp.where(line < 4, pltpu.roll(near, TILE - 4, 0), far).astype(BF16)
            for b in range(TILE // 8):
                to = (first - many) * 2 + b * 16
                out[to : to + 8, wide:] = even[b * 8 : (b + 1) * 8]
                out[to + 8 : to + 16, wide:] = odd[b * 8 : (b + 1) * 8]


def score_stats(sc, qb, qt, pb, pt, scale):
    blocks = qb.shape[0] // LOW
    rows = blocks * BLOCK
    columns = pb.shape[0] + pt.shape[0]
    width = qb.shape[1]
    vmem = pl.BlockSpec(memory_space=pltpu.VMEM)
    return pl.pallas_call(
        functools.partial(stats_kernel, scale=scale),
        in_specs=[pl.BlockSpec(memory_space=pltpu.SMEM)] + [vmem] * 4,
        out_specs=[vmem] * 4,
        out_shape=[
            jax.ShapeDtypeStruct((rows, width), BF16),
            jax.ShapeDtypeStruct((width, columns), BF16),
            jax.ShapeDtypeStruct((1, rows), jnp.int32),
            jax.ShapeDtypeStruct((8 * blocks, rows), F32),
        ],
        name="score_stats",
    )(sc, qb, qt, pb, pt)


def score_grads(stats, q, pb, pt, turned, place, scale):
    rows, width = q.shape
    columns = pb.shape[0] + pt.shape[0]
    vmem = pl.BlockSpec(memory_space=pltpu.VMEM)
    return pl.pallas_call(
        functools.partial(grads_kernel, scale=scale),
        in_specs=[vmem] * 6,
        out_specs=[vmem] * 2,
        out_shape=[
            jax.ShapeDtypeStruct((columns // BLOCK * CHUNK, width), BF16),
            jax.ShapeDtypeStruct((rows // BLOCK * CHUNK, width), BF16),
        ],
        scratch_shapes=[pltpu.VMEM((columns, rows), BF16)],
        name="score_grads",
    )(stats, q, pb, pt, turned, place)


def weight_grads(de_parts, rows, hidden, slope, second):
    vmem = pl.BlockSpec(memory_space=pltpu.VMEM)
    return pl.pallas_call(
        weights_kernel,
        in_specs=[vmem] * 8,
        out_specs=vmem,
        out_shape=jax.ShapeDtypeStruct((512, 1792), BF16),
        scratch_shapes=[pltpu.VMEM((4 * BLOCK, second.shape[1]), BF16)],
        name="weight_grads",
    )(*de_parts, rows, hidden, slope, second)


def body(query_features, passage_features, counts, positives, w_first, w_second):
    width = query_features.shape[1]
    hidden_width, emb_width = w_second.shape
    scale = 2.5 * emb_width ** (-0.5)
    group = lax.axis_index((LINE, CORE))
    core = lax.axis_index(CORE)
    pairs = BLOCK * lax.axis_size(DP)

    heavy = (counts > LOW).astype(jnp.int32)
    offsets = jnp.cumsum(counts) - counts
    devices = jnp.arange(counts.shape[0], dtype=jnp.int32)
    mine = heavy * (devices % 8 == group)
    heavy_at = jnp.sum(mine * (devices // 8))
    over_start = jnp.sum(mine * offsets) + LOW
    group_start = lax.dynamic_slice_in_dim(offsets.reshape(16, 8), group, 1, 1)[:, 0]
    sc = jnp.concatenate([group_start, heavy_at[None], over_start[None]]).astype(jnp.int32)

    pos_high = jnp.right_shift(positives, 7).astype(BF16)
    pos_low = jnp.bitwise_and(positives, 127).astype(BF16)
    lane = jnp.arange(LOW, dtype=jnp.int32)
    line = jnp.arange(UNIT, dtype=jnp.int32)[None, :, None]
    at_group = (lane // UNIT == group)[None, None, :]
    spread_high = jnp.tile(pos_high[LOW:].reshape(16, 1, UNIT), (1, 1, 16))
    spread_low = jnp.tile(pos_low[LOW:].reshape(16, 1, UNIT), (1, 1, 16))
    coded = jnp.where(
        at_group & (line == 2),
        spread_high,
        jnp.where(at_group & (line == 3), spread_low, jnp.zeros((), BF16)),
    ).reshape(LOW, LOW)
    over = jnp.concatenate([query_features[LOW:], passage_features[LOW:], coded], axis=1)
    over = jnp.concatenate([over, over], axis=0)
    over = lax.dynamic_slice_in_dim(over, (16 - heavy_at) * UNIT, LOW, 0)
    arrived = plane_exchange(over)
    tail = lax.dynamic_slice_in_dim(arrived, heavy_at * UNIT, UNIT, 0)

    def tower(x):
        pre = jnp.dot(x, w_first, preferred_element_type=F32)
        hidden = gelu_tanh(pre).astype(BF16)
        return jnp.dot(hidden, w_second, preferred_element_type=F32).astype(BF16)

    base = tower(jnp.concatenate([query_features[:LOW], passage_features[:LOW]], axis=0))
    pb = plane_exchange(jnp.concatenate([base[LOW:]] * 16, axis=0))
    qb = line_exchange(jnp.concatenate([base[:LOW]] * 8, axis=0))

    tail_q, tail_p = tail[:, :width], tail[:, width : 2 * width]
    tail_emb = tower(jnp.concatenate([tail_q, tail_p], axis=0))
    line = line[0]
    codes = jnp.where(
        line == 0, pos_high[None, :LOW], jnp.where(line == 1, pos_low[None, :LOW], tail[:, 2 * width :])
    )
    codes = jnp.pad(codes, ((0, 0), (0, emb_width - LOW)))
    pt = plane_exchange(jnp.concatenate([tail_emb[UNIT:]] * 16, axis=0))
    qt = line_exchange(jnp.concatenate([tail_emb[:UNIT], codes] * 8, axis=0))

    q_all, turned, place, stats = score_stats(sc, qb, qt, pb, pt, scale)
    stats = line_exchange(stats)
    dp_part, dq_part = score_grads(stats, q_all, pb, pt, turned, place, scale)
    dp_sum = jnp.sum(plane_exchange(dp_part).reshape(16, CHUNK, emb_width).astype(F32), axis=0)
    dq_sum = jnp.sum(line_exchange(dq_part).reshape(8, CHUNK, emb_width).astype(F32), axis=0)
    mean_loss = (dp_sum[BLOCK, 0] + dp_sum[BLOCK + 1, 0] + dp_sum[BLOCK + 2, 0]) / pairs
    de_q = dq_sum[:BLOCK].astype(BF16)
    de_p = dp_sum[:BLOCK].astype(BF16)

    late_core, _ = lax.optimization_barrier((core, base))
    each = hidden_width // lax.axis_size(DP)
    half = hidden_width // 2
    unit = jnp.arange(half, dtype=jnp.int32)
    rest = unit - 512
    unit_of = jnp.where(
        unit < 512,
        (unit // 8) * (2 * each) + unit % 8,
        (rest // 4) * (2 * each) + 8 + rest % 4,
    )
    unit_of = unit_of + late_core * each
    pick = (unit_of[:, None] == jnp.arange(hidden_width, dtype=jnp.int32)[None, :]).astype(BF16)
    first_half = lax.dot_general(
        pick, w_first, (((1,), (1,)), ((), ())), preferred_element_type=F32
    ).astype(BF16)
    second_half = jnp.dot(pick, w_second, preferred_element_type=F32).astype(BF16)
    own = jnp.concatenate(
        [query_features[:LOW], tail_q, passage_features[:LOW], tail_p], axis=0
    )
    other = swap_core(own)
    rows = jnp.concatenate([own[:BLOCK], other[:BLOCK], own[BLOCK:], other[BLOCK:]], axis=0)
    pre_half = lax.dot_general(
        first_half, rows, (((1,), (1,)), ((), ())), preferred_element_type=F32
    )
    act, pull_back = jax.vjp(gelu_tanh, pre_half)
    hidden = act.astype(BF16)
    slope = pull_back(jnp.ones_like(pre_half))[0]

    grads = weight_grads(
        (de_q, swap_core(de_q), de_p, swap_core(de_p)), rows, hidden, slope, second_half
    )
    out = jnp.sum(chip_exchange(grads).reshape(64, 8, -1).astype(F32), axis=0)
    wide = width + emb_width
    tail_out = jnp.concatenate([out[:4, wide:], out[4:, wide : 2 * wide - 640]], axis=1)
    out = jnp.concatenate([out[:, :wide], tail_out], axis=0)
    return (mean_loss, out[:, :width].T, out[:, width:])


def solution(mesh):
    finer = Mesh(mesh.devices.reshape(4, 4, 4, 2), DP)
    placed = (P(DP, None), P(DP, None), P(), P(DP), P(), P())
    return jax.shard_map(
        body,
        mesh=finer,
        in_specs=placed,
        out_specs=(P(), P(None, DP), P(DP, None)),
        check_vma=False,
    )
```

time: 811 us -> 246 us (0.30)
  waiting for transfers between devices: 512 us -> 77.4 us
  local copies, waits for them, and re-layouts: 136 us -> 37.7 us
  matrix products: 56.5 us -> 14.6 us
  starting transfers between devices: 11.3 us -> 38.5 us
  Pallas kernels: 0 us -> 25 us
  other arithmetic: 39.7 us -> 17.6 us
  between operations: 17.7 us -> 6 us
    unnamed x8 -> x0, waiting for transfers between devices: 265 us -> none
    reduce_scatter x3 -> x0, waiting for transfers between devices: 238 us -> none  [the longest x1 224 us: summed_rows(): return lax.psum_scatter(tiles, chips, scatter_dimension=0, tiled=True)[0]]
    gather x5 -> x0, local copies, waits for them, and re-layouts: 97.5 us -> none  [the longest x1 96.2 us: body(): anchor = jnp.take(all_pos, slot_grid)]
    all_to_all x0 -> x7, waiting for transfers between devices: none -> 77.4 us  [the longest x4 34.8 us: plane_exchange(): return lax.all_to_all(x, PLANE, 0, 0, tiled=True)]
    dot_general x11 -> x4, matrix products: 56.5 us -> 14.6 us  [the longest x1 6.6 us: body(): lax.dot_general(first_half, rows, (((1,), (1,)), ((), ())), preferred_ele...]
    all_to_all x0 -> x7, starting transfers between devices: none -> 37.9 us  [the longest x4 24.3 us: plane_exchange(): return lax.all_to_all(x, PLANE, 0, 0, tiled=True)]
    all_gather x4 -> x0, blocking collectives: 36.1 us -> none  [stacked_from(): tiles = lax.all_gather(tiles, axes[k], axis=0, tiled=True)]
    all_to_all x0 -> x2, blocking collectives: none -> 28.1 us  [line_exchange(): return lax.all_to_all(x, (LINE, CORE), 0, 0, tiled=True)]
  transfers between devices with their start and end apart: 10 -> 10, of which waited for: 7 -> 6; matrix products, arithmetic and copies ran while one was open for 20% -> 18% of each run, Pallas kernels for 0% -> 0%
where the time goes in v1:
time: 246 us; the launch traced here: 245 us
  waiting for transfers between devices  77.4 us (31%)
  starting transfers between devices  38.5 us (16%)
  local copies, waits for them, and re-layouts  37.7 us (15%)
  blocking collectives  28.1 us (11%)
  Pallas kernels  25 us (10%)
  other arithmetic  17.6 us (7%)
  matrix products  14.6 us (6%)
  between operations  6 us (2%)
    all_to_all x4, waiting for transfers between devices, plane_exchange(): return lax.all_to_all(x, PLANE, 0, 0, tiled=True)  34.8 us
    all_to_all x2, blocking collectives, line_exchange(): return lax.all_to_all(x, (LINE, CORE), 0, 0, tiled=True)  28.1 us
    unnamed x89, local copies, waits for them, and re-layouts  25.8 us
    all_to_all x1, waiting for transfers between devices, chip_exchange(): return lax.all_to_all(x, (*PLANE, LINE), 0, 0, tiled=True)  24.9 us
    all_to_all x4, starting transfers between devices, plane_exchange(): return lax.all_to_all(x, PLANE, 0, 0, tiled=True)  24.3 us
    all_to_all x2, waiting for transfers between devices, line_exchange(): return lax.all_to_all(x, (LINE, CORE), 0, 0, tiled=True)  17.7 us
    pallas_call x1, Pallas kernels, score_grads(): pl.pallas_call(functools.partial(grads_kernel, scale=scale), in_specs=[vm...  11.6 us
    all_to_all x2, starting transfers between devices, line_exchange(): return lax.all_to_all(x, (LINE, CORE), 0, 0, tiled=True)  8.14 us
  transfers between devices with their start and end apart: 10, of which 6 were waited for; matrix products, arithmetic and copies ran while one was open for 18% of the time, Pallas kernels for 0%

profile of v1, /device:TPU:0, one launch (start us, length us, event | category | flops | bytes accessed | tf_op | source)
XLA Modules:
  0.0 245.0 jit_solution(5922330751841078415)
XLA Ops:
  9.7 8.0 %all-to-all-start.1 = ((bf16[16,8,1664]{2,1,0:T(8,128)(2,1)}), bf16[16,8,1664]{2,1,0:T(8,128)(2,1)}, u32[]{:S(2)}, u32[]{:S(2)}) async-start(bf16[16,8,1664]{2,1,0:T(8,128)(2,1)} %fusion.24), calls=%async_computation.1 | async-start | bytes 851968 | tf_op jit(solution)/shard_map/all_to_all | solution.py:35
  17.8 2.6 %convolution_convert_fusion = bf16[256,384]{1,0:T(8,128)(2,1)S(1)} fusion(bf16[1536,384]{1,0:T(8,128)(2,1)} %param.11, bf16[768,1536]{1,0:T(8,128)(2,1)S(1)} %copy-done, bf16[128,768]{1,0:T(8,128)(2,1)S(1)} %get-tuple-element.47, bf16[128,768]{1,0:T(8,128)(2,1)S(1)} %get-tuple-element.27), kind=kOutput, calls=%fused_computation.23 | convolution fusion | flops 910393344 | bytes 4128768 | tf_op jit(solution)/shard_map/dot_general | solution.py:279
  45.7 4.4 %all-to-all-start.2 = ((bf16[8,16,384]{2,1,0:T(8,128)(2,1)}), bf16[8,16,384]{2,1,0:T(8,128)(2,1)S(1)}, u32[]{:S(2)}, u32[]{:S(2)}) async-start(bf16[8,16,384]{2,1,0:T(8,128)(2,1)} %bitcast.10), calls=%async_computation.2 | async-start | bytes 196608 | tf_op jit(solution)/shard_map/all_to_all | solution.py:39
  50.2 5.8 %all-to-all-done.2 = bf16[8,16,384]{2,1,0:T(8,128)(2,1)S(1)} async-done(((bf16[8,16,384]{2,1,0:T(8,128)(2,1)}), bf16[8,16,384]{2,1,0:T(8,128)(2,1)S(1)}, u32[]{:S(2)}, u32[]{:S(2)}) %all-to-all-start.2) | async-done | bytes 98336 | tf_op jit(solution)/shard_map/all_to_all | solution.py:39
  56.0 7.2 %all-to-all-start.4 = ((bf16[16,8,384]{2,1,0:T(8,128)(2,1)}), bf16[16,8,384]{2,1,0:T(8,128)(2,1)S(1)}, u32[]{:S(2)}, u32[]{:S(2)}) async-start(bf16[16,8,384]{2,1,0:T(8,128)(2,1)} %bitcast.45), calls=%async_computation.4 | async-start | bytes 196608 | tf_op jit(solution)/shard_map/all_to_all | solution.py:35
  63.2 7.7 %all-to-all-done.4 = bf16[16,8,384]{2,1,0:T(8,128)(2,1)S(1)} async-done(((bf16[16,8,384]{2,1,0:T(8,128)(2,1)}), bf16[16,8,384]{2,1,0:T(8,128)(2,1)S(1)}, u32[]{:S(2)}, u32[]{:S(2)}) %all-to-all-start.4) | async-done | bytes 98336 | tf_op jit(solution)/shard_map/all_to_all | solution.py:35
  70.9 16.2 %all_to_all.94 = bf16[8,128,384]{2,1,0:T(8,128)(2,1)} all-to-all(bf16[8,128,384]{2,1,0:T(8,128)(2,1)S(1)} %bitcast.39), channel_id=1, replica_groups=mesh['dp_0'=4,'dp_1'=4,'dp_2'=4,'dp_3'=2] {'dp_2','dp_3'}, dimensions={0} | all-to-all | bytes 1572864 | tf_op jit(solution)/shard_map/all_to_all | solution.py:39
  87.2 4.4 %all-to-all-start.3 = ((bf16[16,128,384]{2,1,0:T(8,128)(2,1)}), bf16[16,128,384]{2,1,0:T(8,128)(2,1)}, u32[]{:S(2)}, u32[]{:S(2)}) async-start(bf16[16,128,384]{2,1,0:T(8,128)(2,1)} %bitcast.12), calls=%async_computation.3 | async-start | bytes 3145728 | tf_op jit(solution)/shard_map/all_to_all | solution.py:35
  93.6 21.7 %all-to-all-done.3 = bf16[16,128,384]{2,1,0:T(8,128)(2,1)} async-done(((bf16[16,128,384]{2,1,0:T(8,128)(2,1)}), bf16[16,128,384]{2,1,0:T(8,128)(2,1)}, u32[]{:S(2)}, u32[]{:S(2)}) %all-to-all-start.3) | async-done | bytes 1572896 | tf_op jit(solution)/shard_map/all_to_all | solution.py:35
  115.3 7.4 %score_stats.1 = (bf16[1088,384]{1,0:T(8,128)(2,1)}, bf16[384,2176]{1,0:T(8,128)(2,1)}, s32[1,1088]{1,0:T(1,128)}, f32[64,1088]{1,0:T(8,128)}) custom-call(s32[18]{0:T(128)} %pad_add_fusion.sc, bf16[1024,384]{1,0:T(8,128)(2,1)} %bitcast.36, bf16[128,384]{1,0:T(8,128)(2,1)} %bitcast.43, bf16[2048,384]{1,0:T(8,128)(2,1)} %bitcast.13.pb, bf16[128,384]{1,0:T(8,128)(2,1)} %bitcast.40), custom_call_target="tpu_custom_call" | custom-call | tf_op jit(solution)/shard_map/score_stats/pallas_call | solution.py:198
  122.7 11.9 %all_to_all.95 = f32[8,8,1088]{2,1,0:T(8,128)} all-to-all(f32[8,8,1088]{2,1,0:T(8,128)} %bitcast.44), channel_id=1, replica_groups=mesh['dp_0'=4,'dp_1'=4,'dp_2'=4,'dp_3'=2] {'dp_2','dp_3'}, dimensions={0} | all-to-all | bytes 557056 | tf_op jit(solution)/shard_map/all_to_all | solution.py:39
  134.6 11.6 %score_grads.1 = (bf16[2304,384]{1,0:T(8,128)(2,1)}, bf16[1152,384]{1,0:T(8,128)(2,1)}) custom-call(f32[64,1088]{1,0:T(8,128)} %bitcast.38, bf16[1088,384]{1,0:T(8,128)(2,1)} %get-tuple-element.11.q, bf16[2048,384]{1,0:T(8,128)(2,1)} %bitcast.13.pb, bf16[128,384]{1,0:T(8,128)(2,1)} %bitcast.41, bf16[384,2176]{1,0:T(8,128)(2,1)} %get-tuple-element.12.turned, ...), custom_call_target="tpu_custom_call" | custom-call | tf_op jit(solution)/shard_map/score_grads/pallas_call | solution.py:216
  146.2 3.7 %all-to-all-start.7 = ((bf16[8,144,384]{2,1,0:T(8,128)(2,1)}), bf16[8,144,384]{2,1,0:T(8,128)(2,1)S(1)}, u32[]{:S(2)}, u32[]{:S(2)}) async-start(bf16[8,144,384]{2,1,0:T(8,128)(2,1)} %bitcast.42), calls=%async_computation.7 | async-start | bytes 1769472 | tf_op jit(solution)/shard_map/all_to_all | solution.py:39
  152.1 11.9 %all-to-all-done.7 = bf16[8,144,384]{2,1,0:T(8,128)(2,1)S(1)} async-done(((bf16[8,144,384]{2,1,0:T(8,128)(2,1)}), bf16[8,144,384]{2,1,0:T(8,128)(2,1)S(1)}, u32[]{:S(2)}, u32[]{:S(2)}) %all-to-all-start.7) | async-done | bytes 884768 | tf_op jit(solution)/shard_map/all_to_all | solution.py:39
  164.0 4.6 %all-to-all-start.6 = ((bf16[16,144,384]{2,1,0:T(8,128)(2,1)}), bf16[16,144,384]{2,1,0:T(8,128)(2,1)}, u32[]{:S(2)}, u32[]{:S(2)}) async-start(bf16[16,144,384]{2,1,0:T(8,128)(2,1)} %bitcast.37), calls=%async_computation.6 | async-start | bytes 3538944 | tf_op jit(solution)/shard_map/all_to_all | solution.py:35
  168.7 3.6 %fusion.15.second = bf16[768,384]{1,0:T(8,128)(2,1)} fusion(bf16[1536,384]{1,0:T(8,128)(2,1)} %param.11, s32[768]{0:T(1024)S(1)} %fusion.73), kind=kOutput, calls=%fused_computation.22 | convolution fusion | flops 907444224 | bytes 1772544 | tf_op jit(solution)/shard_map/dot_general | solution.py:319
  176.8 6.6 %fusion.99 = (f32[768,544]{0,1:T(8,128)}, f32[768,544]{0,1:T(8,128)}) fusion(bf16[544,768]{1,0:T(8,128)(2,1)} %slice_dynamic-update-slice_fusion.rows, bf16[768,1536]{1,0:T(8,128)(2,1)S(1)} %copy-done, s32[768]{0:T(1024)S(1)} %fusion.73), kind=kOutput, calls=%fused_computation.201 | convolution fusion | flops 2455855104 | bytes 6540288 | tf_op jit(solution)/shard_map/dot_general | solution.py:325
  183.4 2.8 %copy.32 = f32[768,544]{1,0:T(8,128)} copy(f32[768,544]{0,1:T(8,128)} %get-tuple-element.45) | data formatting | bytes 3342336 | tf_op jit(solution)/shard_map/jvp()/integer_pow | solution.py:27
  186.2 2.8 %copy.35 = f32[768,544]{1,0:T(8,128)} copy(f32[768,544]{0,1:T(8,128)} %get-tuple-element.46) | data formatting | bytes 3342336 | tf_op jit(solution)/shard_map/dot_general | solution.py:325
  189.3 5.4 %all-to-all-done.6 = bf16[16,144,384]{2,1,0:T(8,128)(2,1)} async-done(((bf16[16,144,384]{2,1,0:T(8,128)(2,1)}), bf16[16,144,384]{2,1,0:T(8,128)(2,1)}, u32[]{:S(2)}, u32[]{:S(2)}) %all-to-all-start.6) | async-done | bytes 1769504 | tf_op jit(solution)/shard_map/all_to_all | solution.py:35
  196.8 4.4 %multiply_add_fusion = (f32[768,544]{1,0:T(8,128)}, bf16[768,544]{1,0:T(8,128)(2,1)}) fusion(f32[768,544]{1,0:T(8,128)S(1)} %copy-done.1, f32[768,544]{1,0:T(8,128)} %copy.35), kind=kLoop, calls=%fused_computation.8 | loop fusion | flops 7520256 | bytes 5849088 | tf_op jit(solution)/shard_map/transpose(jvp())/add_any | solution.py:27
  201.9 6.0 %weight_grads.1 = bf16[512,1792]{1,0:T(8,128)(2,1)} custom-call(bf16[136,384]{1,0:T(8,128)(2,1)} %copy-done.7, bf16[136,384]{1,0:T(8,128)(2,1)} %copy-done.15, bf16[136,384]{1,0:T(8,128)(2,1)} %copy-done.8, bf16[136,384]{1,0:T(8,128)(2,1)} %copy-done.16, bf16[544,768]{1,0:T(8,128)(2,1)} %slice_dynamic-update-slice_fusion.rows, ...), custom_call_target="tpu_custom_call" | custom-call | tf_op jit(solution)/shard_map/weight_grads/pallas_call | solution.py:231
  207.9 5.5 %all-to-all-start.8 = ((bf16[64,8,1792]{2,1,0:T(8,128)(2,1)}), bf16[64,8,1792]{2,1,0:T(8,128)(2,1)}, u32[]{:S(2)}, u32[]{:S(2)}) async-start(bf16[64,8,1792]{2,1,0:T(8,128)(2,1)} %bitcast.35), calls=%async_computation.8 | async-start | bytes 3670016 | tf_op jit(solution)/shard_map/all_to_all | solution.py:43
  215.9 24.9 %all-to-all-done.8 = bf16[64,8,1792]{2,1,0:T(8,128)(2,1)} async-done(((bf16[64,8,1792]{2,1,0:T(8,128)(2,1)}), bf16[64,8,1792]{2,1,0:T(8,128)(2,1)}, u32[]{:S(2)}, u32[]{:S(2)}) %all-to-all-start.8) | async-done | bytes 1835040 | tf_op jit(solution)/shard_map/all_to_all | solution.py:43
  (140 shorter events, 47.7 us)
Async XLA Ops:
  0.6 17.1 %copy-start = (bf16[768,1536]{1,0:T(8,128)(2,1)S(1)}, bf16[768,1536]{1,0:T(8,128)(2,1)}, u32[]{:S(2)}) copy-start(bf16[768,1536]{1,0:T(8,128)(2,1)} %param.10) | copy-start | bytes 7077892
  7.1 13.3 %copy-start.4 = (bf16[128,768]{1,0:T(8,128)(2,1)}, bf16[128,768]{1,0:T(8,128)(2,1)S(1)}, u32[]{:S(2)}) copy-start(bf16[128,768]{1,0:T(8,128)(2,1)S(1)} %get-tuple-element.27) | copy-start | bytes 589828
  7.1 13.3 %copy-start.6 = (bf16[128,768]{1,0:T(8,128)(2,1)}, bf16[128,768]{1,0:T(8,128)(2,1)S(1)}, u32[]{:S(2)}) copy-start(bf16[128,768]{1,0:T(8,128)(2,1)S(1)} %get-tuple-element.47) | copy-start | bytes 589828
  9.7 21.8 %all-to-all-start.1 = ((bf16[16,8,1664]{2,1,0:T(8,128)(2,1)}), bf16[16,8,1664]{2,1,0:T(8,128)(2,1)}, u32[]{:S(2)}, u32[]{:S(2)}) async-start(bf16[16,8,1664]{2,1,0:T(8,128)(2,1)} %fusion.24), calls=%async_computation.1 | async-start | bytes 851968 | tf_op jit(solution)/shard_map/all_to_all | solution.py:35
  32.8 1.9 copy-start.10
  32.8 1.9 copy-start.13
  45.7 10.2 %all-to-all-start.2 = ((bf16[8,16,384]{2,1,0:T(8,128)(2,1)}), bf16[8,16,384]{2,1,0:T(8,128)(2,1)S(1)}, u32[]{:S(2)}, u32[]{:S(2)}) async-start(bf16[8,16,384]{2,1,0:T(8,128)(2,1)} %bitcast.10), calls=%async_computation.2 | async-start | bytes 196608 | tf_op jit(solution)/shard_map/all_to_all | solution.py:39
  56.0 31.2 %copy-start.9 = (bf16[8,16,384]{2,1,0:T(8,128)(2,1)}, bf16[8,16,384]{2,1,0:T(8,128)(2,1)S(1)}, u32[]{:S(2)}) copy-start(bf16[8,16,384]{2,1,0:T(8,128)(2,1)S(1)} %all-to-all-done.2) | copy-start | bytes 294916
  56.0 14.9 %all-to-all-start.4 = ((bf16[16,8,384]{2,1,0:T(8,128)(2,1)}), bf16[16,8,384]{2,1,0:T(8,128)(2,1)S(1)}, u32[]{:S(2)}, u32[]{:S(2)}) async-start(bf16[16,8,384]{2,1,0:T(8,128)(2,1)} %bitcast.45), calls=%async_computation.4 | async-start | bytes 196608 | tf_op jit(solution)/shard_map/all_to_all | solution.py:35
  70.9 16.2 %copy-start.3 = (bf16[16,8,384]{2,1,0:T(8,128)(2,1)}, bf16[16,8,384]{2,1,0:T(8,128)(2,1)S(1)}, u32[]{:S(2)}) copy-start(bf16[16,8,384]{2,1,0:T(8,128)(2,1)S(1)} %all-to-all-done.4) | copy-start | bytes 294916
  87.2 28.1 %all-to-all-start.3 = ((bf16[16,128,384]{2,1,0:T(8,128)(2,1)}), bf16[16,128,384]{2,1,0:T(8,128)(2,1)}, u32[]{:S(2)}, u32[]{:S(2)}) async-start(bf16[16,128,384]{2,1,0:T(8,128)(2,1)} %bitcast.12), calls=%async_computation.3 | async-start | bytes 3145728 | tf_op jit(solution)/shard_map/all_to_all | solution.py:35
  146.2 3.7 %copy-start.5 = (bf16[128,768]{1,0:T(8,128)(2,1)S(1)}, bf16[128,768]{1,0:T(8,128)(2,1)}, u32[]{:S(2)}) copy-start(bf16[128,768]{1,0:T(8,128)(2,1)} %copy-done.4) | copy-start | bytes 589828
  146.2 3.7 %copy-start.11 = (bf16[8,768]{1,0:T(8,128)(2,1)S(1)}, bf16[8,768]{1,0:T(8,128)(2,1)}, u32[]{:S(2)}) copy-start(bf16[8,768]{1,0:T(8,128)(2,1)} %copy-done.10) | copy-start | bytes 36868
  146.2 3.7 %copy-start.14 = (bf16[8,768]{1,0:T(8,128)(2,1)S(1)}, bf16[8,768]{1,0:T(8,128)(2,1)}, u32[]{:S(2)}) copy-start(bf16[8,768]{1,0:T(8,128)(2,1)} %copy-done.13) | copy-start | bytes 36868
  146.2 17.8 %all-to-all-start.7 = ((bf16[8,144,384]{2,1,0:T(8,128)(2,1)}), bf16[8,144,384]{2,1,0:T(8,128)(2,1)S(1)}, u32[]{:S(2)}, u32[]{:S(2)}) async-start(bf16[8,144,384]{2,1,0:T(8,128)(2,1)} %bitcast.42), calls=%async_computation.7 | async-start | bytes 1769472 | tf_op jit(solution)/shard_map/all_to_all | solution.py:39
  151.7 20.6 %collective-permute-start.2 = (bf16[272,768]{1,0:T(8,128)(2,1)}, bf16[272,768]{1,0:T(8,128)(2,1)}, u32[]{:S(2)}, u32[]{:S(2)}) collective-permute-start(bf16[272,768]{1,0:T(8,128)(2,1)} %pad_maximum_fusion), channel_id=1, source_target_pairs={{0,1},{1,0},{2,3},{3,2},{4,5},{5,4},{6,7},{7,6},{8,9},{9,8},{10,11... | collective-permute-start | bytes 1253384 | tf_op jit(solution)/shard_map/ppermute | solution.py:31
  164.0 30.7 %all-to-all-start.6 = ((bf16[16,144,384]{2,1,0:T(8,128)(2,1)}), bf16[16,144,384]{2,1,0:T(8,128)(2,1)}, u32[]{:S(2)}, u32[]{:S(2)}) async-start(bf16[16,144,384]{2,1,0:T(8,128)(2,1)} %bitcast.37), calls=%async_computation.6 | async-start | bytes 3538944 | tf_op jit(solution)/shard_map/all_to_all | solution.py:35
  168.7 5.3 %copy-start.2 = (bf16[256,768]{1,0:T(8,128)(2,1)S(1)}, bf16[256,768]{1,0:T(8,128)(2,1)}, u32[]{:S(2)}) copy-start(bf16[256,768]{1,0:T(8,128)(2,1)} %param.7) | copy-start | bytes 1179652
  189.2 12.0 %copy-start.7 = (bf16[136,384]{1,0:T(8,128)(2,1)}, bf16[136,384]{1,0:T(8,128)(2,1)S(1)}, u32[]{:S(2)}) copy-start(bf16[136,384]{1,0:T(8,128)(2,1)S(1)} %slice.145.de_q) | copy-start | bytes 313348
  189.2 12.0 %collective-permute-start = (bf16[136,384]{1,0:T(8,128)(2,1)S(1)}, bf16[136,384]{1,0:T(8,128)(2,1)S(1)}, u32[]{:S(2)}, u32[]{:S(2)}) collective-permute-start(bf16[136,384]{1,0:T(8,128)(2,1)S(1)} %slice.145.de_q), channel_id=1, source_target_pairs={{0,1},{1,0},{2,3},{3,2},{4,5},{5,4},{6,7},{7,6},{8,9},{9,8},{10,11... | collective-permute-start | bytes 313352 | tf_op jit(solution)/shard_map/ppermute | solution.py:31
  194.7 2.1 copy-start.1
  196.6 4.6 %copy-start.8 = (bf16[136,384]{1,0:T(8,128)(2,1)}, bf16[136,384]{1,0:T(8,128)(2,1)S(1)}, u32[]{:S(2)}) copy-start(bf16[136,384]{1,0:T(8,128)(2,1)S(1)} %slice.207.de_p) | copy-start | bytes 313348
  196.6 4.6 %collective-permute-start.1 = (bf16[136,384]{1,0:T(8,128)(2,1)S(1)}, bf16[136,384]{1,0:T(8,128)(2,1)S(1)}, u32[]{:S(2)}, u32[]{:S(2)}) collective-permute-start(bf16[136,384]{1,0:T(8,128)(2,1)S(1)} %slice.207.de_p), channel_id=1, source_target_pairs={{0,1},{1,0},{2,3},{3,2},{4,5},{5,4},{6,7},{7,6},{8,9},{9,8},{10,11... | collective-permute-start | bytes 313352 | tf_op jit(solution)/shard_map/ppermute | solution.py:31
  207.9 32.9 %all-to-all-start.8 = ((bf16[64,8,1792]{2,1,0:T(8,128)(2,1)}), bf16[64,8,1792]{2,1,0:T(8,128)(2,1)}, u32[]{:S(2)}, u32[]{:S(2)}) async-start(bf16[64,8,1792]{2,1,0:T(8,128)(2,1)} %bitcast.35), calls=%async_computation.8 | async-start | bytes 3670016 | tf_op jit(solution)/shard_map/all_to_all | solution.py:43
  (3 other events, 1.9 us)

commit v2 on v1

v2 whole, which is shorter than its diff:
```python
import functools

import jax
import jax.numpy as jnp
from jax import lax
from jax.experimental import pallas as pl
from jax.experimental.pallas import tpu as pltpu
from jax.sharding import Mesh
from jax.sharding import PartitionSpec as P

DP = ("dp_0", "dp_1", "dp_2", "dp_3")
PLANE = ("dp_0", "dp_1")
LINE = "dp_2"
CORE = "dp_3"
F32 = jnp.float32
BF16 = jnp.bfloat16

LOW = 128
UNIT = 8
BLOCK = LOW + UNIT
CHUNK = 144
PAIR = 2 * BLOCK
TILE = 256
LOG2E = 1.4426950408889634


def gelu_tanh(values):
    return jax.nn.gelu(values, approximate=True)


def swap_core(x):
    return lax.ppermute(x, CORE, [(0, 1), (1, 0)])


def plane_exchange(x):
    return lax.all_to_all(x, PLANE, 0, 0, tiled=True)


def stats_exchange(x):
    return lax.all_to_all(x, (LINE, CORE), 0, 0, tiled=True)


def from_line(x, k):
    return lax.ppermute(x, LINE, [((i + k) % 4, i) for i in range(4)])


def to_line(x, k):
    return lax.ppermute(x, LINE, [(i, (i + k) % 4) for i in range(4)])


def along_line(pair):
    return [pair] + [from_line(pair, k) for k in (1, 2, 3)]


def place_of(pos, sc):
    over = pos - sc[17]
    slot = jnp.bitwise_and(lax.shift_right_logical(over, 3) + sc[16], 15)
    place = jnp.where(
        (over >= 0) & (over < LOW), slot * BLOCK + LOW + jnp.bitwise_and(over, 7), -1
    )
    for s in range(16):
        at = pos - sc[s]
        place = jnp.where((at >= 0) & (at < LOW), at + s * BLOCK, place)
    return place


def near_index(sc, j):
    return jnp.bitwise_and(j // 2 - sc[18], 3) * 2 + jnp.bitwise_xor(j % 2, sc[19])


def nt_dot(a, b):
    return lax.dot_general(a, b, (((1,), (1,)), ((), ())), preferred_element_type=F32)


def stats_kernel(
    sc, q0, q1, q2, q3, t0, t1, t2, t3, p, q_out, turned_out, place_out, stats_out, qs, ts, *, scale
):
    width = p.shape[1]
    for k, ref in enumerate((q0, q1, q2, q3)):
        for b in range(2):
            qs[2 * k + b] = ref[b * LOW : (b + 1) * LOW]
    for k, ref in enumerate((t0, t1, t2, t3)):
        for b in range(2):
            ts[2 * k + b] = ref[b * 16 : (b + 1) * 16, :width]
    codes = []
    spread = None
    for j in range(8):
        b = near_index(sc, j)
        q_out[j * LOW : (j + 1) * LOW] = qs[b]
        tail = ts[b]
        q_out[8 * LOW + j * UNIT : 8 * LOW + (j + 1) * UNIT] = tail[:UNIT]
        code = tail[UNIT:, :LOW].astype(F32)
        codes.append(code[0:1] * 128.0 + code[1:2])
        part = code[2:3] * 128.0 + code[3:4]
        spread = part if spread is None else spread + part
    codes.append(spread[:, : 8 * UNIT])
    place_out[...] = place_of(jnp.concatenate(codes, axis=1).astype(jnp.int32), sc)
    rows = q_out.shape[0]
    pull = scale * LOG2E
    top = jnp.full((1, rows), -1e30, F32)
    total = jnp.zeros((1, rows), F32)
    found = jnp.zeros((1, rows), F32)
    for at in range(0, p.shape[0], PAIR):
        tile = p[at : at + PAIR]
        s = nt_dot(tile, q_out[...])
        row = lax.broadcasted_iota(jnp.int32, s.shape, 0)
        found += jnp.sum(jnp.where(row == place_out[...] - at, s, 0.0), axis=0, keepdims=True)
        new_top = jnp.maximum(top, jnp.max(s, axis=0, keepdims=True))
        total = total * jnp.exp2((top - new_top) * pull) + jnp.sum(
            jnp.exp2(s * pull - new_top * pull), axis=0, keepdims=True
        )
        top = new_top
    for at in range(0, p.shape[0], LOW):
        turned_out[:, at : at + LOW] = p[at : at + LOW].T
    line = lax.broadcasted_iota(jnp.int32, (8, rows), 0)
    stats = jnp.where(line == 0, top, jnp.where(line == 1, total, jnp.where(line == 2, found, 0.0)))
    for b in range(8):
        stats_out[b * 8 : (b + 1) * 8] = stats


def grads_kernel(sc, stats, q, p, turned, place, dp_out, dq_out, g_ref, *, scale):
    rows, width = q.shape
    pull = scale * LOG2E
    tops = [stats[b * 8 : b * 8 + 1] for b in range(8)]
    top = functools.reduce(jnp.maximum, tops)
    total = jnp.zeros((1, rows), F32)
    found = jnp.zeros((1, rows), F32)
    for b in range(8):
        total += stats[b * 8 + 1 : b * 8 + 2] * jnp.exp2((tops[b] - top) * pull)
        found += stats[b * 8 + 2 : b * 8 + 3]
    norm = top * scale + jnp.log(total)
    loss = jnp.sum(norm - found * scale, axis=1, keepdims=True)
    norm = norm * LOG2E
    loss_high = loss.astype(BF16).astype(F32)
    loss_mid = (loss - loss_high).astype(BF16).astype(F32)
    loss_low = loss - loss_high - loss_mid
    line = lax.broadcasted_iota(jnp.int32, (UNIT, width), 0)
    loss_tile = jnp.where(
        line == 0,
        loss_high,
        jnp.where(line == 1, loss_mid, jnp.where(line == 2, loss_low, 0.0)),
    ).astype(BF16)
    for at in range(0, p.shape[0], PAIR):
        s = nt_dot(p[at : at + PAIR], q[...])
        row = lax.broadcasted_iota(jnp.int32, s.shape, 0)
        e = jnp.exp2(s * pull - norm)
        g_ref[at : at + PAIR] = jnp.where(row == place[...] - at, e - 1.0, e).astype(BF16)
    for k in range(p.shape[0] // PAIR):
        dp = scale * jnp.dot(g_ref[k * PAIR : (k + 1) * PAIR], q[...], preferred_element_type=F32)
        dp = dp.astype(BF16)
        for half in range(2):
            to = (2 * k + half) * CHUNK
            dp_out[to : to + BLOCK] = dp[half * BLOCK : (half + 1) * BLOCK]
            dp_out[to + BLOCK : to + CHUNK] = loss_tile
    for k in range(4):
        dq = jnp.dot(
            turned[...], g_ref[:, k * TILE : (k + 1) * TILE], preferred_element_type=F32
        )
        dq = (scale * dq).T.astype(BF16)
        for half in range(2):
            dq_out[near_index(sc, 2 * k + half), :LOW] = dq[half * LOW : (half + 1) * LOW]
    dq = jnp.dot(turned[...], g_ref[:, 8 * LOW :], preferred_element_type=F32)
    dq = (scale * dq).T.astype(BF16)
    for j in range(8):
        dq_out[near_index(sc, j), LOW:BLOCK] = dq[j * UNIT : (j + 1) * UNIT]


def weights_kernel(q0, q1, q2, q3, p0, p1, p2, p3, rows, hidden, slope, second, out, de):
    for k, (dq, dp) in enumerate(zip((q0, q1, q2, q3), (p0, p1, p2, p3))):
        for b in range(2):
            to = (2 * k + b) * 2 * LOW
            de[to : to + LOW] = dq[b * BLOCK : b * BLOCK + LOW]
            de[to + LOW : to + 2 * LOW] = dp[b * BLOCK : b * BLOCK + LOW]
            to = 16 * LOW + (2 * k + b) * 2 * UNIT
            de[to : to + UNIT] = dq[b * BLOCK + LOW : (b + 1) * BLOCK]
            de[to + UNIT : to + 2 * UNIT] = dp[b * BLOCK + LOW : (b + 1) * BLOCK]
    many = out.shape[0]
    wide = rows.shape[1] + de.shape[1]
    grad_second = jnp.dot(hidden[...], de[...], preferred_element_type=F32)
    back = nt_dot(second[...], de[...])
    dpre = (slope[...] * back).astype(BF16)
    grad_first = jnp.dot(dpre, rows[...], preferred_element_type=F32)
    out[:, : rows.shape[1]] = grad_first[:many].astype(BF16)
    out[:, rows.shape[1] : wide] = grad_second[:many].astype(BF16)
    rest = grad_first.shape[0] - many
    x = jnp.concatenate(
        [grad_first[many:], grad_second[many:], jnp.zeros((rest, 128), F32)], axis=1
    )
    near, far = x[:, :640], x[:, 640:]
    line = jnp.bitwise_and(lax.broadcasted_iota(jnp.int32, near.shape, 0), 7)
    even = jnp.where(line < 4, near, pltpu.roll(far, 4, 0)).astype(BF16)
    odd = jnp.where(line < 4, pltpu.roll(near, rest - 4, 0), far).astype(BF16)
    for b in range(rest // 8):
        out[b * 16 : b * 16 + 8, wide:] = even[b * 8 : (b + 1) * 8]
        out[b * 16 + 8 : b * 16 + 16, wide:] = odd[b * 8 : (b + 1) * 8]


VMEM = pl.BlockSpec(memory_space=pltpu.VMEM)
SMEM = pl.BlockSpec(memory_space=pltpu.SMEM)


def score_stats(sc, qs, ts, p, scale):
    columns, width = p.shape
    rows = 8 * BLOCK
    return pl.pallas_call(
        functools.partial(stats_kernel, scale=scale),
        in_specs=[SMEM] + [VMEM] * 9,
        out_specs=[VMEM] * 4,
        out_shape=[
            jax.ShapeDtypeStruct((rows, width), BF16),
            jax.ShapeDtypeStruct((width, columns), BF16),
            jax.ShapeDtypeStruct((1, rows), jnp.int32),
            jax.ShapeDtypeStruct((64, rows), F32),
        ],
        scratch_shapes=[pltpu.VMEM((8, LOW, width), BF16), pltpu.VMEM((8, 16, width), BF16)],
        name="score_stats",
    )(sc, *qs, *ts, p)


def score_grads(sc, stats, q, p, turned, place, scale):
    columns, width = p.shape
    rows = q.shape[0]
    return pl.pallas_call(
        functools.partial(grads_kernel, scale=scale),
        in_specs=[SMEM] + [VMEM] * 5,
        out_specs=[VMEM] * 2,
        out_shape=[
            jax.ShapeDtypeStruct((columns // BLOCK * CHUNK, width), BF16),
            jax.ShapeDtypeStruct((8, BLOCK, width), BF16),
        ],
        scratch_shapes=[pltpu.VMEM((columns, rows), BF16)],
        name="score_grads",
    )(sc, stats, q, p, turned, place)


def weight_grads(dqs, dps, rows, hidden, slope, second):
    return pl.pallas_call(
        weights_kernel,
        in_specs=[VMEM] * 12,
        out_specs=VMEM,
        out_shape=jax.ShapeDtypeStruct((128, 1792), BF16),
        scratch_shapes=[pltpu.VMEM((16 * BLOCK, second.shape[1]), BF16)],
        name="weight_grads",
    )(*dqs, *dps, rows, hidden, slope, second)


def body(query_features, passage_features, counts, positives, w_first, w_second):
    width = query_features.shape[1]
    hidden_width, emb_width = w_second.shape
    scale = 2.5 * emb_width ** (-0.5)
    group = lax.axis_index((LINE, CORE))
    pairs = BLOCK * lax.axis_size(DP)

    heavy = (counts > LOW).astype(jnp.int32)
    offsets = jnp.cumsum(counts) - counts
    devices = jnp.arange(counts.shape[0], dtype=jnp.int32)
    mine = heavy * (devices % 8 == group)
    heavy_at = jnp.sum(mine * (devices // 8))
    over_start = jnp.sum(mine * offsets) + LOW
    group_start = lax.dynamic_slice_in_dim(offsets.reshape(16, 8), group, 1, 1)[:, 0]
    scalars = [heavy_at, over_start, lax.axis_index(LINE), lax.axis_index(CORE)]
    sc = jnp.concatenate([group_start, jnp.stack(scalars)]).astype(jnp.int32)

    pos_high = jnp.right_shift(positives, 7).astype(BF16)
    pos_low = jnp.bitwise_and(positives, 127).astype(BF16)
    lane = jnp.arange(LOW, dtype=jnp.int32)
    line = jnp.arange(UNIT, dtype=jnp.int32)[None, :, None]
    at_group = (lane // UNIT == group)[None, None, :]
    spread_high = jnp.tile(pos_high[LOW:].reshape(16, 1, UNIT), (1, 1, 16))
    spread_low = jnp.tile(pos_low[LOW:].reshape(16, 1, UNIT), (1, 1, 16))
    coded = jnp.where(
        at_group & (line == 2),
        spread_high,
        jnp.where(at_group & (line == 3), spread_low, jnp.zeros((), BF16)),
    ).reshape(LOW, LOW)
    over = jnp.concatenate([query_features[LOW:], passage_features[LOW:], coded], axis=1)
    over = jnp.concatenate([over, over], axis=0)
    over = lax.dynamic_slice_in_dim(over, (16 - heavy_at) * UNIT, LOW, 0)
    arrived = plane_exchange(over)
    tail = lax.dynamic_slice_in_dim(arrived, heavy_at * UNIT, UNIT, 0)

    def tower(x):
        pre = jnp.dot(x, w_first, preferred_element_type=F32)
        hidden = gelu_tanh(pre).astype(BF16)
        return jnp.dot(hidden, w_second, preferred_element_type=F32).astype(BF16)

    feats = jnp.concatenate([query_features[:LOW], passage_features[:LOW]], axis=0)
    base = tower(feats)
    q_base = base[:LOW]
    q_pair = jnp.concatenate([q_base, swap_core(q_base)], axis=0)

    feats_tail = jnp.concatenate([tail[:, :width], tail[:, width : 2 * width]], axis=0)
    tail_emb = tower(feats_tail)
    p_send = jnp.concatenate([base[LOW:], tail_emb[UNIT:]], axis=0)
    p_send, q_pair = lax.optimization_barrier((p_send, q_pair))
    qs = along_line(q_pair)
    p_send = jnp.broadcast_to(p_send[None], (16, BLOCK, emb_width))
    p_all = plane_exchange(p_send.reshape(16 * BLOCK, emb_width))

    line = line[0]
    codes = jnp.where(
        line == 0,
        pos_high[None, :LOW],
        jnp.where(line == 1, pos_low[None, :LOW], tail[:, 2 * width :]),
    )
    codes = jnp.pad(codes, ((0, 0), (0, emb_width - LOW)))
    pack = jnp.concatenate(
        [jnp.concatenate([tail_emb[:UNIT], codes], axis=0), feats_tail], axis=1
    )
    ts = along_line(jnp.concatenate([pack, swap_core(pack)], axis=0))

    feats_pair = jnp.concatenate([feats, swap_core(feats)], axis=0)
    feats_pair, _ = lax.optimization_barrier((feats_pair, (qs[1], ts[0])))
    rows = jnp.concatenate(along_line(feats_pair) + [t[:, emb_width:] for t in ts], axis=0)

    late_group, _ = lax.optimization_barrier((group, base))
    each = hidden_width // lax.axis_size(DP)
    unit = jnp.arange(16 * each, dtype=jnp.int32)
    rest = unit - LOW
    unit_of = jnp.where(
        unit < LOW, (unit // 8) * (8 * each) + unit % 8, (rest // 4) * (8 * each) + 8 + rest % 4
    )
    unit_of = unit_of + late_group * each
    pick = (unit_of[:, None] == jnp.arange(hidden_width, dtype=jnp.int32)[None, :]).astype(BF16)
    first_part = lax.dot_general(
        pick, w_first, (((1,), (1,)), ((), ())), preferred_element_type=F32
    ).astype(BF16)
    second_part = jnp.dot(pick, w_second, preferred_element_type=F32).astype(BF16)
    p_all, first_part, second_part = lax.optimization_barrier((p_all, first_part, second_part))

    q_all, turned, place, stats = score_stats(sc, qs, ts, p_all, scale)
    stats = stats_exchange(stats)
    dp_part, dq_part = score_grads(sc, stats, q_all, p_all, turned, place, scale)
    dp_all = plane_exchange(dp_part)

    dq_part = dq_part.reshape(4, 2 * BLOCK, emb_width)
    dq_pair = dq_part[0].astype(F32)
    for k in (1, 2, 3):
        dq_pair = dq_pair + to_line(dq_part[k], k).astype(F32)
    dq_far = swap_core(dq_pair)
    dq_far = jnp.concatenate([dq_far[BLOCK:], dq_far[:BLOCK]], axis=0)
    dqs = along_line((dq_pair + dq_far).astype(BF16))
    pre = lax.dot_general(first_part, rows, (((1,), (1,)), ((), ())), preferred_element_type=F32)
    act, pull_back = jax.vjp(gelu_tanh, pre)
    hidden = act.astype(BF16)
    slope = pull_back(jnp.ones_like(pre))[0]
    dp_all, dqs, hidden, slope = lax.optimization_barrier((dp_all, dqs, hidden, slope))

    dp_sum = jnp.sum(dp_all.reshape(16, CHUNK, emb_width).astype(F32), axis=0)
    mean_loss = (dp_sum[BLOCK, 0] + dp_sum[BLOCK + 1, 0] + dp_sum[BLOCK + 2, 0]) / pairs
    de_p = dp_sum[:BLOCK].astype(BF16)
    dps = along_line(jnp.concatenate([de_p, swap_core(de_p)], axis=0))
    grads = weight_grads(dqs, dps, rows, hidden, slope, second_part)
    out = jnp.sum(plane_exchange(grads).reshape(16, 8, -1).astype(F32), axis=0)
    wide = width + emb_width
    tail_out = jnp.concatenate([out[:4, wide:], out[4:, wide : 2 * wide - 640]], axis=1)
    out = jnp.concatenate([out[:, :wide], tail_out], axis=0)
    return (mean_loss, out[:, :width].T, out[:, width:])


def solution(mesh):
    finer = Mesh(mesh.devices.reshape(4, 4, 4, 2), DP)
    placed = (P(DP, None), P(DP, None), P(), P(DP), P(), P())
    return jax.shard_map(
        body,
        mesh=finer,
        in_specs=placed,
        out_specs=(P(), P(None, DP), P(DP, None)),
        check_vma=False,
    )
```

time: 246 us -> 213 us (0.87)
  blocking collectives: 28.1 us -> 0 us
  starting transfers between devices: 38.5 us -> 57.7 us
  local copies, waits for them, and re-layouts: 37.7 us -> 22.5 us
  other arithmetic: 17.6 us -> 12 us
    ppermute x0 -> x18, waiting for transfers between devices: none -> 51.5 us  [the longest x15 49.3 us: from_line(): return lax.ppermute(x, LINE, [((i + k) % 4, i) for i in range(4)])]
    all_to_all x3 -> x1, waiting for transfers between devices: 42.6 us -> 5.16 us  [stats_exchange(): return lax.all_to_all(x, (LINE, CORE), 0, 0, tiled=True)]
    ppermute x0 -> x18, starting transfers between devices: none -> 29.6 us  [the longest x15 27 us: from_line(): return lax.ppermute(x, LINE, [((i + k) % 4, i) for i in range(4)])]
    all_to_all x2 -> x0, blocking collectives: 28.1 us -> none  [line_exchange(): return lax.all_to_all(x, (LINE, CORE), 0, 0, tiled=True)]
    all_to_all x4, waiting for transfers between devices: 34.8 us -> 17.1 us  [plane_exchange(): return lax.all_to_all(x, PLANE, 0, 0, tiled=True)]
    unnamed x89 -> x47, local copies, waits for them, and re-layouts: 25.8 us -> 11.3 us
    all_to_all x3 -> x1, starting transfers between devices: 13.7 us -> 3.97 us  [stats_exchange(): return lax.all_to_all(x, (LINE, CORE), 0, 0, tiled=True)]
    add_any x1 -> x0, other arithmetic: 4.42 us -> none  [gelu_tanh(): return jax.nn.gelu(values, approximate=True)]
  transfers between devices with their start and end apart: 10 -> 28, of which waited for: 6 -> 15; matrix products, arithmetic and copies ran while one was open for 18% -> 16% of each run, Pallas kernels for 0% -> 4%
where the time goes in v2:
time: 213 us; the launch traced here: 212 us
  waiting for transfers between devices  75 us (35%)
  starting transfers between devices  57.7 us (27%)
  Pallas kernels  25.6 us (12%)
  local copies, waits for them, and re-layouts  22.5 us (11%)
  matrix products  12.9 us (6%)
  other arithmetic  12 us (6%)
  between operations  6.13 us (3%)
    ppermute x15, waiting for transfers between devices, from_line(): return lax.ppermute(x, LINE, [((i + k) % 4, i) for i in range(4)])  49.3 us
    ppermute x15, starting transfers between devices, from_line(): return lax.ppermute(x, LINE, [((i + k) % 4, i) for i in range(4)])  27 us
    all_to_all x4, starting transfers between devices, plane_exchange(): return lax.all_to_all(x, PLANE, 0, 0, tiled=True)  23.2 us
    all_to_all x4, waiting for transfers between devices, plane_exchange(): return lax.all_to_all(x, PLANE, 0, 0, tiled=True)  17.1 us
    pallas_call x1, Pallas kernels, score_grads(): pl.pallas_call(functools.partial(grads_kernel, scale=scale), in_specs=[SM...  12 us
    unnamed x47, local copies, waits for them, and re-layouts  11.3 us
    pallas_call x1, Pallas kernels, score_stats(): pl.pallas_call(functools.partial(stats_kernel, scale=scale), in_specs=[SM...  7.51 us
    pallas_call x1, Pallas kernels, weight_grads(): pl.pallas_call(weights_kernel, in_specs=[VMEM] * 12, out_specs=VMEM, out_...  6.09 us
  transfers between devices with their start and end apart: 28, of which 15 were waited for; matrix products, arithmetic and copies ran while one was open for 16% of the time, Pallas kernels for 4%

profile of v2, /device:TPU:0, one launch (start us, length us, event | category | flops | bytes accessed | tf_op | source)
XLA Modules:
  0.0 212.0 jit_solution(9813667251953581989)
XLA Ops:
  9.1 8.0 %all-to-all-start = ((bf16[16,8,1664]{2,1,0:T(8,128)(2,1)}), bf16[16,8,1664]{2,1,0:T(8,128)(2,1)S(1)}, u32[]{:S(2)}, u32[]{:S(2)}) async-start(bf16[16,8,1664]{2,1,0:T(8,128)(2,1)} %fusion.25), calls=%async_computation | async-start | bytes 851968 | tf_op jit(solution)/shard_map/all_to_all | solution.py:36
  17.1 3.2 %convolution_convert_fusion.1 = bf16[256,384]{1,0:T(8,128)(2,1)} fusion(bf16[1536,384]{1,0:T(8,128)(2,1)} %param.11, bf16[768,1536]{1,0:T(8,128)(2,1)S(1)} %copy-done, bf16[128,768]{1,0:T(8,128)(2,1)S(1)} %get-tuple-element.80, bf16[128,768]{1,0:T(8,128)(2,1)S(1)} %get-tuple-element.56), kind=kOutput, calls=%fused_computation.22 | convolution fusion | flops 910393344 | bytes 4128768 | tf_op jit(solution)/shard_map/dot_general | solution.py:285
  24.0 3.2 %all-to-all-done = bf16[16,8,1664]{2,1,0:T(8,128)(2,1)S(1)} async-done(((bf16[16,8,1664]{2,1,0:T(8,128)(2,1)}), bf16[16,8,1664]{2,1,0:T(8,128)(2,1)S(1)}, u32[]{:S(2)}, u32[]{:S(2)}) %all-to-all-start) | async-done | bytes 426016 | tf_op jit(solution)/shard_map/all_to_all | solution.py:36
  30.5 4.4 %all-to-all-start.1 = ((bf16[16,136,384]{2,1,0:T(8,128)(2,1)}), bf16[16,136,384]{2,1,0:T(8,128)(2,1)}, u32[]{:S(2)}, u32[]{:S(2)}) async-start(bf16[16,136,384]{2,1,0:T(8,128)(2,1)} %broadcast_in_dim.83), calls=%async_computation.1 | async-start | bytes 3342336 | tf_op jit(solution)/shard_map/all_to_all | solution.py:36
  36.4 3.1 %collective-permute-start.1 = (bf16[256,384]{1,0:T(8,128)(2,1)S(1)}, bf16[256,384]{1,0:T(8,128)(2,1)S(1)}, u32[]{:S(2)}, u32[]{:S(2)}) collective-permute-start(bf16[256,384]{1,0:T(8,128)(2,1)S(1)} %copy-done.5), channel_id=1, source_target_pairs={{2,0},{4,2},{6,4},{0,6},{3,1},{5,3},{7,5},{1,7},{10,8},{12,10},{14... | collective-permute-start | bytes 589832 | tf_op jit(solution)/shard_map/ppermute | solution.py:44
  40.2 3.9 %collective-permute-done.1.q1 = bf16[256,384]{1,0:T(8,128)(2,1)S(1)} collective-permute-done((bf16[256,384]{1,0:T(8,128)(2,1)S(1)}, bf16[256,384]{1,0:T(8,128)(2,1)S(1)}, u32[]{:S(2)}, u32[]{:S(2)}) %collective-permute-start.1) | collective-permute-done | bytes 196640 | tf_op jit(solution)/shard_map/ppermute | solution.py:44
  44.2 3.7 %collective-permute-start.16 = (bf16[512,768]{1,0:T(8,128)(2,1)S(1)}, bf16[512,768]{1,0:T(8,128)(2,1)}, u32[]{:S(2)}, u32[]{:S(2)}) collective-permute-start(bf16[512,768]{1,0:T(8,128)(2,1)S(1)} %pad_maximum_fusion), channel_id=1, source_target_pairs={{2,0},{4,2},{6,4},{0,6},{3,1},{5,3},{7,5},{1,7},{10,8},{12,10},{14... | collective-permute-start | bytes 2359304 | tf_op jit(solution)/shard_map/ppermute | solution.py:44
  58.2 27.3 %collective-permute-done.16 = bf16[512,768]{1,0:T(8,128)(2,1)} collective-permute-done((bf16[512,768]{1,0:T(8,128)(2,1)S(1)}, bf16[512,768]{1,0:T(8,128)(2,1)}, u32[]{:S(2)}, u32[]{:S(2)}) %collective-permute-start.16) | collective-permute-done | bytes 786464 | tf_op jit(solution)/shard_map/ppermute | solution.py:44
  85.5 3.8 %collective-permute-start.5 = (bf16[32,1152]{1,0:T(8,128)(2,1)S(1)}, bf16[32,1152]{1,0:T(8,128)(2,1)}, u32[]{:S(2)}, u32[]{:S(2)}) collective-permute-start(bf16[32,1152]{1,0:T(8,128)(2,1)S(1)} %pad_maximum_fusion.5.t0), channel_id=1, source_target_pairs={{2,0},{4,2},{6,4},{0,6},{3,1},{5,3},{7,5},{1,7},{10,8},{12,10},{14... | collective-permute-start | bytes 221192 | tf_op jit(solution)/shard_map/ppermute | solution.py:44
  98.8 7.5 %score_stats.1 = (bf16[1088,384]{1,0:T(8,128)(2,1)}, bf16[384,2176]{1,0:T(8,128)(2,1)}, s32[1,1088]{1,0:T(1,128)}, f32[64,1088]{1,0:T(8,128)}) custom-call(s32[20]{0:T(128)} %concatenate.49.sc, bf16[256,384]{1,0:T(8,128)(2,1)} %pad_maximum_fusion.3.q0, bf16[256,384]{1,0:T(8,128)(2,1)} %copy-done.16, bf16[256,384]{1,0:T(8,128)(2,1)} %collective-permute-done.2.q2, ...), custom_call_target="tpu_custom_call" | custom-call | tf_op jit(solution)/shard_map/score_stats/pallas_call | solution.py:205
  106.4 4.0 %all-to-all-start.2 = ((f32[8,8,1088]{2,1,0:T(8,128)}), f32[8,8,1088]{2,1,0:T(8,128)S(1)}, u32[]{:S(2)}, u32[]{:S(2)}) async-start(f32[8,8,1088]{2,1,0:T(8,128)} %bitcast.44), calls=%async_computation.2 | async-start | bytes 589824 | tf_op jit(solution)/shard_map/all_to_all | solution.py:40
  113.0 5.2 %all-to-all-done.2 = f32[8,8,1088]{2,1,0:T(8,128)S(1)} async-done(((f32[8,8,1088]{2,1,0:T(8,128)}), f32[8,8,1088]{2,1,0:T(8,128)S(1)}, u32[]{:S(2)}, u32[]{:S(2)}) %all-to-all-start.2) | async-done | bytes 278560 | tf_op jit(solution)/shard_map/all_to_all | solution.py:40
  118.9 12.0 %score_grads.1 = (bf16[2304,384]{1,0:T(8,128)(2,1)}, bf16[8,136,384]{2,1,0:T(8,128)(2,1)}) custom-call(s32[20]{0:T(128)} %concatenate.49.sc, f32[64,1088]{1,0:T(8,128)} %bitcast.41, bf16[1088,384]{1,0:T(8,128)(2,1)} %get-tuple-element.28.q, bf16[2176,384]{1,0:T(8,128)(2,1)} %bitcast.10.p, bf16[384,2176]{1,0:T(8,128)(2,1)} %get-tuple-element.29.turned, ...), custom_call_target="tpu_custom_call" | custom-call | tf_op jit(solution)/shard_map/score_grads/pallas_call | solution.py:223
  137.0 7.3 %all-to-all-start.3 = ((bf16[16,144,384]{2,1,0:T(8,128)(2,1)}), bf16[16,144,384]{2,1,0:T(8,128)(2,1)}, u32[]{:S(2)}, u32[]{:S(2)}) async-start(bf16[16,144,384]{2,1,0:T(8,128)(2,1)} %bitcast.40), calls=%async_computation.3 | async-start | bytes 3538944 | tf_op jit(solution)/shard_map/all_to_all | solution.py:36
  152.7 5.0 %fusion.5 = (f32[192,2176]{1,0:T(8,128)}, bf16[192,2176]{1,0:T(8,128)(2,1)}) fusion(bf16[192,768]{1,0:T(8,128)(2,1)S(1)} %copy-done.19, bf16[2176,768]{1,0:T(8,128)(2,1)} %slice_dynamic-update-slice_fusion.rows), kind=kOutput, calls=%fused_computation.9 | convolution fusion | flops 649666560 | bytes 6144000 | tf_op jit(solution)/shard_map/dot_general | solution.py:343
  157.8 2.7 %collective-permute-done.13.q2 = bf16[272,384]{1,0:T(8,128)(2,1)S(1)} collective-permute-done((bf16[272,384]{1,0:T(8,128)(2,1)S(1)}, bf16[272,384]{1,0:T(8,128)(2,1)S(1)}, u32[]{:S(2)}, u32[]{:S(2)}) %collective-permute-start.13) | collective-permute-done | bytes 208928 | tf_op jit(solution)/shard_map/ppermute | solution.py:44
  160.5 3.7 %collective-permute-done.14.q3 = bf16[272,384]{1,0:T(8,128)(2,1)S(1)} collective-permute-done((bf16[272,384]{1,0:T(8,128)(2,1)S(1)}, bf16[272,384]{1,0:T(8,128)(2,1)S(1)}, u32[]{:S(2)}, u32[]{:S(2)}) %collective-permute-start.14) | collective-permute-done | bytes 208928 | tf_op jit(solution)/shard_map/ppermute | solution.py:44
  164.2 5.2 %all-to-all-done.3 = bf16[16,144,384]{2,1,0:T(8,128)(2,1)} async-done(((bf16[16,144,384]{2,1,0:T(8,128)(2,1)}), bf16[16,144,384]{2,1,0:T(8,128)(2,1)}, u32[]{:S(2)}, u32[]{:S(2)}) %all-to-all-start.3) | async-done | bytes 1769504 | tf_op jit(solution)/shard_map/all_to_all | solution.py:36
  172.6 3.0 %collective-permute-start.20 = (bf16[272,384]{1,0:T(8,128)(2,1)S(1)}, bf16[272,384]{1,0:T(8,128)(2,1)S(1)}, u32[]{:S(2)}, u32[]{:S(2)}) collective-permute-start(bf16[272,384]{1,0:T(8,128)(2,1)S(1)} %pad_maximum_fusion.2.p0), channel_id=1, source_target_pairs={{2,0},{4,2},{6,4},{0,6},{3,1},{5,3},{7,5},{1,7},{10,8},{12,10},{14... | collective-permute-start | bytes 626696 | tf_op jit(solution)/shard_map/ppermute | solution.py:44
  177.3 7.5 %collective-permute-done.20.p1 = bf16[272,384]{1,0:T(8,128)(2,1)S(1)} collective-permute-done((bf16[272,384]{1,0:T(8,128)(2,1)S(1)}, bf16[272,384]{1,0:T(8,128)(2,1)S(1)}, u32[]{:S(2)}, u32[]{:S(2)}) %collective-permute-start.20) | collective-permute-done | bytes 208928 | tf_op jit(solution)/shard_map/ppermute | solution.py:44
  185.9 2.8 %collective-permute-done.22.p3 = bf16[272,384]{1,0:T(8,128)(2,1)} collective-permute-done((bf16[272,384]{1,0:T(8,128)(2,1)S(1)}, bf16[272,384]{1,0:T(8,128)(2,1)}, u32[]{:S(2)}, u32[]{:S(2)}) %collective-permute-start.22) | collective-permute-done | bytes 208928 | tf_op jit(solution)/shard_map/ppermute | solution.py:44
  188.6 6.1 %weight_grads.1 = bf16[128,1792]{1,0:T(8,128)(2,1)} custom-call(bf16[272,384]{1,0:T(8,128)(2,1)} %copy-done.4, bf16[272,384]{1,0:T(8,128)(2,1)} %copy-done.9, bf16[272,384]{1,0:T(8,128)(2,1)} %copy-done.10, bf16[272,384]{1,0:T(8,128)(2,1)} %copy-done.11, bf16[272,384]{1,0:T(8,128)(2,1)} %copy-done.3, bf16[272,384]{1,0:T(8,128)(2,1)} %copy-done.12, ...), custom_call_target="tpu_custom_call" | custom-call | tf_op jit(solution)/shard_map/weight_grads/pallas_call | solution.py:237
  194.7 3.6 %all-to-all-start.4 = ((bf16[16,8,1792]{2,1,0:T(8,128)(2,1)}), bf16[16,8,1792]{2,1,0:T(8,128)(2,1)S(1)}, u32[]{:S(2)}, u32[]{:S(2)}) async-start(bf16[16,8,1792]{2,1,0:T(8,128)(2,1)} %bitcast.39), calls=%async_computation.4 | async-start | bytes 917504 | tf_op jit(solution)/shard_map/all_to_all | solution.py:36
  200.8 8.7 %all-to-all-done.4 = bf16[16,8,1792]{2,1,0:T(8,128)(2,1)S(1)} async-done(((bf16[16,8,1792]{2,1,0:T(8,128)(2,1)}), bf16[16,8,1792]{2,1,0:T(8,128)(2,1)S(1)}, u32[]{:S(2)}, u32[]{:S(2)}) %all-to-all-start.4) | async-done | bytes 458784 | tf_op jit(solution)/shard_map/all_to_all | solution.py:36
  (140 shorter events, 61.0 us)
Async XLA Ops:
  9.1 18.1 %all-to-all-start = ((bf16[16,8,1664]{2,1,0:T(8,128)(2,1)}), bf16[16,8,1664]{2,1,0:T(8,128)(2,1)S(1)}, u32[]{:S(2)}, u32[]{:S(2)}) async-start(bf16[16,8,1664]{2,1,0:T(8,128)(2,1)} %fusion.25), calls=%async_computation | async-start | bytes 851968 | tf_op jit(solution)/shard_map/all_to_all | solution.py:36
  22.2 13.0 %collective-permute-start.15 = (bf16[256,768]{1,0:T(8,128)(2,1)}, bf16[256,768]{1,0:T(8,128)(2,1)}, u32[]{:S(2)}, u32[]{:S(2)}) collective-permute-start(bf16[256,768]{1,0:T(8,128)(2,1)} %pad_maximum_fusion.1), channel_id=1, source_target_pairs={{0,1},{1,0},{2,3},{3,2},{4,5},{5,4},{6,7},{7,6},{8,9},{9,8},{10,11... | collective-permute-start | bytes 1179656 | tf_op jit(solution)/shard_map/ppermute | solution.py:32
  30.5 67.3 %all-to-all-start.1 = ((bf16[16,136,384]{2,1,0:T(8,128)(2,1)}), bf16[16,136,384]{2,1,0:T(8,128)(2,1)}, u32[]{:S(2)}, u32[]{:S(2)}) async-start(bf16[16,136,384]{2,1,0:T(8,128)(2,1)} %broadcast_in_dim.83), calls=%async_computation.1 | async-start | bytes 3342336 | tf_op jit(solution)/shard_map/all_to_all | solution.py:36
  36.4 7.7 %collective-permute-start.1 = (bf16[256,384]{1,0:T(8,128)(2,1)S(1)}, bf16[256,384]{1,0:T(8,128)(2,1)S(1)}, u32[]{:S(2)}, u32[]{:S(2)}) collective-permute-start(bf16[256,384]{1,0:T(8,128)(2,1)S(1)} %copy-done.5), channel_id=1, source_target_pairs={{2,0},{4,2},{6,4},{0,6},{3,1},{5,3},{7,5},{1,7},{10,8},{12,10},{14... | collective-permute-start | bytes 589832 | tf_op jit(solution)/shard_map/ppermute | solution.py:44
  44.2 41.3 %collective-permute-start.16 = (bf16[512,768]{1,0:T(8,128)(2,1)S(1)}, bf16[512,768]{1,0:T(8,128)(2,1)}, u32[]{:S(2)}, u32[]{:S(2)}) collective-permute-start(bf16[512,768]{1,0:T(8,128)(2,1)S(1)} %pad_maximum_fusion), channel_id=1, source_target_pairs={{2,0},{4,2},{6,4},{0,6},{3,1},{5,3},{7,5},{1,7},{10,8},{12,10},{14... | collective-permute-start | bytes 2359304 | tf_op jit(solution)/shard_map/ppermute | solution.py:44
  47.9 45.3 %collective-permute-start.17 = (bf16[512,768]{1,0:T(8,128)(2,1)S(1)}, bf16[512,768]{1,0:T(8,128)(2,1)}, u32[]{:S(2)}, u32[]{:S(2)}) collective-permute-start(bf16[512,768]{1,0:T(8,128)(2,1)S(1)} %pad_maximum_fusion), channel_id=1, source_target_pairs={{4,0},{6,2},{0,4},{2,6},{5,1},{7,3},{1,5},{3,7},{12,8},{14,10},{8,... | collective-permute-start | bytes 2359304 | tf_op jit(solution)/shard_map/ppermute | solution.py:44
  48.0 62.4 %collective-permute-start.18 = (bf16[512,768]{1,0:T(8,128)(2,1)S(1)}, bf16[512,768]{1,0:T(8,128)(2,1)}, u32[]{:S(2)}, u32[]{:S(2)}) collective-permute-start(bf16[512,768]{1,0:T(8,128)(2,1)S(1)} %pad_maximum_fusion), channel_id=1, source_target_pairs={{6,0},{0,2},{2,4},{4,6},{7,1},{1,3},{3,5},{5,7},{14,8},{8,10},{10,... | collective-permute-start | bytes 2359304 | tf_op jit(solution)/shard_map/ppermute | solution.py:44
  54.4 44.4 %collective-permute-start.2 = (bf16[256,384]{1,0:T(8,128)(2,1)S(1)}, bf16[256,384]{1,0:T(8,128)(2,1)}, u32[]{:S(2)}, u32[]{:S(2)}) collective-permute-start(bf16[256,384]{1,0:T(8,128)(2,1)S(1)} %copy-done.6), channel_id=1, source_target_pairs={{4,0},{6,2},{0,4},{2,6},{5,1},{7,3},{1,5},{3,7},{12,8},{14,10},{8,... | collective-permute-start | bytes 589832 | tf_op jit(solution)/shard_map/ppermute | solution.py:44
  56.6 42.3 %collective-permute-start.3 = (bf16[256,384]{1,0:T(8,128)(2,1)S(1)}, bf16[256,384]{1,0:T(8,128)(2,1)}, u32[]{:S(2)}, u32[]{:S(2)}) collective-permute-start(bf16[256,384]{1,0:T(8,128)(2,1)S(1)} %copy-done.6), channel_id=1, source_target_pairs={{6,0},{0,2},{2,4},{4,6},{7,1},{1,3},{3,5},{5,7},{14,8},{8,10},{10,... | collective-permute-start | bytes 589832 | tf_op jit(solution)/shard_map/ppermute | solution.py:44
  85.5 5.9 %collective-permute-start.5 = (bf16[32,1152]{1,0:T(8,128)(2,1)S(1)}, bf16[32,1152]{1,0:T(8,128)(2,1)}, u32[]{:S(2)}, u32[]{:S(2)}) collective-permute-start(bf16[32,1152]{1,0:T(8,128)(2,1)S(1)} %pad_maximum_fusion.5.t0), channel_id=1, source_target_pairs={{2,0},{4,2},{6,4},{0,6},{3,1},{5,3},{7,5},{1,7},{10,8},{12,10},{14... | collective-permute-start | bytes 221192 | tf_op jit(solution)/shard_map/ppermute | solution.py:44
  91.3 6.5 %collective-permute-start.6 = (bf16[32,1152]{1,0:T(8,128)(2,1)S(1)}, bf16[32,1152]{1,0:T(8,128)(2,1)S(1)}, u32[]{:S(2)}, u32[]{:S(2)}) collective-permute-start(bf16[32,1152]{1,0:T(8,128)(2,1)S(1)} %pad_maximum_fusion.5.t0), channel_id=1, source_target_pairs={{4,0},{6,2},{0,4},{2,6},{5,1},{7,3},{1,5},{3,7},{12,8},{14,10},{8,... | collective-permute-start | bytes 221192 | tf_op jit(solution)/shard_map/ppermute | solution.py:44
  93.2 5.7 %collective-permute-start.7 = (bf16[32,1152]{1,0:T(8,128)(2,1)S(1)}, bf16[32,1152]{1,0:T(8,128)(2,1)}, u32[]{:S(2)}, u32[]{:S(2)}) collective-permute-start(bf16[32,1152]{1,0:T(8,128)(2,1)S(1)} %pad_maximum_fusion.5.t0), channel_id=1, source_target_pairs={{6,0},{0,2},{2,4},{4,6},{7,1},{1,3},{3,5},{5,7},{14,8},{8,10},{10,... | collective-permute-start | bytes 221192 | tf_op jit(solution)/shard_map/ppermute | solution.py:44
  106.4 11.8 %all-to-all-start.2 = ((f32[8,8,1088]{2,1,0:T(8,128)}), f32[8,8,1088]{2,1,0:T(8,128)S(1)}, u32[]{:S(2)}, u32[]{:S(2)}) async-start(f32[8,8,1088]{2,1,0:T(8,128)} %bitcast.44), calls=%async_computation.2 | async-start | bytes 589824 | tf_op jit(solution)/shard_map/all_to_all | solution.py:40
  132.9 11.3 %collective-permute-start.10 = (bf16[272,384]{1,0:T(8,128)(2,1)}, bf16[272,384]{1,0:T(8,128)(2,1)S(1)}, u32[]{:S(2)}, u32[]{:S(2)}) collective-permute-start(bf16[272,384]{1,0:T(8,128)(2,1)} %bitcast.18), channel_id=1, source_target_pairs={{0,6},{2,0},{4,2},{6,4},{1,7},{3,1},{5,3},{7,5},{8,14},{10,8},{12,... | collective-permute-start | bytes 626696 | tf_op jit(solution)/shard_map/ppermute | solution.py:48
  134.1 10.2 %collective-permute-start.9 = (bf16[272,384]{1,0:T(8,128)(2,1)S(1)}, bf16[272,384]{1,0:T(8,128)(2,1)S(1)}, u32[]{:S(2)}, u32[]{:S(2)}) collective-permute-start(bf16[272,384]{1,0:T(8,128)(2,1)S(1)} %bitcast.46), channel_id=1, source_target_pairs={{0,4},{2,6},{4,0},{6,2},{1,5},{3,7},{5,1},{7,3},{8,12},{10,14},{12... | collective-permute-start | bytes 626696 | tf_op jit(solution)/shard_map/ppermute | solution.py:48
  135.6 10.8 %collective-permute-start.8 = (bf16[272,384]{1,0:T(8,128)(2,1)S(1)}, bf16[272,384]{1,0:T(8,128)(2,1)}, u32[]{:S(2)}, u32[]{:S(2)}) collective-permute-start(bf16[272,384]{1,0:T(8,128)(2,1)S(1)} %bitcast.45), channel_id=1, source_target_pairs={{0,2},{2,4},{4,6},{6,0},{1,3},{3,5},{5,7},{7,1},{8,10},{10,12},{12... | collective-permute-start | bytes 626696 | tf_op jit(solution)/shard_map/ppermute | solution.py:48
  137.0 32.4 %all-to-all-start.3 = ((bf16[16,144,384]{2,1,0:T(8,128)(2,1)}), bf16[16,144,384]{2,1,0:T(8,128)(2,1)}, u32[]{:S(2)}, u32[]{:S(2)}) async-start(bf16[16,144,384]{2,1,0:T(8,128)(2,1)} %bitcast.40), calls=%async_computation.3 | async-start | bytes 3538944 | tf_op jit(solution)/shard_map/all_to_all | solution.py:36
  149.7 8.1 %collective-permute-start.12 = (bf16[272,384]{1,0:T(8,128)(2,1)S(1)}, bf16[272,384]{1,0:T(8,128)(2,1)S(1)}, u32[]{:S(2)}, u32[]{:S(2)}) collective-permute-start(bf16[272,384]{1,0:T(8,128)(2,1)S(1)} %fusion.28.q0), channel_id=1, source_target_pairs={{2,0},{4,2},{6,4},{0,6},{3,1},{5,3},{7,5},{1,7},{10,8},{12,10},{14... | collective-permute-start | bytes 626696 | tf_op jit(solution)/shard_map/ppermute | solution.py:44
  150.9 9.6 %collective-permute-start.13 = (bf16[272,384]{1,0:T(8,128)(2,1)S(1)}, bf16[272,384]{1,0:T(8,128)(2,1)S(1)}, u32[]{:S(2)}, u32[]{:S(2)}) collective-permute-start(bf16[272,384]{1,0:T(8,128)(2,1)S(1)} %fusion.28.q0), channel_id=1, source_target_pairs={{4,0},{6,2},{0,4},{2,6},{5,1},{7,3},{1,5},{3,7},{12,8},{14,10},{8,... | collective-permute-start | bytes 626696 | tf_op jit(solution)/shard_map/ppermute | solution.py:44
  151.8 12.4 %collective-permute-start.14 = (bf16[272,384]{1,0:T(8,128)(2,1)S(1)}, bf16[272,384]{1,0:T(8,128)(2,1)S(1)}, u32[]{:S(2)}, u32[]{:S(2)}) collective-permute-start(bf16[272,384]{1,0:T(8,128)(2,1)S(1)} %fusion.28.q0), channel_id=1, source_target_pairs={{6,0},{0,2},{2,4},{4,6},{7,1},{1,3},{3,5},{5,7},{14,8},{8,10},{10,... | collective-permute-start | bytes 626696 | tf_op jit(solution)/shard_map/ppermute | solution.py:44
  172.6 12.2 %collective-permute-start.20 = (bf16[272,384]{1,0:T(8,128)(2,1)S(1)}, bf16[272,384]{1,0:T(8,128)(2,1)S(1)}, u32[]{:S(2)}, u32[]{:S(2)}) collective-permute-start(bf16[272,384]{1,0:T(8,128)(2,1)S(1)} %pad_maximum_fusion.2.p0), channel_id=1, source_target_pairs={{2,0},{4,2},{6,4},{0,6},{3,1},{5,3},{7,5},{1,7},{10,8},{12,10},{14... | collective-permute-start | bytes 626696 | tf_op jit(solution)/shard_map/ppermute | solution.py:44
  175.6 9.6 %collective-permute-start.21 = (bf16[272,384]{1,0:T(8,128)(2,1)S(1)}, bf16[272,384]{1,0:T(8,128)(2,1)S(1)}, u32[]{:S(2)}, u32[]{:S(2)}) collective-permute-start(bf16[272,384]{1,0:T(8,128)(2,1)S(1)} %pad_maximum_fusion.2.p0), channel_id=1, source_target_pairs={{4,0},{6,2},{0,4},{2,6},{5,1},{7,3},{1,5},{3,7},{12,8},{14,10},{8,... | collective-permute-start | bytes 626696 | tf_op jit(solution)/shard_map/ppermute | solution.py:44
  176.4 12.2 %collective-permute-start.22 = (bf16[272,384]{1,0:T(8,128)(2,1)S(1)}, bf16[272,384]{1,0:T(8,128)(2,1)}, u32[]{:S(2)}, u32[]{:S(2)}) collective-permute-start(bf16[272,384]{1,0:T(8,128)(2,1)S(1)} %pad_maximum_fusion.2.p0), channel_id=1, source_target_pairs={{6,0},{0,2},{2,4},{4,6},{7,1},{1,3},{3,5},{5,7},{14,8},{8,10},{10,... | collective-permute-start | bytes 626696 | tf_op jit(solution)/shard_map/ppermute | solution.py:44
  194.7 14.8 %all-to-all-start.4 = ((bf16[16,8,1792]{2,1,0:T(8,128)(2,1)}), bf16[16,8,1792]{2,1,0:T(8,128)(2,1)S(1)}, u32[]{:S(2)}, u32[]{:S(2)}) async-start(bf16[16,8,1792]{2,1,0:T(8,128)(2,1)} %bitcast.39), calls=%async_computation.4 | async-start | bytes 917504 | tf_op jit(solution)/shard_map/all_to_all | solution.py:36
  (24 other events, 236.0 us)

commit v3 on v2

v3 whole, which is shorter than its diff:
```python
import functools

import jax
import jax.numpy as jnp
from jax import lax
from jax.experimental import pallas as pl
from jax.experimental.pallas import tpu as pltpu
from jax.sharding import Mesh
from jax.sharding import PartitionSpec as P

DP = ("dp_0", "dp_1", "dp_2", "dp_3")
PLANE = ("dp_0", "dp_1")
LINE = "dp_2"
CORE = "dp_3"
F32 = jnp.float32
BF16 = jnp.bfloat16

LOW = 128
UNIT = 8
BLOCK = LOW + UNIT
CHUNK = 144
PAIR = 2 * BLOCK
TILE = 256
LOG2E = 1.4426950408889634


def gelu_tanh(values):
    return jax.nn.gelu(values, approximate=True)


def swap_core(x):
    return lax.ppermute(x, CORE, [(0, 1), (1, 0)])


def plane_exchange(x):
    return lax.all_to_all(x, PLANE, 0, 0, tiled=True)


def stats_exchange(x):
    return lax.all_to_all(x, (LINE, CORE), 0, 0, tiled=True)


def from_line(x, k):
    return lax.ppermute(x, LINE, [((i + k) % 4, i) for i in range(4)])


def to_line(x, k):
    return lax.ppermute(x, LINE, [(i, (i + k) % 4) for i in range(4)])


def along_line(x):
    return [x] + [from_line(x, k) for k in (1, 2, 3)]


def gathered(x):
    own = jnp.concatenate(along_line(x), axis=0)
    return (own, swap_core(own))


def place_of(pos, sc):
    over = pos - sc[17]
    slot = jnp.bitwise_and(lax.shift_right_logical(over, 3) + sc[16], 15)
    place = jnp.where(
        (over >= 0) & (over < LOW), slot * BLOCK + LOW + jnp.bitwise_and(over, 7), -1
    )
    for s in range(16):
        at = pos - sc[s]
        place = jnp.where((at >= 0) & (at < LOW), at + s * BLOCK, place)
    return place


def near_index(sc, j):
    return jnp.bitwise_and(j // 2 - sc[18], 3) + 4 * jnp.bitwise_xor(j % 2, sc[19])


def nt_dot(a, b):
    return lax.dot_general(a, b, (((1,), (1,)), ((), ())), preferred_element_type=F32)


def stats_kernel(
    sc, q_own, q_far, t_own, t_far, p, q_out, place_out, stats_out, qs, ts, *, scale
):
    for k, (q, t) in enumerate(((q_own, t_own), (q_far, t_far))):
        for b in range(4):
            qs[4 * k + b] = q[b * LOW : (b + 1) * LOW]
            ts[4 * k + b] = t[b * 16 : (b + 1) * 16]
    lane = lax.broadcasted_iota(jnp.int32, (1, LOW), 1) // UNIT
    codes = []
    spread = jnp.zeros((1, LOW), F32)
    for j in range(8):
        b = near_index(sc, j)
        q_out[j * LOW : (j + 1) * LOW] = qs[b]
        tail = ts[b]
        q_out[8 * LOW + j * UNIT : 8 * LOW + (j + 1) * UNIT] = tail[:UNIT]
        code = tail[UNIT:, :LOW].astype(F32)
        codes.append(code[0:1] * 128.0 + code[1:2])
        unit = jnp.bitwise_and(sc[20] - sc[21 + j], 15)
        part = pltpu.roll(code, jnp.bitwise_and(j - unit, 15) * UNIT, 1)
        spread = jnp.where(lane == j, part[2:3] * 128.0 + part[3:4], spread)
    codes.append(spread[:, : 8 * UNIT])
    place_out[...] = place_of(jnp.concatenate(codes, axis=1).astype(jnp.int32), sc)
    rows = q_out.shape[0]
    pull = scale * LOG2E
    top = jnp.full((1, rows), -1e30, F32)
    total = jnp.zeros((1, rows), F32)
    found = jnp.zeros((1, rows), F32)
    for at in range(0, p.shape[0], PAIR):
        tile = p[at : at + PAIR]
        s = nt_dot(tile, q_out[...])
        row = lax.broadcasted_iota(jnp.int32, s.shape, 0)
        found += jnp.sum(jnp.where(row == place_out[...] - at, s, 0.0), axis=0, keepdims=True)
        new_top = jnp.maximum(top, jnp.max(s, axis=0, keepdims=True))
        total = total * jnp.exp2((top - new_top) * pull) + jnp.sum(
            jnp.exp2(s * pull - new_top * pull), axis=0, keepdims=True
        )
        top = new_top
    line = lax.broadcasted_iota(jnp.int32, (8, rows), 0)
    stats = jnp.where(line == 0, top, jnp.where(line == 1, total, jnp.where(line == 2, found, 0.0)))
    for b in range(8):
        stats_out[b * 8 : (b + 1) * 8] = stats


def grads_kernel(stats, q, p, place, dp_out, g_ref, *, scale):
    rows, width = q.shape
    pull = scale * LOG2E
    tops = [stats[b * 8 : b * 8 + 1] for b in range(8)]
    top = functools.reduce(jnp.maximum, tops)
    total = jnp.zeros((1, rows), F32)
    found = jnp.zeros((1, rows), F32)
    for b in range(8):
        total += stats[b * 8 + 1 : b * 8 + 2] * jnp.exp2((tops[b] - top) * pull)
        found += stats[b * 8 + 2 : b * 8 + 3]
    norm = top * scale + jnp.log(total)
    loss = jnp.sum(norm - found * scale, axis=1, keepdims=True)
    norm = norm * LOG2E
    loss_high = loss.astype(BF16).astype(F32)
    loss_mid = (loss - loss_high).astype(BF16).astype(F32)
    loss_low = loss - loss_high - loss_mid
    line = lax.broadcasted_iota(jnp.int32, (UNIT, width), 0)
    loss_tile = jnp.where(
        line == 0,
        loss_high,
        jnp.where(line == 1, loss_mid, jnp.where(line == 2, loss_low, 0.0)),
    ).astype(BF16)
    for at in range(0, p.shape[0], PAIR):
        s = nt_dot(p[at : at + PAIR], q[...])
        row = lax.broadcasted_iota(jnp.int32, s.shape, 0)
        e = jnp.exp2(s * pull - norm)
        g_ref[at : at + PAIR] = jnp.where(row == place[...] - at, e - 1.0, e).astype(BF16)
    for k in range(p.shape[0] // PAIR):
        dp = scale * jnp.dot(g_ref[k * PAIR : (k + 1) * PAIR], q[...], preferred_element_type=F32)
        dp = dp.astype(BF16)
        for half in range(2):
            to = (2 * k + half) * CHUNK
            dp_out[to : to + BLOCK] = dp[half * BLOCK : (half + 1) * BLOCK]
            dp_out[to + BLOCK : to + CHUNK] = loss_tile


def query_kernel(sc, p, g, own, far, turned, *, scale):
    for at in range(0, p.shape[0], LOW):
        turned[:, at : at + LOW] = p[at : at + LOW].T

    def put(j, rows, part):
        b = near_index(sc, j)

        @pl.when(b < 4)
        def _():
            own[b, rows] = part

        @pl.when(b >= 4)
        def _():
            far[b - 4, rows] = part

    for k in range(4):
        dq = jnp.dot(turned[...], g[:, k * TILE : (k + 1) * TILE], preferred_element_type=F32)
        dq = (scale * dq).T
        for half in range(2):
            put(2 * k + half, slice(0, LOW), dq[half * LOW : (half + 1) * LOW])
    dq = jnp.dot(turned[...], g[:, 8 * LOW :], preferred_element_type=F32)
    dq = (scale * dq).T
    for j in range(8):
        put(j, slice(LOW, BLOCK), dq[j * UNIT : (j + 1) * UNIT])


def weight_parts(de_own, de_far, rows, hidden, slope, second, de):
    half = de_own.shape[0]
    de[:half] = de_own[...]
    de[half:] = de_far[...]
    grad_second = jnp.dot(hidden[...], de[...], preferred_element_type=F32)
    dpre = (slope[...] * nt_dot(second[...], de[...])).astype(BF16)
    grad_first = jnp.dot(dpre, rows[...], preferred_element_type=F32)
    return (grad_first, grad_second)


def first_weights_kernel(de_own, de_far, rows, hidden, slope, second, out, de):
    grad_first, grad_second = weight_parts(de_own, de_far, rows, hidden, slope, second, de)
    out[:, : rows.shape[1]] = grad_first
    out[:, rows.shape[1] :] = grad_second


def last_weights_kernel(sums, de_own, de_far, rows, hidden, slope, second, out, de):
    grad_first, grad_second = weight_parts(de_own, de_far, rows, hidden, slope, second, de)
    grad_first += sums[:, : rows.shape[1]]
    grad_second += sums[:, rows.shape[1] :]
    many = out.shape[0]
    wide = sums.shape[1]
    out[:, : rows.shape[1]] = grad_first[:many].astype(BF16)
    out[:, rows.shape[1] : wide] = grad_second[:many].astype(BF16)
    rest = grad_first.shape[0] - many
    x = jnp.concatenate(
        [grad_first[many:], grad_second[many:], jnp.zeros((rest, 128), F32)], axis=1
    )
    near, far = x[:, :640], x[:, 640:]
    line = jnp.bitwise_and(lax.broadcasted_iota(jnp.int32, near.shape, 0), 7)
    even = jnp.where(line < 4, near, pltpu.roll(far, 4, 0)).astype(BF16)
    odd = jnp.where(line < 4, pltpu.roll(near, rest - 4, 0), far).astype(BF16)
    for b in range(rest // 8):
        out[b * 16 : b * 16 + 8, wide:] = even[b * 8 : (b + 1) * 8]
        out[b * 16 + 8 : b * 16 + 16, wide:] = odd[b * 8 : (b + 1) * 8]


VMEM = pl.BlockSpec(memory_space=pltpu.VMEM)
SMEM = pl.BlockSpec(memory_space=pltpu.SMEM)


def score_stats(sc, qs, ts, p, scale):
    width = p.shape[1]
    rows = 8 * BLOCK
    return pl.pallas_call(
        functools.partial(stats_kernel, scale=scale),
        in_specs=[SMEM] + [VMEM] * 5,
        out_specs=[VMEM] * 3,
        out_shape=[
            jax.ShapeDtypeStruct((rows, width), BF16),
            jax.ShapeDtypeStruct((1, rows), jnp.int32),
            jax.ShapeDtypeStruct((64, rows), F32),
        ],
        scratch_shapes=[pltpu.VMEM((8, LOW, width), BF16), pltpu.VMEM((8, 16, width), BF16)],
        name="score_stats",
    )(sc, *qs, *ts, p)


def score_grads(stats, q, p, place, scale):
    columns, width = p.shape
    rows = q.shape[0]
    return pl.pallas_call(
        functools.partial(grads_kernel, scale=scale),
        in_specs=[VMEM] * 4,
        out_specs=[VMEM] * 2,
        out_shape=[
            jax.ShapeDtypeStruct((columns // BLOCK * CHUNK, width), BF16),
            jax.ShapeDtypeStruct((columns, rows), BF16),
        ],
        name="score_grads",
    )(stats, q, p, place)


def query_grads(sc, p, g, scale):
    columns, width = p.shape
    return pl.pallas_call(
        functools.partial(query_kernel, scale=scale),
        in_specs=[SMEM] + [VMEM] * 2,
        out_specs=[VMEM] * 2,
        out_shape=[jax.ShapeDtypeStruct((4, BLOCK, width), F32)] * 2,
        scratch_shapes=[pltpu.VMEM((width, columns), BF16)],
        name="query_grads",
    )(sc, p, g)


def weight_grads(sums, des, rows, hidden, slope, second):
    scratch = [pltpu.VMEM((8 * BLOCK, second.shape[1]), BF16)]
    operands = (*des, rows, hidden, slope, second)
    if sums is None:
        shape = (second.shape[0], rows.shape[1] + second.shape[1])
        return pl.pallas_call(
            first_weights_kernel,
            in_specs=[VMEM] * 6,
            out_specs=VMEM,
            out_shape=jax.ShapeDtypeStruct(shape, F32),
            scratch_shapes=scratch,
            name="first_weights",
        )(*operands)
    return pl.pallas_call(
        last_weights_kernel,
        in_specs=[VMEM] * 7,
        out_specs=VMEM,
        out_shape=jax.ShapeDtypeStruct((128, 1792), BF16),
        scratch_shapes=scratch,
        name="last_weights",
    )(sums, *operands)


def body(query_features, passage_features, counts, positives, w_first, w_second):
    width = query_features.shape[1]
    hidden_width, emb_width = w_second.shape
    scale = 2.5 * emb_width ** (-0.5)
    group = lax.axis_index((LINE, CORE))
    pairs = BLOCK * lax.axis_size(DP)

    heavy = (counts > LOW).astype(jnp.int32)
    devices = jnp.arange(counts.shape[0], dtype=jnp.int32)
    mine = heavy * (devices % 8 == group)
    heavy_at = jnp.sum(mine * (devices // 8))
    pos_high = jnp.right_shift(positives, 7).astype(BF16)
    pos_low = jnp.bitwise_and(positives, 127).astype(BF16)
    line = jnp.arange(LOW, dtype=jnp.int32)[:, None] % UNIT
    coded = jnp.where(
        line == 2, pos_high[LOW:], jnp.where(line == 3, pos_low[LOW:], jnp.zeros((), BF16))
    )
    over = jnp.concatenate([query_features[LOW:], passage_features[LOW:], coded], axis=1)
    over = jnp.concatenate([over, over], axis=0)
    over = lax.dynamic_slice_in_dim(over, (16 - heavy_at) * UNIT, LOW, 0)
    arrived = plane_exchange(over)
    tail = lax.dynamic_slice_in_dim(arrived, heavy_at * UNIT, UNIT, 0)

    def tower(x):
        pre = jnp.dot(x, w_first, preferred_element_type=F32)
        hidden = gelu_tanh(pre).astype(BF16)
        return jnp.dot(hidden, w_second, preferred_element_type=F32).astype(BF16)

    base = tower(jnp.concatenate([query_features[:LOW], passage_features[:LOW]], axis=0))
    qs = gathered(base[:LOW])

    tail_q, tail_p = tail[:, :width], tail[:, width : 2 * width]
    tail_emb = tower(jnp.concatenate([tail_q, tail_p], axis=0))
    p_send = jnp.concatenate([base[LOW:], tail_emb[UNIT:]], axis=0)
    p_send = jnp.broadcast_to(p_send[None], (16, BLOCK, emb_width))
    p_all = plane_exchange(p_send.reshape(16 * BLOCK, emb_width))

    line = line[:UNIT]
    codes = jnp.where(
        line == 0,
        pos_high[None, :LOW],
        jnp.where(line == 1, pos_low[None, :LOW], tail[:, 2 * width :]),
    )
    codes = jnp.pad(codes, ((0, 0), (0, emb_width - LOW)))
    ts = gathered(jnp.concatenate([tail_emb[:UNIT], codes], axis=0))

    late_counts, group, _ = lax.optimization_barrier((counts, group, base))
    heavy = (late_counts > LOW).astype(jnp.int32)
    mine = heavy * (devices % 8 == group)
    offsets = jnp.cumsum(late_counts) - late_counts
    over_start = jnp.sum(mine * offsets) + LOW
    group_start = lax.dynamic_slice_in_dim(offsets.reshape(16, 8), group, 1, 1)[:, 0]
    scalars = [heavy_at, over_start, lax.axis_index(LINE), lax.axis_index(CORE)]
    scalars = jnp.stack(scalars + [lax.axis_index(PLANE)])
    heavies = jnp.sum(heavy.reshape(16, 8) * jnp.arange(16, dtype=jnp.int32)[:, None], axis=0)
    sc = jnp.concatenate([group_start, scalars, heavies]).astype(jnp.int32)

    feats = jnp.concatenate(
        [query_features[:LOW], tail_q, passage_features[:LOW], tail_p], axis=0
    )
    feats, _ = lax.optimization_barrier((feats, (qs[1], ts[1])))
    feats = along_line(feats)

    each = hidden_width // lax.axis_size(DP)
    unit = jnp.arange(16 * each, dtype=jnp.int32)
    rest = unit - LOW
    unit_of = jnp.where(
        unit < LOW, (unit // 8) * (8 * each) + unit % 8, (rest // 4) * (8 * each) + 8 + rest % 4
    )
    unit_of = unit_of + group * each
    pick = (unit_of[:, None] == jnp.arange(hidden_width, dtype=jnp.int32)[None, :]).astype(BF16)
    first_part = lax.dot_general(
        pick, w_first, (((1,), (1,)), ((), ())), preferred_element_type=F32
    ).astype(BF16)
    second_part = jnp.dot(pick, w_second, preferred_element_type=F32).astype(BF16)
    p_all, first_part, second_part = lax.optimization_barrier((p_all, first_part, second_part))

    q_all, place, stats = score_stats(sc, qs, ts, p_all, scale)
    stats = stats_exchange(stats)
    dp_part, g = score_grads(stats, q_all, p_all, place, scale)
    dp_all = plane_exchange(dp_part)
    dq_own, dq_far = query_grads(sc, p_all, g, scale)

    dq = dq_own + swap_core(dq_far)
    dq_sum = dq[0].astype(BF16).astype(F32)
    for k in (1, 2, 3):
        dq_sum = dq_sum + to_line(dq[k].astype(BF16), k).astype(F32)
    dqs = gathered(dq_sum.astype(BF16))
    feats, _ = lax.optimization_barrier((feats, dq_far))
    feats_own = jnp.concatenate(
        [x[:BLOCK] for x in feats] + [x[BLOCK:] for x in feats], axis=0
    )
    feats_far = swap_core(feats_own)
    half = 4 * BLOCK

    def units_of(rows):
        pre = lax.dot_general(
            first_part, rows, (((1,), (1,)), ((), ())), preferred_element_type=F32
        )
        act, pull_back = jax.vjp(gelu_tanh, pre)
        return (rows, act.astype(BF16), pull_back(jnp.ones_like(pre))[0])

    q_units = units_of(jnp.concatenate([feats_own[:half], feats_far[:half]], axis=0))
    p_units = units_of(jnp.concatenate([feats_own[half:], feats_far[half:]], axis=0))
    dp_all, dqs, q_units, p_units = lax.optimization_barrier((dp_all, dqs, q_units, p_units))

    dp_sum = jnp.sum(dp_all.reshape(16, CHUNK, emb_width).astype(F32), axis=0)
    mean_loss = (dp_sum[BLOCK, 0] + dp_sum[BLOCK + 1, 0] + dp_sum[BLOCK + 2, 0]) / pairs
    dps = gathered(dp_sum[:BLOCK].astype(BF16))
    sums = weight_grads(None, dqs, *q_units, second_part)
    grads = weight_grads(sums, dps, *p_units, second_part)
    out = jnp.sum(plane_exchange(grads).reshape(16, 8, -1).astype(F32), axis=0)
    wide = width + emb_width
    tail_out = jnp.concatenate([out[:4, wide:], out[4:, wide : 2 * wide - 640]], axis=1)
    out = jnp.concatenate([out[:, :wide], tail_out], axis=0)
    return (mean_loss, out[:, :width].T, out[:, width:])


def solution(mesh):
    finer = Mesh(mesh.devices.reshape(4, 4, 4, 2), DP)
    placed = (P(DP, None), P(DP, None), P(), P(DP), P(), P())
    return jax.shard_map(
        body,
        mesh=finer,
        in_specs=placed,
        out_specs=(P(), P(None, DP), P(DP, None)),
        check_vma=False,
    )
```

time: 213 us -> 204 us (0.958)
  waiting for transfers between devices: 75 us -> 36.6 us
  blocking collectives: 0 us -> 11.9 us
  local copies, waits for them, and re-layouts: 22.5 us -> 31.2 us
  Pallas kernels: 25.6 us -> 34.3 us
  starting transfers between devices: 57.7 us -> 51.1 us
  other arithmetic: 12 us -> 17.3 us
    ppermute x15, waiting for transfers between devices: 49.3 us -> 14.6 us  [from_line(): return lax.ppermute(x, LINE, [((i + k) % 4, i) for i in range(4)])]
    all_to_all x0 -> x1, blocking collectives: none -> 11.9 us  [stats_exchange(): return lax.all_to_all(x, (LINE, CORE), 0, 0, tiled=True)]
    pallas_call x2 -> x4, Pallas kernels: 18.1 us -> 27.7 us  [the longest x1 9.84 us: query_grads(): pl.pallas_call(functools.partial(query_kernel, scale=scale), in_specs=[SM...]
    ppermute x15, starting transfers between devices: 27 us -> 20.2 us  [from_line(): return lax.ppermute(x, LINE, [((i + k) % 4, i) for i in range(4)])]
    all_to_all x1 -> x0, waiting for transfers between devices: 5.16 us -> none  [stats_exchange(): return lax.all_to_all(x, (LINE, CORE), 0, 0, tiled=True)]
    ppermute x3, waiting for transfers between devices: 2.11 us -> 6.18 us  [to_line(): return lax.ppermute(x, LINE, [(i, (i + k) % 4) for i in range(4)])]
    unnamed x47 -> x61, local copies, waits for them, and re-layouts: 11.3 us -> 15.4 us
    all_to_all x1 -> x0, starting transfers between devices: 3.97 us -> none  [stats_exchange(): return lax.all_to_all(x, (LINE, CORE), 0, 0, tiled=True)]
  transfers between devices with their start and end apart: 28 -> 28, of which waited for: 15 -> 13; matrix products, arithmetic and copies ran while one was open for 16% -> 25% of each run, Pallas kernels for 4% -> 15%
where the time goes in v3:
time: 204 us; the launch traced here: 203 us
  starting transfers between devices  51.1 us (25%)
  waiting for transfers between devices  36.6 us (18%)
  Pallas kernels  34.3 us (17%)
  local copies, waits for them, and re-layouts  31.2 us (15%)
  other arithmetic  17.3 us (8%)
  matrix products  14.1 us (7%)
  blocking collectives  11.9 us (6%)
  between operations  6.11 us (3%)
    all_to_all x4, starting transfers between devices, plane_exchange(): return lax.all_to_all(x, PLANE, 0, 0, tiled=True)  26.7 us
    ppermute x15, starting transfers between devices, from_line(): return lax.ppermute(x, LINE, [((i + k) % 4, i) for i in range(4)])  20.2 us
    unnamed x61, local copies, waits for them, and re-layouts  15.4 us
    all_to_all x4, waiting for transfers between devices, plane_exchange(): return lax.all_to_all(x, PLANE, 0, 0, tiled=True)  14.6 us
    ppermute x15, waiting for transfers between devices, from_line(): return lax.ppermute(x, LINE, [((i + k) % 4, i) for i in range(4)])  14.6 us
    all_to_all x1, blocking collectives, stats_exchange(): return lax.all_to_all(x, (LINE, CORE), 0, 0, tiled=True)  11.9 us
    pallas_call x1, Pallas kernels, query_grads(): pl.pallas_call(functools.partial(query_kernel, scale=scale), in_specs=[SM...  9.84 us
    pallas_call x1, Pallas kernels, score_grads(): pl.pallas_call(functools.partial(grads_kernel, scale=scale), in_specs=[VM...  9.23 us
  transfers between devices with their start and end apart: 28, of which 13 were waited for; matrix products, arithmetic and copies ran while one was open for 25% of the time, Pallas kernels for 15%

profile of v3, /device:TPU:0, one launch (start us, length us, event | category | flops | bytes accessed | tf_op | source)
XLA Modules:
  0.0 202.6 jit_solution(12064065373912939412)
XLA Ops:
  3.6 3.3 %convolution_convert_fusion.1 = bf16[256,384]{1,0:T(8,128)(2,1)} fusion(bf16[1536,384]{1,0:T(8,128)(2,1)} %param.11, bf16[768,1536]{1,0:T(8,128)(2,1)S(1)} %copy-done, bf16[128,768]{1,0:T(8,128)(2,1)S(1)} %get-tuple-element.77, bf16[128,768]{1,0:T(8,128)(2,1)S(1)} %get-tuple-element.100), kind=kOutput, calls=%fused_computation.17 | convolution fusion | flops 910393344 | bytes 4128768 | tf_op jit(solution)/shard_map/dot_general | solution.py:319
  10.3 2.9 %collective-permute-start.1 = (bf16[128,384]{1,0:T(8,128)(2,1)}, bf16[128,384]{1,0:T(8,128)(2,1)}, u32[]{:S(2)}, u32[]{:S(2)}) collective-permute-start(bf16[128,384]{1,0:T(8,128)(2,1)} %get-tuple-element.84), channel_id=1, source_target_pairs={{4,0},{6,2},{0,4},{2,6},{5,1},{7,3},{1,5},{3,7},{12,8},{14,10},{8,... | collective-permute-start | bytes 294920 | tf_op jit(solution)/shard_map/ppermute | solution.py:44
  20.1 7.9 %all-to-all-start = ((bf16[16,8,1664]{2,1,0:T(8,128)(2,1)}), bf16[16,8,1664]{2,1,0:T(8,128)(2,1)}, u32[]{:S(2)}, u32[]{:S(2)}) async-start(bf16[16,8,1664]{2,1,0:T(8,128)(2,1)} %fusion.31), calls=%async_computation | async-start | bytes 851968 | tf_op jit(solution)/shard_map/all_to_all | solution.py:36
  45.9 7.4 %all-to-all-start.1 = ((bf16[16,136,384]{2,1,0:T(8,128)(2,1)}), bf16[16,136,384]{2,1,0:T(8,128)(2,1)}, u32[]{:S(2)}, u32[]{:S(2)}) async-start(bf16[16,136,384]{2,1,0:T(8,128)(2,1)} %broadcast_in_dim.81), calls=%async_computation.1 | async-start | bytes 3342336 | tf_op jit(solution)/shard_map/all_to_all | solution.py:36
  59.9 4.4 %collective-permute-done.5 = bf16[16,384]{1,0:T(8,128)(2,1)S(1)} collective-permute-done((bf16[16,384]{1,0:T(8,128)(2,1)S(1)}, bf16[16,384]{1,0:T(8,128)(2,1)S(1)}, u32[]{:S(2)}, u32[]{:S(2)}) %collective-permute-start.5) | collective-permute-done | bytes 12320 | tf_op jit(solution)/shard_map/ppermute | solution.py:44
  71.0 5.7 %all-to-all-done.1 = bf16[16,136,384]{2,1,0:T(8,128)(2,1)} async-done(((bf16[16,136,384]{2,1,0:T(8,128)(2,1)}), bf16[16,136,384]{2,1,0:T(8,128)(2,1)}, u32[]{:S(2)}, u32[]{:S(2)}) %all-to-all-start.1) | async-done | bytes 1671200 | tf_op jit(solution)/shard_map/all_to_all | solution.py:36
  76.7 6.7 %score_stats.1 = (bf16[1088,384]{1,0:T(8,128)(2,1)}, s32[1,1088]{1,0:T(1,128)}, f32[64,1088]{1,0:T(8,128)}) custom-call(s32[29]{0:T(128)} %concatenate.57.sc, bf16[512,384]{1,0:T(8,128)(2,1)} %copy-done.5, bf16[512,384]{1,0:T(8,128)(2,1)} %copy-done.14, bf16[64,384]{1,0:T(8,128)(2,1)} %copy-done.16, bf16[64,384]{1,0:T(8,128)(2,1)} %copy-done.17, ...), custom_call_target="tpu_custom_call" | custom-call | tf_op jit(solution)/shard_map/score_stats/pallas_call | solution.py:229
  83.4 11.9 %all_to_all.53 = f32[8,8,1088]{2,1,0:T(8,128)} all-to-all(f32[8,8,1088]{2,1,0:T(8,128)} %bitcast.48), channel_id=1, replica_groups=mesh['dp_0'=4,'dp_1'=4,'dp_2'=4,'dp_3'=2] {'dp_2','dp_3'}, dimensions={0} | all-to-all | bytes 557056 | tf_op jit(solution)/shard_map/all_to_all | solution.py:40
  95.3 9.2 %score_grads.1 = (bf16[2304,384]{1,0:T(8,128)(2,1)}, bf16[2176,1088]{1,0:T(8,128)(2,1)}) custom-call(f32[64,1088]{1,0:T(8,128)} %bitcast.47, bf16[1088,384]{1,0:T(8,128)(2,1)} %get-tuple-element.33.q, bf16[2176,384]{1,0:T(8,128)(2,1)} %bitcast.10.p, s32[1,1088]{1,0:T(1,128)} %get-tuple-element.34.place), custom_call_target="tpu_custom_call" | custom-call | tf_op jit(solution)/shard_map/score_grads/pallas_call | solution.py:246
  104.5 9.8 %query_grads.1 = (f32[4,136,384]{2,1,0:T(8,128)}, f32[4,136,384]{2,1,0:T(8,128)}) custom-call(s32[29]{0:T(128)} %concatenate.57.sc, bf16[2176,384]{1,0:T(8,128)(2,1)} %bitcast.10.p, bf16[2176,1088]{1,0:T(8,128)(2,1)} %get-tuple-element.36.g), custom_call_target="tpu_custom_call" | custom-call | tf_op jit(solution)/shard_map/query_grads/pallas_call | solution.py:260
  120.0 2.7 %copy.26 = bf16[1088,768]{1,0:T(8,128)(2,1)} copy(bf16[1088,768]{1,0:T(8,128)(2,1)} %slice_dynamic-update-slice_fusion.10) | data formatting | bytes 3342336
  129.3 4.5 %all-to-all-start.3 = ((bf16[16,144,384]{2,1,0:T(8,128)(2,1)}), bf16[16,144,384]{2,1,0:T(8,128)(2,1)}, u32[]{:S(2)}, u32[]{:S(2)}) async-start(bf16[16,144,384]{2,1,0:T(8,128)(2,1)} %bitcast.46), calls=%async_computation.3 | async-start | bytes 3538944 | tf_op jit(solution)/shard_map/all_to_all | solution.py:36
  135.9 2.7 %collective-permute-start.11 = (bf16[136,384]{1,0:T(8,128)(2,1)S(1)}, bf16[136,384]{1,0:T(8,128)(2,1)S(1)}, u32[]{:S(2)}, u32[]{:S(2)}) collective-permute-start(bf16[136,384]{1,0:T(8,128)(2,1)S(1)} %get-tuple-element.74), channel_id=1, source_target_pairs={{0,6},{2,0},{4,2},{6,4},{1,7},{3,1},{5,3},{7,5},{8,14},{10,8},{12,... | collective-permute-start | bytes 313352 | tf_op jit(solution)/shard_map/ppermute | solution.py:48
  138.6 2.8 %collective-permute-done.9 = bf16[136,384]{1,0:T(8,128)(2,1)S(1)} collective-permute-done((bf16[136,384]{1,0:T(8,128)(2,1)S(1)}, bf16[136,384]{1,0:T(8,128)(2,1)S(1)}, u32[]{:S(2)}, u32[]{:S(2)}) %collective-permute-start.9) | collective-permute-done | bytes 104480 | tf_op jit(solution)/shard_map/ppermute | solution.py:48
  144.9 3.3 %collective-permute-start.13 = (bf16[136,384]{1,0:T(8,128)(2,1)S(1)}, bf16[136,384]{1,0:T(8,128)(2,1)S(1)}, u32[]{:S(2)}, u32[]{:S(2)}) collective-permute-start(bf16[136,384]{1,0:T(8,128)(2,1)S(1)} %fusion.46), channel_id=1, source_target_pairs={{4,0},{6,2},{0,4},{2,6},{5,1},{7,3},{1,5},{3,7},{12,8},{14,10},{8,... | collective-permute-start | bytes 313352 | tf_op jit(solution)/shard_map/ppermute | solution.py:44
  148.2 3.4 %collective-permute-done.14 = bf16[136,384]{1,0:T(8,128)(2,1)S(1)} collective-permute-done((bf16[136,384]{1,0:T(8,128)(2,1)S(1)}, bf16[136,384]{1,0:T(8,128)(2,1)S(1)}, u32[]{:S(2)}, u32[]{:S(2)}) %collective-permute-start.14) | collective-permute-done | bytes 104480 | tf_op jit(solution)/shard_map/ppermute | solution.py:44
  155.7 4.1 %fusion.21 = (f32[192,1088]{1,0:T(8,128)}, bf16[192,1088]{1,0:T(8,128)(2,1)}) fusion(bf16[192,768]{1,0:T(8,128)(2,1)S(1)} %copy-done.24, bf16[1088,768]{1,0:T(8,128)(2,1)} %get-tuple-element.52.rows), kind=kOutput, calls=%fused_computation.32 | convolution fusion | flops 324833280 | bytes 3219456 | tf_op jit(solution)/shard_map/dot_general | solution.py:389
  164.4 3.0 %collective-permute-start.21 = (bf16[136,384]{1,0:T(8,128)(2,1)S(1)}, bf16[136,384]{1,0:T(8,128)(2,1)S(1)}, u32[]{:S(2)}, u32[]{:S(2)}) collective-permute-start(bf16[136,384]{1,0:T(8,128)(2,1)S(1)} %slice.216), channel_id=1, source_target_pairs={{4,0},{6,2},{0,4},{2,6},{5,1},{7,3},{1,5},{3,7},{12,8},{14,10},{8,... | collective-permute-start | bytes 313352 | tf_op jit(solution)/shard_map/ppermute | solution.py:44
  167.8 2.6 %collective-permute-done.22 = bf16[136,384]{1,0:T(8,128)(2,1)S(1)} collective-permute-done((bf16[136,384]{1,0:T(8,128)(2,1)S(1)}, bf16[136,384]{1,0:T(8,128)(2,1)S(1)}, u32[]{:S(2)}, u32[]{:S(2)}) %collective-permute-start.22) | collective-permute-done | bytes 104480 | tf_op jit(solution)/shard_map/ppermute | solution.py:44
  170.4 2.5 %collective-permute-done.21 = bf16[136,384]{1,0:T(8,128)(2,1)S(1)} collective-permute-done((bf16[136,384]{1,0:T(8,128)(2,1)S(1)}, bf16[136,384]{1,0:T(8,128)(2,1)S(1)}, u32[]{:S(2)}, u32[]{:S(2)}) %collective-permute-start.21) | collective-permute-done | bytes 104480 | tf_op jit(solution)/shard_map/ppermute | solution.py:44
  173.3 4.3 %first_weights.1.sums = f32[192,1152]{1,0:T(8,128)} custom-call(bf16[544,384]{1,0:T(8,128)(2,1)} %copy-done.3, bf16[544,384]{1,0:T(8,128)(2,1)} %copy-done.13, bf16[1088,768]{1,0:T(8,128)(2,1)} %copy-done.2, bf16[192,1088]{1,0:T(8,128)(2,1)} %get-tuple-element.49.hidden, f32[192,1088]{1,0:T(8,128)} %get-tuple-element.50.slope, bf16[192,384]{1,0:T(8,128)(2,1)} %fusion.9.second), custom_call_target="tpu_custom_call" | custom-call | tf_op jit(solution)/shard_map/first_weights/pallas_call | solution.py:275
  177.6 4.3 %last_weights.1 = bf16[128,1792]{1,0:T(8,128)(2,1)} custom-call(f32[192,1152]{1,0:T(8,128)} %first_weights.1.sums, bf16[544,384]{1,0:T(8,128)(2,1)} %copy-done.4, bf16[544,384]{1,0:T(8,128)(2,1)} %collective-permute-done.23.de_far, bf16[1088,768]{1,0:T(8,128)(2,1)} %get-tuple-element.52.rows, bf16[192,1088]{1,0:T(8,128)(2,1)} %get-tuple-element.53.hidden, ...), custom_call_target="tpu_custom_call" | custom-call | tf_op jit(solution)/shard_map/last_weights/pallas_call | solution.py:283
  181.9 6.9 %all-to-all-start.4 = ((bf16[16,8,1792]{2,1,0:T(8,128)(2,1)}), bf16[16,8,1792]{2,1,0:T(8,128)(2,1)S(1)}, u32[]{:S(2)}, u32[]{:S(2)}) async-start(bf16[16,8,1792]{2,1,0:T(8,128)(2,1)} %bitcast.45), calls=%async_computation.4 | async-start | bytes 917504 | tf_op jit(solution)/shard_map/all_to_all | solution.py:36
  191.2 8.9 %all-to-all-done.4 = bf16[16,8,1792]{2,1,0:T(8,128)(2,1)S(1)} async-done(((bf16[16,8,1792]{2,1,0:T(8,128)(2,1)}), bf16[16,8,1792]{2,1,0:T(8,128)(2,1)S(1)}, u32[]{:S(2)}, u32[]{:S(2)}) %all-to-all-start.4) | async-done | bytes 458784 | tf_op jit(solution)/shard_map/all_to_all | solution.py:36
  (152 shorter events, 71.3 us)
Async XLA Ops:
  8.6 47.3 %collective-permute-start.2 = (bf16[128,384]{1,0:T(8,128)(2,1)}, bf16[128,384]{1,0:T(8,128)(2,1)}, u32[]{:S(2)}, u32[]{:S(2)}) collective-permute-start(bf16[128,384]{1,0:T(8,128)(2,1)} %get-tuple-element.84), channel_id=1, source_target_pairs={{6,0},{0,2},{2,4},{4,6},{7,1},{1,3},{3,5},{5,7},{14,8},{8,10},{10,... | collective-permute-start | bytes 294920 | tf_op jit(solution)/shard_map/ppermute | solution.py:44
  10.3 45.6 %collective-permute-start.1 = (bf16[128,384]{1,0:T(8,128)(2,1)}, bf16[128,384]{1,0:T(8,128)(2,1)}, u32[]{:S(2)}, u32[]{:S(2)}) collective-permute-start(bf16[128,384]{1,0:T(8,128)(2,1)} %get-tuple-element.84), channel_id=1, source_target_pairs={{4,0},{6,2},{0,4},{2,6},{5,1},{7,3},{1,5},{3,7},{12,8},{14,10},{8,... | collective-permute-start | bytes 294920 | tf_op jit(solution)/shard_map/ppermute | solution.py:44
  13.2 42.7 %collective-permute-start = (bf16[128,384]{1,0:T(8,128)(2,1)}, bf16[128,384]{1,0:T(8,128)(2,1)}, u32[]{:S(2)}, u32[]{:S(2)}) collective-permute-start(bf16[128,384]{1,0:T(8,128)(2,1)} %get-tuple-element.84), channel_id=1, source_target_pairs={{2,0},{4,2},{6,4},{0,6},{3,1},{5,3},{7,5},{1,7},{10,8},{12,10},{14... | collective-permute-start | bytes 294920 | tf_op jit(solution)/shard_map/ppermute | solution.py:44
  20.1 19.5 %all-to-all-start = ((bf16[16,8,1664]{2,1,0:T(8,128)(2,1)}), bf16[16,8,1664]{2,1,0:T(8,128)(2,1)}, u32[]{:S(2)}, u32[]{:S(2)}) async-start(bf16[16,8,1664]{2,1,0:T(8,128)(2,1)} %fusion.31), calls=%async_computation | async-start | bytes 851968 | tf_op jit(solution)/shard_map/all_to_all | solution.py:36
  45.9 30.8 %all-to-all-start.1 = ((bf16[16,136,384]{2,1,0:T(8,128)(2,1)}), bf16[16,136,384]{2,1,0:T(8,128)(2,1)}, u32[]{:S(2)}, u32[]{:S(2)}) async-start(bf16[16,136,384]{2,1,0:T(8,128)(2,1)} %broadcast_in_dim.81), calls=%async_computation.1 | async-start | bytes 3342336 | tf_op jit(solution)/shard_map/all_to_all | solution.py:36
  57.0 8.7 %collective-permute-start.3 = (bf16[512,384]{1,0:T(8,128)(2,1)S(1)}, bf16[512,384]{1,0:T(8,128)(2,1)S(1)}, u32[]{:S(2)}, u32[]{:S(2)}) collective-permute-start(bf16[512,384]{1,0:T(8,128)(2,1)S(1)} %pad_maximum_fusion.3.q_own), channel_id=1, source_target_pairs={{0,1},{1,0},{2,3},{3,2},{4,5},{5,4},{6,7},{7,6},{8,9},{9,8},{10,11... | collective-permute-start | bytes 1179656 | tf_op jit(solution)/shard_map/ppermute | solution.py:32
  57.1 7.3 %collective-permute-start.6 = (bf16[16,384]{1,0:T(8,128)(2,1)S(1)}, bf16[16,384]{1,0:T(8,128)(2,1)S(1)}, u32[]{:S(2)}, u32[]{:S(2)}) collective-permute-start(bf16[16,384]{1,0:T(8,128)(2,1)S(1)} %pad_maximum_fusion.6), channel_id=1, source_target_pairs={{6,0},{0,2},{2,4},{4,6},{7,1},{1,3},{3,5},{5,7},{14,8},{8,10},{10,... | collective-permute-start | bytes 36872 | tf_op jit(solution)/shard_map/ppermute | solution.py:44
  59.2 5.2 %collective-permute-start.5 = (bf16[16,384]{1,0:T(8,128)(2,1)S(1)}, bf16[16,384]{1,0:T(8,128)(2,1)S(1)}, u32[]{:S(2)}, u32[]{:S(2)}) collective-permute-start(bf16[16,384]{1,0:T(8,128)(2,1)S(1)} %pad_maximum_fusion.6), channel_id=1, source_target_pairs={{4,0},{6,2},{0,4},{2,6},{5,1},{7,3},{1,5},{3,7},{12,8},{14,10},{8,... | collective-permute-start | bytes 36872 | tf_op jit(solution)/shard_map/ppermute | solution.py:44
  65.7 48.7 %collective-permute-start.18 = (bf16[272,768]{1,0:T(8,128)(2,1)S(1)}, bf16[272,768]{1,0:T(8,128)(2,1)}, u32[]{:S(2)}, u32[]{:S(2)}) collective-permute-start(bf16[272,768]{1,0:T(8,128)(2,1)S(1)} %pad_maximum_fusion.1), channel_id=1, source_target_pairs={{6,0},{0,2},{2,4},{4,6},{7,1},{1,3},{3,5},{5,7},{14,8},{8,10},{10,... | collective-permute-start | bytes 1253384 | tf_op jit(solution)/shard_map/ppermute | solution.py:44
  66.5 47.9 %collective-permute-start.17 = (bf16[272,768]{1,0:T(8,128)(2,1)S(1)}, bf16[272,768]{1,0:T(8,128)(2,1)}, u32[]{:S(2)}, u32[]{:S(2)}) collective-permute-start(bf16[272,768]{1,0:T(8,128)(2,1)S(1)} %pad_maximum_fusion.1), channel_id=1, source_target_pairs={{4,0},{6,2},{0,4},{2,6},{5,1},{7,3},{1,5},{3,7},{12,8},{14,10},{8,... | collective-permute-start | bytes 1253384 | tf_op jit(solution)/shard_map/ppermute | solution.py:44
  68.5 45.9 %collective-permute-start.16 = (bf16[272,768]{1,0:T(8,128)(2,1)S(1)}, bf16[272,768]{1,0:T(8,128)(2,1)}, u32[]{:S(2)}, u32[]{:S(2)}) collective-permute-start(bf16[272,768]{1,0:T(8,128)(2,1)S(1)} %pad_maximum_fusion.1), channel_id=1, source_target_pairs={{2,0},{4,2},{6,4},{0,6},{3,1},{5,3},{7,5},{1,7},{10,8},{12,10},{14... | collective-permute-start | bytes 1253384 | tf_op jit(solution)/shard_map/ppermute | solution.py:44
  114.4 19.5 %collective-permute-start.8 = (f32[4,136,384]{2,1,0:T(8,128)}, f32[4,136,384]{2,1,0:T(8,128)}, u32[]{:S(2)}, u32[]{:S(2)}) collective-permute-start(f32[4,136,384]{2,1,0:T(8,128)} %get-tuple-element.38), channel_id=1, source_target_pairs={{0,1},{1,0},{2,3},{3,2},{4,5},{5,4},{6,7},{7,6},{8,9},{9,8},{10,11... | collective-permute-start | bytes 2506760 | tf_op jit(solution)/shard_map/ppermute | solution.py:32
  128.8 24.4 %collective-permute-start.19 = (bf16[1088,768]{1,0:T(8,128)(2,1)}, bf16[1088,768]{1,0:T(8,128)(2,1)}, u32[]{:S(2)}, u32[]{:S(2)}) collective-permute-start(bf16[1088,768]{1,0:T(8,128)(2,1)} %get-tuple-element.66), channel_id=1, source_target_pairs={{0,1},{1,0},{2,3},{3,2},{4,5},{5,4},{6,7},{7,6},{8,9},{9,8},{10,11... | collective-permute-start | bytes 5013512 | tf_op jit(solution)/shard_map/ppermute | solution.py:32
  129.3 32.5 %all-to-all-start.3 = ((bf16[16,144,384]{2,1,0:T(8,128)(2,1)}), bf16[16,144,384]{2,1,0:T(8,128)(2,1)}, u32[]{:S(2)}, u32[]{:S(2)}) async-start(bf16[16,144,384]{2,1,0:T(8,128)(2,1)} %bitcast.46), calls=%async_computation.3 | async-start | bytes 3538944 | tf_op jit(solution)/shard_map/all_to_all | solution.py:36
  135.3 6.1 %collective-permute-start.9 = (bf16[136,384]{1,0:T(8,128)(2,1)S(1)}, bf16[136,384]{1,0:T(8,128)(2,1)S(1)}, u32[]{:S(2)}, u32[]{:S(2)}) collective-permute-start(bf16[136,384]{1,0:T(8,128)(2,1)S(1)} %get-tuple-element.73), channel_id=1, source_target_pairs={{0,2},{2,4},{4,6},{6,0},{1,3},{3,5},{5,7},{7,1},{8,10},{10,12},{12... | collective-permute-start | bytes 313352 | tf_op jit(solution)/shard_map/ppermute | solution.py:48
  135.9 7.0 %collective-permute-start.11 = (bf16[136,384]{1,0:T(8,128)(2,1)S(1)}, bf16[136,384]{1,0:T(8,128)(2,1)S(1)}, u32[]{:S(2)}, u32[]{:S(2)}) collective-permute-start(bf16[136,384]{1,0:T(8,128)(2,1)S(1)} %get-tuple-element.74), channel_id=1, source_target_pairs={{0,6},{2,0},{4,2},{6,4},{1,7},{3,1},{5,3},{7,5},{8,14},{10,8},{12,... | collective-permute-start | bytes 313352 | tf_op jit(solution)/shard_map/ppermute | solution.py:48
  138.6 6.2 %collective-permute-start.10 = (bf16[136,384]{1,0:T(8,128)(2,1)S(1)}, bf16[136,384]{1,0:T(8,128)(2,1)S(1)}, u32[]{:S(2)}, u32[]{:S(2)}) collective-permute-start(bf16[136,384]{1,0:T(8,128)(2,1)S(1)} %get-tuple-element.75), channel_id=1, source_target_pairs={{0,4},{2,6},{4,0},{6,2},{1,5},{3,7},{5,1},{7,3},{8,12},{10,14},{12... | collective-permute-start | bytes 313352 | tf_op jit(solution)/shard_map/ppermute | solution.py:48
  144.8 6.7 %collective-permute-start.14 = (bf16[136,384]{1,0:T(8,128)(2,1)S(1)}, bf16[136,384]{1,0:T(8,128)(2,1)S(1)}, u32[]{:S(2)}, u32[]{:S(2)}) collective-permute-start(bf16[136,384]{1,0:T(8,128)(2,1)S(1)} %fusion.46), channel_id=1, source_target_pairs={{6,0},{0,2},{2,4},{4,6},{7,1},{1,3},{3,5},{5,7},{14,8},{8,10},{10,... | collective-permute-start | bytes 313352 | tf_op jit(solution)/shard_map/ppermute | solution.py:44
  144.9 7.8 %collective-permute-start.13 = (bf16[136,384]{1,0:T(8,128)(2,1)S(1)}, bf16[136,384]{1,0:T(8,128)(2,1)S(1)}, u32[]{:S(2)}, u32[]{:S(2)}) collective-permute-start(bf16[136,384]{1,0:T(8,128)(2,1)S(1)} %fusion.46), channel_id=1, source_target_pairs={{4,0},{6,2},{0,4},{2,6},{5,1},{7,3},{1,5},{3,7},{12,8},{14,10},{8,... | collective-permute-start | bytes 313352 | tf_op jit(solution)/shard_map/ppermute | solution.py:44
  153.1 8.7 %collective-permute-start.15 = (bf16[544,384]{1,0:T(8,128)(2,1)S(1)}, bf16[544,384]{1,0:T(8,128)(2,1)S(1)}, u32[]{:S(2)}, u32[]{:S(2)}) collective-permute-start(bf16[544,384]{1,0:T(8,128)(2,1)S(1)} %pad_maximum_fusion.de_own), channel_id=1, source_target_pairs={{0,1},{1,0},{2,3},{3,2},{4,5},{5,4},{6,7},{7,6},{8,9},{9,8},{10,11... | collective-permute-start | bytes 1253384 | tf_op jit(solution)/shard_map/ppermute | solution.py:32
  163.7 6.7 %collective-permute-start.22 = (bf16[136,384]{1,0:T(8,128)(2,1)S(1)}, bf16[136,384]{1,0:T(8,128)(2,1)S(1)}, u32[]{:S(2)}, u32[]{:S(2)}) collective-permute-start(bf16[136,384]{1,0:T(8,128)(2,1)S(1)} %slice.216), channel_id=1, source_target_pairs={{6,0},{0,2},{2,4},{4,6},{7,1},{1,3},{3,5},{5,7},{14,8},{8,10},{10,... | collective-permute-start | bytes 313352 | tf_op jit(solution)/shard_map/ppermute | solution.py:44
  164.4 8.5 %collective-permute-start.21 = (bf16[136,384]{1,0:T(8,128)(2,1)S(1)}, bf16[136,384]{1,0:T(8,128)(2,1)S(1)}, u32[]{:S(2)}, u32[]{:S(2)}) collective-permute-start(bf16[136,384]{1,0:T(8,128)(2,1)S(1)} %slice.216), channel_id=1, source_target_pairs={{4,0},{6,2},{0,4},{2,6},{5,1},{7,3},{1,5},{3,7},{12,8},{14,10},{8,... | collective-permute-start | bytes 313352 | tf_op jit(solution)/shard_map/ppermute | solution.py:44
  167.4 5.7 %collective-permute-start.20 = (bf16[136,384]{1,0:T(8,128)(2,1)S(1)}, bf16[136,384]{1,0:T(8,128)(2,1)S(1)}, u32[]{:S(2)}, u32[]{:S(2)}) collective-permute-start(bf16[136,384]{1,0:T(8,128)(2,1)S(1)} %slice.216), channel_id=1, source_target_pairs={{2,0},{4,2},{6,4},{0,6},{3,1},{5,3},{7,5},{1,7},{10,8},{12,10},{14... | collective-permute-start | bytes 313352 | tf_op jit(solution)/shard_map/ppermute | solution.py:44
  181.9 18.3 %all-to-all-start.4 = ((bf16[16,8,1792]{2,1,0:T(8,128)(2,1)}), bf16[16,8,1792]{2,1,0:T(8,128)(2,1)S(1)}, u32[]{:S(2)}, u32[]{:S(2)}) async-start(bf16[16,8,1792]{2,1,0:T(8,128)(2,1)} %bitcast.45), calls=%async_computation.4 | async-start | bytes 917504 | tf_op jit(solution)/shard_map/all_to_all | solution.py:36
  (29 other events, 232.9 us)

commit v4 on v3

--- a/solution.py
+++ b/solution.py
@@ -20,7 +20,6 @@
 BLOCK = LOW + UNIT
 CHUNK = 144
 PAIR = 2 * BLOCK
-TILE = 256
 LOG2E = 1.4426950408889634
 
 
@@ -75,6 +74,65 @@
 
 def nt_dot(a, b):
     return lax.dot_general(a, b, (((1,), (1,)), ((), ())), preferred_element_type=F32)
+
+
+def pack_kernel(counts, where, q, p, pos, out, heavy_out):
+    heavy_at = jnp.int32(0)
+    for s in range(16):
+        heavy_at += jnp.where(counts[s * 8 + where[0]] > LOW, s, 0)
+    heavy_out[0] = heavy_at
+    width = q.shape[1]
+    high = lax.shift_right_logical(pos[1:2], 7).astype(F32)
+    low = jnp.bitwise_and(pos[1:2], 127).astype(F32)
+    line = lax.broadcasted_iota(jnp.int32, (UNIT, LOW), 0)
+    code = jnp.where(line == 2, high, jnp.where(line == 3, low, 0.0)).astype(BF16)
+    for u in range(16):
+        slot = jnp.bitwise_and(heavy_at + u, 15)
+        out[slot, :, :width] = q[u * UNIT : (u + 1) * UNIT]
+        out[slot, :, width : 2 * width] = p[u * UNIT : (u + 1) * UNIT]
+        out[slot, :, 2 * width :] = code
+
+
+def gelu_parts(v):
+    square = v * v
+    t = jnp.tanh(0.7978845608028654 * (v + 0.044715 * (square * v)))
+    grown = 0.5 * (1.0 + t)
+    slope = grown + (0.5 * v) * (1.0 - t * t) * (
+        0.7978845608028654 * (1.0 + 3 * 0.044715 * square)
+    )
+    return (v * grown, slope)
+
+
+def tail_kernel(heavy_at, arrived, base_p, pos, w_first, w_second, p_out, q_out, feats_out):
+    width = w_first.shape[0]
+    tail = arrived[heavy_at[0]]
+    feats = jnp.concatenate([tail[:, :width], tail[:, width : 2 * width]], axis=0)
+    feats_out[...] = feats
+    pre = jnp.dot(feats, w_first[...], preferred_element_type=F32)
+    hidden = gelu_parts(pre)[0].astype(BF16)
+    emb = jnp.dot(hidden, w_second[...], preferred_element_type=F32).astype(BF16)
+    for s in range(p_out.shape[0]):
+        p_out[s, :LOW] = base_p[...]
+        p_out[s, LOW:] = emb[UNIT:]
+    high = lax.shift_right_logical(pos[0:1], 7).astype(F32)
+    low = jnp.bitwise_and(pos[0:1], 127).astype(F32)
+    line = lax.broadcasted_iota(jnp.int32, (UNIT, LOW), 0)
+    code = tail[:, 2 * width :].astype(F32)
+    code = jnp.where(line == 0, high, jnp.where(line == 1, low, code)).astype(BF16)
+    q_out[:UNIT] = emb[:UNIT]
+    q_out[UNIT:] = jnp.zeros((UNIT, q_out.shape[1]), BF16)
+    q_out[UNIT:, :LOW] = code
+
+
+def units_kernel(*refs):
+    blocks, (first, rows_q, rows_p, hidden_q, hidden_p, slope_q, slope_p) = refs[:8], refs[8:]
+    for k, block in enumerate(blocks):
+        rows_q[k * BLOCK : (k + 1) * BLOCK] = block[:BLOCK]
+        rows_p[k * BLOCK : (k + 1) * BLOCK] = block[BLOCK:]
+    for rows, hidden, slope in ((rows_q, hidden_q, slope_q), (rows_p, hidden_p, slope_p)):
+        value, gain = gelu_parts(nt_dot(first[...], rows[...]))
+        hidden[...] = value.astype(BF16)
+        slope[...] = gain
 
 
 def stats_kernel(
@@ -171,13 +229,12 @@
         def _():
             far[b - 4, rows] = part
 
-    for k in range(4):
-        dq = jnp.dot(turned[...], g[:, k * TILE : (k + 1) * TILE], preferred_element_type=F32)
+    for first, size in ((0, 4 * LOW), (4 * LOW, 4 * LOW + 8 * UNIT)):
+        dq = jnp.dot(turned[...], g[:, first : first + size], preferred_element_type=F32)
         dq = (scale * dq).T
-        for half in range(2):
-            put(2 * k + half, slice(0, LOW), dq[half * LOW : (half + 1) * LOW])
-    dq = jnp.dot(turned[...], g[:, 8 * LOW :], preferred_element_type=F32)
-    dq = (scale * dq).T
+        for k in range(4):
+            put(first // LOW + k, slice(0, LOW), dq[k * LOW : (k + 1) * LOW])
+    dq = dq[4 * LOW :]
     for j in range(8):
         put(j, slice(LOW, BLOCK), dq[j * UNIT : (j + 1) * UNIT])
 
@@ -221,6 +278,51 @@
 
 VMEM = pl.BlockSpec(memory_space=pltpu.VMEM)
 SMEM = pl.BlockSpec(memory_space=pltpu.SMEM)
+
+
+def pack_overflow(counts, where, q, p, pos):
+    width = q.shape[1]
+    half = pl.BlockSpec((LOW, width), lambda i: (1, 0))
+    return pl.pallas_call(
+        pack_kernel,
+        grid=(1,),
+        in_specs=[SMEM, SMEM, half, half, pl.BlockSpec((2, LOW), lambda i: (0, 0))],
+        out_specs=[pl.BlockSpec((16, UNIT, 2 * width + LOW), lambda i: (0, 0, 0)), SMEM],
+        out_shape=[
+            jax.ShapeDtypeStruct((16, UNIT, 2 * width + LOW), BF16),
+            jax.ShapeDtypeStruct((1,), jnp.int32),
+        ],
+        name="pack_overflow",
+    )(counts, where, q, p, pos)
+
+
+def tail_rows(heavy_at, arrived, base_p, pos, w_first, w_second):
+    emb_width = w_second.shape[1]
+    return pl.pallas_call(
+        tail_kernel,
+        in_specs=[SMEM] + [VMEM] * 5,
+        out_specs=[VMEM] * 3,
+        out_shape=[
+            jax.ShapeDtypeStruct((16, BLOCK, emb_width), BF16),
+            jax.ShapeDtypeStruct((2 * UNIT, emb_width), BF16),
+            jax.ShapeDtypeStruct((2 * UNIT, w_first.shape[0]), BF16),
+        ],
+        name="tail_rows",
+    )(heavy_at, arrived, base_p, pos, w_first, w_second)
+
+
+def hidden_units(blocks, first):
+    rows = jax.ShapeDtypeStruct((8 * BLOCK, first.shape[1]), BF16)
+    hidden = jax.ShapeDtypeStruct((first.shape[0], 8 * BLOCK), BF16)
+    slope = jax.ShapeDtypeStruct((first.shape[0], 8 * BLOCK), F32)
+    rows_q, rows_p, hidden_q, hidden_p, slope_q, slope_p = pl.pallas_call(
+        units_kernel,
+        in_specs=[VMEM] * 9,
+        out_specs=[VMEM] * 6,
+        out_shape=[rows, rows, hidden, hidden, slope, slope],
+        name="hidden_units",
+    )(*blocks, first)
+    return ((rows_q, hidden_q, slope_q), (rows_p, hidden_p, slope_p))
 
 
 def score_stats(sc, qs, ts, p, scale):
@@ -297,21 +399,11 @@
     group = lax.axis_index((LINE, CORE))
     pairs = BLOCK * lax.axis_size(DP)
 
-    heavy = (counts > LOW).astype(jnp.int32)
-    devices = jnp.arange(counts.shape[0], dtype=jnp.int32)
-    mine = heavy * (devices % 8 == group)
-    heavy_at = jnp.sum(mine * (devices // 8))
-    pos_high = jnp.right_shift(positives, 7).astype(BF16)
-    pos_low = jnp.bitwise_and(positives, 127).astype(BF16)
-    line = jnp.arange(LOW, dtype=jnp.int32)[:, None] % UNIT
-    coded = jnp.where(
-        line == 2, pos_high[LOW:], jnp.where(line == 3, pos_low[LOW:], jnp.zeros((), BF16))
-    )
-    over = jnp.concatenate([query_features[LOW:], passage_features[LOW:], coded], axis=1)
-    over = jnp.concatenate([over, over], axis=0)
-    over = lax.dynamic_slice_in_dim(over, (16 - heavy_at) * UNIT, LOW, 0)
+    pos = positives.reshape(2, LOW)
+    where = jnp.reshape(group, (1,)).astype(jnp.int32)
+    over, heavy_at = pack_overflow(counts, where, query_features, passage_features, pos)
+    over = over.reshape(16 * UNIT, -1)
     arrived = plane_exchange(over)
-    tail = lax.dynamic_slice_in_dim(arrived, heavy_at * UNIT, UNIT, 0)
 
     def tower(x):
         pre = jnp.dot(x, w_first, preferred_element_type=F32)
@@ -321,37 +413,30 @@
     base = tower(jnp.concatenate([query_features[:LOW], passage_features[:LOW]], axis=0))
     qs = gathered(base[:LOW])
 
-    tail_q, tail_p = tail[:, :width], tail[:, width : 2 * width]
-    tail_emb = tower(jnp.concatenate([tail_q, tail_p], axis=0))
-    p_send = jnp.concatenate([base[LOW:], tail_emb[UNIT:]], axis=0)
-    p_send = jnp.broadcast_to(p_send[None], (16, BLOCK, emb_width))
+    p_send, q_tail, tail = tail_rows(
+        heavy_at, arrived.reshape(16, UNIT, -1), base[LOW:], pos, w_first, w_second
+    )
     p_all = plane_exchange(p_send.reshape(16 * BLOCK, emb_width))
-
-    line = line[:UNIT]
-    codes = jnp.where(
-        line == 0,
-        pos_high[None, :LOW],
-        jnp.where(line == 1, pos_low[None, :LOW], tail[:, 2 * width :]),
-    )
-    codes = jnp.pad(codes, ((0, 0), (0, emb_width - LOW)))
-    ts = gathered(jnp.concatenate([tail_emb[:UNIT], codes], axis=0))
-
-    late_counts, group, _ = lax.optimization_barrier((counts, group, base))
+    ts = gathered(q_tail)
+
+    late_counts, group, _ = lax.optimization_barrier((counts, group, q_tail))
     heavy = (late_counts > LOW).astype(jnp.int32)
+    devices = jnp.arange(counts.shape[0], dtype=jnp.int32)
     mine = heavy * (devices % 8 == group)
     offsets = jnp.cumsum(late_counts) - late_counts
     over_start = jnp.sum(mine * offsets) + LOW
     group_start = lax.dynamic_slice_in_dim(offsets.reshape(16, 8), group, 1, 1)[:, 0]
-    scalars = [heavy_at, over_start, lax.axis_index(LINE), lax.axis_index(CORE)]
+    scalars = [heavy_at[0], over_start, lax.axis_index(LINE), lax.axis_index(CORE)]
     scalars = jnp.stack(scalars + [lax.axis_index(PLANE)])
     heavies = jnp.sum(heavy.reshape(16, 8) * jnp.arange(16, dtype=jnp.int32)[:, None], axis=0)
     sc = jnp.concatenate([group_start, scalars, heavies]).astype(jnp.int32)
 
     feats = jnp.concatenate(
-        [query_features[:LOW], tail_q, passage_features[:LOW], tail_p], axis=0
+        [query_features[:LOW], tail[:UNIT], passage_features[:LOW], tail[UNIT:]], axis=0
     )
     feats, _ = lax.optimization_barrier((feats, (qs[1], ts[1])))
     feats = along_line(feats)
+    feats = feats + [swap_core(x) for x in feats]
 
     each = hidden_width // lax.axis_size(DP)
     unit = jnp.arange(16 * each, dtype=jnp.int32)
@@ -379,21 +464,7 @@
         dq_sum = dq_sum + to_line(dq[k].astype(BF16), k).astype(F32)
     dqs = gathered(dq_sum.astype(BF16))
     feats, _ = lax.optimization_barrier((feats, dq_far))
-    feats_own = jnp.concatenate(
-        [x[:BLOCK] for x in feats] + [x[BLOCK:] for x in feats], axis=0
-    )
-    feats_far = swap_core(feats_own)
-    half = 4 * BLOCK
-
-    def units_of(rows):
-        pre = lax.dot_general(
-            first_part, rows, (((1,), (1,)), ((), ())), preferred_element_type=F32
-        )
-        act, pull_back = jax.vjp(gelu_tanh, pre)
-        return (rows, act.astype(BF16), pull_back(jnp.ones_like(pre))[0])
-
-    q_units = units_of(jnp.concatenate([feats_own[:half], feats_far[:half]], axis=0))
-    p_units = units_of(jnp.concatenate([feats_own[half:], feats_far[half:]], axis=0))
+    q_units, p_units = hidden_units(feats, first_part)
     dp_all, dqs, q_units, p_units = lax.optimization_barrier((dp_all, dqs, q_units, p_units))
 
     dp_sum = jnp.sum(dp_all.reshape(16, CHUNK, emb_width).astype(F32), axis=0)

time: 204 us -> 190 us (0.931)
  local copies, waits for them, and re-layouts: 31.2 us -> 10.2 us
  waiting for transfers between devices: 36.6 us -> 54.9 us
  other arithmetic: 17.3 us -> 2.22 us
  Pallas kernels: 34.3 us -> 45.3 us
  matrix products: 14.1 us -> 7.14 us
    pallas_call x0 -> x3, Pallas kernels: none -> 12.9 us  [the longest x1 6.16 us: hidden_units(): pl.pallas_call(units_kernel, in_specs=[VMEM] * 9, out_specs=[VMEM] * 6, o...]
    all_to_all x4, waiting for transfers between devices: 14.6 us -> 25.9 us  [plane_exchange(): return lax.all_to_all(x, PLANE, 0, 0, tiled=True)]
    unnamed x61 -> x53, local copies, waits for them, and re-layouts: 15.4 us -> 4.56 us
    dot_general x2 -> x0, matrix products: 6.1 us -> none  [units_of(): lax.dot_general(first_part, rows, (((1,), (1,)), ((), ())), preferred_ele...]
    ppermute x3, waiting for transfers between devices: 6.18 us -> 11.9 us  [to_line(): return lax.ppermute(x, LINE, [(i, (i + k) % 4) for i in range(4)])]
    slice x5 -> x4, local copies, waits for them, and re-layouts: 6.41 us -> 2.62 us  [the longest x1 1.01 us: body(): query_features[:LOW]]
    another operation x3, other arithmetic: 3.9 us -> 0.36 us
    dot_general x2 -> x1, matrix products: 5.16 us -> 2.62 us  [tower(): return jnp.dot(hidden, w_second, preferred_element_type=F32).astype(BF16)]
  transfers between devices with their start and end apart: 28 -> 31, of which waited for: 13 -> 12; matrix products, arithmetic and copies ran while one was open for 25% -> 7% of each run, Pallas kernels for 15% -> 8%
where the time goes in v4:
time: 190 us; the launch traced here: 189 us
  waiting for transfers between devices  54.9 us (29%)
  starting transfers between devices  52.7 us (28%)
  Pallas kernels  45.3 us (24%)
  blocking collectives  11.9 us (6%)
  local copies, waits for them, and re-layouts  10.2 us (5%)
  matrix products  7.14 us (4%)
  between operations  4.86 us (3%)
  other arithmetic  2.22 us (1%)
    all_to_all x4, starting transfers between devices, plane_exchange(): return lax.all_to_all(x, PLANE, 0, 0, tiled=True)  26 us
    all_to_all x4, waiting for transfers between devices, plane_exchange(): return lax.all_to_all(x, PLANE, 0, 0, tiled=True)  25.9 us
    ppermute x15, starting transfers between devices, from_line(): return lax.ppermute(x, LINE, [((i + k) % 4, i) for i in range(4)])  22.5 us
    ppermute x15, waiting for transfers between devices, from_line(): return lax.ppermute(x, LINE, [((i + k) % 4, i) for i in range(4)])  17.1 us
    all_to_all x1, blocking collectives, stats_exchange(): return lax.all_to_all(x, (LINE, CORE), 0, 0, tiled=True)  11.9 us
    ppermute x3, waiting for transfers between devices, to_line(): return lax.ppermute(x, LINE, [(i, (i + k) % 4) for i in range(4)])  11.9 us
    pallas_call x1, Pallas kernels, score_grads(): pl.pallas_call(functools.partial(grads_kernel, scale=scale), in_specs=[VM...  9.22 us
    pallas_call x1, Pallas kernels, query_grads(): pl.pallas_call(functools.partial(query_kernel, scale=scale), in_specs=[SM...  7.92 us
  transfers between devices with their start and end apart: 31, of which 12 were waited for; matrix products, arithmetic and copies ran while one was open for 7% of the time, Pallas kernels for 8%

profile of v4, /device:TPU:0, one launch (start us, length us, event | category | flops | bytes accessed | tf_op | source)
XLA Modules:
  0.0 189.2 jit_solution(772707508428968071)
XLA Ops:
  2.7 8.0 %all-to-all-start = ((bf16[16,8,1664]{2,1,0:T(8,128)(2,1)}), bf16[16,8,1664]{2,1,0:T(8,128)(2,1)S(1)}, u32[]{:S(2)}, u32[]{:S(2)}) async-start(bf16[16,8,1664]{2,1,0:T(8,128)(2,1)} %get-tuple-element.45), calls=%async_computation | async-start | bytes 851968 | tf_op jit(solution)/shard_map/all_to_all | solution.py:35
  12.7 2.6 %convolution_convert_fusion.1 = bf16[256,384]{1,0:T(8,128)(2,1)S(1)} fusion(bf16[1536,384]{1,0:T(8,128)(2,1)} %w_second.1, bf16[768,1536]{1,0:T(8,128)(2,1)S(1)} %copy-done.1, bf16[128,768]{1,0:T(8,128)(2,1)S(1)} %slice.65, bf16[128,768]{1,0:T(8,128)(2,1)S(1)} %slice.64), kind=kOutput, calls=%fused_computation.13 | convolution fusion | flops 910393344 | bytes 4128768 | tf_op jit(solution)/shard_map/dot_general | solution.py:411
  17.6 2.9 %collective-permute-start.1 = (bf16[128,384]{1,0:T(8,128)(2,1)S(1)}, bf16[128,384]{1,0:T(8,128)(2,1)S(1)}, u32[]{:S(2)}, u32[]{:S(2)}) collective-permute-start(bf16[128,384]{1,0:T(8,128)(2,1)S(1)} %get-tuple-element.93), channel_id=1, source_target_pairs={{4,0},{6,2},{0,4},{2,6},{5,1},{7,3},{1,5},{3,7},{12,8},{14,10},{8,... | collective-permute-start | bytes 294920 | tf_op jit(solution)/shard_map/ppermute | solution.py:43
  22.4 2.4 %collective-permute-done.1 = bf16[128,384]{1,0:T(8,128)(2,1)S(1)} collective-permute-done((bf16[128,384]{1,0:T(8,128)(2,1)S(1)}, bf16[128,384]{1,0:T(8,128)(2,1)S(1)}, u32[]{:S(2)}, u32[]{:S(2)}) %collective-permute-start.1) | collective-permute-done | bytes 98336 | tf_op jit(solution)/shard_map/ppermute | solution.py:43
  26.0 4.7 %tail_rows.1 = (bf16[16,136,384]{2,1,0:T(8,128)(2,1)}, bf16[16,384]{1,0:T(8,128)(2,1)}, bf16[16,768]{1,0:T(8,128)(2,1)}) custom-call(s32[1]{0:T(128)} %get-tuple-element.44.heavy_at, bf16[16,8,1664]{2,1,0:T(8,128)(2,1)} %copy-done.2, bf16[128,384]{1,0:T(8,128)(2,1)} %get-tuple-element.94.base_p, s32[2,128]{1,0:T(2,128)} %bitcast.41, ...), custom_call_target="tpu_custom_call" | custom-call | tf_op jit(solution)/shard_map/tail_rows/pallas_call | solution.py:301
  30.7 2.6 %collective-permute-start.4 = (bf16[16,384]{1,0:T(8,128)(2,1)}, bf16[16,384]{1,0:T(8,128)(2,1)S(1)}, u32[]{:S(2)}, u32[]{:S(2)}) collective-permute-start(bf16[16,384]{1,0:T(8,128)(2,1)} %get-tuple-element.46), channel_id=1, source_target_pairs={{2,0},{4,2},{6,4},{0,6},{3,1},{5,3},{7,5},{1,7},{10,8},{12,10},{14... | collective-permute-start | bytes 36872 | tf_op jit(solution)/shard_map/ppermute | solution.py:43
  34.4 7.1 %all-to-all-start.1 = ((bf16[16,136,384]{2,1,0:T(8,128)(2,1)}), bf16[16,136,384]{2,1,0:T(8,128)(2,1)S(1)}, u32[]{:S(2)}, u32[]{:S(2)}) async-start(bf16[16,136,384]{2,1,0:T(8,128)(2,1)} %get-tuple-element.49), calls=%async_computation.1 | async-start | bytes 3342336 | tf_op jit(solution)/shard_map/all_to_all | solution.py:35
  43.8 3.3 %convolution_convert_fusion.refs_8_ = bf16[192,768]{1,0:T(8,128)(2,1)} fusion(bf16[768,1536]{1,0:T(8,128)(2,1)} %w_first.1, s32[192]{0:T(256)S(1)} %fusion.39), kind=kOutput, calls=%fused_computation.10 | convolution fusion | flops 453427200 | bytes 2654976 | tf_op jit(solution)/shard_map/dot_general | solution.py:449
  49.7 17.0 %all-to-all-done.1 = bf16[16,136,384]{2,1,0:T(8,128)(2,1)S(1)} async-done(((bf16[16,136,384]{2,1,0:T(8,128)(2,1)}), bf16[16,136,384]{2,1,0:T(8,128)(2,1)S(1)}, u32[]{:S(2)}, u32[]{:S(2)}) %all-to-all-start.1) | async-done | bytes 1671200 | tf_op jit(solution)/shard_map/all_to_all | solution.py:35
  67.9 6.7 %score_stats.1 = (bf16[1088,384]{1,0:T(8,128)(2,1)}, s32[1,1088]{1,0:T(1,128)}, f32[64,1088]{1,0:T(8,128)}) custom-call(s32[29]{0:T(128)} %concatenate.28.sc, bf16[512,384]{1,0:T(8,128)(2,1)} %copy-done.6, bf16[512,384]{1,0:T(8,128)(2,1)} %collective-permute-done.3.q_far, bf16[64,384]{1,0:T(8,128)(2,1)} %copy-done.20, bf16[64,384]{1,0:T(8,128)(2,1)} %copy-done.21, ...), custom_call_target="tpu_custom_call" | custom-call | tf_op jit(solution)/shard_map/score_stats/pallas_call | solution.py:331
  74.6 11.9 %all_to_all.47 = f32[8,8,1088]{2,1,0:T(8,128)} all-to-all(f32[8,8,1088]{2,1,0:T(8,128)} %bitcast.38), channel_id=1, replica_groups=mesh['dp_0'=4,'dp_1'=4,'dp_2'=4,'dp_3'=2] {'dp_2','dp_3'}, dimensions={0} | all-to-all | bytes 557056 | tf_op jit(solution)/shard_map/all_to_all | solution.py:39
  86.5 9.2 %score_grads.1 = (bf16[2304,384]{1,0:T(8,128)(2,1)}, bf16[2176,1088]{1,0:T(8,128)(2,1)}) custom-call(f32[64,1088]{1,0:T(8,128)} %bitcast.37, bf16[1088,384]{1,0:T(8,128)(2,1)} %get-tuple-element.52.q, bf16[2176,384]{1,0:T(8,128)(2,1)} %bitcast.34, s32[1,1088]{1,0:T(1,128)} %get-tuple-element.53.place), custom_call_target="tpu_custom_call" | custom-call | tf_op jit(solution)/shard_map/score_grads/pallas_call | solution.py:348
  95.8 7.9 %query_grads.1 = (f32[4,136,384]{2,1,0:T(8,128)}, f32[4,136,384]{2,1,0:T(8,128)}) custom-call(s32[29]{0:T(128)} %concatenate.28.sc, bf16[2176,384]{1,0:T(8,128)(2,1)} %bitcast.35, bf16[2176,1088]{1,0:T(8,128)(2,1)} %get-tuple-element.55.g), custom_call_target="tpu_custom_call" | custom-call | tf_op jit(solution)/shard_map/query_grads/pallas_call | solution.py:362
  103.7 3.9 %all-to-all-start.3 = ((bf16[16,144,384]{2,1,0:T(8,128)(2,1)}), bf16[16,144,384]{2,1,0:T(8,128)(2,1)S(1)}, u32[]{:S(2)}, u32[]{:S(2)}) async-start(bf16[16,144,384]{2,1,0:T(8,128)(2,1)} %bitcast.10), calls=%async_computation.3 | async-start | bytes 3538944 | tf_op jit(solution)/shard_map/all_to_all | solution.py:35
  112.1 3.2 %collective-permute-start.17 = (bf16[272,768]{1,0:T(8,128)(2,1)S(1)}, bf16[272,768]{1,0:T(8,128)(2,1)S(1)}, u32[]{:S(2)}, u32[]{:S(2)}) collective-permute-start(bf16[272,768]{1,0:T(8,128)(2,1)S(1)} %pad_maximum_fusion.1.refs_0_), channel_id=1, source_target_pairs={{4,0},{6,2},{0,4},{2,6},{5,1},{7,3},{1,5},{3,7},{12,8},{14,10},{8,... | collective-permute-start | bytes 1253384 | tf_op jit(solution)/shard_map/ppermute | solution.py:43
  117.2 10.8 %collective-permute-done.9 = bf16[136,384]{1,0:T(8,128)(2,1)S(1)} collective-permute-done((bf16[136,384]{1,0:T(8,128)(2,1)S(1)}, bf16[136,384]{1,0:T(8,128)(2,1)S(1)}, u32[]{:S(2)}, u32[]{:S(2)}) %collective-permute-start.9) | collective-permute-done | bytes 104480 | tf_op jit(solution)/shard_map/ppermute | solution.py:47
  131.5 5.7 %collective-permute-done.18.refs_3_ = bf16[272,768]{1,0:T(8,128)(2,1)S(1)} collective-permute-done((bf16[272,768]{1,0:T(8,128)(2,1)S(1)}, bf16[272,768]{1,0:T(8,128)(2,1)S(1)}, u32[]{:S(2)}, u32[]{:S(2)}) %collective-permute-start.18) | collective-permute-done | bytes 417824 | tf_op jit(solution)/shard_map/ppermute | solution.py:43
  143.4 6.2 %hidden_units.1 = (bf16[1088,768]{1,0:T(8,128)(2,1)}, bf16[1088,768]{1,0:T(8,128)(2,1)}, bf16[192,1088]{1,0:T(8,128)(2,1)}, bf16[192,1088]{1,0:T(8,128)(2,1)}, f32[192,1088]{1,0:T(8,128)}, /*index=5*/f32[192,1088]{1,0:T(8,128)}) custom-call(bf16[272,768]{1,0:T(8,128)(2,1)} %copy-done.3, bf16[272,768]{1,0:T(8,128)(2,1)} %copy-done.13, ...), custom_call_target="tpu_custom_call" | custom-call | tf_op jit(solution)/shard_map/hidden_units/pallas_call | solution.py:318
  152.0 2.5 %collective-permute-start.23 = (bf16[136,384]{1,0:T(8,128)(2,1)S(1)}, bf16[136,384]{1,0:T(8,128)(2,1)S(1)}, u32[]{:S(2)}, u32[]{:S(2)}) collective-permute-start(bf16[136,384]{1,0:T(8,128)(2,1)S(1)} %slice.105), channel_id=1, source_target_pairs={{2,0},{4,2},{6,4},{0,6},{3,1},{5,3},{7,5},{1,7},{10,8},{12,10},{14... | collective-permute-start | bytes 313352 | tf_op jit(solution)/shard_map/ppermute | solution.py:43
  154.5 3.8 %collective-permute-done.25 = bf16[136,384]{1,0:T(8,128)(2,1)S(1)} collective-permute-done((bf16[136,384]{1,0:T(8,128)(2,1)S(1)}, bf16[136,384]{1,0:T(8,128)(2,1)S(1)}, u32[]{:S(2)}, u32[]{:S(2)}) %collective-permute-start.25) | collective-permute-done | bytes 104480 | tf_op jit(solution)/shard_map/ppermute | solution.py:43
  159.0 4.4 %first_weights.1.sums = f32[192,1152]{1,0:T(8,128)} custom-call(bf16[544,384]{1,0:T(8,128)(2,1)} %copy-done.4, bf16[544,384]{1,0:T(8,128)(2,1)} %collective-permute-done.15.de_far, bf16[1088,768]{1,0:T(8,128)(2,1)} %get-tuple-element.78.rows, bf16[192,1088]{1,0:T(8,128)(2,1)} %get-tuple-element.79.hidden, f32[192,1088]{1,0:T(8,128)} %get-tuple-element.80.slope, ...), custom_call_target="tpu_custom_call" | custom-call | tf_op jit(solution)/shard_map/first_weights/pallas_call | solution.py:377
  164.1 4.2 %last_weights.1 = bf16[128,1792]{1,0:T(8,128)(2,1)} custom-call(f32[192,1152]{1,0:T(8,128)} %first_weights.1.sums, bf16[544,384]{1,0:T(8,128)(2,1)} %copy-done.5, bf16[544,384]{1,0:T(8,128)(2,1)} %copy-done.19, bf16[1088,768]{1,0:T(8,128)(2,1)} %get-tuple-element.82.rows, bf16[192,1088]{1,0:T(8,128)(2,1)} %get-tuple-element.83.hidden, ...), custom_call_target="tpu_custom_call" | custom-call | tf_op jit(solution)/shard_map/last_weights/pallas_call | solution.py:385
  168.3 7.0 %all-to-all-start.4 = ((bf16[16,8,1792]{2,1,0:T(8,128)(2,1)}), bf16[16,8,1792]{2,1,0:T(8,128)(2,1)S(1)}, u32[]{:S(2)}, u32[]{:S(2)}) async-start(bf16[16,8,1792]{2,1,0:T(8,128)(2,1)} %bitcast.36), calls=%async_computation.4 | async-start | bytes 917504 | tf_op jit(solution)/shard_map/all_to_all | solution.py:35
  177.8 8.9 %all-to-all-done.4 = bf16[16,8,1792]{2,1,0:T(8,128)(2,1)S(1)} async-done(((bf16[16,8,1792]{2,1,0:T(8,128)(2,1)}), bf16[16,8,1792]{2,1,0:T(8,128)(2,1)S(1)}, u32[]{:S(2)}, u32[]{:S(2)}) %all-to-all-start.4) | async-done | bytes 458784 | tf_op jit(solution)/shard_map/all_to_all | solution.py:35
  (136 shorter events, 37.4 us)
Async XLA Ops:
  2.7 22.6 %all-to-all-start = ((bf16[16,8,1664]{2,1,0:T(8,128)(2,1)}), bf16[16,8,1664]{2,1,0:T(8,128)(2,1)S(1)}, u32[]{:S(2)}, u32[]{:S(2)}) async-start(bf16[16,8,1664]{2,1,0:T(8,128)(2,1)} %get-tuple-element.45), calls=%async_computation | async-start | bytes 851968 | tf_op jit(solution)/shard_map/all_to_all | solution.py:35
  17.6 7.2 %collective-permute-start.1 = (bf16[128,384]{1,0:T(8,128)(2,1)S(1)}, bf16[128,384]{1,0:T(8,128)(2,1)S(1)}, u32[]{:S(2)}, u32[]{:S(2)}) collective-permute-start(bf16[128,384]{1,0:T(8,128)(2,1)S(1)} %get-tuple-element.93), channel_id=1, source_target_pairs={{4,0},{6,2},{0,4},{2,6},{5,1},{7,3},{1,5},{3,7},{12,8},{14,10},{8,... | collective-permute-start | bytes 294920 | tf_op jit(solution)/shard_map/ppermute | solution.py:43
  25.2 41.5 %collective-permute-start.3 = (bf16[512,384]{1,0:T(8,128)(2,1)S(1)}, bf16[512,384]{1,0:T(8,128)(2,1)}, u32[]{:S(2)}, u32[]{:S(2)}) collective-permute-start(bf16[512,384]{1,0:T(8,128)(2,1)S(1)} %pad_maximum_fusion.3.q_own), channel_id=1, source_target_pairs={{0,1},{1,0},{2,3},{3,2},{4,5},{5,4},{6,7},{7,6},{8,9},{9,8},{10,11... | collective-permute-start | bytes 1179656 | tf_op jit(solution)/shard_map/ppermute | solution.py:31
  30.7 16.5 %collective-permute-start.4 = (bf16[16,384]{1,0:T(8,128)(2,1)}, bf16[16,384]{1,0:T(8,128)(2,1)S(1)}, u32[]{:S(2)}, u32[]{:S(2)}) collective-permute-start(bf16[16,384]{1,0:T(8,128)(2,1)} %get-tuple-element.46), channel_id=1, source_target_pairs={{2,0},{4,2},{6,4},{0,6},{3,1},{5,3},{7,5},{1,7},{10,8},{12,10},{14... | collective-permute-start | bytes 36872 | tf_op jit(solution)/shard_map/ppermute | solution.py:43
  33.3 14.0 %collective-permute-start.5 = (bf16[16,384]{1,0:T(8,128)(2,1)}, bf16[16,384]{1,0:T(8,128)(2,1)S(1)}, u32[]{:S(2)}, u32[]{:S(2)}) collective-permute-start(bf16[16,384]{1,0:T(8,128)(2,1)} %get-tuple-element.46), channel_id=1, source_target_pairs={{4,0},{6,2},{0,4},{2,6},{5,1},{7,3},{1,5},{3,7},{12,8},{14,10},{8,... | collective-permute-start | bytes 36872 | tf_op jit(solution)/shard_map/ppermute | solution.py:43
  33.6 13.6 %collective-permute-start.6 = (bf16[16,384]{1,0:T(8,128)(2,1)}, bf16[16,384]{1,0:T(8,128)(2,1)S(1)}, u32[]{:S(2)}, u32[]{:S(2)}) collective-permute-start(bf16[16,384]{1,0:T(8,128)(2,1)} %get-tuple-element.46), channel_id=1, source_target_pairs={{6,0},{0,2},{2,4},{4,6},{7,1},{1,3},{3,5},{5,7},{14,8},{8,10},{10,... | collective-permute-start | bytes 36872 | tf_op jit(solution)/shard_map/ppermute | solution.py:43
  34.4 32.2 %all-to-all-start.1 = ((bf16[16,136,384]{2,1,0:T(8,128)(2,1)}), bf16[16,136,384]{2,1,0:T(8,128)(2,1)S(1)}, u32[]{:S(2)}, u32[]{:S(2)}) async-start(bf16[16,136,384]{2,1,0:T(8,128)(2,1)} %get-tuple-element.49), calls=%async_computation.1 | async-start | bytes 3342336 | tf_op jit(solution)/shard_map/all_to_all | solution.py:35
  47.3 19.4 %collective-permute-start.7 = (bf16[64,384]{1,0:T(8,128)(2,1)S(1)}, bf16[64,384]{1,0:T(8,128)(2,1)S(1)}, u32[]{:S(2)}, u32[]{:S(2)}) collective-permute-start(bf16[64,384]{1,0:T(8,128)(2,1)S(1)} %constant_dynamic-update-slice_fusion.t_own), channel_id=1, source_target_pairs={{0,1},{1,0},{2,3},{3,2},{4,5},{5,4},{6,7},{7,6},{8,9},{9,8},{10,11... | collective-permute-start | bytes 147464 | tf_op jit(solution)/shard_map/ppermute | solution.py:31
  103.7 45.9 %all-to-all-start.3 = ((bf16[16,144,384]{2,1,0:T(8,128)(2,1)}), bf16[16,144,384]{2,1,0:T(8,128)(2,1)S(1)}, u32[]{:S(2)}, u32[]{:S(2)}) async-start(bf16[16,144,384]{2,1,0:T(8,128)(2,1)} %bitcast.10), calls=%async_computation.3 | async-start | bytes 3538944 | tf_op jit(solution)/shard_map/all_to_all | solution.py:35
  107.8 7.5 %collective-permute-start.11 = (bf16[136,384]{1,0:T(8,128)(2,1)S(1)}, bf16[136,384]{1,0:T(8,128)(2,1)S(1)}, u32[]{:S(2)}, u32[]{:S(2)}) collective-permute-start(bf16[136,384]{1,0:T(8,128)(2,1)S(1)} %get-tuple-element.88), channel_id=1, source_target_pairs={{0,6},{2,0},{4,2},{6,4},{1,7},{3,1},{5,3},{7,5},{8,14},{10,8},{12,... | collective-permute-start | bytes 313352 | tf_op jit(solution)/shard_map/ppermute | solution.py:47
  109.1 20.1 %collective-permute-start.16 = (bf16[272,768]{1,0:T(8,128)(2,1)S(1)}, bf16[272,768]{1,0:T(8,128)(2,1)S(1)}, u32[]{:S(2)}, u32[]{:S(2)}) collective-permute-start(bf16[272,768]{1,0:T(8,128)(2,1)S(1)} %pad_maximum_fusion.1.refs_0_), channel_id=1, source_target_pairs={{2,0},{4,2},{6,4},{0,6},{3,1},{5,3},{7,5},{1,7},{10,8},{12,10},{14... | collective-permute-start | bytes 1253384 | tf_op jit(solution)/shard_map/ppermute | solution.py:43
  109.9 7.3 %collective-permute-start.10 = (bf16[136,384]{1,0:T(8,128)(2,1)S(1)}, bf16[136,384]{1,0:T(8,128)(2,1)S(1)}, u32[]{:S(2)}, u32[]{:S(2)}) collective-permute-start(bf16[136,384]{1,0:T(8,128)(2,1)S(1)} %get-tuple-element.89), channel_id=1, source_target_pairs={{0,4},{2,6},{4,0},{6,2},{1,5},{3,7},{5,1},{7,3},{8,12},{10,14},{12... | collective-permute-start | bytes 313352 | tf_op jit(solution)/shard_map/ppermute | solution.py:47
  112.1 16.0 %collective-permute-start.9 = (bf16[136,384]{1,0:T(8,128)(2,1)S(1)}, bf16[136,384]{1,0:T(8,128)(2,1)S(1)}, u32[]{:S(2)}, u32[]{:S(2)}) collective-permute-start(bf16[136,384]{1,0:T(8,128)(2,1)S(1)} %get-tuple-element.87), channel_id=1, source_target_pairs={{0,2},{2,4},{4,6},{6,0},{1,3},{3,5},{5,7},{7,1},{8,10},{10,12},{12... | collective-permute-start | bytes 313352 | tf_op jit(solution)/shard_map/ppermute | solution.py:47
  112.1 19.4 %collective-permute-start.17 = (bf16[272,768]{1,0:T(8,128)(2,1)S(1)}, bf16[272,768]{1,0:T(8,128)(2,1)S(1)}, u32[]{:S(2)}, u32[]{:S(2)}) collective-permute-start(bf16[272,768]{1,0:T(8,128)(2,1)S(1)} %pad_maximum_fusion.1.refs_0_), channel_id=1, source_target_pairs={{4,0},{6,2},{0,4},{2,6},{5,1},{7,3},{1,5},{3,7},{12,8},{14,10},{8,... | collective-permute-start | bytes 1253384 | tf_op jit(solution)/shard_map/ppermute | solution.py:43
  115.3 21.9 %collective-permute-start.18 = (bf16[272,768]{1,0:T(8,128)(2,1)S(1)}, bf16[272,768]{1,0:T(8,128)(2,1)S(1)}, u32[]{:S(2)}, u32[]{:S(2)}) collective-permute-start(bf16[272,768]{1,0:T(8,128)(2,1)S(1)} %pad_maximum_fusion.1.refs_0_), channel_id=1, source_target_pairs={{6,0},{0,2},{2,4},{4,6},{7,1},{1,3},{3,5},{5,7},{14,8},{8,10},{10,... | collective-permute-start | bytes 1253384 | tf_op jit(solution)/shard_map/ppermute | solution.py:43
  128.1 11.5 %collective-permute-start.14 = (bf16[136,384]{1,0:T(8,128)(2,1)S(1)}, bf16[136,384]{1,0:T(8,128)(2,1)S(1)}, u32[]{:S(2)}, u32[]{:S(2)}) collective-permute-start(bf16[136,384]{1,0:T(8,128)(2,1)S(1)} %fusion.28), channel_id=1, source_target_pairs={{6,0},{0,2},{2,4},{4,6},{7,1},{1,3},{3,5},{5,7},{14,8},{8,10},{10,... | collective-permute-start | bytes 313352 | tf_op jit(solution)/shard_map/ppermute | solution.py:43
  128.2 12.8 %collective-permute-start.13 = (bf16[136,384]{1,0:T(8,128)(2,1)S(1)}, bf16[136,384]{1,0:T(8,128)(2,1)S(1)}, u32[]{:S(2)}, u32[]{:S(2)}) collective-permute-start(bf16[136,384]{1,0:T(8,128)(2,1)S(1)} %fusion.28), channel_id=1, source_target_pairs={{4,0},{6,2},{0,4},{2,6},{5,1},{7,3},{1,5},{3,7},{12,8},{14,10},{8,... | collective-permute-start | bytes 313352 | tf_op jit(solution)/shard_map/ppermute | solution.py:43
  129.2 11.9 %collective-permute-start.12 = (bf16[136,384]{1,0:T(8,128)(2,1)S(1)}, bf16[136,384]{1,0:T(8,128)(2,1)S(1)}, u32[]{:S(2)}, u32[]{:S(2)}) collective-permute-start(bf16[136,384]{1,0:T(8,128)(2,1)S(1)} %fusion.28), channel_id=1, source_target_pairs={{2,0},{4,2},{6,4},{0,6},{3,1},{5,3},{7,5},{1,7},{10,8},{12,10},{14... | collective-permute-start | bytes 313352 | tf_op jit(solution)/shard_map/ppermute | solution.py:43
  131.5 10.2 %collective-permute-start.19 = (bf16[272,768]{1,0:T(8,128)(2,1)S(1)}, bf16[272,768]{1,0:T(8,128)(2,1)S(1)}, u32[]{:S(2)}, u32[]{:S(2)}) collective-permute-start(bf16[272,768]{1,0:T(8,128)(2,1)S(1)} %pad_maximum_fusion.1.refs_0_), channel_id=1, source_target_pairs={{0,1},{1,0},{2,3},{3,2},{4,5},{5,4},{6,7},{7,6},{8,9},{9,8},{10,11... | collective-permute-start | bytes 1253384 | tf_op jit(solution)/shard_map/ppermute | solution.py:31
  141.1 8.5 %collective-permute-start.15 = (bf16[544,384]{1,0:T(8,128)(2,1)S(1)}, bf16[544,384]{1,0:T(8,128)(2,1)}, u32[]{:S(2)}, u32[]{:S(2)}) collective-permute-start(bf16[544,384]{1,0:T(8,128)(2,1)S(1)} %pad_maximum_fusion.de_own), channel_id=1, source_target_pairs={{0,1},{1,0},{2,3},{3,2},{4,5},{5,4},{6,7},{7,6},{8,9},{9,8},{10,11... | collective-permute-start | bytes 1253384 | tf_op jit(solution)/shard_map/ppermute | solution.py:31
  149.9 8.4 %collective-permute-start.25 = (bf16[136,384]{1,0:T(8,128)(2,1)S(1)}, bf16[136,384]{1,0:T(8,128)(2,1)S(1)}, u32[]{:S(2)}, u32[]{:S(2)}) collective-permute-start(bf16[136,384]{1,0:T(8,128)(2,1)S(1)} %slice.105), channel_id=1, source_target_pairs={{6,0},{0,2},{2,4},{4,6},{7,1},{1,3},{3,5},{5,7},{14,8},{8,10},{10,... | collective-permute-start | bytes 313352 | tf_op jit(solution)/shard_map/ppermute | solution.py:43
  149.9 8.3 %collective-permute-start.24 = (bf16[136,384]{1,0:T(8,128)(2,1)S(1)}, bf16[136,384]{1,0:T(8,128)(2,1)S(1)}, u32[]{:S(2)}, u32[]{:S(2)}) collective-permute-start(bf16[136,384]{1,0:T(8,128)(2,1)S(1)} %slice.105), channel_id=1, source_target_pairs={{4,0},{6,2},{0,4},{2,6},{5,1},{7,3},{1,5},{3,7},{12,8},{14,10},{8,... | collective-permute-start | bytes 313352 | tf_op jit(solution)/shard_map/ppermute | solution.py:43
  152.0 6.9 %collective-permute-start.23 = (bf16[136,384]{1,0:T(8,128)(2,1)S(1)}, bf16[136,384]{1,0:T(8,128)(2,1)S(1)}, u32[]{:S(2)}, u32[]{:S(2)}) collective-permute-start(bf16[136,384]{1,0:T(8,128)(2,1)S(1)} %slice.105), channel_id=1, source_target_pairs={{2,0},{4,2},{6,4},{0,6},{3,1},{5,3},{7,5},{1,7},{10,8},{12,10},{14... | collective-permute-start | bytes 313352 | tf_op jit(solution)/shard_map/ppermute | solution.py:43
  168.3 18.4 %all-to-all-start.4 = ((bf16[16,8,1792]{2,1,0:T(8,128)(2,1)}), bf16[16,8,1792]{2,1,0:T(8,128)(2,1)S(1)}, u32[]{:S(2)}, u32[]{:S(2)}) async-start(bf16[16,8,1792]{2,1,0:T(8,128)(2,1)} %bitcast.36), calls=%async_computation.4 | async-start | bytes 917504 | tf_op jit(solution)/shard_map/all_to_all | solution.py:35
  (32 other events, 206.0 us)

commit v5 on v4

--- a/solution.py
+++ b/solution.py
@@ -103,11 +103,11 @@
     return (v * grown, slope)
 
 
-def tail_kernel(heavy_at, arrived, base_p, pos, w_first, w_second, p_out, q_out, feats_out):
-    width = w_first.shape[0]
+def tail_kernel(heavy_at, arrived, base_p, pos, w_first, w_second, p_out, q_out):
+    width, emb_width = w_first.shape[0], w_second.shape[1]
     tail = arrived[heavy_at[0]]
     feats = jnp.concatenate([tail[:, :width], tail[:, width : 2 * width]], axis=0)
-    feats_out[...] = feats
+    q_out[:, emb_width:] = feats
     pre = jnp.dot(feats, w_first[...], preferred_element_type=F32)
     hidden = gelu_parts(pre)[0].astype(BF16)
     emb = jnp.dot(hidden, w_second[...], preferred_element_type=F32).astype(BF16)
@@ -119,16 +119,25 @@
     line = lax.broadcasted_iota(jnp.int32, (UNIT, LOW), 0)
     code = tail[:, 2 * width :].astype(F32)
     code = jnp.where(line == 0, high, jnp.where(line == 1, low, code)).astype(BF16)
-    q_out[:UNIT] = emb[:UNIT]
-    q_out[UNIT:] = jnp.zeros((UNIT, q_out.shape[1]), BF16)
+    q_out[:UNIT, :emb_width] = emb[:UNIT]
+    q_out[UNIT:, LOW:emb_width] = jnp.zeros((UNIT, emb_width - LOW), BF16)
     q_out[UNIT:, :LOW] = code
 
 
 def units_kernel(*refs):
-    blocks, (first, rows_q, rows_p, hidden_q, hidden_p, slope_q, slope_p) = refs[:8], refs[8:]
+    blocks, tails, (first, rows_q, rows_p, hidden_q, hidden_p, slope_q, slope_p) = (
+        refs[:8],
+        refs[8:10],
+        refs[10:],
+    )
+    skip = tails[0].shape[1] - rows_q.shape[1]
     for k, block in enumerate(blocks):
-        rows_q[k * BLOCK : (k + 1) * BLOCK] = block[:BLOCK]
-        rows_p[k * BLOCK : (k + 1) * BLOCK] = block[BLOCK:]
+        tail = tails[k // 4][(k % 4) * 2 * UNIT : (k % 4 + 1) * 2 * UNIT, skip:]
+        at = k * BLOCK
+        rows_q[at : at + LOW] = block[:LOW]
+        rows_q[at + LOW : at + BLOCK] = tail[:UNIT]
+        rows_p[at : at + LOW] = block[LOW:]
+        rows_p[at + LOW : at + BLOCK] = tail[UNIT:]
     for rows, hidden, slope in ((rows_q, hidden_q, slope_q), (rows_p, hidden_p, slope_p)):
         value, gain = gelu_parts(nt_dot(first[...], rows[...]))
         hidden[...] = value.astype(BF16)
@@ -141,7 +150,7 @@
     for k, (q, t) in enumerate(((q_own, t_own), (q_far, t_far))):
         for b in range(4):
             qs[4 * k + b] = q[b * LOW : (b + 1) * LOW]
-            ts[4 * k + b] = t[b * 16 : (b + 1) * 16]
+            ts[4 * k + b] = t[b * 16 : (b + 1) * 16, : p.shape[1]]
     lane = lax.broadcasted_iota(jnp.int32, (1, LOW), 1) // UNIT
     codes = []
     spread = jnp.zeros((1, LOW), F32)
@@ -301,27 +310,26 @@
     return pl.pallas_call(
         tail_kernel,
         in_specs=[SMEM] + [VMEM] * 5,
-        out_specs=[VMEM] * 3,
+        out_specs=[VMEM] * 2,
         out_shape=[
             jax.ShapeDtypeStruct((16, BLOCK, emb_width), BF16),
-            jax.ShapeDtypeStruct((2 * UNIT, emb_width), BF16),
-            jax.ShapeDtypeStruct((2 * UNIT, w_first.shape[0]), BF16),
+            jax.ShapeDtypeStruct((2 * UNIT, emb_width + w_first.shape[0]), BF16),
         ],
         name="tail_rows",
     )(heavy_at, arrived, base_p, pos, w_first, w_second)
 
 
-def hidden_units(blocks, first):
+def hidden_units(blocks, tails, first):
     rows = jax.ShapeDtypeStruct((8 * BLOCK, first.shape[1]), BF16)
     hidden = jax.ShapeDtypeStruct((first.shape[0], 8 * BLOCK), BF16)
     slope = jax.ShapeDtypeStruct((first.shape[0], 8 * BLOCK), F32)
     rows_q, rows_p, hidden_q, hidden_p, slope_q, slope_p = pl.pallas_call(
         units_kernel,
-        in_specs=[VMEM] * 9,
+        in_specs=[VMEM] * 11,
         out_specs=[VMEM] * 6,
         out_shape=[rows, rows, hidden, hidden, slope, slope],
         name="hidden_units",
-    )(*blocks, first)
+    )(*blocks, *tails, first)
     return ((rows_q, hidden_q, slope_q), (rows_p, hidden_p, slope_p))
 
 
@@ -410,10 +418,14 @@
         hidden = gelu_tanh(pre).astype(BF16)
         return jnp.dot(hidden, w_second, preferred_element_type=F32).astype(BF16)
 
-    base = tower(jnp.concatenate([query_features[:LOW], passage_features[:LOW]], axis=0))
+    feats = jnp.concatenate([query_features[:LOW], passage_features[:LOW]], axis=0)
+    base = tower(feats)
     qs = gathered(base[:LOW])
 
-    p_send, q_tail, tail = tail_rows(
+    feats = along_line(feats)
+    feats = feats + [swap_core(x) for x in feats]
+
+    p_send, q_tail = tail_rows(
         heavy_at, arrived.reshape(16, UNIT, -1), base[LOW:], pos, w_first, w_second
     )
     p_all = plane_exchange(p_send.reshape(16 * BLOCK, emb_width))
@@ -431,13 +443,6 @@
     heavies = jnp.sum(heavy.reshape(16, 8) * jnp.arange(16, dtype=jnp.int32)[:, None], axis=0)
     sc = jnp.concatenate([group_start, scalars, heavies]).astype(jnp.int32)
 
-    feats = jnp.concatenate(
-        [query_features[:LOW], tail[:UNIT], passage_features[:LOW], tail[UNIT:]], axis=0
-    )
-    feats, _ = lax.optimization_barrier((feats, (qs[1], ts[1])))
-    feats = along_line(feats)
-    feats = feats + [swap_core(x) for x in feats]
-
     each = hidden_width // lax.axis_size(DP)
     unit = jnp.arange(16 * each, dtype=jnp.int32)
     rest = unit - LOW
@@ -450,7 +455,8 @@
         pick, w_first, (((1,), (1,)), ((), ())), preferred_element_type=F32
     ).astype(BF16)
     second_part = jnp.dot(pick, w_second, preferred_element_type=F32).astype(BF16)
-    p_all, first_part, second_part = lax.optimization_barrier((p_all, first_part, second_part))
+    q_units, p_units = hidden_units(feats, ts, first_part)
+    p_all, second_part = lax.optimization_barrier((p_all, second_part))
 
     q_all, place, stats = score_stats(sc, qs, ts, p_all, scale)
     stats = stats_exchange(stats)
@@ -463,9 +469,6 @@
     for k in (1, 2, 3):
         dq_sum = dq_sum + to_line(dq[k].astype(BF16), k).astype(F32)
     dqs = gathered(dq_sum.astype(BF16))
-    feats, _ = lax.optimization_barrier((feats, dq_far))
-    q_units, p_units = hidden_units(feats, first_part)
-    dp_all, dqs, q_units, p_units = lax.optimization_barrier((dp_all, dqs, q_units, p_units))
 
     dp_sum = jnp.sum(dp_all.reshape(16, CHUNK, emb_width).astype(F32), axis=0)
     mean_loss = (dp_sum[BLOCK, 0] + dp_sum[BLOCK + 1, 0] + dp_sum[BLOCK + 2, 0]) / pairs

time: 190 us -> 207 us (1.089)
  waiting for transfers between devices: 54.9 us -> 76.3 us
  starting transfers between devices: 52.7 us -> 47.6 us
  local copies, waits for them, and re-layouts: 10.2 us -> 12.3 us
    all_to_all x4, waiting for transfers between devices: 25.9 us -> 42.5 us  [plane_exchange(): return lax.all_to_all(x, PLANE, 0, 0, tiled=True)]
    ppermute x15, waiting for transfers between devices: 17.1 us -> 26.5 us  [from_line(): return lax.ppermute(x, LINE, [((i + k) % 4, i) for i in range(4)])]
    ppermute x3, waiting for transfers between devices: 11.9 us -> 7.26 us  [to_line(): return lax.ppermute(x, LINE, [(i, (i + k) % 4) for i in range(4)])]
    ppermute x15, starting transfers between devices: 22.5 us -> 19.2 us  [from_line(): return lax.ppermute(x, LINE, [((i + k) % 4, i) for i in range(4)])]
    unnamed x53 -> x55, local copies, waits for them, and re-layouts: 4.56 us -> 6.63 us
  transfers between devices with their start and end apart: 31 -> 31, of which waited for: 12 -> 12; matrix products, arithmetic and copies ran while one was open for 7% -> 6% of each run, Pallas kernels for 8% -> 7%
where the time goes in v5:
time: 207 us; the launch traced here: 206 us
  waiting for transfers between devices  76.3 us (37%)
  starting transfers between devices  47.6 us (23%)
  Pallas kernels  44.8 us (22%)
  local copies, waits for them, and re-layouts  12.3 us (6%)
  blocking collectives  11.9 us (6%)
  matrix products  5.46 us (3%)
  between operations  4.81 us (2%)
  other arithmetic  3.09 us (1%)
    all_to_all x4, waiting for transfers between devices, plane_exchange(): return lax.all_to_all(x, PLANE, 0, 0, tiled=True)  42.5 us
    ppermute x15, waiting for transfers between devices, from_line(): return lax.ppermute(x, LINE, [((i + k) % 4, i) for i in range(4)])  26.5 us
    all_to_all x4, starting transfers between devices, plane_exchange(): return lax.all_to_all(x, PLANE, 0, 0, tiled=True)  24.2 us
    ppermute x15, starting transfers between devices, from_line(): return lax.ppermute(x, LINE, [((i + k) % 4, i) for i in range(4)])  19.2 us
    all_to_all x1, blocking collectives, stats_exchange(): return lax.all_to_all(x, (LINE, CORE), 0, 0, tiled=True)  11.9 us
    pallas_call x1, Pallas kernels, score_grads(): pl.pallas_call(functools.partial(grads_kernel, scale=scale), in_specs=[VM...  9.22 us
    pallas_call x1, Pallas kernels, query_grads(): pl.pallas_call(functools.partial(query_kernel, scale=scale), in_specs=[SM...  7.91 us
    ppermute x3, waiting for transfers between devices, to_line(): return lax.ppermute(x, LINE, [(i, (i + k) % 4) for i in range(4)])  7.26 us
  transfers between devices with their start and end apart: 31, of which 12 were waited for; matrix products, arithmetic and copies ran while one was open for 6% of the time, Pallas kernels for 7%

profile of v5, /device:TPU:0, one launch (start us, length us, event | category | flops | bytes accessed | tf_op | source)
XLA Modules:
  0.0 206.2 jit_solution(3859604679486271114)
XLA Ops:
  2.7 8.0 %all-to-all-start = ((bf16[16,8,1664]{2,1,0:T(8,128)(2,1)}), bf16[16,8,1664]{2,1,0:T(8,128)(2,1)S(1)}, u32[]{:S(2)}, u32[]{:S(2)}) async-start(bf16[16,8,1664]{2,1,0:T(8,128)(2,1)} %get-tuple-element.25), calls=%async_computation | async-start | bytes 851968 | tf_op jit(solution)/shard_map/all_to_all | solution.py:35
  12.7 2.6 %convolution_convert_fusion.1 = bf16[256,384]{1,0:T(8,128)(2,1)S(1)} fusion(bf16[1536,384]{1,0:T(8,128)(2,1)} %w_second.1, bf16[768,1536]{1,0:T(8,128)(2,1)S(1)} %copy-done.1, bf16[128,768]{1,0:T(8,128)(2,1)S(1)} %slice.57, bf16[128,768]{1,0:T(8,128)(2,1)S(1)} %slice.56), kind=kOutput, calls=%fused_computation.13 | convolution fusion | flops 910393344 | bytes 4128768 | tf_op jit(solution)/shard_map/dot_general | solution.py:419
  17.6 2.9 %collective-permute-start.1 = (bf16[128,384]{1,0:T(8,128)(2,1)S(1)}, bf16[128,384]{1,0:T(8,128)(2,1)S(1)}, u32[]{:S(2)}, u32[]{:S(2)}) collective-permute-start(bf16[128,384]{1,0:T(8,128)(2,1)S(1)} %get-tuple-element.53), channel_id=1, source_target_pairs={{4,0},{6,2},{0,4},{2,6},{5,1},{7,3},{1,5},{3,7},{12,8},{14,10},{8,... | collective-permute-start | bytes 294920 | tf_op jit(solution)/shard_map/ppermute | solution.py:43
  22.4 2.4 %collective-permute-done.1 = bf16[128,384]{1,0:T(8,128)(2,1)S(1)} collective-permute-done((bf16[128,384]{1,0:T(8,128)(2,1)S(1)}, bf16[128,384]{1,0:T(8,128)(2,1)S(1)}, u32[]{:S(2)}, u32[]{:S(2)}) %collective-permute-start.1) | collective-permute-done | bytes 98336 | tf_op jit(solution)/shard_map/ppermute | solution.py:43
  26.0 4.7 %tail_rows.1 = (bf16[16,136,384]{2,1,0:T(8,128)(2,1)}, bf16[16,1152]{1,0:T(8,128)(2,1)}) custom-call(s32[1]{0:T(128)} %get-tuple-element.24.heavy_at, bf16[16,8,1664]{2,1,0:T(8,128)(2,1)} %copy-done.3, bf16[128,384]{1,0:T(8,128)(2,1)} %get-tuple-element.54.base_p, s32[2,128]{1,0:T(2,128)} %bitcast.38, bf16[768,1536]{1,0:T(8,128)(2,1)} %w_first.1, ...), custom_call_target="tpu_custom_call" | custom-call | tf_op jit(solution)/shard_map/tail_rows/pallas_call | solution.py:310
  30.8 2.6 %collective-permute-start.4 = (bf16[16,1152]{1,0:T(8,128)(2,1)}, bf16[16,1152]{1,0:T(8,128)(2,1)S(1)}, u32[]{:S(2)}, u32[]{:S(2)}) collective-permute-start(bf16[16,1152]{1,0:T(8,128)(2,1)} %get-tuple-element.26), channel_id=1, source_target_pairs={{2,0},{4,2},{6,4},{0,6},{3,1},{5,3},{7,5},{1,7},{10,8},{12,10},{14... | collective-permute-start | bytes 110600 | tf_op jit(solution)/shard_map/ppermute | solution.py:43
  35.0 7.1 %all-to-all-start.1 = ((bf16[16,136,384]{2,1,0:T(8,128)(2,1)}), bf16[16,136,384]{2,1,0:T(8,128)(2,1)S(1)}, u32[]{:S(2)}, u32[]{:S(2)}) async-start(bf16[16,136,384]{2,1,0:T(8,128)(2,1)} %get-tuple-element.29), calls=%async_computation.1 | async-start | bytes 3342336 | tf_op jit(solution)/shard_map/all_to_all | solution.py:35
  46.4 20.8 %all-to-all-done.1 = bf16[16,136,384]{2,1,0:T(8,128)(2,1)S(1)} async-done(((bf16[16,136,384]{2,1,0:T(8,128)(2,1)}), bf16[16,136,384]{2,1,0:T(8,128)(2,1)S(1)}, u32[]{:S(2)}, u32[]{:S(2)}) %all-to-all-start.1) | async-done | bytes 1671200 | tf_op jit(solution)/shard_map/all_to_all | solution.py:35
  69.1 6.8 %score_stats.1 = (bf16[1088,384]{1,0:T(8,128)(2,1)}, s32[1,1088]{1,0:T(1,128)}, f32[64,1088]{1,0:T(8,128)}) custom-call(s32[29]{0:T(128)} %concatenate.25.sc, bf16[512,384]{1,0:T(8,128)(2,1)} %copy-done.7, bf16[512,384]{1,0:T(8,128)(2,1)} %collective-permute-done.3.q_far, bf16[64,1152]{1,0:T(8,128)(2,1)} %copy-done.14, bf16[64,1152]{1,0:T(8,128)(2,1)} %copy-done.15, ...), custom_call_target="tpu_custom_call" | custom-call | tf_op jit(solution)/shard_map/score_stats/pallas_call | solution.py:339
  75.9 11.9 %all_to_all.44 = f32[8,8,1088]{2,1,0:T(8,128)} all-to-all(f32[8,8,1088]{2,1,0:T(8,128)} %bitcast.35), channel_id=1, replica_groups=mesh['dp_0'=4,'dp_1'=4,'dp_2'=4,'dp_3'=2] {'dp_2','dp_3'}, dimensions={0} | all-to-all | bytes 557056 | tf_op jit(solution)/shard_map/all_to_all | solution.py:39
  87.8 9.2 %score_grads.1 = (bf16[2304,384]{1,0:T(8,128)(2,1)}, bf16[2176,1088]{1,0:T(8,128)(2,1)}) custom-call(f32[64,1088]{1,0:T(8,128)} %bitcast.34, bf16[1088,384]{1,0:T(8,128)(2,1)} %get-tuple-element.32.q, bf16[2176,384]{1,0:T(8,128)(2,1)} %bitcast.31, s32[1,1088]{1,0:T(1,128)} %get-tuple-element.33.place), custom_call_target="tpu_custom_call" | custom-call | tf_op jit(solution)/shard_map/score_grads/pallas_call | solution.py:356
  97.0 7.9 %query_grads.1 = (f32[4,136,384]{2,1,0:T(8,128)}, f32[4,136,384]{2,1,0:T(8,128)}) custom-call(s32[29]{0:T(128)} %concatenate.25.sc, bf16[2176,384]{1,0:T(8,128)(2,1)} %bitcast.32, bf16[2176,1088]{1,0:T(8,128)(2,1)} %get-tuple-element.35.g), custom_call_target="tpu_custom_call" | custom-call | tf_op jit(solution)/shard_map/query_grads/pallas_call | solution.py:370
  104.9 3.9 %all-to-all-start.3 = ((bf16[16,144,384]{2,1,0:T(8,128)(2,1)}), bf16[16,144,384]{2,1,0:T(8,128)(2,1)S(1)}, u32[]{:S(2)}, u32[]{:S(2)}) async-start(bf16[16,144,384]{2,1,0:T(8,128)(2,1)} %bitcast.10), calls=%async_computation.3 | async-start | bytes 3538944 | tf_op jit(solution)/shard_map/all_to_all | solution.py:35
  111.7 3.2 %collective-permute-done.11 = bf16[136,384]{1,0:T(8,128)(2,1)S(1)} collective-permute-done((bf16[136,384]{1,0:T(8,128)(2,1)S(1)}, bf16[136,384]{1,0:T(8,128)(2,1)S(1)}, u32[]{:S(2)}, u32[]{:S(2)}) %collective-permute-start.11) | collective-permute-done | bytes 104480 | tf_op jit(solution)/shard_map/ppermute | solution.py:47
  114.9 2.7 %collective-permute-done.10 = bf16[136,384]{1,0:T(8,128)(2,1)S(1)} collective-permute-done((bf16[136,384]{1,0:T(8,128)(2,1)S(1)}, bf16[136,384]{1,0:T(8,128)(2,1)S(1)}, u32[]{:S(2)}, u32[]{:S(2)}) %collective-permute-start.10) | collective-permute-done | bytes 104480 | tf_op jit(solution)/shard_map/ppermute | solution.py:47
  123.2 12.8 %all-to-all-done.3 = bf16[16,144,384]{2,1,0:T(8,128)(2,1)S(1)} async-done(((bf16[16,144,384]{2,1,0:T(8,128)(2,1)}), bf16[16,144,384]{2,1,0:T(8,128)(2,1)S(1)}, u32[]{:S(2)}, u32[]{:S(2)}) %all-to-all-start.3) | async-done | bytes 1769504 | tf_op jit(solution)/shard_map/all_to_all | solution.py:35
  137.0 2.7 %collective-permute-start.16 = (bf16[256,768]{1,0:T(8,128)(2,1)S(1)}, bf16[256,768]{1,0:T(8,128)(2,1)S(1)}, u32[]{:S(2)}, u32[]{:S(2)}) collective-permute-start(bf16[256,768]{1,0:T(8,128)(2,1)S(1)} %pad_maximum_fusion.2.refs_0_), channel_id=1, source_target_pairs={{2,0},{4,2},{6,4},{0,6},{3,1},{5,3},{7,5},{1,7},{10,8},{12,10},{14... | collective-permute-start | bytes 1179656 | tf_op jit(solution)/shard_map/ppermute | solution.py:43
  143.5 17.9 %collective-permute-done.24 = bf16[136,384]{1,0:T(8,128)(2,1)S(1)} collective-permute-done((bf16[136,384]{1,0:T(8,128)(2,1)S(1)}, bf16[136,384]{1,0:T(8,128)(2,1)S(1)}, u32[]{:S(2)}, u32[]{:S(2)}) %collective-permute-start.24) | collective-permute-done | bytes 104480 | tf_op jit(solution)/shard_map/ppermute | solution.py:43
  162.4 3.7 %collective-permute-done.23 = bf16[136,384]{1,0:T(8,128)(2,1)S(1)} collective-permute-done((bf16[136,384]{1,0:T(8,128)(2,1)S(1)}, bf16[136,384]{1,0:T(8,128)(2,1)S(1)}, u32[]{:S(2)}, u32[]{:S(2)}) %collective-permute-start.23) | collective-permute-done | bytes 104480 | tf_op jit(solution)/shard_map/ppermute | solution.py:43
  171.4 5.6 %hidden_units.1 = (bf16[1088,768]{1,0:T(8,128)(2,1)}, bf16[1088,768]{1,0:T(8,128)(2,1)}, bf16[192,1088]{1,0:T(8,128)(2,1)}, bf16[192,1088]{1,0:T(8,128)(2,1)}, f32[192,1088]{1,0:T(8,128)}, /*index=5*/f32[192,1088]{1,0:T(8,128)}) custom-call(bf16[256,768]{1,0:T(8,128)(2,1)} %copy-done.6, bf16[256,768]{1,0:T(8,128)(2,1)} %copy-done.18, ...), custom_call_target="tpu_custom_call" | custom-call | tf_op jit(solution)/shard_map/hidden_units/pallas_call | solution.py:326
  177.8 4.3 %first_weights.1.sums = f32[192,1152]{1,0:T(8,128)} custom-call(bf16[544,384]{1,0:T(8,128)(2,1)} %copy-done.4, bf16[544,384]{1,0:T(8,128)(2,1)} %copy-done.16, bf16[1088,768]{1,0:T(8,128)(2,1)} %get-tuple-element.38.rows, bf16[192,1088]{1,0:T(8,128)(2,1)} %get-tuple-element.39.hidden, f32[192,1088]{1,0:T(8,128)} %get-tuple-element.40.slope, ...), custom_call_target="tpu_custom_call" | custom-call | tf_op jit(solution)/shard_map/first_weights/pallas_call | solution.py:385
  183.0 4.2 %last_weights.1 = bf16[128,1792]{1,0:T(8,128)(2,1)} custom-call(f32[192,1152]{1,0:T(8,128)} %first_weights.1.sums, bf16[544,384]{1,0:T(8,128)(2,1)} %copy-done.5, bf16[544,384]{1,0:T(8,128)(2,1)} %copy-done.17, bf16[1088,768]{1,0:T(8,128)(2,1)} %get-tuple-element.42.rows, bf16[192,1088]{1,0:T(8,128)(2,1)} %get-tuple-element.43.hidden, ...), custom_call_target="tpu_custom_call" | custom-call | tf_op jit(solution)/shard_map/last_weights/pallas_call | solution.py:393
  187.2 5.2 %all-to-all-start.4 = ((bf16[16,8,1792]{2,1,0:T(8,128)(2,1)}), bf16[16,8,1792]{2,1,0:T(8,128)(2,1)S(1)}, u32[]{:S(2)}, u32[]{:S(2)}) async-start(bf16[16,8,1792]{2,1,0:T(8,128)(2,1)} %bitcast.33), calls=%async_computation.4 | async-start | bytes 917504 | tf_op jit(solution)/shard_map/all_to_all | solution.py:35
  194.9 8.8 %all-to-all-done.4 = bf16[16,8,1792]{2,1,0:T(8,128)(2,1)S(1)} async-done(((bf16[16,8,1792]{2,1,0:T(8,128)(2,1)}), bf16[16,8,1792]{2,1,0:T(8,128)(2,1)S(1)}, u32[]{:S(2)}, u32[]{:S(2)}) %all-to-all-start.4) | async-done | bytes 458784 | tf_op jit(solution)/shard_map/all_to_all | solution.py:35
  (137 shorter events, 39.3 us)
Async XLA Ops:
  2.7 22.6 %all-to-all-start = ((bf16[16,8,1664]{2,1,0:T(8,128)(2,1)}), bf16[16,8,1664]{2,1,0:T(8,128)(2,1)S(1)}, u32[]{:S(2)}, u32[]{:S(2)}) async-start(bf16[16,8,1664]{2,1,0:T(8,128)(2,1)} %get-tuple-element.25), calls=%async_computation | async-start | bytes 851968 | tf_op jit(solution)/shard_map/all_to_all | solution.py:35
  16.0 6.4 %collective-permute-start.2 = (bf16[128,384]{1,0:T(8,128)(2,1)S(1)}, bf16[128,384]{1,0:T(8,128)(2,1)S(1)}, u32[]{:S(2)}, u32[]{:S(2)}) collective-permute-start(bf16[128,384]{1,0:T(8,128)(2,1)S(1)} %get-tuple-element.53), channel_id=1, source_target_pairs={{6,0},{0,2},{2,4},{4,6},{7,1},{1,3},{3,5},{5,7},{14,8},{8,10},{10,... | collective-permute-start | bytes 294920 | tf_op jit(solution)/shard_map/ppermute | solution.py:43
  17.6 7.2 %collective-permute-start.1 = (bf16[128,384]{1,0:T(8,128)(2,1)S(1)}, bf16[128,384]{1,0:T(8,128)(2,1)S(1)}, u32[]{:S(2)}, u32[]{:S(2)}) collective-permute-start(bf16[128,384]{1,0:T(8,128)(2,1)S(1)} %get-tuple-element.53), channel_id=1, source_target_pairs={{4,0},{6,2},{0,4},{2,6},{5,1},{7,3},{1,5},{3,7},{12,8},{14,10},{8,... | collective-permute-start | bytes 294920 | tf_op jit(solution)/shard_map/ppermute | solution.py:43
  25.2 42.1 %collective-permute-start.3 = (bf16[512,384]{1,0:T(8,128)(2,1)S(1)}, bf16[512,384]{1,0:T(8,128)(2,1)}, u32[]{:S(2)}, u32[]{:S(2)}) collective-permute-start(bf16[512,384]{1,0:T(8,128)(2,1)S(1)} %pad_maximum_fusion.3.q_own), channel_id=1, source_target_pairs={{0,1},{1,0},{2,3},{3,2},{4,5},{5,4},{6,7},{7,6},{8,9},{9,8},{10,11... | collective-permute-start | bytes 1179656 | tf_op jit(solution)/shard_map/ppermute | solution.py:31
  30.8 14.3 %collective-permute-start.4 = (bf16[16,1152]{1,0:T(8,128)(2,1)}, bf16[16,1152]{1,0:T(8,128)(2,1)S(1)}, u32[]{:S(2)}, u32[]{:S(2)}) collective-permute-start(bf16[16,1152]{1,0:T(8,128)(2,1)} %get-tuple-element.26), channel_id=1, source_target_pairs={{2,0},{4,2},{6,4},{0,6},{3,1},{5,3},{7,5},{1,7},{10,8},{12,10},{14... | collective-permute-start | bytes 110600 | tf_op jit(solution)/shard_map/ppermute | solution.py:43
  33.3 11.7 %collective-permute-start.5 = (bf16[16,1152]{1,0:T(8,128)(2,1)}, bf16[16,1152]{1,0:T(8,128)(2,1)S(1)}, u32[]{:S(2)}, u32[]{:S(2)}) collective-permute-start(bf16[16,1152]{1,0:T(8,128)(2,1)} %get-tuple-element.26), channel_id=1, source_target_pairs={{4,0},{6,2},{0,4},{2,6},{5,1},{7,3},{1,5},{3,7},{12,8},{14,10},{8,... | collective-permute-start | bytes 110600 | tf_op jit(solution)/shard_map/ppermute | solution.py:43
  33.7 11.4 %collective-permute-start.6 = (bf16[16,1152]{1,0:T(8,128)(2,1)}, bf16[16,1152]{1,0:T(8,128)(2,1)S(1)}, u32[]{:S(2)}, u32[]{:S(2)}) collective-permute-start(bf16[16,1152]{1,0:T(8,128)(2,1)} %get-tuple-element.26), channel_id=1, source_target_pairs={{6,0},{0,2},{2,4},{4,6},{7,1},{1,3},{3,5},{5,7},{14,8},{8,10},{10,... | collective-permute-start | bytes 110600 | tf_op jit(solution)/shard_map/ppermute | solution.py:43
  35.0 32.3 %all-to-all-start.1 = ((bf16[16,136,384]{2,1,0:T(8,128)(2,1)}), bf16[16,136,384]{2,1,0:T(8,128)(2,1)S(1)}, u32[]{:S(2)}, u32[]{:S(2)}) async-start(bf16[16,136,384]{2,1,0:T(8,128)(2,1)} %get-tuple-element.29), calls=%async_computation.1 | async-start | bytes 3342336 | tf_op jit(solution)/shard_map/all_to_all | solution.py:35
  45.1 22.1 %collective-permute-start.7 = (bf16[64,1152]{1,0:T(8,128)(2,1)S(1)}, bf16[64,1152]{1,0:T(8,128)(2,1)S(1)}, u32[]{:S(2)}, u32[]{:S(2)}) collective-permute-start(bf16[64,1152]{1,0:T(8,128)(2,1)S(1)} %constant_dynamic-update-slice_fusion.t_own.refs_8_), channel_id=1, source_target_pairs={{0,1},{1,0},{2,3},{3,2},{4,5},{5,4},{6,7},{7,6},{8,9},{9,8},{10,11... | collective-permute-start | bytes 442376 | tf_op jit(solution)/shard_map/ppermute | solution.py:31
  104.9 31.1 %all-to-all-start.3 = ((bf16[16,144,384]{2,1,0:T(8,128)(2,1)}), bf16[16,144,384]{2,1,0:T(8,128)(2,1)S(1)}, u32[]{:S(2)}, u32[]{:S(2)}) async-start(bf16[16,144,384]{2,1,0:T(8,128)(2,1)} %bitcast.10), calls=%async_computation.3 | async-start | bytes 3538944 | tf_op jit(solution)/shard_map/all_to_all | solution.py:35
  110.3 7.3 %collective-permute-start.10 = (bf16[136,384]{1,0:T(8,128)(2,1)S(1)}, bf16[136,384]{1,0:T(8,128)(2,1)S(1)}, u32[]{:S(2)}, u32[]{:S(2)}) collective-permute-start(bf16[136,384]{1,0:T(8,128)(2,1)S(1)} %get-tuple-element.49), channel_id=1, source_target_pairs={{0,4},{2,6},{4,0},{6,2},{1,5},{3,7},{5,1},{7,3},{8,12},{10,14},{12... | collective-permute-start | bytes 313352 | tf_op jit(solution)/shard_map/ppermute | solution.py:47
  111.7 7.3 %collective-permute-start.9 = (bf16[136,384]{1,0:T(8,128)(2,1)S(1)}, bf16[136,384]{1,0:T(8,128)(2,1)S(1)}, u32[]{:S(2)}, u32[]{:S(2)}) collective-permute-start(bf16[136,384]{1,0:T(8,128)(2,1)S(1)} %get-tuple-element.47), channel_id=1, source_target_pairs={{0,2},{2,4},{4,6},{6,0},{1,3},{3,5},{5,7},{7,1},{8,10},{10,12},{12... | collective-permute-start | bytes 313352 | tf_op jit(solution)/shard_map/ppermute | solution.py:47
  119.1 20.7 %collective-permute-start.14 = (bf16[136,384]{1,0:T(8,128)(2,1)S(1)}, bf16[136,384]{1,0:T(8,128)(2,1)S(1)}, u32[]{:S(2)}, u32[]{:S(2)}) collective-permute-start(bf16[136,384]{1,0:T(8,128)(2,1)S(1)} %fusion.18), channel_id=1, source_target_pairs={{6,0},{0,2},{2,4},{4,6},{7,1},{1,3},{3,5},{5,7},{14,8},{8,10},{10,... | collective-permute-start | bytes 313352 | tf_op jit(solution)/shard_map/ppermute | solution.py:43
  119.1 20.6 %collective-permute-start.13 = (bf16[136,384]{1,0:T(8,128)(2,1)S(1)}, bf16[136,384]{1,0:T(8,128)(2,1)S(1)}, u32[]{:S(2)}, u32[]{:S(2)}) collective-permute-start(bf16[136,384]{1,0:T(8,128)(2,1)S(1)} %fusion.18), channel_id=1, source_target_pairs={{4,0},{6,2},{0,4},{2,6},{5,1},{7,3},{1,5},{3,7},{12,8},{14,10},{8,... | collective-permute-start | bytes 313352 | tf_op jit(solution)/shard_map/ppermute | solution.py:43
  121.2 19.5 %collective-permute-start.12 = (bf16[136,384]{1,0:T(8,128)(2,1)S(1)}, bf16[136,384]{1,0:T(8,128)(2,1)}, u32[]{:S(2)}, u32[]{:S(2)}) collective-permute-start(bf16[136,384]{1,0:T(8,128)(2,1)S(1)} %fusion.18), channel_id=1, source_target_pairs={{2,0},{4,2},{6,4},{0,6},{3,1},{5,3},{7,5},{1,7},{10,8},{12,10},{14... | collective-permute-start | bytes 313352 | tf_op jit(solution)/shard_map/ppermute | solution.py:43
  136.3 6.0 %collective-permute-start.25 = (bf16[136,384]{1,0:T(8,128)(2,1)S(1)}, bf16[136,384]{1,0:T(8,128)(2,1)S(1)}, u32[]{:S(2)}, u32[]{:S(2)}) collective-permute-start(bf16[136,384]{1,0:T(8,128)(2,1)S(1)} %slice.95), channel_id=1, source_target_pairs={{6,0},{0,2},{2,4},{4,6},{7,1},{1,3},{3,5},{5,7},{14,8},{8,10},{10,... | collective-permute-start | bytes 313352 | tf_op jit(solution)/shard_map/ppermute | solution.py:43
  137.0 29.2 %collective-permute-start.16 = (bf16[256,768]{1,0:T(8,128)(2,1)S(1)}, bf16[256,768]{1,0:T(8,128)(2,1)S(1)}, u32[]{:S(2)}, u32[]{:S(2)}) collective-permute-start(bf16[256,768]{1,0:T(8,128)(2,1)S(1)} %pad_maximum_fusion.2.refs_0_), channel_id=1, source_target_pairs={{2,0},{4,2},{6,4},{0,6},{3,1},{5,3},{7,5},{1,7},{10,8},{12,10},{14... | collective-permute-start | bytes 1179656 | tf_op jit(solution)/shard_map/ppermute | solution.py:43
  139.7 27.0 %collective-permute-start.17 = (bf16[256,768]{1,0:T(8,128)(2,1)S(1)}, bf16[256,768]{1,0:T(8,128)(2,1)S(1)}, u32[]{:S(2)}, u32[]{:S(2)}) collective-permute-start(bf16[256,768]{1,0:T(8,128)(2,1)S(1)} %pad_maximum_fusion.2.refs_0_), channel_id=1, source_target_pairs={{4,0},{6,2},{0,4},{2,6},{5,1},{7,3},{1,5},{3,7},{12,8},{14,10},{8,... | collective-permute-start | bytes 1179656 | tf_op jit(solution)/shard_map/ppermute | solution.py:43
  139.7 27.1 %collective-permute-start.18 = (bf16[256,768]{1,0:T(8,128)(2,1)S(1)}, bf16[256,768]{1,0:T(8,128)(2,1)S(1)}, u32[]{:S(2)}, u32[]{:S(2)}) collective-permute-start(bf16[256,768]{1,0:T(8,128)(2,1)S(1)} %pad_maximum_fusion.2.refs_0_), channel_id=1, source_target_pairs={{6,0},{0,2},{2,4},{4,6},{7,1},{1,3},{3,5},{5,7},{14,8},{8,10},{10,... | collective-permute-start | bytes 1179656 | tf_op jit(solution)/shard_map/ppermute | solution.py:43
  140.7 26.6 %collective-permute-start.19 = (bf16[256,768]{1,0:T(8,128)(2,1)S(1)}, bf16[256,768]{1,0:T(8,128)(2,1)S(1)}, u32[]{:S(2)}, u32[]{:S(2)}) collective-permute-start(bf16[256,768]{1,0:T(8,128)(2,1)S(1)} %pad_maximum_fusion.2.refs_0_), channel_id=1, source_target_pairs={{0,1},{1,0},{2,3},{3,2},{4,5},{5,4},{6,7},{7,6},{8,9},{9,8},{10,11... | collective-permute-start | bytes 1179656 | tf_op jit(solution)/shard_map/ppermute | solution.py:31
  142.3 19.1 %collective-permute-start.24 = (bf16[136,384]{1,0:T(8,128)(2,1)S(1)}, bf16[136,384]{1,0:T(8,128)(2,1)S(1)}, u32[]{:S(2)}, u32[]{:S(2)}) collective-permute-start(bf16[136,384]{1,0:T(8,128)(2,1)S(1)} %slice.95), channel_id=1, source_target_pairs={{4,0},{6,2},{0,4},{2,6},{5,1},{7,3},{1,5},{3,7},{12,8},{14,10},{8,... | collective-permute-start | bytes 313352 | tf_op jit(solution)/shard_map/ppermute | solution.py:43
  166.1 10.9 %collective-permute-start.15 = (bf16[544,384]{1,0:T(8,128)(2,1)S(1)}, bf16[544,384]{1,0:T(8,128)(2,1)S(1)}, u32[]{:S(2)}, u32[]{:S(2)}) collective-permute-start(bf16[544,384]{1,0:T(8,128)(2,1)S(1)} %pad_maximum_fusion.de_own), channel_id=1, source_target_pairs={{0,1},{1,0},{2,3},{3,2},{4,5},{5,4},{6,7},{7,6},{8,9},{9,8},{10,11... | collective-permute-start | bytes 1253384 | tf_op jit(solution)/shard_map/ppermute | solution.py:31
  166.2 16.0 %collective-permute-start.26 = (bf16[544,384]{1,0:T(8,128)(2,1)S(1)}, bf16[544,384]{1,0:T(8,128)(2,1)S(1)}, u32[]{:S(2)}, u32[]{:S(2)}) collective-permute-start(bf16[544,384]{1,0:T(8,128)(2,1)S(1)} %pad_maximum_fusion.1.de_own), channel_id=1, source_target_pairs={{0,1},{1,0},{2,3},{3,2},{4,5},{5,4},{6,7},{7,6},{8,9},{9,8},{10,11... | collective-permute-start | bytes 1253384 | tf_op jit(solution)/shard_map/ppermute | solution.py:31
  187.2 16.6 %all-to-all-start.4 = ((bf16[16,8,1792]{2,1,0:T(8,128)(2,1)}), bf16[16,8,1792]{2,1,0:T(8,128)(2,1)S(1)}, u32[]{:S(2)}, u32[]{:S(2)}) async-start(bf16[16,8,1792]{2,1,0:T(8,128)(2,1)} %bitcast.33), calls=%async_computation.4 | async-start | bytes 917504 | tf_op jit(solution)/shard_map/all_to_all | solution.py:35
  (33 other events, 280.7 us)

commit v6 on v5

--- a/solution.py
+++ b/solution.py
@@ -20,6 +20,7 @@
 BLOCK = LOW + UNIT
 CHUNK = 144
 PAIR = 2 * BLOCK
+TILE = 256
 LOG2E = 1.4426950408889634
 
 
@@ -187,7 +188,7 @@
         stats_out[b * 8 : (b + 1) * 8] = stats
 
 
-def grads_kernel(stats, q, p, place, dp_out, g_ref, *, scale):
+def grads_kernel(stats, q, p, place, dp_out, g_out, dp_ref, g_ref, sems, *, scale):
     rows, width = q.shape
     pull = scale * LOG2E
     tops = [stats[b * 8 : b * 8 + 1] for b in range(8)]
@@ -209,21 +210,39 @@
         loss_high,
         jnp.where(line == 1, loss_mid, jnp.where(line == 2, loss_low, 0.0)),
     ).astype(BF16)
+    copies = []
+
+    def send(src, dst, rows):
+        copy = pltpu.make_async_copy(src.at[rows], dst.at[rows], sems.at[len(copies)])
+        copy.start()
+        copies.append(copy)
+
     for at in range(0, p.shape[0], PAIR):
         s = nt_dot(p[at : at + PAIR], q[...])
         row = lax.broadcasted_iota(jnp.int32, s.shape, 0)
         e = jnp.exp2(s * pull - norm)
         g_ref[at : at + PAIR] = jnp.where(row == place[...] - at, e - 1.0, e).astype(BF16)
+        send(g_ref, g_out, pl.ds(at, PAIR))
     for k in range(p.shape[0] // PAIR):
         dp = scale * jnp.dot(g_ref[k * PAIR : (k + 1) * PAIR], q[...], preferred_element_type=F32)
         dp = dp.astype(BF16)
         for half in range(2):
             to = (2 * k + half) * CHUNK
-            dp_out[to : to + BLOCK] = dp[half * BLOCK : (half + 1) * BLOCK]
-            dp_out[to + BLOCK : to + CHUNK] = loss_tile
-
-
-def query_kernel(sc, p, g, own, far, turned, *, scale):
+            dp_ref[to : to + BLOCK] = dp[half * BLOCK : (half + 1) * BLOCK]
+            dp_ref[to + BLOCK : to + CHUNK] = loss_tile
+        send(dp_ref, dp_out, pl.ds(2 * k * CHUNK, 2 * CHUNK))
+    for copy in copies:
+        copy.wait()
+
+
+def query_kernel(sc, p, g_in, own, far, turned, g, sems, *, scale):
+    cut = p.shape[0] // 2 // TILE * TILE
+    spans = (pl.ds(0, cut), pl.ds(cut, p.shape[0] - cut))
+    copies = [
+        pltpu.make_async_copy(g_in.at[span], g.at[span], sems.at[k]) for k, span in enumerate(spans)
+    ]
+    for copy in copies:
+        copy.start()
     for at in range(0, p.shape[0], LOW):
         turned[:, at : at + LOW] = p[at : at + LOW].T
 
@@ -238,12 +257,14 @@
         def _():
             far[b - 4, rows] = part
 
-    for first, size in ((0, 4 * LOW), (4 * LOW, 4 * LOW + 8 * UNIT)):
-        dq = jnp.dot(turned[...], g[:, first : first + size], preferred_element_type=F32)
-        dq = (scale * dq).T
-        for k in range(4):
-            put(first // LOW + k, slice(0, LOW), dq[k * LOW : (k + 1) * LOW])
-    dq = dq[4 * LOW :]
+    copies[0].wait()
+    early = jnp.dot(turned[:, :cut], g[:cut], preferred_element_type=F32)
+    copies[1].wait()
+    dq = early + jnp.dot(turned[:, cut:], g[cut:], preferred_element_type=F32)
+    dq = (scale * dq).T
+    for j in range(8):
+        put(j, slice(0, LOW), dq[j * LOW : (j + 1) * LOW])
+    dq = dq[8 * LOW :]
     for j in range(8):
         put(j, slice(LOW, BLOCK), dq[j * UNIT : (j + 1) * UNIT])
 
@@ -287,6 +308,7 @@
 
 VMEM = pl.BlockSpec(memory_space=pltpu.VMEM)
 SMEM = pl.BlockSpec(memory_space=pltpu.SMEM)
+HBM = pl.BlockSpec(memory_space=pltpu.HBM)
 
 
 def pack_overflow(counts, where, q, p, pos):
@@ -353,13 +375,19 @@
 def score_grads(stats, q, p, place, scale):
     columns, width = p.shape
     rows = q.shape[0]
+    steps = columns // PAIR
     return pl.pallas_call(
         functools.partial(grads_kernel, scale=scale),
         in_specs=[VMEM] * 4,
-        out_specs=[VMEM] * 2,
+        out_specs=[HBM] * 2,
         out_shape=[
-            jax.ShapeDtypeStruct((columns // BLOCK * CHUNK, width), BF16),
+            jax.ShapeDtypeStruct((2 * steps * CHUNK, width), BF16),
             jax.ShapeDtypeStruct((columns, rows), BF16),
+        ],
+        scratch_shapes=[
+            pltpu.VMEM((2 * steps * CHUNK, width), BF16),
+            pltpu.VMEM((columns, rows), BF16),
+            pltpu.SemaphoreType.DMA((2 * steps,)),
         ],
         name="score_grads",
     )(stats, q, p, place)
@@ -369,10 +397,14 @@
     columns, width = p.shape
     return pl.pallas_call(
         functools.partial(query_kernel, scale=scale),
-        in_specs=[SMEM] + [VMEM] * 2,
+        in_specs=[SMEM, VMEM, HBM],
         out_specs=[VMEM] * 2,
         out_shape=[jax.ShapeDtypeStruct((4, BLOCK, width), F32)] * 2,
-        scratch_shapes=[pltpu.VMEM((width, columns), BF16)],
+        scratch_shapes=[
+            pltpu.VMEM((width, columns), BF16),
+            pltpu.VMEM(g.shape, BF16),
+            pltpu.SemaphoreType.DMA((2,)),
+        ],
         name="query_grads",
     )(sc, p, g)
 
@@ -455,11 +487,11 @@
         pick, w_first, (((1,), (1,)), ((), ())), preferred_element_type=F32
     ).astype(BF16)
     second_part = jnp.dot(pick, w_second, preferred_element_type=F32).astype(BF16)
-    q_units, p_units = hidden_units(feats, ts, first_part)
-    p_all, second_part = lax.optimization_barrier((p_all, second_part))
+    p_all, first_part = lax.optimization_barrier((p_all, first_part))
 
     q_all, place, stats = score_stats(sc, qs, ts, p_all, scale)
     stats = stats_exchange(stats)
+    q_units, p_units = hidden_units(feats, ts, first_part)
     dp_part, g = score_grads(stats, q_all, p_all, place, scale)
     dp_all = plane_exchange(dp_part)
     dq_own, dq_far = query_grads(sc, p_all, g, scale)

time: 207 us -> 206 us (level)
    all_to_all x4, waiting for transfers between devices: 42.5 us -> 40 us  [plane_exchange(): return lax.all_to_all(x, PLANE, 0, 0, tiled=True)]
  transfers between devices with their start and end apart: 31 -> 31, of which waited for: 12 -> 14; matrix products, arithmetic and copies ran while one was open for 6% -> 7% of each run, Pallas kernels for 7% -> 7%
where the time goes in v6:
time: 206 us; the launch traced here: 205 us
  waiting for transfers between devices  74.5 us (36%)
  starting transfers between devices  47.9 us (23%)
  Pallas kernels  44.5 us (22%)
  blocking collectives  11.9 us (6%)
  local copies, waits for them, and re-layouts  11 us (5%)
  matrix products  7.13 us (3%)
  between operations  4.76 us (2%)
  other arithmetic  3.09 us (2%)
    all_to_all x4, waiting for transfers between devices, plane_exchange(): return lax.all_to_all(x, PLANE, 0, 0, tiled=True)  40 us
    ppermute x15, waiting for transfers between devices, from_line(): return lax.ppermute(x, LINE, [((i + k) % 4, i) for i in range(4)])  26.3 us
    all_to_all x4, starting transfers between devices, plane_exchange(): return lax.all_to_all(x, PLANE, 0, 0, tiled=True)  24.1 us
    ppermute x15, starting transfers between devices, from_line(): return lax.ppermute(x, LINE, [((i + k) % 4, i) for i in range(4)])  19.6 us
    all_to_all x1, blocking collectives, stats_exchange(): return lax.all_to_all(x, (LINE, CORE), 0, 0, tiled=True)  11.9 us
    pallas_call x1, Pallas kernels, score_grads(): pl.pallas_call(functools.partial(grads_kernel, scale=scale), in_specs=[VM...  8.83 us
    pallas_call x1, Pallas kernels, query_grads(): pl.pallas_call(functools.partial(query_kernel, scale=scale), in_specs=[SM...  8.02 us
    ppermute x3, waiting for transfers between devices, to_line(): return lax.ppermute(x, LINE, [(i, (i + k) % 4) for i in range(4)])  7.22 us
  transfers between devices with their start and end apart: 31, of which 14 were waited for; matrix products, arithmetic and copies ran while one was open for 7% of the time, Pallas kernels for 7%

profile of v6, /device:TPU:0, one launch (start us, length us, event | category | flops | bytes accessed | tf_op | source)
XLA Modules:
  0.0 204.7 jit_solution(14953115820867596144)
XLA Ops:
  2.7 8.0 %all-to-all-start = ((bf16[16,8,1664]{2,1,0:T(8,128)(2,1)}), bf16[16,8,1664]{2,1,0:T(8,128)(2,1)S(1)}, u32[]{:S(2)}, u32[]{:S(2)}) async-start(bf16[16,8,1664]{2,1,0:T(8,128)(2,1)} %get-tuple-element.25), calls=%async_computation | async-start | bytes 851968 | tf_op jit(solution)/shard_map/all_to_all | solution.py:36
  12.7 2.6 %convolution_convert_fusion.1 = bf16[256,384]{1,0:T(8,128)(2,1)S(1)} fusion(bf16[1536,384]{1,0:T(8,128)(2,1)} %w_second.1, bf16[768,1536]{1,0:T(8,128)(2,1)S(1)} %copy-done.1, bf16[128,768]{1,0:T(8,128)(2,1)S(1)} %slice.57, bf16[128,768]{1,0:T(8,128)(2,1)S(1)} %slice.56), kind=kOutput, calls=%fused_computation.13 | convolution fusion | flops 910393344 | bytes 4128768 | tf_op jit(solution)/shard_map/dot_general | solution.py:451
  17.6 2.9 %collective-permute-start.1 = (bf16[128,384]{1,0:T(8,128)(2,1)S(1)}, bf16[128,384]{1,0:T(8,128)(2,1)S(1)}, u32[]{:S(2)}, u32[]{:S(2)}) collective-permute-start(bf16[128,384]{1,0:T(8,128)(2,1)S(1)} %get-tuple-element.53), channel_id=1, source_target_pairs={{4,0},{6,2},{0,4},{2,6},{5,1},{7,3},{1,5},{3,7},{12,8},{14,10},{8,... | collective-permute-start | bytes 294920 | tf_op jit(solution)/shard_map/ppermute | solution.py:44
  26.0 4.7 %tail_rows.1 = (bf16[16,136,384]{2,1,0:T(8,128)(2,1)}, bf16[16,1152]{1,0:T(8,128)(2,1)}) custom-call(s32[1]{0:T(128)} %get-tuple-element.24.heavy_at, bf16[16,8,1664]{2,1,0:T(8,128)(2,1)} %copy-done.2, bf16[128,384]{1,0:T(8,128)(2,1)} %get-tuple-element.54.base_p, s32[2,128]{1,0:T(2,128)} %bitcast.38, bf16[768,1536]{1,0:T(8,128)(2,1)} %w_first.1, ...), custom_call_target="tpu_custom_call" | custom-call | tf_op jit(solution)/shard_map/tail_rows/pallas_call | solution.py:332
  30.7 2.6 %collective-permute-start.4 = (bf16[16,1152]{1,0:T(8,128)(2,1)}, bf16[16,1152]{1,0:T(8,128)(2,1)S(1)}, u32[]{:S(2)}, u32[]{:S(2)}) collective-permute-start(bf16[16,1152]{1,0:T(8,128)(2,1)} %get-tuple-element.26), channel_id=1, source_target_pairs={{2,0},{4,2},{6,4},{0,6},{3,1},{5,3},{7,5},{1,7},{10,8},{12,10},{14... | collective-permute-start | bytes 110600 | tf_op jit(solution)/shard_map/ppermute | solution.py:44
  34.5 7.1 %all-to-all-start.1 = ((bf16[16,136,384]{2,1,0:T(8,128)(2,1)}), bf16[16,136,384]{2,1,0:T(8,128)(2,1)S(1)}, u32[]{:S(2)}, u32[]{:S(2)}) async-start(bf16[16,136,384]{2,1,0:T(8,128)(2,1)} %get-tuple-element.29), calls=%async_computation.1 | async-start | bytes 3342336 | tf_op jit(solution)/shard_map/all_to_all | solution.py:36
  44.9 3.3 %convolution_convert_fusion.refs_10_ = bf16[192,768]{1,0:T(8,128)(2,1)} fusion(bf16[768,1536]{1,0:T(8,128)(2,1)} %w_first.1, s32[192]{0:T(256)S(1)} %fusion.29), kind=kOutput, calls=%fused_computation.10 | convolution fusion | flops 453427200 | bytes 2654976 | tf_op jit(solution)/shard_map/dot_general | solution.py:486
  48.3 18.5 %all-to-all-done.1 = bf16[16,136,384]{2,1,0:T(8,128)(2,1)S(1)} async-done(((bf16[16,136,384]{2,1,0:T(8,128)(2,1)}), bf16[16,136,384]{2,1,0:T(8,128)(2,1)S(1)}, u32[]{:S(2)}, u32[]{:S(2)}) %all-to-all-start.1) | async-done | bytes 1671200 | tf_op jit(solution)/shard_map/all_to_all | solution.py:36
  68.8 6.8 %score_stats.1 = (bf16[1088,384]{1,0:T(8,128)(2,1)}, s32[1,1088]{1,0:T(1,128)}, f32[64,1088]{1,0:T(8,128)}) custom-call(s32[29]{0:T(128)} %concatenate.25.sc, bf16[512,384]{1,0:T(8,128)(2,1)} %copy-done.6, bf16[512,384]{1,0:T(8,128)(2,1)} %copy-done.23, bf16[64,1152]{1,0:T(8,128)(2,1)} %copy-done.13, bf16[64,1152]{1,0:T(8,128)(2,1)} %copy-done.14, ...), custom_call_target="tpu_custom_call" | custom-call | tf_op jit(solution)/shard_map/score_stats/pallas_call | solution.py:361
  75.5 11.9 %all_to_all.44 = f32[8,8,1088]{2,1,0:T(8,128)} all-to-all(f32[8,8,1088]{2,1,0:T(8,128)} %bitcast.35), channel_id=1, replica_groups=mesh['dp_0'=4,'dp_1'=4,'dp_2'=4,'dp_3'=2] {'dp_2','dp_3'}, dimensions={0} | all-to-all | bytes 557056 | tf_op jit(solution)/shard_map/all_to_all | solution.py:40
  87.4 8.8 %score_grads.1 = (bf16[2304,384]{1,0:T(8,128)(2,1)}, bf16[2176,1088]{1,0:T(8,128)(2,1)}) custom-call(f32[64,1088]{1,0:T(8,128)} %bitcast.34, bf16[1088,384]{1,0:T(8,128)(2,1)} %get-tuple-element.32.q, bf16[2176,384]{1,0:T(8,128)(2,1)} %bitcast.31, s32[1,1088]{1,0:T(1,128)} %get-tuple-element.33.place), custom_call_target="tpu_custom_call" | custom-call | tf_op jit(solution)/shard_map/score_grads/pallas_call | solution.py:379
  96.3 8.0 %query_grads.1 = (f32[4,136,384]{2,1,0:T(8,128)}, f32[4,136,384]{2,1,0:T(8,128)}) custom-call(s32[29]{0:T(128)} %concatenate.25.sc, bf16[2176,384]{1,0:T(8,128)(2,1)} %bitcast.32, bf16[2176,1088]{1,0:T(8,128)(2,1)} %get-tuple-element.35.g_in), custom_call_target="tpu_custom_call" | custom-call | tf_op jit(solution)/shard_map/query_grads/pallas_call | solution.py:398
  104.4 3.9 %all-to-all-start.3 = ((bf16[16,144,384]{2,1,0:T(8,128)(2,1)}), bf16[16,144,384]{2,1,0:T(8,128)(2,1)S(1)}, u32[]{:S(2)}, u32[]{:S(2)}) async-start(bf16[16,144,384]{2,1,0:T(8,128)(2,1)} %bitcast.10), calls=%async_computation.3 | async-start | bytes 3538944 | tf_op jit(solution)/shard_map/all_to_all | solution.py:36
  111.2 3.2 %collective-permute-done.11 = bf16[136,384]{1,0:T(8,128)(2,1)S(1)} collective-permute-done((bf16[136,384]{1,0:T(8,128)(2,1)S(1)}, bf16[136,384]{1,0:T(8,128)(2,1)S(1)}, u32[]{:S(2)}, u32[]{:S(2)}) %collective-permute-start.11) | collective-permute-done | bytes 104480 | tf_op jit(solution)/shard_map/ppermute | solution.py:48
  114.4 2.7 %collective-permute-done.10 = bf16[136,384]{1,0:T(8,128)(2,1)S(1)} collective-permute-done((bf16[136,384]{1,0:T(8,128)(2,1)S(1)}, bf16[136,384]{1,0:T(8,128)(2,1)S(1)}, u32[]{:S(2)}, u32[]{:S(2)}) %collective-permute-start.10) | collective-permute-done | bytes 104480 | tf_op jit(solution)/shard_map/ppermute | solution.py:48
  122.7 12.8 %all-to-all-done.3 = bf16[16,144,384]{2,1,0:T(8,128)(2,1)S(1)} async-done(((bf16[16,144,384]{2,1,0:T(8,128)(2,1)}), bf16[16,144,384]{2,1,0:T(8,128)(2,1)S(1)}, u32[]{:S(2)}, u32[]{:S(2)}) %all-to-all-start.3) | async-done | bytes 1769504 | tf_op jit(solution)/shard_map/all_to_all | solution.py:36
  136.5 3.0 %collective-permute-start.16 = (bf16[256,768]{1,0:T(8,128)(2,1)S(1)}, bf16[256,768]{1,0:T(8,128)(2,1)S(1)}, u32[]{:S(2)}, u32[]{:S(2)}) collective-permute-start(bf16[256,768]{1,0:T(8,128)(2,1)S(1)} %pad_maximum_fusion.2.refs_0_), channel_id=1, source_target_pairs={{2,0},{4,2},{6,4},{0,6},{3,1},{5,3},{7,5},{1,7},{10,8},{12,10},{14... | collective-permute-start | bytes 1179656 | tf_op jit(solution)/shard_map/ppermute | solution.py:44
  143.2 17.9 %collective-permute-done.24 = bf16[136,384]{1,0:T(8,128)(2,1)S(1)} collective-permute-done((bf16[136,384]{1,0:T(8,128)(2,1)S(1)}, bf16[136,384]{1,0:T(8,128)(2,1)S(1)}, u32[]{:S(2)}, u32[]{:S(2)}) %collective-permute-start.24) | collective-permute-done | bytes 104480 | tf_op jit(solution)/shard_map/ppermute | solution.py:44
  162.1 3.7 %collective-permute-done.23 = bf16[136,384]{1,0:T(8,128)(2,1)S(1)} collective-permute-done((bf16[136,384]{1,0:T(8,128)(2,1)S(1)}, bf16[136,384]{1,0:T(8,128)(2,1)S(1)}, u32[]{:S(2)}, u32[]{:S(2)}) %collective-permute-start.23) | collective-permute-done | bytes 104480 | tf_op jit(solution)/shard_map/ppermute | solution.py:44
  170.2 5.6 %hidden_units.1 = (bf16[1088,768]{1,0:T(8,128)(2,1)}, bf16[1088,768]{1,0:T(8,128)(2,1)}, bf16[192,1088]{1,0:T(8,128)(2,1)}, bf16[192,1088]{1,0:T(8,128)(2,1)}, f32[192,1088]{1,0:T(8,128)}, /*index=5*/f32[192,1088]{1,0:T(8,128)}) custom-call(bf16[256,768]{1,0:T(8,128)(2,1)} %copy-done.5, bf16[256,768]{1,0:T(8,128)(2,1)} %copy-done.17, ...), custom_call_target="tpu_custom_call" | custom-call | tf_op jit(solution)/shard_map/hidden_units/pallas_call | solution.py:348
  176.7 4.3 %first_weights.1.sums = f32[192,1152]{1,0:T(8,128)} custom-call(bf16[544,384]{1,0:T(8,128)(2,1)} %copy-done.3, bf16[544,384]{1,0:T(8,128)(2,1)} %copy-done.15, bf16[1088,768]{1,0:T(8,128)(2,1)} %get-tuple-element.39.rows, bf16[192,1088]{1,0:T(8,128)(2,1)} %get-tuple-element.40.hidden, f32[192,1088]{1,0:T(8,128)} %get-tuple-element.41.slope, ...), custom_call_target="tpu_custom_call" | custom-call | tf_op jit(solution)/shard_map/first_weights/pallas_call | solution.py:417
  181.8 4.2 %last_weights.1 = bf16[128,1792]{1,0:T(8,128)(2,1)} custom-call(f32[192,1152]{1,0:T(8,128)} %first_weights.1.sums, bf16[544,384]{1,0:T(8,128)(2,1)} %copy-done.4, bf16[544,384]{1,0:T(8,128)(2,1)} %copy-done.16, bf16[1088,768]{1,0:T(8,128)(2,1)} %get-tuple-element.42.rows, bf16[192,1088]{1,0:T(8,128)(2,1)} %get-tuple-element.43.hidden, ...), custom_call_target="tpu_custom_call" | custom-call | tf_op jit(solution)/shard_map/last_weights/pallas_call | solution.py:425
  186.0 5.1 %all-to-all-start.4 = ((bf16[16,8,1792]{2,1,0:T(8,128)(2,1)}), bf16[16,8,1792]{2,1,0:T(8,128)(2,1)S(1)}, u32[]{:S(2)}, u32[]{:S(2)}) async-start(bf16[16,8,1792]{2,1,0:T(8,128)(2,1)} %bitcast.33), calls=%async_computation.4 | async-start | bytes 917504 | tf_op jit(solution)/shard_map/all_to_all | solution.py:36
  193.6 8.6 %all-to-all-done.4 = bf16[16,8,1792]{2,1,0:T(8,128)(2,1)S(1)} async-done(((bf16[16,8,1792]{2,1,0:T(8,128)(2,1)}), bf16[16,8,1792]{2,1,0:T(8,128)(2,1)S(1)}, u32[]{:S(2)}, u32[]{:S(2)}) %all-to-all-start.4) | async-done | bytes 458784 | tf_op jit(solution)/shard_map/all_to_all | solution.py:36
  (137 shorter events, 39.7 us)
Async XLA Ops:
  2.7 22.6 %all-to-all-start = ((bf16[16,8,1664]{2,1,0:T(8,128)(2,1)}), bf16[16,8,1664]{2,1,0:T(8,128)(2,1)S(1)}, u32[]{:S(2)}, u32[]{:S(2)}) async-start(bf16[16,8,1664]{2,1,0:T(8,128)(2,1)} %get-tuple-element.25), calls=%async_computation | async-start | bytes 851968 | tf_op jit(solution)/shard_map/all_to_all | solution.py:36
  16.0 6.4 %collective-permute-start.2 = (bf16[128,384]{1,0:T(8,128)(2,1)S(1)}, bf16[128,384]{1,0:T(8,128)(2,1)S(1)}, u32[]{:S(2)}, u32[]{:S(2)}) collective-permute-start(bf16[128,384]{1,0:T(8,128)(2,1)S(1)} %get-tuple-element.53), channel_id=1, source_target_pairs={{6,0},{0,2},{2,4},{4,6},{7,1},{1,3},{3,5},{5,7},{14,8},{8,10},{10,... | collective-permute-start | bytes 294920 | tf_op jit(solution)/shard_map/ppermute | solution.py:44
  17.6 7.2 %collective-permute-start.1 = (bf16[128,384]{1,0:T(8,128)(2,1)S(1)}, bf16[128,384]{1,0:T(8,128)(2,1)S(1)}, u32[]{:S(2)}, u32[]{:S(2)}) collective-permute-start(bf16[128,384]{1,0:T(8,128)(2,1)S(1)} %get-tuple-element.53), channel_id=1, source_target_pairs={{4,0},{6,2},{0,4},{2,6},{5,1},{7,3},{1,5},{3,7},{12,8},{14,10},{8,... | collective-permute-start | bytes 294920 | tf_op jit(solution)/shard_map/ppermute | solution.py:44
  25.1 41.6 %collective-permute-start.3 = (bf16[512,384]{1,0:T(8,128)(2,1)S(1)}, bf16[512,384]{1,0:T(8,128)(2,1)S(1)}, u32[]{:S(2)}, u32[]{:S(2)}) collective-permute-start(bf16[512,384]{1,0:T(8,128)(2,1)S(1)} %pad_maximum_fusion.3.q_own), channel_id=1, source_target_pairs={{0,1},{1,0},{2,3},{3,2},{4,5},{5,4},{6,7},{7,6},{8,9},{9,8},{10,11... | collective-permute-start | bytes 1179656 | tf_op jit(solution)/shard_map/ppermute | solution.py:32
  30.7 14.1 %collective-permute-start.4 = (bf16[16,1152]{1,0:T(8,128)(2,1)}, bf16[16,1152]{1,0:T(8,128)(2,1)S(1)}, u32[]{:S(2)}, u32[]{:S(2)}) collective-permute-start(bf16[16,1152]{1,0:T(8,128)(2,1)} %get-tuple-element.26), channel_id=1, source_target_pairs={{2,0},{4,2},{6,4},{0,6},{3,1},{5,3},{7,5},{1,7},{10,8},{12,10},{14... | collective-permute-start | bytes 110600 | tf_op jit(solution)/shard_map/ppermute | solution.py:44
  33.3 11.5 %collective-permute-start.5 = (bf16[16,1152]{1,0:T(8,128)(2,1)}, bf16[16,1152]{1,0:T(8,128)(2,1)S(1)}, u32[]{:S(2)}, u32[]{:S(2)}) collective-permute-start(bf16[16,1152]{1,0:T(8,128)(2,1)} %get-tuple-element.26), channel_id=1, source_target_pairs={{4,0},{6,2},{0,4},{2,6},{5,1},{7,3},{1,5},{3,7},{12,8},{14,10},{8,... | collective-permute-start | bytes 110600 | tf_op jit(solution)/shard_map/ppermute | solution.py:44
  33.6 11.2 %collective-permute-start.6 = (bf16[16,1152]{1,0:T(8,128)(2,1)}, bf16[16,1152]{1,0:T(8,128)(2,1)S(1)}, u32[]{:S(2)}, u32[]{:S(2)}) collective-permute-start(bf16[16,1152]{1,0:T(8,128)(2,1)} %get-tuple-element.26), channel_id=1, source_target_pairs={{6,0},{0,2},{2,4},{4,6},{7,1},{1,3},{3,5},{5,7},{14,8},{8,10},{10,... | collective-permute-start | bytes 110600 | tf_op jit(solution)/shard_map/ppermute | solution.py:44
  34.5 32.3 %all-to-all-start.1 = ((bf16[16,136,384]{2,1,0:T(8,128)(2,1)}), bf16[16,136,384]{2,1,0:T(8,128)(2,1)S(1)}, u32[]{:S(2)}, u32[]{:S(2)}) async-start(bf16[16,136,384]{2,1,0:T(8,128)(2,1)} %get-tuple-element.29), calls=%async_computation.1 | async-start | bytes 3342336 | tf_op jit(solution)/shard_map/all_to_all | solution.py:36
  44.8 21.9 %collective-permute-start.7 = (bf16[64,1152]{1,0:T(8,128)(2,1)S(1)}, bf16[64,1152]{1,0:T(8,128)(2,1)S(1)}, u32[]{:S(2)}, u32[]{:S(2)}) collective-permute-start(bf16[64,1152]{1,0:T(8,128)(2,1)S(1)} %constant_dynamic-update-slice_fusion.t_own.refs_8_), channel_id=1, source_target_pairs={{0,1},{1,0},{2,3},{3,2},{4,5},{5,4},{6,7},{7,6},{8,9},{9,8},{10,11... | collective-permute-start | bytes 442376 | tf_op jit(solution)/shard_map/ppermute | solution.py:32
  104.4 31.1 %all-to-all-start.3 = ((bf16[16,144,384]{2,1,0:T(8,128)(2,1)}), bf16[16,144,384]{2,1,0:T(8,128)(2,1)S(1)}, u32[]{:S(2)}, u32[]{:S(2)}) async-start(bf16[16,144,384]{2,1,0:T(8,128)(2,1)} %bitcast.10), calls=%async_computation.3 | async-start | bytes 3538944 | tf_op jit(solution)/shard_map/all_to_all | solution.py:36
  109.7 7.3 %collective-permute-start.10 = (bf16[136,384]{1,0:T(8,128)(2,1)S(1)}, bf16[136,384]{1,0:T(8,128)(2,1)S(1)}, u32[]{:S(2)}, u32[]{:S(2)}) collective-permute-start(bf16[136,384]{1,0:T(8,128)(2,1)S(1)} %get-tuple-element.49), channel_id=1, source_target_pairs={{0,4},{2,6},{4,0},{6,2},{1,5},{3,7},{5,1},{7,3},{8,12},{10,14},{12... | collective-permute-start | bytes 313352 | tf_op jit(solution)/shard_map/ppermute | solution.py:48
  111.2 7.2 %collective-permute-start.9 = (bf16[136,384]{1,0:T(8,128)(2,1)S(1)}, bf16[136,384]{1,0:T(8,128)(2,1)S(1)}, u32[]{:S(2)}, u32[]{:S(2)}) collective-permute-start(bf16[136,384]{1,0:T(8,128)(2,1)S(1)} %get-tuple-element.47), channel_id=1, source_target_pairs={{0,2},{2,4},{4,6},{6,0},{1,3},{3,5},{5,7},{7,1},{8,10},{10,12},{12... | collective-permute-start | bytes 313352 | tf_op jit(solution)/shard_map/ppermute | solution.py:48
  118.5 20.9 %collective-permute-start.14 = (bf16[136,384]{1,0:T(8,128)(2,1)S(1)}, bf16[136,384]{1,0:T(8,128)(2,1)S(1)}, u32[]{:S(2)}, u32[]{:S(2)}) collective-permute-start(bf16[136,384]{1,0:T(8,128)(2,1)S(1)} %fusion.18), channel_id=1, source_target_pairs={{6,0},{0,2},{2,4},{4,6},{7,1},{1,3},{3,5},{5,7},{14,8},{8,10},{10,... | collective-permute-start | bytes 313352 | tf_op jit(solution)/shard_map/ppermute | solution.py:44
  118.6 20.9 %collective-permute-start.13 = (bf16[136,384]{1,0:T(8,128)(2,1)S(1)}, bf16[136,384]{1,0:T(8,128)(2,1)S(1)}, u32[]{:S(2)}, u32[]{:S(2)}) collective-permute-start(bf16[136,384]{1,0:T(8,128)(2,1)S(1)} %fusion.18), channel_id=1, source_target_pairs={{4,0},{6,2},{0,4},{2,6},{5,1},{7,3},{1,5},{3,7},{12,8},{14,10},{8,... | collective-permute-start | bytes 313352 | tf_op jit(solution)/shard_map/ppermute | solution.py:44
  120.6 19.8 %collective-permute-start.12 = (bf16[136,384]{1,0:T(8,128)(2,1)S(1)}, bf16[136,384]{1,0:T(8,128)(2,1)}, u32[]{:S(2)}, u32[]{:S(2)}) collective-permute-start(bf16[136,384]{1,0:T(8,128)(2,1)S(1)} %fusion.18), channel_id=1, source_target_pairs={{2,0},{4,2},{6,4},{0,6},{3,1},{5,3},{7,5},{1,7},{10,8},{12,10},{14... | collective-permute-start | bytes 313352 | tf_op jit(solution)/shard_map/ppermute | solution.py:44
  135.8 6.0 %collective-permute-start.25 = (bf16[136,384]{1,0:T(8,128)(2,1)S(1)}, bf16[136,384]{1,0:T(8,128)(2,1)S(1)}, u32[]{:S(2)}, u32[]{:S(2)}) collective-permute-start(bf16[136,384]{1,0:T(8,128)(2,1)S(1)} %slice.95), channel_id=1, source_target_pairs={{6,0},{0,2},{2,4},{4,6},{7,1},{1,3},{3,5},{5,7},{14,8},{8,10},{10,... | collective-permute-start | bytes 313352 | tf_op jit(solution)/shard_map/ppermute | solution.py:44
  136.5 29.3 %collective-permute-start.16 = (bf16[256,768]{1,0:T(8,128)(2,1)S(1)}, bf16[256,768]{1,0:T(8,128)(2,1)S(1)}, u32[]{:S(2)}, u32[]{:S(2)}) collective-permute-start(bf16[256,768]{1,0:T(8,128)(2,1)S(1)} %pad_maximum_fusion.2.refs_0_), channel_id=1, source_target_pairs={{2,0},{4,2},{6,4},{0,6},{3,1},{5,3},{7,5},{1,7},{10,8},{12,10},{14... | collective-permute-start | bytes 1179656 | tf_op jit(solution)/shard_map/ppermute | solution.py:44
  139.5 27.0 %collective-permute-start.17 = (bf16[256,768]{1,0:T(8,128)(2,1)S(1)}, bf16[256,768]{1,0:T(8,128)(2,1)S(1)}, u32[]{:S(2)}, u32[]{:S(2)}) collective-permute-start(bf16[256,768]{1,0:T(8,128)(2,1)S(1)} %pad_maximum_fusion.2.refs_0_), channel_id=1, source_target_pairs={{4,0},{6,2},{0,4},{2,6},{5,1},{7,3},{1,5},{3,7},{12,8},{14,10},{8,... | collective-permute-start | bytes 1179656 | tf_op jit(solution)/shard_map/ppermute | solution.py:44
  139.5 27.1 %collective-permute-start.18 = (bf16[256,768]{1,0:T(8,128)(2,1)S(1)}, bf16[256,768]{1,0:T(8,128)(2,1)S(1)}, u32[]{:S(2)}, u32[]{:S(2)}) collective-permute-start(bf16[256,768]{1,0:T(8,128)(2,1)S(1)} %pad_maximum_fusion.2.refs_0_), channel_id=1, source_target_pairs={{6,0},{0,2},{2,4},{4,6},{7,1},{1,3},{3,5},{5,7},{14,8},{8,10},{10,... | collective-permute-start | bytes 1179656 | tf_op jit(solution)/shard_map/ppermute | solution.py:44
  140.4 26.5 %collective-permute-start.19 = (bf16[256,768]{1,0:T(8,128)(2,1)S(1)}, bf16[256,768]{1,0:T(8,128)(2,1)S(1)}, u32[]{:S(2)}, u32[]{:S(2)}) collective-permute-start(bf16[256,768]{1,0:T(8,128)(2,1)S(1)} %pad_maximum_fusion.2.refs_0_), channel_id=1, source_target_pairs={{0,1},{1,0},{2,3},{3,2},{4,5},{5,4},{6,7},{7,6},{8,9},{9,8},{10,11... | collective-permute-start | bytes 1179656 | tf_op jit(solution)/shard_map/ppermute | solution.py:32
  141.8 19.3 %collective-permute-start.24 = (bf16[136,384]{1,0:T(8,128)(2,1)S(1)}, bf16[136,384]{1,0:T(8,128)(2,1)S(1)}, u32[]{:S(2)}, u32[]{:S(2)}) collective-permute-start(bf16[136,384]{1,0:T(8,128)(2,1)S(1)} %slice.95), channel_id=1, source_target_pairs={{4,0},{6,2},{0,4},{2,6},{5,1},{7,3},{1,5},{3,7},{12,8},{14,10},{8,... | collective-permute-start | bytes 313352 | tf_op jit(solution)/shard_map/ppermute | solution.py:44
  165.8 10.1 %collective-permute-start.15 = (bf16[544,384]{1,0:T(8,128)(2,1)S(1)}, bf16[544,384]{1,0:T(8,128)(2,1)S(1)}, u32[]{:S(2)}, u32[]{:S(2)}) collective-permute-start(bf16[544,384]{1,0:T(8,128)(2,1)S(1)} %pad_maximum_fusion.de_own), channel_id=1, source_target_pairs={{0,1},{1,0},{2,3},{3,2},{4,5},{5,4},{6,7},{7,6},{8,9},{9,8},{10,11... | collective-permute-start | bytes 1253384 | tf_op jit(solution)/shard_map/ppermute | solution.py:32
  165.9 15.1 %collective-permute-start.26 = (bf16[544,384]{1,0:T(8,128)(2,1)S(1)}, bf16[544,384]{1,0:T(8,128)(2,1)S(1)}, u32[]{:S(2)}, u32[]{:S(2)}) collective-permute-start(bf16[544,384]{1,0:T(8,128)(2,1)S(1)} %pad_maximum_fusion.1.de_own), channel_id=1, source_target_pairs={{0,1},{1,0},{2,3},{3,2},{4,5},{5,4},{6,7},{7,6},{8,9},{9,8},{10,11... | collective-permute-start | bytes 1253384 | tf_op jit(solution)/shard_map/ppermute | solution.py:32
  186.0 16.2 %all-to-all-start.4 = ((bf16[16,8,1792]{2,1,0:T(8,128)(2,1)}), bf16[16,8,1792]{2,1,0:T(8,128)(2,1)S(1)}, u32[]{:S(2)}, u32[]{:S(2)}) async-start(bf16[16,8,1792]{2,1,0:T(8,128)(2,1)} %bitcast.33), calls=%async_computation.4 | async-start | bytes 917504 | tf_op jit(solution)/shard_map/all_to_all | solution.py:36
  (33 other events, 275.6 us)

commit v7 on v6

--- a/solution.py
+++ b/solution.py
@@ -8,6 +8,7 @@
 from jax.sharding import Mesh
 from jax.sharding import PartitionSpec as P
 
+
 DP = ("dp_0", "dp_1", "dp_2", "dp_3")
 PLANE = ("dp_0", "dp_1")
 LINE = "dp_2"
@@ -42,10 +43,6 @@
 
 def from_line(x, k):
     return lax.ppermute(x, LINE, [((i + k) % 4, i) for i in range(4)])
-
-
-def to_line(x, k):
-    return lax.ppermute(x, LINE, [(i, (i + k) % 4) for i in range(4)])
 
 
 def along_line(x):
@@ -269,6 +266,14 @@
         put(j, slice(LOW, BLOCK), dq[j * UNIT : (j + 1) * UNIT])
 
 
+def total_kernel(*refs):
+    parts, out = refs[:4], refs[4]
+    for b in range(4):
+        blocks = [part[(b - k) % 4].astype(F32) for k, part in enumerate(parts)]
+        total = (blocks[0] + blocks[1]) + (blocks[2] + blocks[3])
+        out[b * BLOCK : (b + 1) * BLOCK] = total.astype(BF16)
+
+
 def weight_parts(de_own, de_far, rows, hidden, slope, second, de):
     half = de_own.shape[0]
     de[:half] = de_own[...]
@@ -409,6 +414,17 @@
     )(sc, p, g)
 
 
+def line_total(parts):
+    blocks, rows, width = parts[0].shape
+    return pl.pallas_call(
+        total_kernel,
+        in_specs=[VMEM] * 4,
+        out_specs=VMEM,
+        out_shape=jax.ShapeDtypeStruct((blocks * rows, width), BF16),
+        name="line_total",
+    )(*parts)
+
+
 def weight_grads(sums, des, rows, hidden, slope, second):
     scratch = [pltpu.VMEM((8 * BLOCK, second.shape[1]), BF16)]
     operands = (*des, rows, hidden, slope, second)
@@ -497,10 +513,9 @@
     dq_own, dq_far = query_grads(sc, p_all, g, scale)
 
     dq = dq_own + swap_core(dq_far)
-    dq_sum = dq[0].astype(BF16).astype(F32)
-    for k in (1, 2, 3):
-        dq_sum = dq_sum + to_line(dq[k].astype(BF16), k).astype(F32)
-    dqs = gathered(dq_sum.astype(BF16))
+    parts = along_line(dq.astype(BF16))
+    dq_sum = line_total(parts)
+    dqs = (dq_sum, swap_core(dq_sum))
 
     dp_sum = jnp.sum(dp_all.reshape(16, CHUNK, emb_width).astype(F32), axis=0)
     mean_loss = (dp_sum[BLOCK, 0] + dp_sum[BLOCK + 1, 0] + dp_sum[BLOCK + 2, 0]) / pairs

time: 206 us -> 203 us (0.985)
  waiting for transfers between devices: 74.5 us -> 69 us
  Pallas kernels: 44.5 us -> 46.8 us
    ppermute x3 -> x0, waiting for transfers between devices: 7.22 us -> none  [to_line(): return lax.ppermute(x, LINE, [(i, (i + k) % 4) for i in range(4)])]
    ppermute x9, waiting for transfers between devices: 1.01 us -> 4.49 us  [swap_core(): return lax.ppermute(x, CORE, [(0, 1), (1, 0)])]
    ppermute x3 -> x0, starting transfers between devices: 2.71 us -> none  [to_line(): return lax.ppermute(x, LINE, [(i, (i + k) % 4) for i in range(4)])]
    pallas_call x0 -> x1, Pallas kernels: none -> 2.36 us  [line_total(): pl.pallas_call(total_kernel, in_specs=[VMEM] * 4, out_specs=VMEM, out_sha...]
    unnamed x55 -> x37, local copies, waits for them, and re-layouts: 5.43 us -> 4.49 us
  transfers between devices with their start and end apart: 31 -> 28, of which waited for: 14 -> 14; matrix products, arithmetic and copies ran while one was open for 7% -> 8% of each run, Pallas kernels for 7% -> 12%
where the time goes in v7:
time: 203 us; the launch traced here: 202 us
  waiting for transfers between devices  69 us (34%)
  starting transfers between devices  48.4 us (24%)
  Pallas kernels  46.8 us (23%)
  blocking collectives  11.9 us (6%)
  local copies, waits for them, and re-layouts  10.7 us (5%)
  matrix products  7.08 us (3%)
  between operations  4.77 us (2%)
  other arithmetic  3.31 us (2%)
    all_to_all x4, waiting for transfers between devices, plane_exchange(): return lax.all_to_all(x, PLANE, 0, 0, tiled=True)  38.1 us
    ppermute x15, waiting for transfers between devices, from_line(): return lax.ppermute(x, LINE, [((i + k) % 4, i) for i in range(4)])  26.5 us
    all_to_all x4, starting transfers between devices, plane_exchange(): return lax.all_to_all(x, PLANE, 0, 0, tiled=True)  26.1 us
    ppermute x15, starting transfers between devices, from_line(): return lax.ppermute(x, LINE, [((i + k) % 4, i) for i in range(4)])  20.8 us
    all_to_all x1, blocking collectives, stats_exchange(): return lax.all_to_all(x, (LINE, CORE), 0, 0, tiled=True)  11.9 us
    pallas_call x1, Pallas kernels, score_grads(): pl.pallas_call(functools.partial(grads_kernel, scale=scale), in_specs=[VM...  8.85 us
    pallas_call x1, Pallas kernels, query_grads(): pl.pallas_call(functools.partial(query_kernel, scale=scale), in_specs=[SM...  8.02 us
    pallas_call x1, Pallas kernels, score_stats(): pl.pallas_call(functools.partial(stats_kernel, scale=scale), in_specs=[SM...  6.76 us
  transfers between devices with their start and end apart: 28, of which 14 were waited for; matrix products, arithmetic and copies ran while one was open for 8% of the time, Pallas kernels for 12%

profile of v7, /device:TPU:0, one launch (start us, length us, event | category | flops | bytes accessed | tf_op | source)
XLA Modules:
  0.0 201.9 jit_solution(12713077453670226407)
XLA Ops:
  2.7 8.0 %all-to-all-start = ((bf16[16,8,1664]{2,1,0:T(8,128)(2,1)}), bf16[16,8,1664]{2,1,0:T(8,128)(2,1)S(1)}, u32[]{:S(2)}, u32[]{:S(2)}) async-start(bf16[16,8,1664]{2,1,0:T(8,128)(2,1)} %get-tuple-element.25), calls=%async_computation | async-start | bytes 851968 | tf_op jit(solution)/shard_map/all_to_all | solution.py:37
  12.6 2.6 %convolution_convert_fusion.1 = bf16[256,384]{1,0:T(8,128)(2,1)S(1)} fusion(bf16[1536,384]{1,0:T(8,128)(2,1)} %w_second.1, bf16[768,1536]{1,0:T(8,128)(2,1)S(1)} %copy-done.1, bf16[128,768]{1,0:T(8,128)(2,1)S(1)} %slice.41, bf16[128,768]{1,0:T(8,128)(2,1)S(1)} %slice.40), kind=kOutput, calls=%fused_computation.13 | convolution fusion | flops 910393344 | bytes 4128768 | tf_op jit(solution)/shard_map/dot_general | solution.py:467
  17.4 2.9 %collective-permute-start.1 = (bf16[128,384]{1,0:T(8,128)(2,1)S(1)}, bf16[128,384]{1,0:T(8,128)(2,1)S(1)}, u32[]{:S(2)}, u32[]{:S(2)}) collective-permute-start(bf16[128,384]{1,0:T(8,128)(2,1)S(1)} %get-tuple-element.50), channel_id=1, source_target_pairs={{4,0},{6,2},{0,4},{2,6},{5,1},{7,3},{1,5},{3,7},{12,8},{14,10},{8,... | collective-permute-start | bytes 294920 | tf_op jit(solution)/shard_map/ppermute | solution.py:45
  25.9 4.6 %tail_rows.1 = (bf16[16,136,384]{2,1,0:T(8,128)(2,1)}, bf16[16,1152]{1,0:T(8,128)(2,1)}) custom-call(s32[1]{0:T(128)} %get-tuple-element.24.heavy_at, bf16[16,8,1664]{2,1,0:T(8,128)(2,1)} %copy-done.2, bf16[128,384]{1,0:T(8,128)(2,1)} %get-tuple-element.51.base_p, s32[2,128]{1,0:T(2,128)} %bitcast.28, bf16[768,1536]{1,0:T(8,128)(2,1)} %w_first.1, ...), custom_call_target="tpu_custom_call" | custom-call | tf_op jit(solution)/shard_map/tail_rows/pallas_call | solution.py:337
  30.5 2.6 %collective-permute-start.4 = (bf16[16,1152]{1,0:T(8,128)(2,1)}, bf16[16,1152]{1,0:T(8,128)(2,1)S(1)}, u32[]{:S(2)}, u32[]{:S(2)}) collective-permute-start(bf16[16,1152]{1,0:T(8,128)(2,1)} %get-tuple-element.26), channel_id=1, source_target_pairs={{2,0},{4,2},{6,4},{0,6},{3,1},{5,3},{7,5},{1,7},{10,8},{12,10},{14... | collective-permute-start | bytes 110600 | tf_op jit(solution)/shard_map/ppermute | solution.py:45
  34.3 7.1 %all-to-all-start.1 = ((bf16[16,136,384]{2,1,0:T(8,128)(2,1)}), bf16[16,136,384]{2,1,0:T(8,128)(2,1)S(1)}, u32[]{:S(2)}, u32[]{:S(2)}) async-start(bf16[16,136,384]{2,1,0:T(8,128)(2,1)} %get-tuple-element.29), calls=%async_computation.1 | async-start | bytes 3342336 | tf_op jit(solution)/shard_map/all_to_all | solution.py:37
  44.9 3.3 %convolution_convert_fusion.refs_10_ = bf16[192,768]{1,0:T(8,128)(2,1)} fusion(bf16[768,1536]{1,0:T(8,128)(2,1)} %w_first.1, s32[192]{0:T(256)S(1)} %fusion.26), kind=kOutput, calls=%fused_computation.10 | convolution fusion | flops 453427200 | bytes 2654976 | tf_op jit(solution)/shard_map/dot_general | solution.py:502
  48.2 18.2 %all-to-all-done.1 = bf16[16,136,384]{2,1,0:T(8,128)(2,1)S(1)} async-done(((bf16[16,136,384]{2,1,0:T(8,128)(2,1)}), bf16[16,136,384]{2,1,0:T(8,128)(2,1)S(1)}, u32[]{:S(2)}, u32[]{:S(2)}) %all-to-all-start.1) | async-done | bytes 1671200 | tf_op jit(solution)/shard_map/all_to_all | solution.py:37
  68.5 6.8 %score_stats.1 = (bf16[1088,384]{1,0:T(8,128)(2,1)}, s32[1,1088]{1,0:T(1,128)}, f32[64,1088]{1,0:T(8,128)}) custom-call(s32[29]{0:T(128)} %concatenate.22.sc, bf16[512,384]{1,0:T(8,128)(2,1)} %copy-done.6, bf16[512,384]{1,0:T(8,128)(2,1)} %copy-done.14, bf16[64,1152]{1,0:T(8,128)(2,1)} %copy-done.8, bf16[64,1152]{1,0:T(8,128)(2,1)} %copy-done.9, ...), custom_call_target="tpu_custom_call" | custom-call | tf_op jit(solution)/shard_map/score_stats/pallas_call | solution.py:366
  75.2 11.9 %all_to_all.44 = f32[8,8,1088]{2,1,0:T(8,128)} all-to-all(f32[8,8,1088]{2,1,0:T(8,128)} %bitcast.25), channel_id=1, replica_groups=mesh['dp_0'=4,'dp_1'=4,'dp_2'=4,'dp_3'=2] {'dp_2','dp_3'}, dimensions={0} | all-to-all | bytes 557056 | tf_op jit(solution)/shard_map/all_to_all | solution.py:41
  87.1 8.9 %score_grads.1 = (bf16[2304,384]{1,0:T(8,128)(2,1)}, bf16[2176,1088]{1,0:T(8,128)(2,1)}) custom-call(f32[64,1088]{1,0:T(8,128)} %bitcast.24, bf16[1088,384]{1,0:T(8,128)(2,1)} %get-tuple-element.32.q, bf16[2176,384]{1,0:T(8,128)(2,1)} %bitcast.20, s32[1,1088]{1,0:T(1,128)} %get-tuple-element.33.place), custom_call_target="tpu_custom_call" | custom-call | tf_op jit(solution)/shard_map/score_grads/pallas_call | solution.py:384
  96.0 3.8 %all-to-all-start.3 = ((bf16[16,144,384]{2,1,0:T(8,128)(2,1)}), bf16[16,144,384]{2,1,0:T(8,128)(2,1)S(1)}, u32[]{:S(2)}, u32[]{:S(2)}) async-start(bf16[16,144,384]{2,1,0:T(8,128)(2,1)} %bitcast.23), calls=%async_computation.3 | async-start | bytes 3538944 | tf_op jit(solution)/shard_map/all_to_all | solution.py:37
  99.8 8.0 %query_grads.1 = (f32[4,136,384]{2,1,0:T(8,128)}, f32[4,136,384]{2,1,0:T(8,128)}) custom-call(s32[29]{0:T(128)} %concatenate.22.sc, bf16[2176,384]{1,0:T(8,128)(2,1)} %bitcast.21, bf16[2176,1088]{1,0:T(8,128)(2,1)} %get-tuple-element.35.g_in), custom_call_target="tpu_custom_call" | custom-call | tf_op jit(solution)/shard_map/query_grads/pallas_call | solution.py:403
  108.0 2.6 %collective-permute-done.8 = f32[4,136,384]{2,1,0:T(8,128)S(1)} collective-permute-done((f32[4,136,384]{2,1,0:T(8,128)}, f32[4,136,384]{2,1,0:T(8,128)S(1)}, u32[]{:S(2)}, u32[]{:S(2)}) %collective-permute-start.8) | collective-permute-done | bytes 835616 | tf_op jit(solution)/shard_map/ppermute | solution.py:33
  114.5 12.0 %all-to-all-done.3 = bf16[16,144,384]{2,1,0:T(8,128)(2,1)S(1)} async-done(((bf16[16,144,384]{2,1,0:T(8,128)(2,1)}), bf16[16,144,384]{2,1,0:T(8,128)(2,1)S(1)}, u32[]{:S(2)}, u32[]{:S(2)}) %all-to-all-start.3) | async-done | bytes 1769504 | tf_op jit(solution)/shard_map/all_to_all | solution.py:37
  127.5 2.7 %collective-permute-start.13 = (bf16[256,768]{1,0:T(8,128)(2,1)S(1)}, bf16[256,768]{1,0:T(8,128)(2,1)}, u32[]{:S(2)}, u32[]{:S(2)}) collective-permute-start(bf16[256,768]{1,0:T(8,128)(2,1)S(1)} %pad_maximum_fusion.1.refs_0_), channel_id=1, source_target_pairs={{2,0},{4,2},{6,4},{0,6},{3,1},{5,3},{7,5},{1,7},{10,8},{12,10},{14... | collective-permute-start | bytes 1179656 | tf_op jit(solution)/shard_map/ppermute | solution.py:45
  130.2 3.7 %collective-permute-start.15 = (bf16[256,768]{1,0:T(8,128)(2,1)S(1)}, bf16[256,768]{1,0:T(8,128)(2,1)}, u32[]{:S(2)}, u32[]{:S(2)}) collective-permute-start(bf16[256,768]{1,0:T(8,128)(2,1)S(1)} %pad_maximum_fusion.1.refs_0_), channel_id=1, source_target_pairs={{6,0},{0,2},{2,4},{4,6},{7,1},{1,3},{3,5},{5,7},{14,8},{8,10},{10,... | collective-permute-start | bytes 1179656 | tf_op jit(solution)/shard_map/ppermute | solution.py:45
  135.1 3.3 %collective-permute-done.22 = bf16[136,384]{1,0:T(8,128)(2,1)S(1)} collective-permute-done((bf16[136,384]{1,0:T(8,128)(2,1)S(1)}, bf16[136,384]{1,0:T(8,128)(2,1)S(1)}, u32[]{:S(2)}, u32[]{:S(2)}) %collective-permute-start.22) | collective-permute-done | bytes 104480 | tf_op jit(solution)/shard_map/ppermute | solution.py:45
  139.8 16.5 %collective-permute-done.21 = bf16[136,384]{1,0:T(8,128)(2,1)S(1)} collective-permute-done((bf16[136,384]{1,0:T(8,128)(2,1)S(1)}, bf16[136,384]{1,0:T(8,128)(2,1)S(1)}, u32[]{:S(2)}, u32[]{:S(2)}) %collective-permute-start.21) | collective-permute-done | bytes 104480 | tf_op jit(solution)/shard_map/ppermute | solution.py:45
  165.3 5.7 %hidden_units.1 = (bf16[1088,768]{1,0:T(8,128)(2,1)}, bf16[1088,768]{1,0:T(8,128)(2,1)}, bf16[192,1088]{1,0:T(8,128)(2,1)}, bf16[192,1088]{1,0:T(8,128)(2,1)}, f32[192,1088]{1,0:T(8,128)}, /*index=5*/f32[192,1088]{1,0:T(8,128)}) custom-call(bf16[256,768]{1,0:T(8,128)(2,1)} %copy-done.5, bf16[256,768]{1,0:T(8,128)(2,1)} %collective-permute-done.13.refs_1_, ...), custom_call_target="tpu_custom_call" | custom-call | tf_op jit(solution)/shard_map/hidden_units/pallas_call | solution.py:353
  171.8 4.3 %first_weights.1.sums = f32[192,1152]{1,0:T(8,128)} custom-call(bf16[544,384]{1,0:T(8,128)(2,1)} %line_total.1.de_own, bf16[544,384]{1,0:T(8,128)(2,1)} %copy-done.11, bf16[1088,768]{1,0:T(8,128)(2,1)} %get-tuple-element.39.rows, bf16[192,1088]{1,0:T(8,128)(2,1)} %get-tuple-element.40.hidden, f32[192,1088]{1,0:T(8,128)} %get-tuple-element.41.slope, ...), custom_call_target="tpu_custom_call" | custom-call | tf_op jit(solution)/shard_map/first_weights/pallas_call | solution.py:433
  176.9 4.2 %last_weights.1 = bf16[128,1792]{1,0:T(8,128)(2,1)} custom-call(f32[192,1152]{1,0:T(8,128)} %first_weights.1.sums, bf16[544,384]{1,0:T(8,128)(2,1)} %copy-done.4, bf16[544,384]{1,0:T(8,128)(2,1)} %copy-done.12, bf16[1088,768]{1,0:T(8,128)(2,1)} %get-tuple-element.42.rows, bf16[192,1088]{1,0:T(8,128)(2,1)} %get-tuple-element.43.hidden, ...), custom_call_target="tpu_custom_call" | custom-call | tf_op jit(solution)/shard_map/last_weights/pallas_call | solution.py:441
  181.1 7.2 %all-to-all-start.4 = ((bf16[16,8,1792]{2,1,0:T(8,128)(2,1)}), bf16[16,8,1792]{2,1,0:T(8,128)(2,1)S(1)}, u32[]{:S(2)}, u32[]{:S(2)}) async-start(bf16[16,8,1792]{2,1,0:T(8,128)(2,1)} %bitcast.22), calls=%async_computation.4 | async-start | bytes 917504 | tf_op jit(solution)/shard_map/all_to_all | solution.py:37
  191.6 7.8 %all-to-all-done.4 = bf16[16,8,1792]{2,1,0:T(8,128)(2,1)S(1)} async-done(((bf16[16,8,1792]{2,1,0:T(8,128)(2,1)}), bf16[16,8,1792]{2,1,0:T(8,128)(2,1)S(1)}, u32[]{:S(2)}, u32[]{:S(2)}) %all-to-all-start.4) | async-done | bytes 458784 | tf_op jit(solution)/shard_map/all_to_all | solution.py:37
  (111 shorter events, 38.6 us)
Async XLA Ops:
  2.7 22.4 %all-to-all-start = ((bf16[16,8,1664]{2,1,0:T(8,128)(2,1)}), bf16[16,8,1664]{2,1,0:T(8,128)(2,1)S(1)}, u32[]{:S(2)}, u32[]{:S(2)}) async-start(bf16[16,8,1664]{2,1,0:T(8,128)(2,1)} %get-tuple-element.25), calls=%async_computation | async-start | bytes 851968 | tf_op jit(solution)/shard_map/all_to_all | solution.py:37
  15.8 6.4 %collective-permute-start.2 = (bf16[128,384]{1,0:T(8,128)(2,1)S(1)}, bf16[128,384]{1,0:T(8,128)(2,1)S(1)}, u32[]{:S(2)}, u32[]{:S(2)}) collective-permute-start(bf16[128,384]{1,0:T(8,128)(2,1)S(1)} %get-tuple-element.50), channel_id=1, source_target_pairs={{6,0},{0,2},{2,4},{4,6},{7,1},{1,3},{3,5},{5,7},{14,8},{8,10},{10,... | collective-permute-start | bytes 294920 | tf_op jit(solution)/shard_map/ppermute | solution.py:45
  17.4 7.2 %collective-permute-start.1 = (bf16[128,384]{1,0:T(8,128)(2,1)S(1)}, bf16[128,384]{1,0:T(8,128)(2,1)S(1)}, u32[]{:S(2)}, u32[]{:S(2)}) collective-permute-start(bf16[128,384]{1,0:T(8,128)(2,1)S(1)} %get-tuple-element.50), channel_id=1, source_target_pairs={{4,0},{6,2},{0,4},{2,6},{5,1},{7,3},{1,5},{3,7},{12,8},{14,10},{8,... | collective-permute-start | bytes 294920 | tf_op jit(solution)/shard_map/ppermute | solution.py:45
  20.3 4.6 %collective-permute-start = (bf16[128,384]{1,0:T(8,128)(2,1)S(1)}, bf16[128,384]{1,0:T(8,128)(2,1)S(1)}, u32[]{:S(2)}, u32[]{:S(2)}) collective-permute-start(bf16[128,384]{1,0:T(8,128)(2,1)S(1)} %get-tuple-element.50), channel_id=1, source_target_pairs={{2,0},{4,2},{6,4},{0,6},{3,1},{5,3},{7,5},{1,7},{10,8},{12,10},{14... | collective-permute-start | bytes 294920 | tf_op jit(solution)/shard_map/ppermute | solution.py:45
  25.0 41.4 %collective-permute-start.3 = (bf16[512,384]{1,0:T(8,128)(2,1)S(1)}, bf16[512,384]{1,0:T(8,128)(2,1)S(1)}, u32[]{:S(2)}, u32[]{:S(2)}) collective-permute-start(bf16[512,384]{1,0:T(8,128)(2,1)S(1)} %pad_maximum_fusion.2.q_own), channel_id=1, source_target_pairs={{0,1},{1,0},{2,3},{3,2},{4,5},{5,4},{6,7},{7,6},{8,9},{9,8},{10,11... | collective-permute-start | bytes 1179656 | tf_op jit(solution)/shard_map/ppermute | solution.py:33
  30.5 14.3 %collective-permute-start.4 = (bf16[16,1152]{1,0:T(8,128)(2,1)}, bf16[16,1152]{1,0:T(8,128)(2,1)S(1)}, u32[]{:S(2)}, u32[]{:S(2)}) collective-permute-start(bf16[16,1152]{1,0:T(8,128)(2,1)} %get-tuple-element.26), channel_id=1, source_target_pairs={{2,0},{4,2},{6,4},{0,6},{3,1},{5,3},{7,5},{1,7},{10,8},{12,10},{14... | collective-permute-start | bytes 110600 | tf_op jit(solution)/shard_map/ppermute | solution.py:45
  33.0 11.7 %collective-permute-start.5 = (bf16[16,1152]{1,0:T(8,128)(2,1)}, bf16[16,1152]{1,0:T(8,128)(2,1)S(1)}, u32[]{:S(2)}, u32[]{:S(2)}) collective-permute-start(bf16[16,1152]{1,0:T(8,128)(2,1)} %get-tuple-element.26), channel_id=1, source_target_pairs={{4,0},{6,2},{0,4},{2,6},{5,1},{7,3},{1,5},{3,7},{12,8},{14,10},{8,... | collective-permute-start | bytes 110600 | tf_op jit(solution)/shard_map/ppermute | solution.py:45
  33.4 11.4 %collective-permute-start.6 = (bf16[16,1152]{1,0:T(8,128)(2,1)}, bf16[16,1152]{1,0:T(8,128)(2,1)S(1)}, u32[]{:S(2)}, u32[]{:S(2)}) collective-permute-start(bf16[16,1152]{1,0:T(8,128)(2,1)} %get-tuple-element.26), channel_id=1, source_target_pairs={{6,0},{0,2},{2,4},{4,6},{7,1},{1,3},{3,5},{5,7},{14,8},{8,10},{10,... | collective-permute-start | bytes 110600 | tf_op jit(solution)/shard_map/ppermute | solution.py:45
  34.3 32.1 %all-to-all-start.1 = ((bf16[16,136,384]{2,1,0:T(8,128)(2,1)}), bf16[16,136,384]{2,1,0:T(8,128)(2,1)S(1)}, u32[]{:S(2)}, u32[]{:S(2)}) async-start(bf16[16,136,384]{2,1,0:T(8,128)(2,1)} %get-tuple-element.29), calls=%async_computation.1 | async-start | bytes 3342336 | tf_op jit(solution)/shard_map/all_to_all | solution.py:37
  44.8 21.6 %collective-permute-start.7 = (bf16[64,1152]{1,0:T(8,128)(2,1)S(1)}, bf16[64,1152]{1,0:T(8,128)(2,1)S(1)}, u32[]{:S(2)}, u32[]{:S(2)}) collective-permute-start(bf16[64,1152]{1,0:T(8,128)(2,1)S(1)} %constant_dynamic-update-slice_fusion.t_own.refs_8_), channel_id=1, source_target_pairs={{0,1},{1,0},{2,3},{3,2},{4,5},{5,4},{6,7},{7,6},{8,9},{9,8},{10,11... | collective-permute-start | bytes 442376 | tf_op jit(solution)/shard_map/ppermute | solution.py:33
  96.0 30.5 %all-to-all-start.3 = ((bf16[16,144,384]{2,1,0:T(8,128)(2,1)}), bf16[16,144,384]{2,1,0:T(8,128)(2,1)S(1)}, u32[]{:S(2)}, u32[]{:S(2)}) async-start(bf16[16,144,384]{2,1,0:T(8,128)(2,1)} %bitcast.23), calls=%async_computation.3 | async-start | bytes 3538944 | tf_op jit(solution)/shard_map/all_to_all | solution.py:37
  111.8 18.5 %collective-permute-start.9 = (bf16[4,136,384]{2,1,0:T(8,128)(2,1)S(1)}, bf16[4,136,384]{2,1,0:T(8,128)(2,1)}, u32[]{:S(2)}, u32[]{:S(2)}) collective-permute-start(bf16[4,136,384]{2,1,0:T(8,128)(2,1)S(1)} %add_convert_fusion.refs_0_), channel_id=1, source_target_pairs={{2,0},{4,2},{6,4},{0,6},{3,1},{5,3},{7,5},{1,7},{10,8},{12,10},{14... | collective-permute-start | bytes 1253384 | tf_op jit(solution)/shard_map/ppermute | solution.py:45
  113.0 17.2 %collective-permute-start.10 = (bf16[4,136,384]{2,1,0:T(8,128)(2,1)S(1)}, bf16[4,136,384]{2,1,0:T(8,128)(2,1)}, u32[]{:S(2)}, u32[]{:S(2)}) collective-permute-start(bf16[4,136,384]{2,1,0:T(8,128)(2,1)S(1)} %add_convert_fusion.refs_0_), channel_id=1, source_target_pairs={{4,0},{6,2},{0,4},{2,6},{5,1},{7,3},{1,5},{3,7},{12,8},{14,10},{8,... | collective-permute-start | bytes 1253384 | tf_op jit(solution)/shard_map/ppermute | solution.py:45
  114.5 20.6 %collective-permute-start.11 = (bf16[4,136,384]{2,1,0:T(8,128)(2,1)S(1)}, bf16[4,136,384]{2,1,0:T(8,128)(2,1)}, u32[]{:S(2)}, u32[]{:S(2)}) collective-permute-start(bf16[4,136,384]{2,1,0:T(8,128)(2,1)S(1)} %add_convert_fusion.refs_0_), channel_id=1, source_target_pairs={{6,0},{0,2},{2,4},{4,6},{7,1},{1,3},{3,5},{5,7},{14,8},{8,10},{10,... | collective-permute-start | bytes 1253384 | tf_op jit(solution)/shard_map/ppermute | solution.py:45
  126.8 11.5 %collective-permute-start.22 = (bf16[136,384]{1,0:T(8,128)(2,1)S(1)}, bf16[136,384]{1,0:T(8,128)(2,1)S(1)}, u32[]{:S(2)}, u32[]{:S(2)}) collective-permute-start(bf16[136,384]{1,0:T(8,128)(2,1)S(1)} %slice.65), channel_id=1, source_target_pairs={{6,0},{0,2},{2,4},{4,6},{7,1},{1,3},{3,5},{5,7},{14,8},{8,10},{10,... | collective-permute-start | bytes 313352 | tf_op jit(solution)/shard_map/ppermute | solution.py:45
  127.5 33.5 %collective-permute-start.13 = (bf16[256,768]{1,0:T(8,128)(2,1)S(1)}, bf16[256,768]{1,0:T(8,128)(2,1)}, u32[]{:S(2)}, u32[]{:S(2)}) collective-permute-start(bf16[256,768]{1,0:T(8,128)(2,1)S(1)} %pad_maximum_fusion.1.refs_0_), channel_id=1, source_target_pairs={{2,0},{4,2},{6,4},{0,6},{3,1},{5,3},{7,5},{1,7},{10,8},{12,10},{14... | collective-permute-start | bytes 1179656 | tf_op jit(solution)/shard_map/ppermute | solution.py:45
  130.2 31.4 %collective-permute-start.14 = (bf16[256,768]{1,0:T(8,128)(2,1)S(1)}, bf16[256,768]{1,0:T(8,128)(2,1)}, u32[]{:S(2)}, u32[]{:S(2)}) collective-permute-start(bf16[256,768]{1,0:T(8,128)(2,1)S(1)} %pad_maximum_fusion.1.refs_0_), channel_id=1, source_target_pairs={{4,0},{6,2},{0,4},{2,6},{5,1},{7,3},{1,5},{3,7},{12,8},{14,10},{8,... | collective-permute-start | bytes 1179656 | tf_op jit(solution)/shard_map/ppermute | solution.py:45
  130.2 31.5 %collective-permute-start.15 = (bf16[256,768]{1,0:T(8,128)(2,1)S(1)}, bf16[256,768]{1,0:T(8,128)(2,1)}, u32[]{:S(2)}, u32[]{:S(2)}) collective-permute-start(bf16[256,768]{1,0:T(8,128)(2,1)S(1)} %pad_maximum_fusion.1.refs_0_), channel_id=1, source_target_pairs={{6,0},{0,2},{2,4},{4,6},{7,1},{1,3},{3,5},{5,7},{14,8},{8,10},{10,... | collective-permute-start | bytes 1179656 | tf_op jit(solution)/shard_map/ppermute | solution.py:45
  135.0 27.1 %collective-permute-start.16 = (bf16[256,768]{1,0:T(8,128)(2,1)S(1)}, bf16[256,768]{1,0:T(8,128)(2,1)}, u32[]{:S(2)}, u32[]{:S(2)}) collective-permute-start(bf16[256,768]{1,0:T(8,128)(2,1)S(1)} %pad_maximum_fusion.1.refs_0_), channel_id=1, source_target_pairs={{0,1},{1,0},{2,3},{3,2},{4,5},{5,4},{6,7},{7,6},{8,9},{9,8},{10,11... | collective-permute-start | bytes 1179656 | tf_op jit(solution)/shard_map/ppermute | solution.py:33
  138.3 18.0 %collective-permute-start.21 = (bf16[136,384]{1,0:T(8,128)(2,1)S(1)}, bf16[136,384]{1,0:T(8,128)(2,1)S(1)}, u32[]{:S(2)}, u32[]{:S(2)}) collective-permute-start(bf16[136,384]{1,0:T(8,128)(2,1)S(1)} %slice.65), channel_id=1, source_target_pairs={{4,0},{6,2},{0,4},{2,6},{5,1},{7,3},{1,5},{3,7},{12,8},{14,10},{8,... | collective-permute-start | bytes 313352 | tf_op jit(solution)/shard_map/ppermute | solution.py:45
  156.3 4.7 %collective-permute-start.20 = (bf16[136,384]{1,0:T(8,128)(2,1)S(1)}, bf16[136,384]{1,0:T(8,128)(2,1)S(1)}, u32[]{:S(2)}, u32[]{:S(2)}) collective-permute-start(bf16[136,384]{1,0:T(8,128)(2,1)S(1)} %slice.65), channel_id=1, source_target_pairs={{2,0},{4,2},{6,4},{0,6},{3,1},{5,3},{7,5},{1,7},{10,8},{12,10},{14... | collective-permute-start | bytes 313352 | tf_op jit(solution)/shard_map/ppermute | solution.py:45
  160.9 10.1 %collective-permute-start.12 = (bf16[544,384]{1,0:T(8,128)(2,1)}, bf16[544,384]{1,0:T(8,128)(2,1)S(1)}, u32[]{:S(2)}, u32[]{:S(2)}) collective-permute-start(bf16[544,384]{1,0:T(8,128)(2,1)} %line_total.1.de_own), channel_id=1, source_target_pairs={{0,1},{1,0},{2,3},{3,2},{4,5},{5,4},{6,7},{7,6},{8,9},{9,8},{10,11... | collective-permute-start | bytes 1253384 | tf_op jit(solution)/shard_map/ppermute | solution.py:33
  161.0 15.1 %collective-permute-start.23 = (bf16[544,384]{1,0:T(8,128)(2,1)S(1)}, bf16[544,384]{1,0:T(8,128)(2,1)S(1)}, u32[]{:S(2)}, u32[]{:S(2)}) collective-permute-start(bf16[544,384]{1,0:T(8,128)(2,1)S(1)} %pad_maximum_fusion.de_own), channel_id=1, source_target_pairs={{0,1},{1,0},{2,3},{3,2},{4,5},{5,4},{6,7},{7,6},{8,9},{9,8},{10,11... | collective-permute-start | bytes 1253384 | tf_op jit(solution)/shard_map/ppermute | solution.py:33
  181.1 18.3 %all-to-all-start.4 = ((bf16[16,8,1792]{2,1,0:T(8,128)(2,1)}), bf16[16,8,1792]{2,1,0:T(8,128)(2,1)S(1)}, u32[]{:S(2)}, u32[]{:S(2)}) async-start(bf16[16,8,1792]{2,1,0:T(8,128)(2,1)} %bitcast.22), calls=%async_computation.4 | async-start | bytes 917504 | tf_op jit(solution)/shard_map/all_to_all | solution.py:37
  (21 other events, 217.7 us)

commit v8 on v6

--- a/solution.py
+++ b/solution.py
@@ -8,6 +8,7 @@
 from jax.sharding import Mesh
 from jax.sharding import PartitionSpec as P
 
+
 DP = ("dp_0", "dp_1", "dp_2", "dp_3")
 PLANE = ("dp_0", "dp_1")
 LINE = "dp_2"
@@ -20,7 +21,6 @@
 BLOCK = LOW + UNIT
 CHUNK = 144
 PAIR = 2 * BLOCK
-TILE = 256
 LOG2E = 1.4426950408889634
 
 
@@ -235,17 +235,7 @@
         copy.wait()
 
 
-def query_kernel(sc, p, g_in, own, far, turned, g, sems, *, scale):
-    cut = p.shape[0] // 2 // TILE * TILE
-    spans = (pl.ds(0, cut), pl.ds(cut, p.shape[0] - cut))
-    copies = [
-        pltpu.make_async_copy(g_in.at[span], g.at[span], sems.at[k]) for k, span in enumerate(spans)
-    ]
-    for copy in copies:
-        copy.start()
-    for at in range(0, p.shape[0], LOW):
-        turned[:, at : at + LOW] = p[at : at + LOW].T
-
+def query_kernel(sc, p, g, own, far, *, scale):
     def put(j, rows, part):
         b = near_index(sc, j)
 
@@ -257,14 +247,17 @@
         def _():
             far[b - 4, rows] = part
 
-    copies[0].wait()
-    early = jnp.dot(turned[:, :cut], g[:cut], preferred_element_type=F32)
-    copies[1].wait()
-    dq = early + jnp.dot(turned[:, cut:], g[cut:], preferred_element_type=F32)
-    dq = (scale * dq).T
-    for j in range(8):
-        put(j, slice(0, LOW), dq[j * LOW : (j + 1) * LOW])
-    dq = dq[8 * LOW :]
+    def part(first, size):
+        dq = lax.dot_general(
+            g[:, first : first + size], p[...], (((0,), (0,)), ((), ())), preferred_element_type=F32
+        )
+        return scale * dq
+
+    for k in range(2):
+        dq = part(4 * k * LOW, 4 * LOW)
+        for j in range(4):
+            put(4 * k + j, slice(0, LOW), dq[j * LOW : (j + 1) * LOW])
+    dq = part(8 * LOW, 8 * UNIT)
     for j in range(8):
         put(j, slice(LOW, BLOCK), dq[j * UNIT : (j + 1) * UNIT])
 
@@ -279,20 +272,17 @@
     return (grad_first, grad_second)
 
 
-def first_weights_kernel(de_own, de_far, rows, hidden, slope, second, out, de):
-    grad_first, grad_second = weight_parts(de_own, de_far, rows, hidden, slope, second, de)
-    out[:, : rows.shape[1]] = grad_first
-    out[:, rows.shape[1] :] = grad_second
-
-
-def last_weights_kernel(sums, de_own, de_far, rows, hidden, slope, second, out, de):
-    grad_first, grad_second = weight_parts(de_own, de_far, rows, hidden, slope, second, de)
-    grad_first += sums[:, : rows.shape[1]]
-    grad_second += sums[:, rows.shape[1] :]
+def weights_kernel(*refs):
+    second, out, de = refs[10:]
+    first_q, second_q = weight_parts(*refs[:5], second, de)
+    grad_first, grad_second = weight_parts(*refs[5:10], second, de)
+    grad_first += first_q
+    grad_second += second_q
     many = out.shape[0]
-    wide = sums.shape[1]
-    out[:, : rows.shape[1]] = grad_first[:many].astype(BF16)
-    out[:, rows.shape[1] : wide] = grad_second[:many].astype(BF16)
+    width = grad_first.shape[1]
+    wide = width + grad_second.shape[1]
+    out[:, :width] = grad_first[:many].astype(BF16)
+    out[:, width:wide] = grad_second[:many].astype(BF16)
     rest = grad_first.shape[0] - many
     x = jnp.concatenate(
         [grad_first[many:], grad_second[many:], jnp.zeros((rest, 128), F32)], axis=1
@@ -394,42 +384,25 @@
 
 
 def query_grads(sc, p, g, scale):
-    columns, width = p.shape
+    width = p.shape[1]
     return pl.pallas_call(
         functools.partial(query_kernel, scale=scale),
-        in_specs=[SMEM, VMEM, HBM],
+        in_specs=[SMEM, VMEM, VMEM],
         out_specs=[VMEM] * 2,
         out_shape=[jax.ShapeDtypeStruct((4, BLOCK, width), F32)] * 2,
-        scratch_shapes=[
-            pltpu.VMEM((width, columns), BF16),
-            pltpu.VMEM(g.shape, BF16),
-            pltpu.SemaphoreType.DMA((2,)),
-        ],
         name="query_grads",
     )(sc, p, g)
 
 
-def weight_grads(sums, des, rows, hidden, slope, second):
-    scratch = [pltpu.VMEM((8 * BLOCK, second.shape[1]), BF16)]
-    operands = (*des, rows, hidden, slope, second)
-    if sums is None:
-        shape = (second.shape[0], rows.shape[1] + second.shape[1])
-        return pl.pallas_call(
-            first_weights_kernel,
-            in_specs=[VMEM] * 6,
-            out_specs=VMEM,
-            out_shape=jax.ShapeDtypeStruct(shape, F32),
-            scratch_shapes=scratch,
-            name="first_weights",
-        )(*operands)
-    return pl.pallas_call(
-        last_weights_kernel,
-        in_specs=[VMEM] * 7,
+def weight_grads(dqs, q_units, dps, p_units, second):
+    return pl.pallas_call(
+        weights_kernel,
+        in_specs=[VMEM] * 11,
         out_specs=VMEM,
         out_shape=jax.ShapeDtypeStruct((128, 1792), BF16),
-        scratch_shapes=scratch,
-        name="last_weights",
-    )(sums, *operands)
+        scratch_shapes=[pltpu.VMEM((8 * BLOCK, second.shape[1]), BF16)],
+        name="weight_grads",
+    )(*dqs, *q_units, *dps, *p_units, second)
 
 
 def body(query_features, passage_features, counts, positives, w_first, w_second):
@@ -505,8 +478,7 @@
     dp_sum = jnp.sum(dp_all.reshape(16, CHUNK, emb_width).astype(F32), axis=0)
     mean_loss = (dp_sum[BLOCK, 0] + dp_sum[BLOCK + 1, 0] + dp_sum[BLOCK + 2, 0]) / pairs
     dps = gathered(dp_sum[:BLOCK].astype(BF16))
-    sums = weight_grads(None, dqs, *q_units, second_part)
-    grads = weight_grads(sums, dps, *p_units, second_part)
+    grads = weight_grads(dqs, q_units, dps, p_units, second_part)
     out = jnp.sum(plane_exchange(grads).reshape(16, 8, -1).astype(F32), axis=0)
     wide = width + emb_width
     tail_out = jnp.concatenate([out[:4, wide:], out[4:, wide : 2 * wide - 640]], axis=1)

time: 206 us -> 202 us (0.981)
  Pallas kernels: 44.5 us -> 41.9 us
    pallas_call x2 -> x1, Pallas kernels: 8.52 us -> 6.2 us  [weight_grads(): pl.pallas_call(weights_kernel, in_specs=[VMEM] * 11, out_specs=VMEM, out_...]
  transfers between devices with their start and end apart: 31 -> 31, of which waited for: 14 -> 14; matrix products, arithmetic and copies ran while one was open for 7% -> 7% of each run, Pallas kernels for 7% -> 5%
where the time goes in v8:
time: 202 us
  waiting for transfers between devices  74.5 us (37%)
  starting transfers between devices  48 us (24%)
  Pallas kernels  41.9 us (21%)
  blocking collectives  11.9 us (6%)
  local copies, waits for them, and re-layouts  10.3 us (5%)
  matrix products  7.13 us (4%)
  between operations  4.74 us (2%)
  other arithmetic  3.09 us (2%)
    all_to_all x4, waiting for transfers between devices, plane_exchange(): return lax.all_to_all(x, PLANE, 0, 0, tiled=True)  39.9 us
    ppermute x15, waiting for transfers between devices, from_line(): return lax.ppermute(x, LINE, [((i + k) % 4, i) for i in range(4)])  26.3 us
    all_to_all x4, starting transfers between devices, plane_exchange(): return lax.all_to_all(x, PLANE, 0, 0, tiled=True)  24.2 us
    ppermute x15, starting transfers between devices, from_line(): return lax.ppermute(x, LINE, [((i + k) % 4, i) for i in range(4)])  19.7 us
    all_to_all x1, blocking collectives, stats_exchange(): return lax.all_to_all(x, (LINE, CORE), 0, 0, tiled=True)  11.9 us
    pallas_call x1, Pallas kernels, score_grads(): pl.pallas_call(functools.partial(grads_kernel, scale=scale), in_specs=[VM...  8.83 us
    pallas_call x1, Pallas kernels, query_grads(): pl.pallas_call(functools.partial(query_kernel, scale=scale), in_specs=[SM...  7.76 us
    ppermute x3, waiting for transfers between devices, to_line(): return lax.ppermute(x, LINE, [(i, (i + k) % 4) for i in range(4)])  7.25 us
  transfers between devices with their start and end apart: 31, of which 14 were waited for; matrix products, arithmetic and copies ran while one was open for 7% of the time, Pallas kernels for 5%

profile of v8, /device:TPU:0, one launch (start us, length us, event | category | flops | bytes accessed | tf_op | source)
XLA Modules:
  0.0 201.5 jit_solution(15085467330605154095)
XLA Ops:
  2.7 8.0 %all-to-all-start = ((bf16[16,8,1664]{2,1,0:T(8,128)(2,1)}), bf16[16,8,1664]{2,1,0:T(8,128)(2,1)S(1)}, u32[]{:S(2)}, u32[]{:S(2)}) async-start(bf16[16,8,1664]{2,1,0:T(8,128)(2,1)} %get-tuple-element.25), calls=%async_computation | async-start | bytes 851968 | tf_op jit(solution)/shard_map/all_to_all | solution.py:36
  12.7 2.6 %convolution_convert_fusion.1 = bf16[256,384]{1,0:T(8,128)(2,1)S(1)} fusion(bf16[1536,384]{1,0:T(8,128)(2,1)} %w_second.1, bf16[768,1536]{1,0:T(8,128)(2,1)S(1)} %copy-done.1, bf16[128,768]{1,0:T(8,128)(2,1)S(1)} %slice.57, bf16[128,768]{1,0:T(8,128)(2,1)S(1)} %slice.56), kind=kOutput, calls=%fused_computation.13 | convolution fusion | flops 910393344 | bytes 4128768 | tf_op jit(solution)/shard_map/dot_general | solution.py:424
  17.6 2.9 %collective-permute-start.1 = (bf16[128,384]{1,0:T(8,128)(2,1)S(1)}, bf16[128,384]{1,0:T(8,128)(2,1)S(1)}, u32[]{:S(2)}, u32[]{:S(2)}) collective-permute-start(bf16[128,384]{1,0:T(8,128)(2,1)S(1)} %get-tuple-element.53), channel_id=1, source_target_pairs={{4,0},{6,2},{0,4},{2,6},{5,1},{7,3},{1,5},{3,7},{12,8},{14,10},{8,... | collective-permute-start | bytes 294920 | tf_op jit(solution)/shard_map/ppermute | solution.py:44
  22.4 2.4 %collective-permute-done.1 = bf16[128,384]{1,0:T(8,128)(2,1)S(1)} collective-permute-done((bf16[128,384]{1,0:T(8,128)(2,1)S(1)}, bf16[128,384]{1,0:T(8,128)(2,1)S(1)}, u32[]{:S(2)}, u32[]{:S(2)}) %collective-permute-start.1) | collective-permute-done | bytes 98336 | tf_op jit(solution)/shard_map/ppermute | solution.py:44
  26.0 4.7 %tail_rows.1 = (bf16[16,136,384]{2,1,0:T(8,128)(2,1)}, bf16[16,1152]{1,0:T(8,128)(2,1)}) custom-call(s32[1]{0:T(128)} %get-tuple-element.24.heavy_at, bf16[16,8,1664]{2,1,0:T(8,128)(2,1)} %copy-done.2, bf16[128,384]{1,0:T(8,128)(2,1)} %get-tuple-element.54.base_p, s32[2,128]{1,0:T(2,128)} %bitcast.38, bf16[768,1536]{1,0:T(8,128)(2,1)} %w_first.1, ...), custom_call_target="tpu_custom_call" | custom-call | tf_op jit(solution)/shard_map/tail_rows/pallas_call | solution.py:322
  30.7 2.6 %collective-permute-start.4 = (bf16[16,1152]{1,0:T(8,128)(2,1)}, bf16[16,1152]{1,0:T(8,128)(2,1)S(1)}, u32[]{:S(2)}, u32[]{:S(2)}) collective-permute-start(bf16[16,1152]{1,0:T(8,128)(2,1)} %get-tuple-element.26), channel_id=1, source_target_pairs={{2,0},{4,2},{6,4},{0,6},{3,1},{5,3},{7,5},{1,7},{10,8},{12,10},{14... | collective-permute-start | bytes 110600 | tf_op jit(solution)/shard_map/ppermute | solution.py:44
  34.5 7.1 %all-to-all-start.1 = ((bf16[16,136,384]{2,1,0:T(8,128)(2,1)}), bf16[16,136,384]{2,1,0:T(8,128)(2,1)S(1)}, u32[]{:S(2)}, u32[]{:S(2)}) async-start(bf16[16,136,384]{2,1,0:T(8,128)(2,1)} %get-tuple-element.29), calls=%async_computation.1 | async-start | bytes 3342336 | tf_op jit(solution)/shard_map/all_to_all | solution.py:36
  44.9 3.3 %convolution_convert_fusion.refs_10_ = bf16[192,768]{1,0:T(8,128)(2,1)} fusion(bf16[768,1536]{1,0:T(8,128)(2,1)} %w_first.1, s32[192]{0:T(256)S(1)} %fusion.29), kind=kOutput, calls=%fused_computation.10 | convolution fusion | flops 453427200 | bytes 2654976 | tf_op jit(solution)/shard_map/dot_general | solution.py:459
  48.3 18.5 %all-to-all-done.1 = bf16[16,136,384]{2,1,0:T(8,128)(2,1)S(1)} async-done(((bf16[16,136,384]{2,1,0:T(8,128)(2,1)}), bf16[16,136,384]{2,1,0:T(8,128)(2,1)S(1)}, u32[]{:S(2)}, u32[]{:S(2)}) %all-to-all-start.1) | async-done | bytes 1671200 | tf_op jit(solution)/shard_map/all_to_all | solution.py:36
  68.8 6.8 %score_stats.1 = (bf16[1088,384]{1,0:T(8,128)(2,1)}, s32[1,1088]{1,0:T(1,128)}, f32[64,1088]{1,0:T(8,128)}) custom-call(s32[29]{0:T(128)} %concatenate.25.sc, bf16[512,384]{1,0:T(8,128)(2,1)} %copy-done.6, bf16[512,384]{1,0:T(8,128)(2,1)} %copy-done.23, bf16[64,1152]{1,0:T(8,128)(2,1)} %copy-done.13, bf16[64,1152]{1,0:T(8,128)(2,1)} %copy-done.14, ...), custom_call_target="tpu_custom_call" | custom-call | tf_op jit(solution)/shard_map/score_stats/pallas_call | solution.py:351
  75.5 11.9 %all_to_all.44 = f32[8,8,1088]{2,1,0:T(8,128)} all-to-all(f32[8,8,1088]{2,1,0:T(8,128)} %bitcast.35), channel_id=1, replica_groups=mesh['dp_0'=4,'dp_1'=4,'dp_2'=4,'dp_3'=2] {'dp_2','dp_3'}, dimensions={0} | all-to-all | bytes 557056 | tf_op jit(solution)/shard_map/all_to_all | solution.py:40
  87.4 8.8 %score_grads.1 = (bf16[2304,384]{1,0:T(8,128)(2,1)}, bf16[2176,1088]{1,0:T(8,128)(2,1)}) custom-call(f32[64,1088]{1,0:T(8,128)} %bitcast.34, bf16[1088,384]{1,0:T(8,128)(2,1)} %get-tuple-element.32.q, bf16[2176,384]{1,0:T(8,128)(2,1)} %bitcast.31, s32[1,1088]{1,0:T(1,128)} %get-tuple-element.33.place), custom_call_target="tpu_custom_call" | custom-call | tf_op jit(solution)/shard_map/score_grads/pallas_call | solution.py:369
  96.3 7.8 %query_grads.1 = (f32[4,136,384]{2,1,0:T(8,128)}, f32[4,136,384]{2,1,0:T(8,128)}) custom-call(s32[29]{0:T(128)} %concatenate.25.sc, bf16[2176,384]{1,0:T(8,128)(2,1)} %bitcast.32, bf16[2176,1088]{1,0:T(8,128)(2,1)} %get-tuple-element.35.g), custom_call_target="tpu_custom_call" | custom-call | tf_op jit(solution)/shard_map/query_grads/pallas_call | solution.py:388
  104.0 3.9 %all-to-all-start.3 = ((bf16[16,144,384]{2,1,0:T(8,128)(2,1)}), bf16[16,144,384]{2,1,0:T(8,128)(2,1)S(1)}, u32[]{:S(2)}, u32[]{:S(2)}) async-start(bf16[16,144,384]{2,1,0:T(8,128)(2,1)} %bitcast.10), calls=%async_computation.3 | async-start | bytes 3538944 | tf_op jit(solution)/shard_map/all_to_all | solution.py:36
  110.8 3.2 %collective-permute-done.11 = bf16[136,384]{1,0:T(8,128)(2,1)S(1)} collective-permute-done((bf16[136,384]{1,0:T(8,128)(2,1)S(1)}, bf16[136,384]{1,0:T(8,128)(2,1)S(1)}, u32[]{:S(2)}, u32[]{:S(2)}) %collective-permute-start.11) | collective-permute-done | bytes 104480 | tf_op jit(solution)/shard_map/ppermute | solution.py:48
  114.0 2.7 %collective-permute-done.10 = bf16[136,384]{1,0:T(8,128)(2,1)S(1)} collective-permute-done((bf16[136,384]{1,0:T(8,128)(2,1)S(1)}, bf16[136,384]{1,0:T(8,128)(2,1)S(1)}, u32[]{:S(2)}, u32[]{:S(2)}) %collective-permute-start.10) | collective-permute-done | bytes 104480 | tf_op jit(solution)/shard_map/ppermute | solution.py:48
  122.3 12.8 %all-to-all-done.3 = bf16[16,144,384]{2,1,0:T(8,128)(2,1)S(1)} async-done(((bf16[16,144,384]{2,1,0:T(8,128)(2,1)}), bf16[16,144,384]{2,1,0:T(8,128)(2,1)S(1)}, u32[]{:S(2)}, u32[]{:S(2)}) %all-to-all-start.3) | async-done | bytes 1769504 | tf_op jit(solution)/shard_map/all_to_all | solution.py:36
  136.1 3.0 %collective-permute-start.16 = (bf16[256,768]{1,0:T(8,128)(2,1)S(1)}, bf16[256,768]{1,0:T(8,128)(2,1)S(1)}, u32[]{:S(2)}, u32[]{:S(2)}) collective-permute-start(bf16[256,768]{1,0:T(8,128)(2,1)S(1)} %pad_maximum_fusion.2.refs_0_), channel_id=1, source_target_pairs={{2,0},{4,2},{6,4},{0,6},{3,1},{5,3},{7,5},{1,7},{10,8},{12,10},{14... | collective-permute-start | bytes 1179656 | tf_op jit(solution)/shard_map/ppermute | solution.py:44
  142.8 17.9 %collective-permute-done.24 = bf16[136,384]{1,0:T(8,128)(2,1)S(1)} collective-permute-done((bf16[136,384]{1,0:T(8,128)(2,1)S(1)}, bf16[136,384]{1,0:T(8,128)(2,1)S(1)}, u32[]{:S(2)}, u32[]{:S(2)}) %collective-permute-start.24) | collective-permute-done | bytes 104480 | tf_op jit(solution)/shard_map/ppermute | solution.py:44
  161.7 3.7 %collective-permute-done.23 = bf16[136,384]{1,0:T(8,128)(2,1)S(1)} collective-permute-done((bf16[136,384]{1,0:T(8,128)(2,1)S(1)}, bf16[136,384]{1,0:T(8,128)(2,1)S(1)}, u32[]{:S(2)}, u32[]{:S(2)}) %collective-permute-start.23) | collective-permute-done | bytes 104480 | tf_op jit(solution)/shard_map/ppermute | solution.py:44
  169.9 5.7 %hidden_units.1 = (bf16[1088,768]{1,0:T(8,128)(2,1)}, bf16[1088,768]{1,0:T(8,128)(2,1)}, bf16[192,1088]{1,0:T(8,128)(2,1)}, bf16[192,1088]{1,0:T(8,128)(2,1)}, f32[192,1088]{1,0:T(8,128)}, /*index=5*/f32[192,1088]{1,0:T(8,128)}) custom-call(bf16[256,768]{1,0:T(8,128)(2,1)} %copy-done.5, bf16[256,768]{1,0:T(8,128)(2,1)} %copy-done.17, ...), custom_call_target="tpu_custom_call" | custom-call | tf_op jit(solution)/shard_map/hidden_units/pallas_call | solution.py:338
  176.5 6.2 %weight_grads.1 = bf16[128,1792]{1,0:T(8,128)(2,1)} custom-call(bf16[544,384]{1,0:T(8,128)(2,1)} %copy-done.3, bf16[544,384]{1,0:T(8,128)(2,1)} %copy-done.15, bf16[1088,768]{1,0:T(8,128)(2,1)} %get-tuple-element.39.refs_2_, bf16[192,1088]{1,0:T(8,128)(2,1)} %get-tuple-element.40.refs_3_, f32[192,1088]{1,0:T(8,128)} %get-tuple-element.41.refs_4_, ...), custom_call_target="tpu_custom_call" | custom-call | tf_op jit(solution)/shard_map/weight_grads/pallas_call | solution.py:398
  182.7 5.2 %all-to-all-start.4 = ((bf16[16,8,1792]{2,1,0:T(8,128)(2,1)}), bf16[16,8,1792]{2,1,0:T(8,128)(2,1)S(1)}, u32[]{:S(2)}, u32[]{:S(2)}) async-start(bf16[16,8,1792]{2,1,0:T(8,128)(2,1)} %bitcast.33), calls=%async_computation.4 | async-start | bytes 917504 | tf_op jit(solution)/shard_map/all_to_all | solution.py:36
  190.4 8.6 %all-to-all-done.4 = bf16[16,8,1792]{2,1,0:T(8,128)(2,1)S(1)} async-done(((bf16[16,8,1792]{2,1,0:T(8,128)(2,1)}), bf16[16,8,1792]{2,1,0:T(8,128)(2,1)S(1)}, u32[]{:S(2)}, u32[]{:S(2)}) %all-to-all-start.4) | async-done | bytes 458784 | tf_op jit(solution)/shard_map/all_to_all | solution.py:36
  (136 shorter events, 36.6 us)
Async XLA Ops:
  2.7 22.6 %all-to-all-start = ((bf16[16,8,1664]{2,1,0:T(8,128)(2,1)}), bf16[16,8,1664]{2,1,0:T(8,128)(2,1)S(1)}, u32[]{:S(2)}, u32[]{:S(2)}) async-start(bf16[16,8,1664]{2,1,0:T(8,128)(2,1)} %get-tuple-element.25), calls=%async_computation | async-start | bytes 851968 | tf_op jit(solution)/shard_map/all_to_all | solution.py:36
  16.0 6.4 %collective-permute-start.2 = (bf16[128,384]{1,0:T(8,128)(2,1)S(1)}, bf16[128,384]{1,0:T(8,128)(2,1)S(1)}, u32[]{:S(2)}, u32[]{:S(2)}) collective-permute-start(bf16[128,384]{1,0:T(8,128)(2,1)S(1)} %get-tuple-element.53), channel_id=1, source_target_pairs={{6,0},{0,2},{2,4},{4,6},{7,1},{1,3},{3,5},{5,7},{14,8},{8,10},{10,... | collective-permute-start | bytes 294920 | tf_op jit(solution)/shard_map/ppermute | solution.py:44
  17.6 7.2 %collective-permute-start.1 = (bf16[128,384]{1,0:T(8,128)(2,1)S(1)}, bf16[128,384]{1,0:T(8,128)(2,1)S(1)}, u32[]{:S(2)}, u32[]{:S(2)}) collective-permute-start(bf16[128,384]{1,0:T(8,128)(2,1)S(1)} %get-tuple-element.53), channel_id=1, source_target_pairs={{4,0},{6,2},{0,4},{2,6},{5,1},{7,3},{1,5},{3,7},{12,8},{14,10},{8,... | collective-permute-start | bytes 294920 | tf_op jit(solution)/shard_map/ppermute | solution.py:44
  25.1 41.6 %collective-permute-start.3 = (bf16[512,384]{1,0:T(8,128)(2,1)S(1)}, bf16[512,384]{1,0:T(8,128)(2,1)S(1)}, u32[]{:S(2)}, u32[]{:S(2)}) collective-permute-start(bf16[512,384]{1,0:T(8,128)(2,1)S(1)} %pad_maximum_fusion.3.q_own), channel_id=1, source_target_pairs={{0,1},{1,0},{2,3},{3,2},{4,5},{5,4},{6,7},{7,6},{8,9},{9,8},{10,11... | collective-permute-start | bytes 1179656 | tf_op jit(solution)/shard_map/ppermute | solution.py:32
  30.7 14.1 %collective-permute-start.4 = (bf16[16,1152]{1,0:T(8,128)(2,1)}, bf16[16,1152]{1,0:T(8,128)(2,1)S(1)}, u32[]{:S(2)}, u32[]{:S(2)}) collective-permute-start(bf16[16,1152]{1,0:T(8,128)(2,1)} %get-tuple-element.26), channel_id=1, source_target_pairs={{2,0},{4,2},{6,4},{0,6},{3,1},{5,3},{7,5},{1,7},{10,8},{12,10},{14... | collective-permute-start | bytes 110600 | tf_op jit(solution)/shard_map/ppermute | solution.py:44
  33.3 11.5 %collective-permute-start.5 = (bf16[16,1152]{1,0:T(8,128)(2,1)}, bf16[16,1152]{1,0:T(8,128)(2,1)S(1)}, u32[]{:S(2)}, u32[]{:S(2)}) collective-permute-start(bf16[16,1152]{1,0:T(8,128)(2,1)} %get-tuple-element.26), channel_id=1, source_target_pairs={{4,0},{6,2},{0,4},{2,6},{5,1},{7,3},{1,5},{3,7},{12,8},{14,10},{8,... | collective-permute-start | bytes 110600 | tf_op jit(solution)/shard_map/ppermute | solution.py:44
  33.6 11.2 %collective-permute-start.6 = (bf16[16,1152]{1,0:T(8,128)(2,1)}, bf16[16,1152]{1,0:T(8,128)(2,1)S(1)}, u32[]{:S(2)}, u32[]{:S(2)}) collective-permute-start(bf16[16,1152]{1,0:T(8,128)(2,1)} %get-tuple-element.26), channel_id=1, source_target_pairs={{6,0},{0,2},{2,4},{4,6},{7,1},{1,3},{3,5},{5,7},{14,8},{8,10},{10,... | collective-permute-start | bytes 110600 | tf_op jit(solution)/shard_map/ppermute | solution.py:44
  34.5 32.3 %all-to-all-start.1 = ((bf16[16,136,384]{2,1,0:T(8,128)(2,1)}), bf16[16,136,384]{2,1,0:T(8,128)(2,1)S(1)}, u32[]{:S(2)}, u32[]{:S(2)}) async-start(bf16[16,136,384]{2,1,0:T(8,128)(2,1)} %get-tuple-element.29), calls=%async_computation.1 | async-start | bytes 3342336 | tf_op jit(solution)/shard_map/all_to_all | solution.py:36
  44.8 21.9 %collective-permute-start.7 = (bf16[64,1152]{1,0:T(8,128)(2,1)S(1)}, bf16[64,1152]{1,0:T(8,128)(2,1)S(1)}, u32[]{:S(2)}, u32[]{:S(2)}) collective-permute-start(bf16[64,1152]{1,0:T(8,128)(2,1)S(1)} %constant_dynamic-update-slice_fusion.t_own.refs_8_), channel_id=1, source_target_pairs={{0,1},{1,0},{2,3},{3,2},{4,5},{5,4},{6,7},{7,6},{8,9},{9,8},{10,11... | collective-permute-start | bytes 442376 | tf_op jit(solution)/shard_map/ppermute | solution.py:32
  104.0 31.1 %all-to-all-start.3 = ((bf16[16,144,384]{2,1,0:T(8,128)(2,1)}), bf16[16,144,384]{2,1,0:T(8,128)(2,1)S(1)}, u32[]{:S(2)}, u32[]{:S(2)}) async-start(bf16[16,144,384]{2,1,0:T(8,128)(2,1)} %bitcast.10), calls=%async_computation.3 | async-start | bytes 3538944 | tf_op jit(solution)/shard_map/all_to_all | solution.py:36
  109.4 7.3 %collective-permute-start.10 = (bf16[136,384]{1,0:T(8,128)(2,1)S(1)}, bf16[136,384]{1,0:T(8,128)(2,1)S(1)}, u32[]{:S(2)}, u32[]{:S(2)}) collective-permute-start(bf16[136,384]{1,0:T(8,128)(2,1)S(1)} %get-tuple-element.49), channel_id=1, source_target_pairs={{0,4},{2,6},{4,0},{6,2},{1,5},{3,7},{5,1},{7,3},{8,12},{10,14},{12... | collective-permute-start | bytes 313352 | tf_op jit(solution)/shard_map/ppermute | solution.py:48
  110.8 7.3 %collective-permute-start.9 = (bf16[136,384]{1,0:T(8,128)(2,1)S(1)}, bf16[136,384]{1,0:T(8,128)(2,1)S(1)}, u32[]{:S(2)}, u32[]{:S(2)}) collective-permute-start(bf16[136,384]{1,0:T(8,128)(2,1)S(1)} %get-tuple-element.47), channel_id=1, source_target_pairs={{0,2},{2,4},{4,6},{6,0},{1,3},{3,5},{5,7},{7,1},{8,10},{10,12},{12... | collective-permute-start | bytes 313352 | tf_op jit(solution)/shard_map/ppermute | solution.py:48
  118.2 20.9 %collective-permute-start.14 = (bf16[136,384]{1,0:T(8,128)(2,1)S(1)}, bf16[136,384]{1,0:T(8,128)(2,1)S(1)}, u32[]{:S(2)}, u32[]{:S(2)}) collective-permute-start(bf16[136,384]{1,0:T(8,128)(2,1)S(1)} %fusion.18), channel_id=1, source_target_pairs={{6,0},{0,2},{2,4},{4,6},{7,1},{1,3},{3,5},{5,7},{14,8},{8,10},{10,... | collective-permute-start | bytes 313352 | tf_op jit(solution)/shard_map/ppermute | solution.py:44
  118.2 20.8 %collective-permute-start.13 = (bf16[136,384]{1,0:T(8,128)(2,1)S(1)}, bf16[136,384]{1,0:T(8,128)(2,1)S(1)}, u32[]{:S(2)}, u32[]{:S(2)}) collective-permute-start(bf16[136,384]{1,0:T(8,128)(2,1)S(1)} %fusion.18), channel_id=1, source_target_pairs={{4,0},{6,2},{0,4},{2,6},{5,1},{7,3},{1,5},{3,7},{12,8},{14,10},{8,... | collective-permute-start | bytes 313352 | tf_op jit(solution)/shard_map/ppermute | solution.py:44
  120.3 19.8 %collective-permute-start.12 = (bf16[136,384]{1,0:T(8,128)(2,1)S(1)}, bf16[136,384]{1,0:T(8,128)(2,1)}, u32[]{:S(2)}, u32[]{:S(2)}) collective-permute-start(bf16[136,384]{1,0:T(8,128)(2,1)S(1)} %fusion.18), channel_id=1, source_target_pairs={{2,0},{4,2},{6,4},{0,6},{3,1},{5,3},{7,5},{1,7},{10,8},{12,10},{14... | collective-permute-start | bytes 313352 | tf_op jit(solution)/shard_map/ppermute | solution.py:44
  135.4 6.0 %collective-permute-start.25 = (bf16[136,384]{1,0:T(8,128)(2,1)S(1)}, bf16[136,384]{1,0:T(8,128)(2,1)S(1)}, u32[]{:S(2)}, u32[]{:S(2)}) collective-permute-start(bf16[136,384]{1,0:T(8,128)(2,1)S(1)} %slice.95), channel_id=1, source_target_pairs={{6,0},{0,2},{2,4},{4,6},{7,1},{1,3},{3,5},{5,7},{14,8},{8,10},{10,... | collective-permute-start | bytes 313352 | tf_op jit(solution)/shard_map/ppermute | solution.py:44
  136.1 29.4 %collective-permute-start.16 = (bf16[256,768]{1,0:T(8,128)(2,1)S(1)}, bf16[256,768]{1,0:T(8,128)(2,1)S(1)}, u32[]{:S(2)}, u32[]{:S(2)}) collective-permute-start(bf16[256,768]{1,0:T(8,128)(2,1)S(1)} %pad_maximum_fusion.2.refs_0_), channel_id=1, source_target_pairs={{2,0},{4,2},{6,4},{0,6},{3,1},{5,3},{7,5},{1,7},{10,8},{12,10},{14... | collective-permute-start | bytes 1179656 | tf_op jit(solution)/shard_map/ppermute | solution.py:44
  139.1 27.0 %collective-permute-start.17 = (bf16[256,768]{1,0:T(8,128)(2,1)S(1)}, bf16[256,768]{1,0:T(8,128)(2,1)S(1)}, u32[]{:S(2)}, u32[]{:S(2)}) collective-permute-start(bf16[256,768]{1,0:T(8,128)(2,1)S(1)} %pad_maximum_fusion.2.refs_0_), channel_id=1, source_target_pairs={{4,0},{6,2},{0,4},{2,6},{5,1},{7,3},{1,5},{3,7},{12,8},{14,10},{8,... | collective-permute-start | bytes 1179656 | tf_op jit(solution)/shard_map/ppermute | solution.py:44
  139.1 27.1 %collective-permute-start.18 = (bf16[256,768]{1,0:T(8,128)(2,1)S(1)}, bf16[256,768]{1,0:T(8,128)(2,1)S(1)}, u32[]{:S(2)}, u32[]{:S(2)}) collective-permute-start(bf16[256,768]{1,0:T(8,128)(2,1)S(1)} %pad_maximum_fusion.2.refs_0_), channel_id=1, source_target_pairs={{6,0},{0,2},{2,4},{4,6},{7,1},{1,3},{3,5},{5,7},{14,8},{8,10},{10,... | collective-permute-start | bytes 1179656 | tf_op jit(solution)/shard_map/ppermute | solution.py:44
  140.0 26.6 %collective-permute-start.19 = (bf16[256,768]{1,0:T(8,128)(2,1)S(1)}, bf16[256,768]{1,0:T(8,128)(2,1)S(1)}, u32[]{:S(2)}, u32[]{:S(2)}) collective-permute-start(bf16[256,768]{1,0:T(8,128)(2,1)S(1)} %pad_maximum_fusion.2.refs_0_), channel_id=1, source_target_pairs={{0,1},{1,0},{2,3},{3,2},{4,5},{5,4},{6,7},{7,6},{8,9},{9,8},{10,11... | collective-permute-start | bytes 1179656 | tf_op jit(solution)/shard_map/ppermute | solution.py:32
  141.4 19.4 %collective-permute-start.24 = (bf16[136,384]{1,0:T(8,128)(2,1)S(1)}, bf16[136,384]{1,0:T(8,128)(2,1)S(1)}, u32[]{:S(2)}, u32[]{:S(2)}) collective-permute-start(bf16[136,384]{1,0:T(8,128)(2,1)S(1)} %slice.95), channel_id=1, source_target_pairs={{4,0},{6,2},{0,4},{2,6},{5,1},{7,3},{1,5},{3,7},{12,8},{14,10},{8,... | collective-permute-start | bytes 313352 | tf_op jit(solution)/shard_map/ppermute | solution.py:44
  165.4 10.1 %collective-permute-start.15 = (bf16[544,384]{1,0:T(8,128)(2,1)S(1)}, bf16[544,384]{1,0:T(8,128)(2,1)S(1)}, u32[]{:S(2)}, u32[]{:S(2)}) collective-permute-start(bf16[544,384]{1,0:T(8,128)(2,1)S(1)} %pad_maximum_fusion.refs_0_), channel_id=1, source_target_pairs={{0,1},{1,0},{2,3},{3,2},{4,5},{5,4},{6,7},{7,6},{8,9},{9,8},{10,11... | collective-permute-start | bytes 1253384 | tf_op jit(solution)/shard_map/ppermute | solution.py:32
  165.5 10.1 %collective-permute-start.26 = (bf16[544,384]{1,0:T(8,128)(2,1)S(1)}, bf16[544,384]{1,0:T(8,128)(2,1)S(1)}, u32[]{:S(2)}, u32[]{:S(2)}) collective-permute-start(bf16[544,384]{1,0:T(8,128)(2,1)S(1)} %pad_maximum_fusion.1.refs_5_), channel_id=1, source_target_pairs={{0,1},{1,0},{2,3},{3,2},{4,5},{5,4},{6,7},{7,6},{8,9},{9,8},{10,11... | collective-permute-start | bytes 1253384 | tf_op jit(solution)/shard_map/ppermute | solution.py:32
  182.7 16.3 %all-to-all-start.4 = ((bf16[16,8,1792]{2,1,0:T(8,128)(2,1)}), bf16[16,8,1792]{2,1,0:T(8,128)(2,1)S(1)}, u32[]{:S(2)}, u32[]{:S(2)}) async-start(bf16[16,8,1792]{2,1,0:T(8,128)(2,1)} %bitcast.33), calls=%async_computation.4 | async-start | bytes 917504 | tf_op jit(solution)/shard_map/all_to_all | solution.py:36
  (33 other events, 274.7 us)

commit v9 on v8

--- a/solution.py
+++ b/solution.py
@@ -471,8 +471,9 @@
 
     dq = dq_own + swap_core(dq_far)
     dq_sum = dq[0].astype(BF16).astype(F32)
-    for k in (1, 2, 3):
-        dq_sum = dq_sum + to_line(dq[k].astype(BF16), k).astype(F32)
+    arrived = [to_line(dq[k].astype(BF16), k) for k in (1, 2, 3)]
+    for part in arrived:
+        dq_sum = dq_sum + part.astype(F32)
     dqs = gathered(dq_sum.astype(BF16))
 
     dp_sum = jnp.sum(dp_all.reshape(16, CHUNK, emb_width).astype(F32), axis=0)

time: 202 us -> 202 us (level)
  no operation moved by 1% of the time
where the time goes in v9:
time: 202 us
  waiting for transfers between devices  74.5 us (37%)
  starting transfers between devices  48 us (24%)
  Pallas kernels  41.9 us (21%)
  blocking collectives  11.9 us (6%)
  local copies, waits for them, and re-layouts  10.3 us (5%)
  matrix products  7.13 us (4%)
  between operations  4.74 us (2%)
  other arithmetic  3.09 us (2%)
    all_to_all x4, waiting for transfers between devices, plane_exchange(): return lax.all_to_all(x, PLANE, 0, 0, tiled=True)  39.9 us
    ppermute x15, waiting for transfers between devices, from_line(): return lax.ppermute(x, LINE, [((i + k) % 4, i) for i in range(4)])  26.3 us
    all_to_all x4, starting transfers between devices, plane_exchange(): return lax.all_to_all(x, PLANE, 0, 0, tiled=True)  24.2 us
    ppermute x15, starting transfers between devices, from_line(): return lax.ppermute(x, LINE, [((i + k) % 4, i) for i in range(4)])  19.7 us
    all_to_all x1, blocking collectives, stats_exchange(): return lax.all_to_all(x, (LINE, CORE), 0, 0, tiled=True)  11.9 us
    pallas_call x1, Pallas kernels, score_grads(): pl.pallas_call(functools.partial(grads_kernel, scale=scale), in_specs=[VM...  8.83 us
    pallas_call x1, Pallas kernels, query_grads(): pl.pallas_call(functools.partial(query_kernel, scale=scale), in_specs=[SM...  7.76 us
    ppermute x3, waiting for transfers between devices, to_line(): return lax.ppermute(x, LINE, [(i, (i + k) % 4) for i in range(4)])  7.25 us
  transfers between devices with their start and end apart: 31, of which 14 were waited for; matrix products, arithmetic and copies ran while one was open for 7% of the time, Pallas kernels for 5%

profile of v9, /device:TPU:0, one launch (start us, length us, event | category | flops | bytes accessed | tf_op | source)
XLA Modules:
  0.0 201.5 jit_solution(15085467330605154095)
XLA Ops:
  2.7 8.0 %all-to-all-start = ((bf16[16,8,1664]{2,1,0:T(8,128)(2,1)}), bf16[16,8,1664]{2,1,0:T(8,128)(2,1)S(1)}, u32[]{:S(2)}, u32[]{:S(2)}) async-start(bf16[16,8,1664]{2,1,0:T(8,128)(2,1)} %get-tuple-element.25), calls=%async_computation | async-start | bytes 851968 | tf_op jit(solution)/shard_map/all_to_all | solution.py:36
  12.7 2.6 %convolution_convert_fusion.1 = bf16[256,384]{1,0:T(8,128)(2,1)S(1)} fusion(bf16[1536,384]{1,0:T(8,128)(2,1)} %w_second.1, bf16[768,1536]{1,0:T(8,128)(2,1)S(1)} %copy-done.1, bf16[128,768]{1,0:T(8,128)(2,1)S(1)} %slice.57, bf16[128,768]{1,0:T(8,128)(2,1)S(1)} %slice.56), kind=kOutput, calls=%fused_computation.13 | convolution fusion | flops 910393344 | bytes 4128768 | tf_op jit(solution)/shard_map/dot_general | solution.py:424
  17.6 2.9 %collective-permute-start.1 = (bf16[128,384]{1,0:T(8,128)(2,1)S(1)}, bf16[128,384]{1,0:T(8,128)(2,1)S(1)}, u32[]{:S(2)}, u32[]{:S(2)}) collective-permute-start(bf16[128,384]{1,0:T(8,128)(2,1)S(1)} %get-tuple-element.53), channel_id=1, source_target_pairs={{4,0},{6,2},{0,4},{2,6},{5,1},{7,3},{1,5},{3,7},{12,8},{14,10},{8,... | collective-permute-start | bytes 294920 | tf_op jit(solution)/shard_map/ppermute | solution.py:44
  22.4 2.4 %collective-permute-done.1 = bf16[128,384]{1,0:T(8,128)(2,1)S(1)} collective-permute-done((bf16[128,384]{1,0:T(8,128)(2,1)S(1)}, bf16[128,384]{1,0:T(8,128)(2,1)S(1)}, u32[]{:S(2)}, u32[]{:S(2)}) %collective-permute-start.1) | collective-permute-done | bytes 98336 | tf_op jit(solution)/shard_map/ppermute | solution.py:44
  26.0 4.7 %tail_rows.1 = (bf16[16,136,384]{2,1,0:T(8,128)(2,1)}, bf16[16,1152]{1,0:T(8,128)(2,1)}) custom-call(s32[1]{0:T(128)} %get-tuple-element.24.heavy_at, bf16[16,8,1664]{2,1,0:T(8,128)(2,1)} %copy-done.2, bf16[128,384]{1,0:T(8,128)(2,1)} %get-tuple-element.54.base_p, s32[2,128]{1,0:T(2,128)} %bitcast.38, bf16[768,1536]{1,0:T(8,128)(2,1)} %w_first.1, ...), custom_call_target="tpu_custom_call" | custom-call | tf_op jit(solution)/shard_map/tail_rows/pallas_call | solution.py:322
  30.7 2.6 %collective-permute-start.4 = (bf16[16,1152]{1,0:T(8,128)(2,1)}, bf16[16,1152]{1,0:T(8,128)(2,1)S(1)}, u32[]{:S(2)}, u32[]{:S(2)}) collective-permute-start(bf16[16,1152]{1,0:T(8,128)(2,1)} %get-tuple-element.26), channel_id=1, source_target_pairs={{2,0},{4,2},{6,4},{0,6},{3,1},{5,3},{7,5},{1,7},{10,8},{12,10},{14... | collective-permute-start | bytes 110600 | tf_op jit(solution)/shard_map/ppermute | solution.py:44
  34.5 7.1 %all-to-all-start.1 = ((bf16[16,136,384]{2,1,0:T(8,128)(2,1)}), bf16[16,136,384]{2,1,0:T(8,128)(2,1)S(1)}, u32[]{:S(2)}, u32[]{:S(2)}) async-start(bf16[16,136,384]{2,1,0:T(8,128)(2,1)} %get-tuple-element.29), calls=%async_computation.1 | async-start | bytes 3342336 | tf_op jit(solution)/shard_map/all_to_all | solution.py:36
  44.9 3.3 %convolution_convert_fusion.refs_10_ = bf16[192,768]{1,0:T(8,128)(2,1)} fusion(bf16[768,1536]{1,0:T(8,128)(2,1)} %w_first.1, s32[192]{0:T(256)S(1)} %fusion.29), kind=kOutput, calls=%fused_computation.10 | convolution fusion | flops 453427200 | bytes 2654976 | tf_op jit(solution)/shard_map/dot_general | solution.py:459
  48.3 18.5 %all-to-all-done.1 = bf16[16,136,384]{2,1,0:T(8,128)(2,1)S(1)} async-done(((bf16[16,136,384]{2,1,0:T(8,128)(2,1)}), bf16[16,136,384]{2,1,0:T(8,128)(2,1)S(1)}, u32[]{:S(2)}, u32[]{:S(2)}) %all-to-all-start.1) | async-done | bytes 1671200 | tf_op jit(solution)/shard_map/all_to_all | solution.py:36
  68.8 6.8 %score_stats.1 = (bf16[1088,384]{1,0:T(8,128)(2,1)}, s32[1,1088]{1,0:T(1,128)}, f32[64,1088]{1,0:T(8,128)}) custom-call(s32[29]{0:T(128)} %concatenate.25.sc, bf16[512,384]{1,0:T(8,128)(2,1)} %copy-done.6, bf16[512,384]{1,0:T(8,128)(2,1)} %copy-done.23, bf16[64,1152]{1,0:T(8,128)(2,1)} %copy-done.13, bf16[64,1152]{1,0:T(8,128)(2,1)} %copy-done.14, ...), custom_call_target="tpu_custom_call" | custom-call | tf_op jit(solution)/shard_map/score_stats/pallas_call | solution.py:351
  75.5 11.9 %all_to_all.44 = f32[8,8,1088]{2,1,0:T(8,128)} all-to-all(f32[8,8,1088]{2,1,0:T(8,128)} %bitcast.35), channel_id=1, replica_groups=mesh['dp_0'=4,'dp_1'=4,'dp_2'=4,'dp_3'=2] {'dp_2','dp_3'}, dimensions={0} | all-to-all | bytes 557056 | tf_op jit(solution)/shard_map/all_to_all | solution.py:40
  87.4 8.8 %score_grads.1 = (bf16[2304,384]{1,0:T(8,128)(2,1)}, bf16[2176,1088]{1,0:T(8,128)(2,1)}) custom-call(f32[64,1088]{1,0:T(8,128)} %bitcast.34, bf16[1088,384]{1,0:T(8,128)(2,1)} %get-tuple-element.32.q, bf16[2176,384]{1,0:T(8,128)(2,1)} %bitcast.31, s32[1,1088]{1,0:T(1,128)} %get-tuple-element.33.place), custom_call_target="tpu_custom_call" | custom-call | tf_op jit(solution)/shard_map/score_grads/pallas_call | solution.py:369
  96.3 7.8 %query_grads.1 = (f32[4,136,384]{2,1,0:T(8,128)}, f32[4,136,384]{2,1,0:T(8,128)}) custom-call(s32[29]{0:T(128)} %concatenate.25.sc, bf16[2176,384]{1,0:T(8,128)(2,1)} %bitcast.32, bf16[2176,1088]{1,0:T(8,128)(2,1)} %get-tuple-element.35.g), custom_call_target="tpu_custom_call" | custom-call | tf_op jit(solution)/shard_map/query_grads/pallas_call | solution.py:388
  104.0 3.9 %all-to-all-start.3 = ((bf16[16,144,384]{2,1,0:T(8,128)(2,1)}), bf16[16,144,384]{2,1,0:T(8,128)(2,1)S(1)}, u32[]{:S(2)}, u32[]{:S(2)}) async-start(bf16[16,144,384]{2,1,0:T(8,128)(2,1)} %bitcast.10), calls=%async_computation.3 | async-start | bytes 3538944 | tf_op jit(solution)/shard_map/all_to_all | solution.py:36
  110.8 3.2 %collective-permute-done.11 = bf16[136,384]{1,0:T(8,128)(2,1)S(1)} collective-permute-done((bf16[136,384]{1,0:T(8,128)(2,1)S(1)}, bf16[136,384]{1,0:T(8,128)(2,1)S(1)}, u32[]{:S(2)}, u32[]{:S(2)}) %collective-permute-start.11) | collective-permute-done | bytes 104480 | tf_op jit(solution)/shard_map/ppermute | solution.py:48
  114.0 2.7 %collective-permute-done.10 = bf16[136,384]{1,0:T(8,128)(2,1)S(1)} collective-permute-done((bf16[136,384]{1,0:T(8,128)(2,1)S(1)}, bf16[136,384]{1,0:T(8,128)(2,1)S(1)}, u32[]{:S(2)}, u32[]{:S(2)}) %collective-permute-start.10) | collective-permute-done | bytes 104480 | tf_op jit(solution)/shard_map/ppermute | solution.py:48
  122.3 12.8 %all-to-all-done.3 = bf16[16,144,384]{2,1,0:T(8,128)(2,1)S(1)} async-done(((bf16[16,144,384]{2,1,0:T(8,128)(2,1)}), bf16[16,144,384]{2,1,0:T(8,128)(2,1)S(1)}, u32[]{:S(2)}, u32[]{:S(2)}) %all-to-all-start.3) | async-done | bytes 1769504 | tf_op jit(solution)/shard_map/all_to_all | solution.py:36
  136.1 3.0 %collective-permute-start.16 = (bf16[256,768]{1,0:T(8,128)(2,1)S(1)}, bf16[256,768]{1,0:T(8,128)(2,1)S(1)}, u32[]{:S(2)}, u32[]{:S(2)}) collective-permute-start(bf16[256,768]{1,0:T(8,128)(2,1)S(1)} %pad_maximum_fusion.2.refs_0_), channel_id=1, source_target_pairs={{2,0},{4,2},{6,4},{0,6},{3,1},{5,3},{7,5},{1,7},{10,8},{12,10},{14... | collective-permute-start | bytes 1179656 | tf_op jit(solution)/shard_map/ppermute | solution.py:44
  142.8 17.9 %collective-permute-done.24 = bf16[136,384]{1,0:T(8,128)(2,1)S(1)} collective-permute-done((bf16[136,384]{1,0:T(8,128)(2,1)S(1)}, bf16[136,384]{1,0:T(8,128)(2,1)S(1)}, u32[]{:S(2)}, u32[]{:S(2)}) %collective-permute-start.24) | collective-permute-done | bytes 104480 | tf_op jit(solution)/shard_map/ppermute | solution.py:44
  161.7 3.7 %collective-permute-done.23 = bf16[136,384]{1,0:T(8,128)(2,1)S(1)} collective-permute-done((bf16[136,384]{1,0:T(8,128)(2,1)S(1)}, bf16[136,384]{1,0:T(8,128)(2,1)S(1)}, u32[]{:S(2)}, u32[]{:S(2)}) %collective-permute-start.23) | collective-permute-done | bytes 104480 | tf_op jit(solution)/shard_map/ppermute | solution.py:44
  169.9 5.7 %hidden_units.1 = (bf16[1088,768]{1,0:T(8,128)(2,1)}, bf16[1088,768]{1,0:T(8,128)(2,1)}, bf16[192,1088]{1,0:T(8,128)(2,1)}, bf16[192,1088]{1,0:T(8,128)(2,1)}, f32[192,1088]{1,0:T(8,128)}, /*index=5*/f32[192,1088]{1,0:T(8,128)}) custom-call(bf16[256,768]{1,0:T(8,128)(2,1)} %copy-done.5, bf16[256,768]{1,0:T(8,128)(2,1)} %copy-done.17, ...), custom_call_target="tpu_custom_call" | custom-call | tf_op jit(solution)/shard_map/hidden_units/pallas_call | solution.py:338
  176.5 6.2 %weight_grads.1 = bf16[128,1792]{1,0:T(8,128)(2,1)} custom-call(bf16[544,384]{1,0:T(8,128)(2,1)} %copy-done.3, bf16[544,384]{1,0:T(8,128)(2,1)} %copy-done.15, bf16[1088,768]{1,0:T(8,128)(2,1)} %get-tuple-element.39.refs_2_, bf16[192,1088]{1,0:T(8,128)(2,1)} %get-tuple-element.40.refs_3_, f32[192,1088]{1,0:T(8,128)} %get-tuple-element.41.refs_4_, ...), custom_call_target="tpu_custom_call" | custom-call | tf_op jit(solution)/shard_map/weight_grads/pallas_call | solution.py:398
  182.7 5.2 %all-to-all-start.4 = ((bf16[16,8,1792]{2,1,0:T(8,128)(2,1)}), bf16[16,8,1792]{2,1,0:T(8,128)(2,1)S(1)}, u32[]{:S(2)}, u32[]{:S(2)}) async-start(bf16[16,8,1792]{2,1,0:T(8,128)(2,1)} %bitcast.33), calls=%async_computation.4 | async-start | bytes 917504 | tf_op jit(solution)/shard_map/all_to_all | solution.py:36
  190.4 8.6 %all-to-all-done.4 = bf16[16,8,1792]{2,1,0:T(8,128)(2,1)S(1)} async-done(((bf16[16,8,1792]{2,1,0:T(8,128)(2,1)}), bf16[16,8,1792]{2,1,0:T(8,128)(2,1)S(1)}, u32[]{:S(2)}, u32[]{:S(2)}) %all-to-all-start.4) | async-done | bytes 458784 | tf_op jit(solution)/shard_map/all_to_all | solution.py:36
  (136 shorter events, 36.6 us)
Async XLA Ops:
  2.7 22.6 %all-to-all-start = ((bf16[16,8,1664]{2,1,0:T(8,128)(2,1)}), bf16[16,8,1664]{2,1,0:T(8,128)(2,1)S(1)}, u32[]{:S(2)}, u32[]{:S(2)}) async-start(bf16[16,8,1664]{2,1,0:T(8,128)(2,1)} %get-tuple-element.25), calls=%async_computation | async-start | bytes 851968 | tf_op jit(solution)/shard_map/all_to_all | solution.py:36
  16.0 6.4 %collective-permute-start.2 = (bf16[128,384]{1,0:T(8,128)(2,1)S(1)}, bf16[128,384]{1,0:T(8,128)(2,1)S(1)}, u32[]{:S(2)}, u32[]{:S(2)}) collective-permute-start(bf16[128,384]{1,0:T(8,128)(2,1)S(1)} %get-tuple-element.53), channel_id=1, source_target_pairs={{6,0},{0,2},{2,4},{4,6},{7,1},{1,3},{3,5},{5,7},{14,8},{8,10},{10,... | collective-permute-start | bytes 294920 | tf_op jit(solution)/shard_map/ppermute | solution.py:44
  17.6 7.2 %collective-permute-start.1 = (bf16[128,384]{1,0:T(8,128)(2,1)S(1)}, bf16[128,384]{1,0:T(8,128)(2,1)S(1)}, u32[]{:S(2)}, u32[]{:S(2)}) collective-permute-start(bf16[128,384]{1,0:T(8,128)(2,1)S(1)} %get-tuple-element.53), channel_id=1, source_target_pairs={{4,0},{6,2},{0,4},{2,6},{5,1},{7,3},{1,5},{3,7},{12,8},{14,10},{8,... | collective-permute-start | bytes 294920 | tf_op jit(solution)/shard_map/ppermute | solution.py:44
  25.1 41.6 %collective-permute-start.3 = (bf16[512,384]{1,0:T(8,128)(2,1)S(1)}, bf16[512,384]{1,0:T(8,128)(2,1)S(1)}, u32[]{:S(2)}, u32[]{:S(2)}) collective-permute-start(bf16[512,384]{1,0:T(8,128)(2,1)S(1)} %pad_maximum_fusion.3.q_own), channel_id=1, source_target_pairs={{0,1},{1,0},{2,3},{3,2},{4,5},{5,4},{6,7},{7,6},{8,9},{9,8},{10,11... | collective-permute-start | bytes 1179656 | tf_op jit(solution)/shard_map/ppermute | solution.py:32
  30.7 14.1 %collective-permute-start.4 = (bf16[16,1152]{1,0:T(8,128)(2,1)}, bf16[16,1152]{1,0:T(8,128)(2,1)S(1)}, u32[]{:S(2)}, u32[]{:S(2)}) collective-permute-start(bf16[16,1152]{1,0:T(8,128)(2,1)} %get-tuple-element.26), channel_id=1, source_target_pairs={{2,0},{4,2},{6,4},{0,6},{3,1},{5,3},{7,5},{1,7},{10,8},{12,10},{14... | collective-permute-start | bytes 110600 | tf_op jit(solution)/shard_map/ppermute | solution.py:44
  33.3 11.5 %collective-permute-start.5 = (bf16[16,1152]{1,0:T(8,128)(2,1)}, bf16[16,1152]{1,0:T(8,128)(2,1)S(1)}, u32[]{:S(2)}, u32[]{:S(2)}) collective-permute-start(bf16[16,1152]{1,0:T(8,128)(2,1)} %get-tuple-element.26), channel_id=1, source_target_pairs={{4,0},{6,2},{0,4},{2,6},{5,1},{7,3},{1,5},{3,7},{12,8},{14,10},{8,... | collective-permute-start | bytes 110600 | tf_op jit(solution)/shard_map/ppermute | solution.py:44
  33.6 11.2 %collective-permute-start.6 = (bf16[16,1152]{1,0:T(8,128)(2,1)}, bf16[16,1152]{1,0:T(8,128)(2,1)S(1)}, u32[]{:S(2)}, u32[]{:S(2)}) collective-permute-start(bf16[16,1152]{1,0:T(8,128)(2,1)} %get-tuple-element.26), channel_id=1, source_target_pairs={{6,0},{0,2},{2,4},{4,6},{7,1},{1,3},{3,5},{5,7},{14,8},{8,10},{10,... | collective-permute-start | bytes 110600 | tf_op jit(solution)/shard_map/ppermute | solution.py:44
  34.5 32.3 %all-to-all-start.1 = ((bf16[16,136,384]{2,1,0:T(8,128)(2,1)}), bf16[16,136,384]{2,1,0:T(8,128)(2,1)S(1)}, u32[]{:S(2)}, u32[]{:S(2)}) async-start(bf16[16,136,384]{2,1,0:T(8,128)(2,1)} %get-tuple-element.29), calls=%async_computation.1 | async-start | bytes 3342336 | tf_op jit(solution)/shard_map/all_to_all | solution.py:36
  44.8 21.9 %collective-permute-start.7 = (bf16[64,1152]{1,0:T(8,128)(2,1)S(1)}, bf16[64,1152]{1,0:T(8,128)(2,1)S(1)}, u32[]{:S(2)}, u32[]{:S(2)}) collective-permute-start(bf16[64,1152]{1,0:T(8,128)(2,1)S(1)} %constant_dynamic-update-slice_fusion.t_own.refs_8_), channel_id=1, source_target_pairs={{0,1},{1,0},{2,3},{3,2},{4,5},{5,4},{6,7},{7,6},{8,9},{9,8},{10,11... | collective-permute-start | bytes 442376 | tf_op jit(solution)/shard_map/ppermute | solution.py:32
  104.0 31.1 %all-to-all-start.3 = ((bf16[16,144,384]{2,1,0:T(8,128)(2,1)}), bf16[16,144,384]{2,1,0:T(8,128)(2,1)S(1)}, u32[]{:S(2)}, u32[]{:S(2)}) async-start(bf16[16,144,384]{2,1,0:T(8,128)(2,1)} %bitcast.10), calls=%async_computation.3 | async-start | bytes 3538944 | tf_op jit(solution)/shard_map/all_to_all | solution.py:36
  109.4 7.3 %collective-permute-start.10 = (bf16[136,384]{1,0:T(8,128)(2,1)S(1)}, bf16[136,384]{1,0:T(8,128)(2,1)S(1)}, u32[]{:S(2)}, u32[]{:S(2)}) collective-permute-start(bf16[136,384]{1,0:T(8,128)(2,1)S(1)} %get-tuple-element.49), channel_id=1, source_target_pairs={{0,4},{2,6},{4,0},{6,2},{1,5},{3,7},{5,1},{7,3},{8,12},{10,14},{12... | collective-permute-start | bytes 313352 | tf_op jit(solution)/shard_map/ppermute | solution.py:48
  110.8 7.3 %collective-permute-start.9 = (bf16[136,384]{1,0:T(8,128)(2,1)S(1)}, bf16[136,384]{1,0:T(8,128)(2,1)S(1)}, u32[]{:S(2)}, u32[]{:S(2)}) collective-permute-start(bf16[136,384]{1,0:T(8,128)(2,1)S(1)} %get-tuple-element.47), channel_id=1, source_target_pairs={{0,2},{2,4},{4,6},{6,0},{1,3},{3,5},{5,7},{7,1},{8,10},{10,12},{12... | collective-permute-start | bytes 313352 | tf_op jit(solution)/shard_map/ppermute | solution.py:48
  118.2 20.9 %collective-permute-start.14 = (bf16[136,384]{1,0:T(8,128)(2,1)S(1)}, bf16[136,384]{1,0:T(8,128)(2,1)S(1)}, u32[]{:S(2)}, u32[]{:S(2)}) collective-permute-start(bf16[136,384]{1,0:T(8,128)(2,1)S(1)} %fusion.18), channel_id=1, source_target_pairs={{6,0},{0,2},{2,4},{4,6},{7,1},{1,3},{3,5},{5,7},{14,8},{8,10},{10,... | collective-permute-start | bytes 313352 | tf_op jit(solution)/shard_map/ppermute | solution.py:44
  118.2 20.8 %collective-permute-start.13 = (bf16[136,384]{1,0:T(8,128)(2,1)S(1)}, bf16[136,384]{1,0:T(8,128)(2,1)S(1)}, u32[]{:S(2)}, u32[]{:S(2)}) collective-permute-start(bf16[136,384]{1,0:T(8,128)(2,1)S(1)} %fusion.18), channel_id=1, source_target_pairs={{4,0},{6,2},{0,4},{2,6},{5,1},{7,3},{1,5},{3,7},{12,8},{14,10},{8,... | collective-permute-start | bytes 313352 | tf_op jit(solution)/shard_map/ppermute | solution.py:44
  120.3 19.8 %collective-permute-start.12 = (bf16[136,384]{1,0:T(8,128)(2,1)S(1)}, bf16[136,384]{1,0:T(8,128)(2,1)}, u32[]{:S(2)}, u32[]{:S(2)}) collective-permute-start(bf16[136,384]{1,0:T(8,128)(2,1)S(1)} %fusion.18), channel_id=1, source_target_pairs={{2,0},{4,2},{6,4},{0,6},{3,1},{5,3},{7,5},{1,7},{10,8},{12,10},{14... | collective-permute-start | bytes 313352 | tf_op jit(solution)/shard_map/ppermute | solution.py:44
  135.4 6.0 %collective-permute-start.25 = (bf16[136,384]{1,0:T(8,128)(2,1)S(1)}, bf16[136,384]{1,0:T(8,128)(2,1)S(1)}, u32[]{:S(2)}, u32[]{:S(2)}) collective-permute-start(bf16[136,384]{1,0:T(8,128)(2,1)S(1)} %slice.95), channel_id=1, source_target_pairs={{6,0},{0,2},{2,4},{4,6},{7,1},{1,3},{3,5},{5,7},{14,8},{8,10},{10,... | collective-permute-start | bytes 313352 | tf_op jit(solution)/shard_map/ppermute | solution.py:44
  136.1 29.4 %collective-permute-start.16 = (bf16[256,768]{1,0:T(8,128)(2,1)S(1)}, bf16[256,768]{1,0:T(8,128)(2,1)S(1)}, u32[]{:S(2)}, u32[]{:S(2)}) collective-permute-start(bf16[256,768]{1,0:T(8,128)(2,1)S(1)} %pad_maximum_fusion.2.refs_0_), channel_id=1, source_target_pairs={{2,0},{4,2},{6,4},{0,6},{3,1},{5,3},{7,5},{1,7},{10,8},{12,10},{14... | collective-permute-start | bytes 1179656 | tf_op jit(solution)/shard_map/ppermute | solution.py:44
  139.1 27.0 %collective-permute-start.17 = (bf16[256,768]{1,0:T(8,128)(2,1)S(1)}, bf16[256,768]{1,0:T(8,128)(2,1)S(1)}, u32[]{:S(2)}, u32[]{:S(2)}) collective-permute-start(bf16[256,768]{1,0:T(8,128)(2,1)S(1)} %pad_maximum_fusion.2.refs_0_), channel_id=1, source_target_pairs={{4,0},{6,2},{0,4},{2,6},{5,1},{7,3},{1,5},{3,7},{12,8},{14,10},{8,... | collective-permute-start | bytes 1179656 | tf_op jit(solution)/shard_map/ppermute | solution.py:44
  139.1 27.1 %collective-permute-start.18 = (bf16[256,768]{1,0:T(8,128)(2,1)S(1)}, bf16[256,768]{1,0:T(8,128)(2,1)S(1)}, u32[]{:S(2)}, u32[]{:S(2)}) collective-permute-start(bf16[256,768]{1,0:T(8,128)(2,1)S(1)} %pad_maximum_fusion.2.refs_0_), channel_id=1, source_target_pairs={{6,0},{0,2},{2,4},{4,6},{7,1},{1,3},{3,5},{5,7},{14,8},{8,10},{10,... | collective-permute-start | bytes 1179656 | tf_op jit(solution)/shard_map/ppermute | solution.py:44
  140.0 26.6 %collective-permute-start.19 = (bf16[256,768]{1,0:T(8,128)(2,1)S(1)}, bf16[256,768]{1,0:T(8,128)(2,1)S(1)}, u32[]{:S(2)}, u32[]{:S(2)}) collective-permute-start(bf16[256,768]{1,0:T(8,128)(2,1)S(1)} %pad_maximum_fusion.2.refs_0_), channel_id=1, source_target_pairs={{0,1},{1,0},{2,3},{3,2},{4,5},{5,4},{6,7},{7,6},{8,9},{9,8},{10,11... | collective-permute-start | bytes 1179656 | tf_op jit(solution)/shard_map/ppermute | solution.py:32
  141.4 19.4 %collective-permute-start.24 = (bf16[136,384]{1,0:T(8,128)(2,1)S(1)}, bf16[136,384]{1,0:T(8,128)(2,1)S(1)}, u32[]{:S(2)}, u32[]{:S(2)}) collective-permute-start(bf16[136,384]{1,0:T(8,128)(2,1)S(1)} %slice.95), channel_id=1, source_target_pairs={{4,0},{6,2},{0,4},{2,6},{5,1},{7,3},{1,5},{3,7},{12,8},{14,10},{8,... | collective-permute-start | bytes 313352 | tf_op jit(solution)/shard_map/ppermute | solution.py:44
  165.4 10.1 %collective-permute-start.15 = (bf16[544,384]{1,0:T(8,128)(2,1)S(1)}, bf16[544,384]{1,0:T(8,128)(2,1)S(1)}, u32[]{:S(2)}, u32[]{:S(2)}) collective-permute-start(bf16[544,384]{1,0:T(8,128)(2,1)S(1)} %pad_maximum_fusion.refs_0_), channel_id=1, source_target_pairs={{0,1},{1,0},{2,3},{3,2},{4,5},{5,4},{6,7},{7,6},{8,9},{9,8},{10,11... | collective-permute-start | bytes 1253384 | tf_op jit(solution)/shard_map/ppermute | solution.py:32
  165.5 10.1 %collective-permute-start.26 = (bf16[544,384]{1,0:T(8,128)(2,1)S(1)}, bf16[544,384]{1,0:T(8,128)(2,1)S(1)}, u32[]{:S(2)}, u32[]{:S(2)}) collective-permute-start(bf16[544,384]{1,0:T(8,128)(2,1)S(1)} %pad_maximum_fusion.1.refs_5_), channel_id=1, source_target_pairs={{0,1},{1,0},{2,3},{3,2},{4,5},{5,4},{6,7},{7,6},{8,9},{9,8},{10,11... | collective-permute-start | bytes 1253384 | tf_op jit(solution)/shard_map/ppermute | solution.py:32
  182.7 16.3 %all-to-all-start.4 = ((bf16[16,8,1792]{2,1,0:T(8,128)(2,1)}), bf16[16,8,1792]{2,1,0:T(8,128)(2,1)S(1)}, u32[]{:S(2)}, u32[]{:S(2)}) async-start(bf16[16,8,1792]{2,1,0:T(8,128)(2,1)} %bitcast.33), calls=%async_computation.4 | async-start | bytes 917504 | tf_op jit(solution)/shard_map/all_to_all | solution.py:36
  (33 other events, 274.7 us)

commit v10 on v9

--- a/solution.py
+++ b/solution.py
@@ -19,13 +19,8 @@
 LOW = 128
 UNIT = 8
 BLOCK = LOW + UNIT
-CHUNK = 144
 PAIR = 2 * BLOCK
 LOG2E = 1.4426950408889634
-
-
-def gelu_tanh(values):
-    return jax.nn.gelu(values, approximate=True)
 
 
 def swap_core(x):
@@ -102,6 +97,16 @@
         0.7978845608028654 * (1.0 + 3 * 0.044715 * square)
     )
     return (v * grown, slope)
+
+
+def base_kernel(q, p, w_first, w_second, q_out, p_out, feats):
+    feats[:LOW] = q[...]
+    feats[LOW:] = p[...]
+    pre = jnp.dot(feats[...], w_first[...], preferred_element_type=F32)
+    hidden = gelu_parts(pre)[0].astype(BF16)
+    emb = jnp.dot(hidden, w_second[...], preferred_element_type=F32).astype(BF16)
+    q_out[...] = emb[:LOW]
+    p_out[...] = emb[LOW:]
 
 
 def tail_kernel(heavy_at, arrived, base_p, pos, w_first, w_second, p_out, q_out):
@@ -188,8 +193,8 @@
         stats_out[b * 8 : (b + 1) * 8] = stats
 
 
-def grads_kernel(stats, q, p, place, dp_out, g_out, dp_ref, g_ref, sems, *, scale):
-    rows, width = q.shape
+def grads_kernel(stats, q, p, place, dp_out, g_out, loss_out, dp_ref, g_ref, sems, *, scale):
+    rows = q.shape[0]
     pull = scale * LOG2E
     tops = [stats[b * 8 : b * 8 + 1] for b in range(8)]
     top = functools.reduce(jnp.maximum, tops)
@@ -204,12 +209,12 @@
     loss_high = loss.astype(BF16).astype(F32)
     loss_mid = (loss - loss_high).astype(BF16).astype(F32)
     loss_low = loss - loss_high - loss_mid
-    line = lax.broadcasted_iota(jnp.int32, (UNIT, width), 0)
-    loss_tile = jnp.where(
+    line = jnp.bitwise_and(lax.broadcasted_iota(jnp.int32, loss_out.shape, 0), 3)
+    loss_out[...] = jnp.where(
         line == 0,
         loss_high,
         jnp.where(line == 1, loss_mid, jnp.where(line == 2, loss_low, 0.0)),
-    ).astype(BF16)
+    )
     copies = []
 
     def send(src, dst, rows):
@@ -225,12 +230,8 @@
         send(g_ref, g_out, pl.ds(at, PAIR))
     for k in range(p.shape[0] // PAIR):
         dp = scale * jnp.dot(g_ref[k * PAIR : (k + 1) * PAIR], q[...], preferred_element_type=F32)
-        dp = dp.astype(BF16)
-        for half in range(2):
-            to = (2 * k + half) * CHUNK
-            dp_ref[to : to + BLOCK] = dp[half * BLOCK : (half + 1) * BLOCK]
-            dp_ref[to + BLOCK : to + CHUNK] = loss_tile
-        send(dp_ref, dp_out, pl.ds(2 * k * CHUNK, 2 * CHUNK))
+        dp_ref[k * PAIR : (k + 1) * PAIR] = dp.astype(BF16)
+        send(dp_ref, dp_out, pl.ds(k * PAIR, PAIR))
     for copy in copies:
         copy.wait()
 
@@ -262,20 +263,44 @@
         put(j, slice(LOW, BLOCK), dq[j * UNIT : (j + 1) * UNIT])
 
 
-def weight_parts(de_own, de_far, rows, hidden, slope, second, de):
+def total_kernel(parts, out):
+    total = parts[:BLOCK].astype(F32)
+    for k in range(1, 16):
+        total += parts[k * BLOCK : (k + 1) * BLOCK].astype(F32)
+    out[...] = total.astype(BF16)
+
+
+def weight_parts(de_own, de_far, hidden, slope, rows, second, de, copies):
     half = de_own.shape[0]
     de[:half] = de_own[...]
     de[half:] = de_far[...]
+    back = nt_dot(second[...], de[...])
+    copies[0].wait()
     grad_second = jnp.dot(hidden[...], de[...], preferred_element_type=F32)
-    dpre = (slope[...] * nt_dot(second[...], de[...])).astype(BF16)
+    copies[1].wait()
+    dpre = (slope[...] * back).astype(BF16)
+    copies[2].wait()
     grad_first = jnp.dot(dpre, rows[...], preferred_element_type=F32)
     return (grad_first, grad_second)
 
 
 def weights_kernel(*refs):
-    second, out, de = refs[10:]
-    first_q, second_q = weight_parts(*refs[:5], second, de)
-    grad_first, grad_second = weight_parts(*refs[5:10], second, de)
+    des, (second, loss), units, (out, de), held, sems = (
+        refs[:4],
+        refs[4:6],
+        refs[6:12],
+        refs[12:14],
+        refs[14:20],
+        refs[20],
+    )
+    copies = [
+        pltpu.make_async_copy(unit, hold, sems.at[k])
+        for k, (unit, hold) in enumerate(zip(units, held))
+    ]
+    for copy in copies:
+        copy.start()
+    first_q, second_q = weight_parts(*des[:2], *held[:3], second, de, copies[:3])
+    grad_first, grad_second = weight_parts(*des[2:], *held[3:], second, de, copies[3:])
     grad_first += first_q
     grad_second += second_q
     many = out.shape[0]
@@ -285,7 +310,8 @@
     out[:, width:wide] = grad_second[:many].astype(BF16)
     rest = grad_first.shape[0] - many
     x = jnp.concatenate(
-        [grad_first[many:], grad_second[many:], jnp.zeros((rest, 128), F32)], axis=1
+        [grad_first[many:], grad_second[many:], jnp.concatenate([loss[...]] * (rest // UNIT))],
+        axis=1,
     )
     near, far = x[:, :640], x[:, 640:]
     line = jnp.bitwise_and(lax.broadcasted_iota(jnp.int32, near.shape, 0), 7)
@@ -315,6 +341,24 @@
         ],
         name="pack_overflow",
     )(counts, where, q, p, pos)
+
+
+def base_rows(q, p, w_first, w_second):
+    width, emb_width = w_first.shape[0], w_second.shape[1]
+    rows = pl.BlockSpec((LOW, width), lambda i: (0, 0))
+
+    def whole(shape):
+        return pl.BlockSpec(shape, lambda i: (0, 0))
+
+    shapes = [(LOW, emb_width), (LOW, emb_width), (2 * LOW, width)]
+    return pl.pallas_call(
+        base_kernel,
+        grid=(1,),
+        in_specs=[rows, rows, whole(w_first.shape), whole(w_second.shape)],
+        out_specs=[whole(shape) for shape in shapes],
+        out_shape=[jax.ShapeDtypeStruct(shape, BF16) for shape in shapes],
+        name="base_rows",
+    )(q, p, w_first, w_second)
 
 
 def tail_rows(heavy_at, arrived, base_p, pos, w_first, w_second):
@@ -342,7 +386,7 @@
         out_shape=[rows, rows, hidden, hidden, slope, slope],
         name="hidden_units",
     )(*blocks, *tails, first)
-    return ((rows_q, hidden_q, slope_q), (rows_p, hidden_p, slope_p))
+    return ((hidden_q, slope_q, rows_q), (hidden_p, slope_p, rows_p))
 
 
 def score_stats(sc, qs, ts, p, scale):
@@ -369,13 +413,14 @@
     return pl.pallas_call(
         functools.partial(grads_kernel, scale=scale),
         in_specs=[VMEM] * 4,
-        out_specs=[HBM] * 2,
+        out_specs=[HBM, HBM, VMEM],
         out_shape=[
-            jax.ShapeDtypeStruct((2 * steps * CHUNK, width), BF16),
+            jax.ShapeDtypeStruct((columns, width), BF16),
             jax.ShapeDtypeStruct((columns, rows), BF16),
+            jax.ShapeDtypeStruct((UNIT, LOW), F32),
         ],
         scratch_shapes=[
-            pltpu.VMEM((2 * steps * CHUNK, width), BF16),
+            pltpu.VMEM((columns, width), BF16),
             pltpu.VMEM((columns, rows), BF16),
             pltpu.SemaphoreType.DMA((2 * steps,)),
         ],
@@ -394,15 +439,28 @@
     )(sc, p, g)
 
 
-def weight_grads(dqs, q_units, dps, p_units, second):
+def plane_total(parts):
+    return pl.pallas_call(
+        total_kernel,
+        in_specs=[VMEM],
+        out_specs=VMEM,
+        out_shape=jax.ShapeDtypeStruct((BLOCK, parts.shape[1]), BF16),
+        name="plane_total",
+    )(parts)
+
+
+def weight_grads(dqs, q_units, dps, p_units, second, loss):
+    held = [pltpu.VMEM(x.shape, x.dtype) for x in (*q_units, *p_units)]
     return pl.pallas_call(
         weights_kernel,
-        in_specs=[VMEM] * 11,
+        in_specs=[VMEM] * 6 + [HBM] * 6,
         out_specs=VMEM,
-        out_shape=jax.ShapeDtypeStruct((128, 1792), BF16),
-        scratch_shapes=[pltpu.VMEM((8 * BLOCK, second.shape[1]), BF16)],
+        out_shape=jax.ShapeDtypeStruct((LOW, 1792), BF16),
+        scratch_shapes=[pltpu.VMEM((8 * BLOCK, second.shape[1]), BF16)]
+        + held
+        + [pltpu.SemaphoreType.DMA((6,))],
         name="weight_grads",
-    )(*dqs, *q_units, *dps, *p_units, second)
+    )(*dqs, *dps, second, loss, *q_units, *p_units)
 
 
 def body(query_features, passage_features, counts, positives, w_first, w_second):
@@ -418,20 +476,14 @@
     over = over.reshape(16 * UNIT, -1)
     arrived = plane_exchange(over)
 
-    def tower(x):
-        pre = jnp.dot(x, w_first, preferred_element_type=F32)
-        hidden = gelu_tanh(pre).astype(BF16)
-        return jnp.dot(hidden, w_second, preferred_element_type=F32).astype(BF16)
-
-    feats = jnp.concatenate([query_features[:LOW], passage_features[:LOW]], axis=0)
-    base = tower(feats)
-    qs = gathered(base[:LOW])
+    q_base, p_base, feats = base_rows(query_features, passage_features, w_first, w_second)
+    qs = gathered(q_base)
 
     feats = along_line(feats)
     feats = feats + [swap_core(x) for x in feats]
 
     p_send, q_tail = tail_rows(
-        heavy_at, arrived.reshape(16, UNIT, -1), base[LOW:], pos, w_first, w_second
+        heavy_at, arrived.reshape(16, UNIT, -1), p_base, pos, w_first, w_second
     )
     p_all = plane_exchange(p_send.reshape(16 * BLOCK, emb_width))
     ts = gathered(q_tail)
@@ -465,7 +517,7 @@
     q_all, place, stats = score_stats(sc, qs, ts, p_all, scale)
     stats = stats_exchange(stats)
     q_units, p_units = hidden_units(feats, ts, first_part)
-    dp_part, g = score_grads(stats, q_all, p_all, place, scale)
+    dp_part, g, loss = score_grads(stats, q_all, p_all, place, scale)
     dp_all = plane_exchange(dp_part)
     dq_own, dq_far = query_grads(sc, p_all, g, scale)
 
@@ -476,12 +528,12 @@
         dq_sum = dq_sum + part.astype(F32)
     dqs = gathered(dq_sum.astype(BF16))
 
-    dp_sum = jnp.sum(dp_all.reshape(16, CHUNK, emb_width).astype(F32), axis=0)
-    mean_loss = (dp_sum[BLOCK, 0] + dp_sum[BLOCK + 1, 0] + dp_sum[BLOCK + 2, 0]) / pairs
-    dps = gathered(dp_sum[:BLOCK].astype(BF16))
-    grads = weight_grads(dqs, q_units, dps, p_units, second_part)
+    dp_sum = plane_total(dp_all)
+    dps = gathered(dp_sum)
+    grads = weight_grads(dqs, q_units, dps, p_units, second_part, loss)
     out = jnp.sum(plane_exchange(grads).reshape(16, 8, -1).astype(F32), axis=0)
     wide = width + emb_width
+    mean_loss = (out[4, -1] + out[5, -1] + out[6, -1]) / pairs
     tail_out = jnp.concatenate([out[:4, wide:], out[4:, wide : 2 * wide - 640]], axis=1)
     out = jnp.concatenate([out[:, :wide], tail_out], axis=0)
     return (mean_loss, out[:, :width].T, out[:, width:])

time: 202 us -> 206 us (1.020)
  blocking collectives: 11.9 us -> 28.3 us
  starting transfers between devices: 48 us -> 37 us
  waiting for transfers between devices: 74.5 us -> 67.6 us
  Pallas kernels: 41.9 us -> 48.5 us
  matrix products: 7.13 us -> 4.5 us
    all_to_all x0 -> x1, blocking collectives: none -> 16.1 us  [plane_exchange(): return lax.all_to_all(x, PLANE, 0, 0, tiled=True)]
    all_to_all x4 -> x3, starting transfers between devices: 24.2 us -> 15.7 us  [plane_exchange(): return lax.all_to_all(x, PLANE, 0, 0, tiled=True)]
    pallas_call x1 -> x3, Pallas kernels: 6.2 us -> 12.5 us  [the longest x1 5.93 us: weight_grads(): pl.pallas_call(weights_kernel, in_specs=[VMEM] * 6 + [HBM] * 6, out_specs...]
    all_to_all x4 -> x3, waiting for transfers between devices: 39.9 us -> 35.1 us  [plane_exchange(): return lax.all_to_all(x, PLANE, 0, 0, tiled=True)]
    dot_general x1 -> x0, matrix products: 2.62 us -> none  [tower(): return jnp.dot(hidden, w_second, preferred_element_type=F32).astype(BF16)]
    slice x5 -> x1, local copies, waits for them, and re-layouts: 3.15 us -> 0.65 us  [body(): mean_loss = (out[4, -1] + out[5, -1] + out[6, -1]) / pairs]
    ppermute x15, starting transfers between devices: 19.7 us -> 17.2 us  [from_line(): return lax.ppermute(x, LINE, [((i + k) % 4, i) for i in range(4)])]
    unnamed x55 -> x54, local copies, waits for them, and re-layouts: 4.78 us -> 6.71 us
  transfers between devices with their start and end apart: 31 -> 30, of which waited for: 14 -> 11; matrix products, arithmetic and copies ran while one was open for 7% -> 5% of each run, Pallas kernels for 5% -> 7%
where the time goes in v10:
time: 206 us; the launch traced here: 205 us
  waiting for transfers between devices  67.6 us (33%)
  Pallas kernels  48.5 us (24%)
  starting transfers between devices  37 us (18%)
  blocking collectives  28.3 us (14%)
  local copies, waits for them, and re-layouts  9.71 us (5%)
  other arithmetic  4.86 us (2%)
  between operations  4.63 us (2%)
  matrix products  4.5 us (2%)
    all_to_all x3, waiting for transfers between devices, plane_exchange(): return lax.all_to_all(x, PLANE, 0, 0, tiled=True)  35.1 us
    ppermute x15, waiting for transfers between devices, from_line(): return lax.ppermute(x, LINE, [((i + k) % 4, i) for i in range(4)])  24.6 us
    ppermute x15, starting transfers between devices, from_line(): return lax.ppermute(x, LINE, [((i + k) % 4, i) for i in range(4)])  17.2 us
    all_to_all x1, blocking collectives, plane_exchange(): return lax.all_to_all(x, PLANE, 0, 0, tiled=True)  16.1 us
    all_to_all x3, starting transfers between devices, plane_exchange(): return lax.all_to_all(x, PLANE, 0, 0, tiled=True)  15.7 us
    all_to_all x1, blocking collectives, stats_exchange(): return lax.all_to_all(x, (LINE, CORE), 0, 0, tiled=True)  12.1 us
    pallas_call x1, Pallas kernels, score_grads(): pl.pallas_call(functools.partial(grads_kernel, scale=scale), in_specs=[VM...  9.42 us
    pallas_call x1, Pallas kernels, query_grads(): pl.pallas_call(functools.partial(query_kernel, scale=scale), in_specs=[SM...  7.75 us
  transfers between devices with their start and end apart: 30, of which 11 were waited for; matrix products, arithmetic and copies ran while one was open for 5% of the time, Pallas kernels for 7%

profile of v10, /device:TPU:0, one launch (start us, length us, event | category | flops | bytes accessed | tf_op | source)
XLA Modules:
  0.0 205.1 jit_solution(170369128739076822)
XLA Ops:
  0.6 4.2 %base_rows.1 = (bf16[128,384]{1,0:T(8,128)(2,1)}, bf16[128,384]{1,0:T(8,128)(2,1)}, bf16[256,768]{1,0:T(8,128)(2,1)}) custom-call(bf16[256,768]{1,0:T(8,128)(2,1)} %q.3, bf16[256,768]{1,0:T(8,128)(2,1)} %p.3, bf16[768,1536]{1,0:T(8,128)(2,1)} %w_first.3, bf16[1536,384]{1,0:T(8,128)(2,1)} %w_second.3), custom_call_target="tpu_custom_call" | custom-call | tf_op jit(solution)/shard_map/base_rows/pallas_call | solution.py:354
  4.8 3.1 %collective-permute-start = (bf16[128,384]{1,0:T(8,128)(2,1)}, bf16[128,384]{1,0:T(8,128)(2,1)S(1)}, u32[]{:S(2)}, u32[]{:S(2)}) collective-permute-start(bf16[128,384]{1,0:T(8,128)(2,1)} %get-tuple-element.36), channel_id=1, source_target_pairs={{2,0},{4,2},{6,4},{0,6},{3,1},{5,3},{7,5},{1,7},{10,8},{12,10},{14... | collective-permute-start | bytes 294920 | tf_op jit(solution)/shard_map/ppermute | solution.py:39
  11.4 7.9 %all-to-all-start = ((bf16[16,8,1664]{2,1,0:T(8,128)(2,1)}), bf16[16,8,1664]{2,1,0:T(8,128)(2,1)S(1)}, u32[]{:S(2)}, u32[]{:S(2)}) async-start(bf16[16,8,1664]{2,1,0:T(8,128)(2,1)} %get-tuple-element.29), calls=%async_computation | async-start | bytes 851968 | tf_op jit(solution)/shard_map/all_to_all | solution.py:31
  19.6 9.1 %all-to-all-done.arrived = bf16[16,8,1664]{2,1,0:T(8,128)(2,1)S(1)} async-done(((bf16[16,8,1664]{2,1,0:T(8,128)(2,1)}), bf16[16,8,1664]{2,1,0:T(8,128)(2,1)S(1)}, u32[]{:S(2)}, u32[]{:S(2)}) %all-to-all-start) | async-done | bytes 426016 | tf_op jit(solution)/shard_map/all_to_all | solution.py:31
  29.4 4.6 %tail_rows.1 = (bf16[16,136,384]{2,1,0:T(8,128)(2,1)}, bf16[16,1152]{1,0:T(8,128)(2,1)}) custom-call(s32[1]{0:T(128)} %get-tuple-element.28.heavy_at, bf16[16,8,1664]{2,1,0:T(8,128)(2,1)} %copy-done.3, bf16[128,384]{1,0:T(8,128)(2,1)} %get-tuple-element.30.base_p, s32[2,128]{1,0:T(2,128)} %bitcast.39, bf16[768,1536]{1,0:T(8,128)(2,1)} %w_first.3, ...), custom_call_target="tpu_custom_call" | custom-call | tf_op jit(solution)/shard_map/tail_rows/pallas_call | solution.py:366
  38.0 3.9 %all-to-all-start.1 = ((bf16[16,136,384]{2,1,0:T(8,128)(2,1)}), bf16[16,136,384]{2,1,0:T(8,128)(2,1)S(1)}, u32[]{:S(2)}, u32[]{:S(2)}) async-start(bf16[16,136,384]{2,1,0:T(8,128)(2,1)} %get-tuple-element.34), calls=%async_computation.1 | async-start | bytes 3342336 | tf_op jit(solution)/shard_map/all_to_all | solution.py:31
  45.2 3.3 %convolution_convert_fusion.refs_10_ = bf16[192,768]{1,0:T(8,128)(2,1)} fusion(bf16[768,1536]{1,0:T(8,128)(2,1)} %w_first.3, s32[192]{0:T(256)S(1)} %fusion.17), kind=kOutput, calls=%fused_computation | convolution fusion | flops 453427200 | bytes 2654976 | tf_op jit(solution)/shard_map/dot_general | solution.py:511
  48.5 15.4 %all-to-all-done.1 = bf16[16,136,384]{2,1,0:T(8,128)(2,1)S(1)} async-done(((bf16[16,136,384]{2,1,0:T(8,128)(2,1)}), bf16[16,136,384]{2,1,0:T(8,128)(2,1)S(1)}, u32[]{:S(2)}, u32[]{:S(2)}) %all-to-all-start.1) | async-done | bytes 1671200 | tf_op jit(solution)/shard_map/all_to_all | solution.py:31
  65.9 6.7 %score_stats.1 = (bf16[1088,384]{1,0:T(8,128)(2,1)}, s32[1,1088]{1,0:T(1,128)}, f32[64,1088]{1,0:T(8,128)}) custom-call(s32[29]{0:T(128)} %concatenate.21.sc, bf16[512,384]{1,0:T(8,128)(2,1)} %copy-done.8, bf16[512,384]{1,0:T(8,128)(2,1)} %copy-done.20, bf16[64,1152]{1,0:T(8,128)(2,1)} %copy-done.7, bf16[64,1152]{1,0:T(8,128)(2,1)} %copy-done.9, ...), custom_call_target="tpu_custom_call" | custom-call | tf_op jit(solution)/shard_map/score_stats/pallas_call | solution.py:395
  72.6 12.1 %all_to_all.46 = f32[8,8,1088]{2,1,0:T(8,128)} all-to-all(f32[8,8,1088]{2,1,0:T(8,128)} %bitcast.36), channel_id=1, replica_groups=mesh['dp_0'=4,'dp_1'=4,'dp_2'=4,'dp_3'=2] {'dp_2','dp_3'}, dimensions={0} | all-to-all | bytes 557056 | tf_op jit(solution)/shard_map/all_to_all | solution.py:35
  84.8 9.4 %score_grads.1 = (bf16[2176,384]{1,0:T(8,128)(2,1)}, bf16[2176,1088]{1,0:T(8,128)(2,1)}, f32[8,128]{1,0:T(8,128)}) custom-call(f32[64,1088]{1,0:T(8,128)} %bitcast.35, bf16[1088,384]{1,0:T(8,128)(2,1)} %get-tuple-element.38.q, bf16[2176,384]{1,0:T(8,128)(2,1)} %bitcast.30, s32[1,1088]{1,0:T(1,128)} %get-tuple-element.39.place), custom_call_target="tpu_custom_call" | custom-call | tf_op jit(solution)/shard_map/score_grads/pallas_call | solution.py:413
  94.2 7.8 %query_grads.1 = (f32[4,136,384]{2,1,0:T(8,128)}, f32[4,136,384]{2,1,0:T(8,128)}) custom-call(s32[29]{0:T(128)} %concatenate.21.sc, bf16[2176,384]{1,0:T(8,128)(2,1)} %bitcast.31, bf16[2176,1088]{1,0:T(8,128)(2,1)} %get-tuple-element.40.g), custom_call_target="tpu_custom_call" | custom-call | tf_op jit(solution)/shard_map/query_grads/pallas_call | solution.py:433
  101.9 3.9 %all-to-all-start.3 = ((bf16[16,136,384]{2,1,0:T(8,128)(2,1)}), bf16[16,136,384]{2,1,0:T(8,128)(2,1)S(1)}, u32[]{:S(2)}, u32[]{:S(2)}) async-start(bf16[16,136,384]{2,1,0:T(8,128)(2,1)} %bitcast.34), calls=%async_computation.3 | async-start | bytes 3342336 | tf_op jit(solution)/shard_map/all_to_all | solution.py:31
  109.8 3.2 %collective-permute-done.11 = bf16[136,384]{1,0:T(8,128)(2,1)S(1)} collective-permute-done((bf16[136,384]{1,0:T(8,128)(2,1)S(1)}, bf16[136,384]{1,0:T(8,128)(2,1)S(1)}, u32[]{:S(2)}, u32[]{:S(2)}) %collective-permute-start.11) | collective-permute-done | bytes 104480 | tf_op jit(solution)/shard_map/ppermute | solution.py:43
  113.0 2.7 %collective-permute-done.10 = bf16[136,384]{1,0:T(8,128)(2,1)S(1)} collective-permute-done((bf16[136,384]{1,0:T(8,128)(2,1)S(1)}, bf16[136,384]{1,0:T(8,128)(2,1)S(1)}, u32[]{:S(2)}, u32[]{:S(2)}) %collective-permute-start.10) | collective-permute-done | bytes 104480 | tf_op jit(solution)/shard_map/ppermute | solution.py:43
  121.4 10.6 %all-to-all-done.3 = bf16[16,136,384]{2,1,0:T(8,128)(2,1)S(1)} async-done(((bf16[16,136,384]{2,1,0:T(8,128)(2,1)}), bf16[16,136,384]{2,1,0:T(8,128)(2,1)S(1)}, u32[]{:S(2)}, u32[]{:S(2)}) %all-to-all-start.3) | async-done | bytes 1671200 | tf_op jit(solution)/shard_map/all_to_all | solution.py:31
  133.2 2.4 %plane_total.1 = bf16[136,384]{1,0:T(8,128)(2,1)} custom-call(bf16[2176,384]{1,0:T(8,128)(2,1)} %bitcast.32), custom_call_target="tpu_custom_call" | custom-call | tf_op jit(solution)/shard_map/plane_total/pallas_call | solution.py:443
  136.2 2.7 %collective-permute-start.20 = (bf16[256,768]{1,0:T(8,128)(2,1)S(1)}, bf16[256,768]{1,0:T(8,128)(2,1)S(1)}, u32[]{:S(2)}, u32[]{:S(2)}) collective-permute-start(bf16[256,768]{1,0:T(8,128)(2,1)S(1)} %copy-done.12), channel_id=1, source_target_pairs={{2,0},{4,2},{6,4},{0,6},{3,1},{5,3},{7,5},{1,7},{10,8},{12,10},{14... | collective-permute-start | bytes 1179656 | tf_op jit(solution)/shard_map/ppermute | solution.py:39
  140.0 8.9 %collective-permute-done.18 = bf16[136,384]{1,0:T(8,128)(2,1)S(1)} collective-permute-done((bf16[136,384]{1,0:T(8,128)(2,1)}, bf16[136,384]{1,0:T(8,128)(2,1)S(1)}, u32[]{:S(2)}, u32[]{:S(2)}) %collective-permute-start.18) | collective-permute-done | bytes 104480 | tf_op jit(solution)/shard_map/ppermute | solution.py:39
  148.9 11.8 %collective-permute-done.17 = bf16[136,384]{1,0:T(8,128)(2,1)S(1)} collective-permute-done((bf16[136,384]{1,0:T(8,128)(2,1)}, bf16[136,384]{1,0:T(8,128)(2,1)S(1)}, u32[]{:S(2)}, u32[]{:S(2)}) %collective-permute-start.17) | collective-permute-done | bytes 104480 | tf_op jit(solution)/shard_map/ppermute | solution.py:39
  161.7 3.9 %collective-permute-done.16 = bf16[136,384]{1,0:T(8,128)(2,1)S(1)} collective-permute-done((bf16[136,384]{1,0:T(8,128)(2,1)}, bf16[136,384]{1,0:T(8,128)(2,1)S(1)}, u32[]{:S(2)}, u32[]{:S(2)}) %collective-permute-start.16) | collective-permute-done | bytes 104480 | tf_op jit(solution)/shard_map/ppermute | solution.py:39
  171.3 5.7 %hidden_units.1 = (bf16[1088,768]{1,0:T(8,128)(2,1)}, bf16[1088,768]{1,0:T(8,128)(2,1)}, bf16[192,1088]{1,0:T(8,128)(2,1)}, bf16[192,1088]{1,0:T(8,128)(2,1)}, f32[192,1088]{1,0:T(8,128)}, /*index=5*/f32[192,1088]{1,0:T(8,128)}) custom-call(bf16[256,768]{1,0:T(8,128)(2,1)} %get-tuple-element.45.refs_0_, bf16[256,768]{1,0:T(8,128)(2,1)} %copy-done.13, ...), custom_call_target="tpu_custom_call" | custom-call | tf_op jit(solution)/shard_map/hidden_units/pallas_call | solution.py:382
  178.0 5.9 %weight_grads.1 = bf16[128,1792]{1,0:T(8,128)(2,1)} custom-call(bf16[544,384]{1,0:T(8,128)(2,1)} %copy-done.4, bf16[544,384]{1,0:T(8,128)(2,1)} %copy-done.10, bf16[544,384]{1,0:T(8,128)(2,1)} %copy-done.5, bf16[544,384]{1,0:T(8,128)(2,1)} %copy-done.11, bf16[192,384]{1,0:T(8,128)(2,1)} %fusion.1.refs_4_, f32[8,128]{1,0:T(8,128)} %get-tuple-element.44.refs_5_, ...), custom_call_target="tpu_custom_call" | custom-call | tf_op jit(solution)/shard_map/weight_grads/pallas_call | solution.py:454
  183.9 16.1 %all_to_all.47 = bf16[16,8,1792]{2,1,0:T(8,128)(2,1)S(1)} all-to-all(bf16[16,8,1792]{2,1,0:T(8,128)(2,1)} %bitcast.33), channel_id=1, replica_groups=mesh['dp_0'=4,'dp_1'=4,'dp_2'=4,'dp_3'=2] {'dp_0','dp_1'}, dimensions={0} | all-to-all | bytes 917504 | tf_op jit(solution)/shard_map/all_to_all | solution.py:31
  (129 shorter events, 35.3 us)
Async XLA Ops:
  4.8 14.5 %collective-permute-start = (bf16[128,384]{1,0:T(8,128)(2,1)}, bf16[128,384]{1,0:T(8,128)(2,1)S(1)}, u32[]{:S(2)}, u32[]{:S(2)}) collective-permute-start(bf16[128,384]{1,0:T(8,128)(2,1)} %get-tuple-element.36), channel_id=1, source_target_pairs={{2,0},{4,2},{6,4},{0,6},{3,1},{5,3},{7,5},{1,7},{10,8},{12,10},{14... | collective-permute-start | bytes 294920 | tf_op jit(solution)/shard_map/ppermute | solution.py:39
  8.0 11.4 %collective-permute-start.1 = (bf16[128,384]{1,0:T(8,128)(2,1)}, bf16[128,384]{1,0:T(8,128)(2,1)S(1)}, u32[]{:S(2)}, u32[]{:S(2)}) collective-permute-start(bf16[128,384]{1,0:T(8,128)(2,1)} %get-tuple-element.36), channel_id=1, source_target_pairs={{4,0},{6,2},{0,4},{2,6},{5,1},{7,3},{1,5},{3,7},{12,8},{14,10},{8,... | collective-permute-start | bytes 294920 | tf_op jit(solution)/shard_map/ppermute | solution.py:39
  8.6 10.9 %collective-permute-start.2 = (bf16[128,384]{1,0:T(8,128)(2,1)}, bf16[128,384]{1,0:T(8,128)(2,1)S(1)}, u32[]{:S(2)}, u32[]{:S(2)}) collective-permute-start(bf16[128,384]{1,0:T(8,128)(2,1)} %get-tuple-element.36), channel_id=1, source_target_pairs={{6,0},{0,2},{2,4},{4,6},{7,1},{1,3},{3,5},{5,7},{14,8},{8,10},{10,... | collective-permute-start | bytes 294920 | tf_op jit(solution)/shard_map/ppermute | solution.py:39
  11.4 17.2 %all-to-all-start = ((bf16[16,8,1664]{2,1,0:T(8,128)(2,1)}), bf16[16,8,1664]{2,1,0:T(8,128)(2,1)S(1)}, u32[]{:S(2)}, u32[]{:S(2)}) async-start(bf16[16,8,1664]{2,1,0:T(8,128)(2,1)} %get-tuple-element.29), calls=%async_computation | async-start | bytes 851968 | tf_op jit(solution)/shard_map/all_to_all | solution.py:31
  19.5 44.4 %collective-permute-start.3 = (bf16[512,384]{1,0:T(8,128)(2,1)S(1)}, bf16[512,384]{1,0:T(8,128)(2,1)S(1)}, u32[]{:S(2)}, u32[]{:S(2)}) collective-permute-start(bf16[512,384]{1,0:T(8,128)(2,1)S(1)} %constant_dynamic-update-slice_fusion.q_own), channel_id=1, source_target_pairs={{0,1},{1,0},{2,3},{3,2},{4,5},{5,4},{6,7},{7,6},{8,9},{9,8},{10,11... | collective-permute-start | bytes 1179656 | tf_op jit(solution)/shard_map/ppermute | solution.py:27
  34.0 11.1 %collective-permute-start.4 = (bf16[16,1152]{1,0:T(8,128)(2,1)}, bf16[16,1152]{1,0:T(8,128)(2,1)S(1)}, u32[]{:S(2)}, u32[]{:S(2)}) collective-permute-start(bf16[16,1152]{1,0:T(8,128)(2,1)} %get-tuple-element.31), channel_id=1, source_target_pairs={{2,0},{4,2},{6,4},{0,6},{3,1},{5,3},{7,5},{1,7},{10,8},{12,10},{14... | collective-permute-start | bytes 110600 | tf_op jit(solution)/shard_map/ppermute | solution.py:39
  36.2 8.8 %collective-permute-start.5 = (bf16[16,1152]{1,0:T(8,128)(2,1)}, bf16[16,1152]{1,0:T(8,128)(2,1)S(1)}, u32[]{:S(2)}, u32[]{:S(2)}) collective-permute-start(bf16[16,1152]{1,0:T(8,128)(2,1)} %get-tuple-element.31), channel_id=1, source_target_pairs={{4,0},{6,2},{0,4},{2,6},{5,1},{7,3},{1,5},{3,7},{12,8},{14,10},{8,... | collective-permute-start | bytes 110600 | tf_op jit(solution)/shard_map/ppermute | solution.py:39
  37.9 7.1 %collective-permute-start.6 = (bf16[16,1152]{1,0:T(8,128)(2,1)}, bf16[16,1152]{1,0:T(8,128)(2,1)S(1)}, u32[]{:S(2)}, u32[]{:S(2)}) collective-permute-start(bf16[16,1152]{1,0:T(8,128)(2,1)} %get-tuple-element.31), channel_id=1, source_target_pairs={{6,0},{0,2},{2,4},{4,6},{7,1},{1,3},{3,5},{5,7},{14,8},{8,10},{10,... | collective-permute-start | bytes 110600 | tf_op jit(solution)/shard_map/ppermute | solution.py:39
  38.0 25.9 %all-to-all-start.1 = ((bf16[16,136,384]{2,1,0:T(8,128)(2,1)}), bf16[16,136,384]{2,1,0:T(8,128)(2,1)S(1)}, u32[]{:S(2)}, u32[]{:S(2)}) async-start(bf16[16,136,384]{2,1,0:T(8,128)(2,1)} %get-tuple-element.34), calls=%async_computation.1 | async-start | bytes 3342336 | tf_op jit(solution)/shard_map/all_to_all | solution.py:31
  45.1 18.8 %collective-permute-start.7 = (bf16[64,1152]{1,0:T(8,128)(2,1)S(1)}, bf16[64,1152]{1,0:T(8,128)(2,1)S(1)}, u32[]{:S(2)}, u32[]{:S(2)}) collective-permute-start(bf16[64,1152]{1,0:T(8,128)(2,1)S(1)} %constant_dynamic-update-slice_fusion.4.t_own.refs_8_), channel_id=1, source_target_pairs={{0,1},{1,0},{2,3},{3,2},{4,5},{5,4},{6,7},{7,6},{8,9},{9,8},{10,11... | collective-permute-start | bytes 442376 | tf_op jit(solution)/shard_map/ppermute | solution.py:27
  101.9 30.1 %all-to-all-start.3 = ((bf16[16,136,384]{2,1,0:T(8,128)(2,1)}), bf16[16,136,384]{2,1,0:T(8,128)(2,1)S(1)}, u32[]{:S(2)}, u32[]{:S(2)}) async-start(bf16[16,136,384]{2,1,0:T(8,128)(2,1)} %bitcast.34), calls=%async_computation.3 | async-start | bytes 3342336 | tf_op jit(solution)/shard_map/all_to_all | solution.py:31
  108.4 7.3 %collective-permute-start.10 = (bf16[136,384]{1,0:T(8,128)(2,1)S(1)}, bf16[136,384]{1,0:T(8,128)(2,1)S(1)}, u32[]{:S(2)}, u32[]{:S(2)}) collective-permute-start(bf16[136,384]{1,0:T(8,128)(2,1)S(1)} %get-tuple-element.57), channel_id=1, source_target_pairs={{0,4},{2,6},{4,0},{6,2},{1,5},{3,7},{5,1},{7,3},{8,12},{10,14},{12... | collective-permute-start | bytes 313352 | tf_op jit(solution)/shard_map/ppermute | solution.py:43
  109.8 7.3 %collective-permute-start.9 = (bf16[136,384]{1,0:T(8,128)(2,1)S(1)}, bf16[136,384]{1,0:T(8,128)(2,1)S(1)}, u32[]{:S(2)}, u32[]{:S(2)}) collective-permute-start(bf16[136,384]{1,0:T(8,128)(2,1)S(1)} %get-tuple-element.55), channel_id=1, source_target_pairs={{0,2},{2,4},{4,6},{6,0},{1,3},{3,5},{5,7},{7,1},{8,10},{10,12},{12... | collective-permute-start | bytes 313352 | tf_op jit(solution)/shard_map/ppermute | solution.py:43
  117.2 21.6 %collective-permute-start.14 = (bf16[136,384]{1,0:T(8,128)(2,1)S(1)}, bf16[136,384]{1,0:T(8,128)(2,1)S(1)}, u32[]{:S(2)}, u32[]{:S(2)}) collective-permute-start(bf16[136,384]{1,0:T(8,128)(2,1)S(1)} %fusion.6), channel_id=1, source_target_pairs={{6,0},{0,2},{2,4},{4,6},{7,1},{1,3},{3,5},{5,7},{14,8},{8,10},{10,... | collective-permute-start | bytes 313352 | tf_op jit(solution)/shard_map/ppermute | solution.py:39
  117.3 21.6 %collective-permute-start.13 = (bf16[136,384]{1,0:T(8,128)(2,1)S(1)}, bf16[136,384]{1,0:T(8,128)(2,1)}, u32[]{:S(2)}, u32[]{:S(2)}) collective-permute-start(bf16[136,384]{1,0:T(8,128)(2,1)S(1)} %fusion.6), channel_id=1, source_target_pairs={{4,0},{6,2},{0,4},{2,6},{5,1},{7,3},{1,5},{3,7},{12,8},{14,10},{8,... | collective-permute-start | bytes 313352 | tf_op jit(solution)/shard_map/ppermute | solution.py:39
  119.3 20.7 %collective-permute-start.12 = (bf16[136,384]{1,0:T(8,128)(2,1)S(1)}, bf16[136,384]{1,0:T(8,128)(2,1)}, u32[]{:S(2)}, u32[]{:S(2)}) collective-permute-start(bf16[136,384]{1,0:T(8,128)(2,1)S(1)} %fusion.6), channel_id=1, source_target_pairs={{2,0},{4,2},{6,4},{0,6},{3,1},{5,3},{7,5},{1,7},{10,8},{12,10},{14... | collective-permute-start | bytes 313352 | tf_op jit(solution)/shard_map/ppermute | solution.py:39
  135.6 13.3 %collective-permute-start.18 = (bf16[136,384]{1,0:T(8,128)(2,1)}, bf16[136,384]{1,0:T(8,128)(2,1)S(1)}, u32[]{:S(2)}, u32[]{:S(2)}) collective-permute-start(bf16[136,384]{1,0:T(8,128)(2,1)} %plane_total.1), channel_id=1, source_target_pairs={{6,0},{0,2},{2,4},{4,6},{7,1},{1,3},{3,5},{5,7},{14,8},{8,10},{10,... | collective-permute-start | bytes 313352 | tf_op jit(solution)/shard_map/ppermute | solution.py:39
  136.2 30.4 %collective-permute-start.20 = (bf16[256,768]{1,0:T(8,128)(2,1)S(1)}, bf16[256,768]{1,0:T(8,128)(2,1)S(1)}, u32[]{:S(2)}, u32[]{:S(2)}) collective-permute-start(bf16[256,768]{1,0:T(8,128)(2,1)S(1)} %copy-done.12), channel_id=1, source_target_pairs={{2,0},{4,2},{6,4},{0,6},{3,1},{5,3},{7,5},{1,7},{10,8},{12,10},{14... | collective-permute-start | bytes 1179656 | tf_op jit(solution)/shard_map/ppermute | solution.py:39
  138.8 28.3 %collective-permute-start.21 = (bf16[256,768]{1,0:T(8,128)(2,1)S(1)}, bf16[256,768]{1,0:T(8,128)(2,1)S(1)}, u32[]{:S(2)}, u32[]{:S(2)}) collective-permute-start(bf16[256,768]{1,0:T(8,128)(2,1)S(1)} %copy-done.12), channel_id=1, source_target_pairs={{4,0},{6,2},{0,4},{2,6},{5,1},{7,3},{1,5},{3,7},{12,8},{14,10},{8,... | collective-permute-start | bytes 1179656 | tf_op jit(solution)/shard_map/ppermute | solution.py:39
  138.8 28.4 %collective-permute-start.22 = (bf16[256,768]{1,0:T(8,128)(2,1)S(1)}, bf16[256,768]{1,0:T(8,128)(2,1)S(1)}, u32[]{:S(2)}, u32[]{:S(2)}) collective-permute-start(bf16[256,768]{1,0:T(8,128)(2,1)S(1)} %copy-done.12), channel_id=1, source_target_pairs={{6,0},{0,2},{2,4},{4,6},{7,1},{1,3},{3,5},{5,7},{14,8},{8,10},{10,... | collective-permute-start | bytes 1179656 | tf_op jit(solution)/shard_map/ppermute | solution.py:39
  140.0 27.6 %collective-permute-start.23 = (bf16[256,768]{1,0:T(8,128)(2,1)S(1)}, bf16[256,768]{1,0:T(8,128)(2,1)S(1)}, u32[]{:S(2)}, u32[]{:S(2)}) collective-permute-start(bf16[256,768]{1,0:T(8,128)(2,1)S(1)} %copy-done.12), channel_id=1, source_target_pairs={{0,1},{1,0},{2,3},{3,2},{4,5},{5,4},{6,7},{7,6},{8,9},{9,8},{10,11... | collective-permute-start | bytes 1179656 | tf_op jit(solution)/shard_map/ppermute | solution.py:27
  148.9 11.8 %collective-permute-start.17 = (bf16[136,384]{1,0:T(8,128)(2,1)}, bf16[136,384]{1,0:T(8,128)(2,1)S(1)}, u32[]{:S(2)}, u32[]{:S(2)}) collective-permute-start(bf16[136,384]{1,0:T(8,128)(2,1)} %plane_total.1), channel_id=1, source_target_pairs={{4,0},{6,2},{0,4},{2,6},{5,1},{7,3},{1,5},{3,7},{12,8},{14,10},{8,... | collective-permute-start | bytes 313352 | tf_op jit(solution)/shard_map/ppermute | solution.py:39
  165.6 11.5 %collective-permute-start.15 = (bf16[544,384]{1,0:T(8,128)(2,1)S(1)}, bf16[544,384]{1,0:T(8,128)(2,1)S(1)}, u32[]{:S(2)}, u32[]{:S(2)}) collective-permute-start(bf16[544,384]{1,0:T(8,128)(2,1)S(1)} %pad_maximum_fusion.refs_0_), channel_id=1, source_target_pairs={{0,1},{1,0},{2,3},{3,2},{4,5},{5,4},{6,7},{7,6},{8,9},{9,8},{10,11... | collective-permute-start | bytes 1253384 | tf_op jit(solution)/shard_map/ppermute | solution.py:27
  166.5 10.5 %collective-permute-start.19 = (bf16[544,384]{1,0:T(8,128)(2,1)S(1)}, bf16[544,384]{1,0:T(8,128)(2,1)S(1)}, u32[]{:S(2)}, u32[]{:S(2)}) collective-permute-start(bf16[544,384]{1,0:T(8,128)(2,1)S(1)} %pad_maximum_fusion.1.refs_2_), channel_id=1, source_target_pairs={{0,1},{1,0},{2,3},{3,2},{4,5},{5,4},{6,7},{7,6},{8,9},{9,8},{10,11... | collective-permute-start | bytes 1253384 | tf_op jit(solution)/shard_map/ppermute | solution.py:27
  (30 other events, 209.1 us)

commit v11 on v9

--- a/solution.py
+++ b/solution.py
@@ -22,10 +22,6 @@
 CHUNK = 144
 PAIR = 2 * BLOCK
 LOG2E = 1.4426950408889634
-
-
-def gelu_tanh(values):
-    return jax.nn.gelu(values, approximate=True)
 
 
 def swap_core(x):
@@ -102,6 +98,14 @@
         0.7978845608028654 * (1.0 + 3 * 0.044715 * square)
     )
     return (v * grown, slope)
+
+
+def base_kernel(q, p, w_first, w_second, emb, feats):
+    feats[:LOW] = q[...]
+    feats[LOW:] = p[...]
+    pre = jnp.dot(feats[...], w_first[...], preferred_element_type=F32)
+    hidden = gelu_parts(pre)[0].astype(BF16)
+    emb[...] = jnp.dot(hidden, w_second[...], preferred_element_type=F32).astype(BF16)
 
 
 def tail_kernel(heavy_at, arrived, base_p, pos, w_first, w_second, p_out, q_out):
@@ -262,20 +266,37 @@
         put(j, slice(LOW, BLOCK), dq[j * UNIT : (j + 1) * UNIT])
 
 
-def weight_parts(de_own, de_far, rows, hidden, slope, second, de):
+def weight_parts(de_own, de_far, hidden, slope, rows, second, de, copies):
     half = de_own.shape[0]
     de[:half] = de_own[...]
     de[half:] = de_far[...]
+    back = nt_dot(second[...], de[...])
+    copies[0].wait()
     grad_second = jnp.dot(hidden[...], de[...], preferred_element_type=F32)
-    dpre = (slope[...] * nt_dot(second[...], de[...])).astype(BF16)
+    copies[1].wait()
+    dpre = (slope[...] * back).astype(BF16)
+    copies[2].wait()
     grad_first = jnp.dot(dpre, rows[...], preferred_element_type=F32)
     return (grad_first, grad_second)
 
 
 def weights_kernel(*refs):
-    second, out, de = refs[10:]
-    first_q, second_q = weight_parts(*refs[:5], second, de)
-    grad_first, grad_second = weight_parts(*refs[5:10], second, de)
+    des, second, units, (out, de), held, sems = (
+        refs[:4],
+        refs[4],
+        refs[5:11],
+        refs[11:13],
+        refs[13:19],
+        refs[19],
+    )
+    copies = [
+        pltpu.make_async_copy(unit, hold, sems.at[k])
+        for k, (unit, hold) in enumerate(zip(units, held))
+    ]
+    for copy in copies:
+        copy.start()
+    first_q, second_q = weight_parts(*des[:2], *held[:3], second, de, copies[:3])
+    grad_first, grad_second = weight_parts(*des[2:], *held[3:], second, de, copies[3:])
     grad_first += first_q
     grad_second += second_q
     many = out.shape[0]
@@ -315,6 +336,24 @@
         ],
         name="pack_overflow",
     )(counts, where, q, p, pos)
+
+
+def base_rows(q, p, w_first, w_second):
+    width, emb_width = w_first.shape[0], w_second.shape[1]
+    rows = pl.BlockSpec((LOW, width), lambda i: (0, 0))
+
+    def whole(shape):
+        return pl.BlockSpec(shape, lambda i: (0, 0))
+
+    shapes = [(2 * LOW, emb_width), (2 * LOW, width)]
+    return pl.pallas_call(
+        base_kernel,
+        grid=(1,),
+        in_specs=[rows, rows, whole(w_first.shape), whole(w_second.shape)],
+        out_specs=[whole(shape) for shape in shapes],
+        out_shape=[jax.ShapeDtypeStruct(shape, BF16) for shape in shapes],
+        name="base_rows",
+    )(q, p, w_first, w_second)
 
 
 def tail_rows(heavy_at, arrived, base_p, pos, w_first, w_second):
@@ -342,7 +381,7 @@
         out_shape=[rows, rows, hidden, hidden, slope, slope],
         name="hidden_units",
     )(*blocks, *tails, first)
-    return ((rows_q, hidden_q, slope_q), (rows_p, hidden_p, slope_p))
+    return ((hidden_q, slope_q, rows_q), (hidden_p, slope_p, rows_p))
 
 
 def score_stats(sc, qs, ts, p, scale):
@@ -395,14 +434,17 @@
 
 
 def weight_grads(dqs, q_units, dps, p_units, second):
+    held = [pltpu.VMEM(x.shape, x.dtype) for x in (*q_units, *p_units)]
     return pl.pallas_call(
         weights_kernel,
-        in_specs=[VMEM] * 11,
+        in_specs=[VMEM] * 5 + [HBM] * 6,
         out_specs=VMEM,
-        out_shape=jax.ShapeDtypeStruct((128, 1792), BF16),
-        scratch_shapes=[pltpu.VMEM((8 * BLOCK, second.shape[1]), BF16)],
+        out_shape=jax.ShapeDtypeStruct((LOW, 1792), BF16),
+        scratch_shapes=[pltpu.VMEM((8 * BLOCK, second.shape[1]), BF16)]
+        + held
+        + [pltpu.SemaphoreType.DMA((6,))],
         name="weight_grads",
-    )(*dqs, *q_units, *dps, *p_units, second)
+    )(*dqs, *dps, second, *q_units, *p_units)
 
 
 def body(query_features, passage_features, counts, positives, w_first, w_second):
@@ -418,13 +460,7 @@
     over = over.reshape(16 * UNIT, -1)
     arrived = plane_exchange(over)
 
-    def tower(x):
-        pre = jnp.dot(x, w_first, preferred_element_type=F32)
-        hidden = gelu_tanh(pre).astype(BF16)
-        return jnp.dot(hidden, w_second, preferred_element_type=F32).astype(BF16)
-
-    feats = jnp.concatenate([query_features[:LOW], passage_features[:LOW]], axis=0)
-    base = tower(feats)
+    base, feats = base_rows(query_features, passage_features, w_first, w_second)
     qs = gathered(base[:LOW])
 
     feats = along_line(feats)

time: 202 us -> 202 us (level)
  Pallas kernels: 41.9 us -> 45.7 us
  matrix products: 7.13 us -> 4.5 us
    pallas_call x1 -> x2, Pallas kernels: 6.2 us -> 10.1 us  [the longest x1 5.94 us: weight_grads(): pl.pallas_call(weights_kernel, in_specs=[VMEM] * 5 + [HBM] * 6, out_specs...]
    dot_general x1 -> x0, matrix products: 2.62 us -> none  [tower(): return jnp.dot(hidden, w_second, preferred_element_type=F32).astype(BF16)]
    unnamed x55 -> x41, local copies, waits for them, and re-layouts: 4.78 us -> 4.6 us
  transfers between devices with their start and end apart: 31 -> 31, of which waited for: 14 -> 14; matrix products, arithmetic and copies ran while one was open for 7% -> 6% of each run, Pallas kernels for 5% -> 7%
where the time goes in v11:
time: 202 us; the launch traced here: 201 us
  waiting for transfers between devices  74.1 us (37%)
  starting transfers between devices  47.1 us (23%)
  Pallas kernels  45.7 us (23%)
  blocking collectives  11.9 us (6%)
  local copies, waits for them, and re-layouts  9.14 us (5%)
  between operations  4.64 us (2%)
  matrix products  4.5 us (2%)
  other arithmetic  4.21 us (2%)
    all_to_all x4, waiting for transfers between devices, plane_exchange(): return lax.all_to_all(x, PLANE, 0, 0, tiled=True)  38.8 us
    ppermute x15, waiting for transfers between devices, from_line(): return lax.ppermute(x, LINE, [((i + k) % 4, i) for i in range(4)])  27.1 us
    all_to_all x4, starting transfers between devices, plane_exchange(): return lax.all_to_all(x, PLANE, 0, 0, tiled=True)  24.2 us
    ppermute x15, starting transfers between devices, from_line(): return lax.ppermute(x, LINE, [((i + k) % 4, i) for i in range(4)])  18.8 us
    all_to_all x1, blocking collectives, stats_exchange(): return lax.all_to_all(x, (LINE, CORE), 0, 0, tiled=True)  11.9 us
    pallas_call x1, Pallas kernels, score_grads(): pl.pallas_call(functools.partial(grads_kernel, scale=scale), in_specs=[VM...  8.84 us
    pallas_call x1, Pallas kernels, query_grads(): pl.pallas_call(functools.partial(query_kernel, scale=scale), in_specs=[SM...  7.75 us
    ppermute x3, waiting for transfers between devices, to_line(): return lax.ppermute(x, LINE, [(i, (i + k) % 4) for i in range(4)])  7.23 us
  transfers between devices with their start and end apart: 31, of which 14 were waited for; matrix products, arithmetic and copies ran while one was open for 6% of the time, Pallas kernels for 7%

profile of v11, /device:TPU:0, one launch (start us, length us, event | category | flops | bytes accessed | tf_op | source)
XLA Modules:
  0.0 201.2 jit_solution(10300315991134178489)
XLA Ops:
  2.5 8.0 %all-to-all-start = ((bf16[16,8,1664]{2,1,0:T(8,128)(2,1)}), bf16[16,8,1664]{2,1,0:T(8,128)(2,1)S(1)}, u32[]{:S(2)}, u32[]{:S(2)}) async-start(bf16[16,8,1664]{2,1,0:T(8,128)(2,1)} %get-tuple-element.27), calls=%async_computation | async-start | bytes 851968 | tf_op jit(solution)/shard_map/all_to_all | solution.py:32
  10.5 4.1 %base_rows.1 = (bf16[256,384]{1,0:T(8,128)(2,1)}, bf16[256,768]{1,0:T(8,128)(2,1)}) custom-call(bf16[256,768]{1,0:T(8,128)(2,1)} %q.3, bf16[256,768]{1,0:T(8,128)(2,1)} %p.3, bf16[768,1536]{1,0:T(8,128)(2,1)} %w_first.3, bf16[1536,384]{1,0:T(8,128)(2,1)} %w_second.3), custom_call_target="tpu_custom_call" | custom-call | tf_op jit(solution)/shard_map/base_rows/pallas_call | solution.py:349
  17.8 2.9 %collective-permute-start.1 = (bf16[128,384]{1,0:T(8,128)(2,1)S(1)}, bf16[128,384]{1,0:T(8,128)(2,1)S(1)}, u32[]{:S(2)}, u32[]{:S(2)}) collective-permute-start(bf16[128,384]{1,0:T(8,128)(2,1)S(1)} %get-tuple-element.57), channel_id=1, source_target_pairs={{4,0},{6,2},{0,4},{2,6},{5,1},{7,3},{1,5},{3,7},{12,8},{14,10},{8,... | collective-permute-start | bytes 294920 | tf_op jit(solution)/shard_map/ppermute | solution.py:40
  22.6 2.4 %collective-permute-done.1 = bf16[128,384]{1,0:T(8,128)(2,1)S(1)} collective-permute-done((bf16[128,384]{1,0:T(8,128)(2,1)S(1)}, bf16[128,384]{1,0:T(8,128)(2,1)S(1)}, u32[]{:S(2)}, u32[]{:S(2)}) %collective-permute-start.1) | collective-permute-done | bytes 98336 | tf_op jit(solution)/shard_map/ppermute | solution.py:40
  26.3 4.7 %tail_rows.1 = (bf16[16,136,384]{2,1,0:T(8,128)(2,1)}, bf16[16,1152]{1,0:T(8,128)(2,1)}) custom-call(s32[1]{0:T(128)} %get-tuple-element.26.heavy_at, bf16[16,8,1664]{2,1,0:T(8,128)(2,1)} %copy-done.2, bf16[128,384]{1,0:T(8,128)(2,1)} %get-tuple-element.58.base_p, s32[2,128]{1,0:T(2,128)} %bitcast.37, bf16[768,1536]{1,0:T(8,128)(2,1)} %w_first.3, ...), custom_call_target="tpu_custom_call" | custom-call | tf_op jit(solution)/shard_map/tail_rows/pallas_call | solution.py:361
  31.0 2.6 %collective-permute-start.4 = (bf16[16,1152]{1,0:T(8,128)(2,1)}, bf16[16,1152]{1,0:T(8,128)(2,1)S(1)}, u32[]{:S(2)}, u32[]{:S(2)}) collective-permute-start(bf16[16,1152]{1,0:T(8,128)(2,1)} %get-tuple-element.29), channel_id=1, source_target_pairs={{2,0},{4,2},{6,4},{0,6},{3,1},{5,3},{7,5},{1,7},{10,8},{12,10},{14... | collective-permute-start | bytes 110600 | tf_op jit(solution)/shard_map/ppermute | solution.py:40
  34.8 7.1 %all-to-all-start.1 = ((bf16[16,136,384]{2,1,0:T(8,128)(2,1)}), bf16[16,136,384]{2,1,0:T(8,128)(2,1)S(1)}, u32[]{:S(2)}, u32[]{:S(2)}) async-start(bf16[16,136,384]{2,1,0:T(8,128)(2,1)} %get-tuple-element.32), calls=%async_computation.1 | async-start | bytes 3342336 | tf_op jit(solution)/shard_map/all_to_all | solution.py:32
  45.2 3.3 %convolution_convert_fusion.refs_10_ = bf16[192,768]{1,0:T(8,128)(2,1)} fusion(bf16[768,1536]{1,0:T(8,128)(2,1)} %w_first.3, s32[192]{0:T(256)S(1)} %fusion.17), kind=kOutput, calls=%fused_computation.1 | convolution fusion | flops 453427200 | bytes 2654976 | tf_op jit(solution)/shard_map/dot_general | solution.py:495
  48.6 18.4 %all-to-all-done.1 = bf16[16,136,384]{2,1,0:T(8,128)(2,1)S(1)} async-done(((bf16[16,136,384]{2,1,0:T(8,128)(2,1)}), bf16[16,136,384]{2,1,0:T(8,128)(2,1)S(1)}, u32[]{:S(2)}, u32[]{:S(2)}) %all-to-all-start.1) | async-done | bytes 1671200 | tf_op jit(solution)/shard_map/all_to_all | solution.py:32
  69.0 6.8 %score_stats.1 = (bf16[1088,384]{1,0:T(8,128)(2,1)}, s32[1,1088]{1,0:T(1,128)}, f32[64,1088]{1,0:T(8,128)}) custom-call(s32[29]{0:T(128)} %concatenate.21.sc, bf16[512,384]{1,0:T(8,128)(2,1)} %copy-done.5, bf16[512,384]{1,0:T(8,128)(2,1)} %copy-done.16, bf16[64,1152]{1,0:T(8,128)(2,1)} %copy-done.7, bf16[64,1152]{1,0:T(8,128)(2,1)} %copy-done.8, ...), custom_call_target="tpu_custom_call" | custom-call | tf_op jit(solution)/shard_map/score_stats/pallas_call | solution.py:390
  75.8 11.9 %all_to_all.44 = f32[8,8,1088]{2,1,0:T(8,128)} all-to-all(f32[8,8,1088]{2,1,0:T(8,128)} %bitcast.34), channel_id=1, replica_groups=mesh['dp_0'=4,'dp_1'=4,'dp_2'=4,'dp_3'=2] {'dp_2','dp_3'}, dimensions={0} | all-to-all | bytes 557056 | tf_op jit(solution)/shard_map/all_to_all | solution.py:36
  87.7 8.8 %score_grads.1 = (bf16[2304,384]{1,0:T(8,128)(2,1)}, bf16[2176,1088]{1,0:T(8,128)(2,1)}) custom-call(f32[64,1088]{1,0:T(8,128)} %bitcast.33, bf16[1088,384]{1,0:T(8,128)(2,1)} %get-tuple-element.35.q, bf16[2176,384]{1,0:T(8,128)(2,1)} %bitcast.29, s32[1,1088]{1,0:T(1,128)} %get-tuple-element.36.place), custom_call_target="tpu_custom_call" | custom-call | tf_op jit(solution)/shard_map/score_grads/pallas_call | solution.py:408
  96.5 7.7 %query_grads.1 = (f32[4,136,384]{2,1,0:T(8,128)}, f32[4,136,384]{2,1,0:T(8,128)}) custom-call(s32[29]{0:T(128)} %concatenate.21.sc, bf16[2176,384]{1,0:T(8,128)(2,1)} %bitcast.30, bf16[2176,1088]{1,0:T(8,128)(2,1)} %get-tuple-element.38.g), custom_call_target="tpu_custom_call" | custom-call | tf_op jit(solution)/shard_map/query_grads/pallas_call | solution.py:427
  104.3 3.9 %all-to-all-start.3 = ((bf16[16,144,384]{2,1,0:T(8,128)(2,1)}), bf16[16,144,384]{2,1,0:T(8,128)(2,1)S(1)}, u32[]{:S(2)}, u32[]{:S(2)}) async-start(bf16[16,144,384]{2,1,0:T(8,128)(2,1)} %bitcast.32), calls=%async_computation.3 | async-start | bytes 3538944 | tf_op jit(solution)/shard_map/all_to_all | solution.py:32
  112.2 3.2 %collective-permute-done.11 = bf16[136,384]{1,0:T(8,128)(2,1)S(1)} collective-permute-done((bf16[136,384]{1,0:T(8,128)(2,1)S(1)}, bf16[136,384]{1,0:T(8,128)(2,1)S(1)}, u32[]{:S(2)}, u32[]{:S(2)}) %collective-permute-start.11) | collective-permute-done | bytes 104480 | tf_op jit(solution)/shard_map/ppermute | solution.py:44
  115.4 2.7 %collective-permute-done.10 = bf16[136,384]{1,0:T(8,128)(2,1)S(1)} collective-permute-done((bf16[136,384]{1,0:T(8,128)(2,1)S(1)}, bf16[136,384]{1,0:T(8,128)(2,1)S(1)}, u32[]{:S(2)}, u32[]{:S(2)}) %collective-permute-start.10) | collective-permute-done | bytes 104480 | tf_op jit(solution)/shard_map/ppermute | solution.py:44
  123.7 11.7 %all-to-all-done.3 = bf16[16,144,384]{2,1,0:T(8,128)(2,1)S(1)} async-done(((bf16[16,144,384]{2,1,0:T(8,128)(2,1)}), bf16[16,144,384]{2,1,0:T(8,128)(2,1)S(1)}, u32[]{:S(2)}, u32[]{:S(2)}) %all-to-all-start.3) | async-done | bytes 1769504 | tf_op jit(solution)/shard_map/all_to_all | solution.py:32
  136.3 2.7 %collective-permute-start.20 = (bf16[256,768]{1,0:T(8,128)(2,1)}, bf16[256,768]{1,0:T(8,128)(2,1)S(1)}, u32[]{:S(2)}, u32[]{:S(2)}) collective-permute-start(bf16[256,768]{1,0:T(8,128)(2,1)} %get-tuple-element.41.refs_0_), channel_id=1, source_target_pairs={{2,0},{4,2},{6,4},{0,6},{3,1},{5,3},{7,5},{1,7},{10,8},{12,10},{14... | collective-permute-start | bytes 1179656 | tf_op jit(solution)/shard_map/ppermute | solution.py:40
  142.7 18.1 %collective-permute-done.17 = bf16[136,384]{1,0:T(8,128)(2,1)S(1)} collective-permute-done((bf16[136,384]{1,0:T(8,128)(2,1)S(1)}, bf16[136,384]{1,0:T(8,128)(2,1)S(1)}, u32[]{:S(2)}, u32[]{:S(2)}) %collective-permute-start.17) | collective-permute-done | bytes 104480 | tf_op jit(solution)/shard_map/ppermute | solution.py:40
  161.8 3.7 %collective-permute-done.16 = bf16[136,384]{1,0:T(8,128)(2,1)S(1)} collective-permute-done((bf16[136,384]{1,0:T(8,128)(2,1)S(1)}, bf16[136,384]{1,0:T(8,128)(2,1)S(1)}, u32[]{:S(2)}, u32[]{:S(2)}) %collective-permute-start.16) | collective-permute-done | bytes 104480 | tf_op jit(solution)/shard_map/ppermute | solution.py:40
  170.0 5.7 %hidden_units.1 = (bf16[1088,768]{1,0:T(8,128)(2,1)}, bf16[1088,768]{1,0:T(8,128)(2,1)}, bf16[192,1088]{1,0:T(8,128)(2,1)}, bf16[192,1088]{1,0:T(8,128)(2,1)}, f32[192,1088]{1,0:T(8,128)}, /*index=5*/f32[192,1088]{1,0:T(8,128)}) custom-call(bf16[256,768]{1,0:T(8,128)(2,1)} %get-tuple-element.41.refs_0_, bf16[256,768]{1,0:T(8,128)(2,1)} %copy-done.10, ...), custom_call_target="tpu_custom_call" | custom-call | tf_op jit(solution)/shard_map/hidden_units/pallas_call | solution.py:377
  176.5 5.9 %weight_grads.1 = bf16[128,1792]{1,0:T(8,128)(2,1)} custom-call(bf16[544,384]{1,0:T(8,128)(2,1)} %copy-done.3, bf16[544,384]{1,0:T(8,128)(2,1)} %copy-done.9, bf16[544,384]{1,0:T(8,128)(2,1)} %copy-done.4, bf16[544,384]{1,0:T(8,128)(2,1)} %collective-permute-done.19.refs_3_, bf16[192,384]{1,0:T(8,128)(2,1)} %fusion.1.refs_4_, ...), custom_call_target="tpu_custom_call" | custom-call | tf_op jit(solution)/shard_map/weight_grads/pallas_call | solution.py:438
  182.5 5.2 %all-to-all-start.4 = ((bf16[16,8,1792]{2,1,0:T(8,128)(2,1)}), bf16[16,8,1792]{2,1,0:T(8,128)(2,1)S(1)}, u32[]{:S(2)}, u32[]{:S(2)}) async-start(bf16[16,8,1792]{2,1,0:T(8,128)(2,1)} %bitcast.31), calls=%async_computation.4 | async-start | bytes 917504 | tf_op jit(solution)/shard_map/all_to_all | solution.py:32
  190.1 8.6 %all-to-all-done.4 = bf16[16,8,1792]{2,1,0:T(8,128)(2,1)S(1)} async-done(((bf16[16,8,1792]{2,1,0:T(8,128)(2,1)}), bf16[16,8,1792]{2,1,0:T(8,128)(2,1)S(1)}, u32[]{:S(2)}, u32[]{:S(2)}) %all-to-all-start.4) | async-done | bytes 458784 | tf_op jit(solution)/shard_map/all_to_all | solution.py:32
  (119 shorter events, 36.3 us)
Async XLA Ops:
  2.5 23.0 %all-to-all-start = ((bf16[16,8,1664]{2,1,0:T(8,128)(2,1)}), bf16[16,8,1664]{2,1,0:T(8,128)(2,1)S(1)}, u32[]{:S(2)}, u32[]{:S(2)}) async-start(bf16[16,8,1664]{2,1,0:T(8,128)(2,1)} %get-tuple-element.27), calls=%async_computation | async-start | bytes 851968 | tf_op jit(solution)/shard_map/all_to_all | solution.py:32
  16.2 6.4 %collective-permute-start.2 = (bf16[128,384]{1,0:T(8,128)(2,1)S(1)}, bf16[128,384]{1,0:T(8,128)(2,1)S(1)}, u32[]{:S(2)}, u32[]{:S(2)}) collective-permute-start(bf16[128,384]{1,0:T(8,128)(2,1)S(1)} %get-tuple-element.57), channel_id=1, source_target_pairs={{6,0},{0,2},{2,4},{4,6},{7,1},{1,3},{3,5},{5,7},{14,8},{8,10},{10,... | collective-permute-start | bytes 294920 | tf_op jit(solution)/shard_map/ppermute | solution.py:40
  17.8 7.2 %collective-permute-start.1 = (bf16[128,384]{1,0:T(8,128)(2,1)S(1)}, bf16[128,384]{1,0:T(8,128)(2,1)S(1)}, u32[]{:S(2)}, u32[]{:S(2)}) collective-permute-start(bf16[128,384]{1,0:T(8,128)(2,1)S(1)} %get-tuple-element.57), channel_id=1, source_target_pairs={{4,0},{6,2},{0,4},{2,6},{5,1},{7,3},{1,5},{3,7},{12,8},{14,10},{8,... | collective-permute-start | bytes 294920 | tf_op jit(solution)/shard_map/ppermute | solution.py:40
  25.4 41.6 %collective-permute-start.3 = (bf16[512,384]{1,0:T(8,128)(2,1)S(1)}, bf16[512,384]{1,0:T(8,128)(2,1)S(1)}, u32[]{:S(2)}, u32[]{:S(2)}) collective-permute-start(bf16[512,384]{1,0:T(8,128)(2,1)S(1)} %pad_maximum_fusion.2.q_own), channel_id=1, source_target_pairs={{0,1},{1,0},{2,3},{3,2},{4,5},{5,4},{6,7},{7,6},{8,9},{9,8},{10,11... | collective-permute-start | bytes 1179656 | tf_op jit(solution)/shard_map/ppermute | solution.py:28
  31.0 14.1 %collective-permute-start.4 = (bf16[16,1152]{1,0:T(8,128)(2,1)}, bf16[16,1152]{1,0:T(8,128)(2,1)S(1)}, u32[]{:S(2)}, u32[]{:S(2)}) collective-permute-start(bf16[16,1152]{1,0:T(8,128)(2,1)} %get-tuple-element.29), channel_id=1, source_target_pairs={{2,0},{4,2},{6,4},{0,6},{3,1},{5,3},{7,5},{1,7},{10,8},{12,10},{14... | collective-permute-start | bytes 110600 | tf_op jit(solution)/shard_map/ppermute | solution.py:40
  33.5 11.5 %collective-permute-start.5 = (bf16[16,1152]{1,0:T(8,128)(2,1)}, bf16[16,1152]{1,0:T(8,128)(2,1)S(1)}, u32[]{:S(2)}, u32[]{:S(2)}) collective-permute-start(bf16[16,1152]{1,0:T(8,128)(2,1)} %get-tuple-element.29), channel_id=1, source_target_pairs={{4,0},{6,2},{0,4},{2,6},{5,1},{7,3},{1,5},{3,7},{12,8},{14,10},{8,... | collective-permute-start | bytes 110600 | tf_op jit(solution)/shard_map/ppermute | solution.py:40
  33.9 11.2 %collective-permute-start.6 = (bf16[16,1152]{1,0:T(8,128)(2,1)}, bf16[16,1152]{1,0:T(8,128)(2,1)S(1)}, u32[]{:S(2)}, u32[]{:S(2)}) collective-permute-start(bf16[16,1152]{1,0:T(8,128)(2,1)} %get-tuple-element.29), channel_id=1, source_target_pairs={{6,0},{0,2},{2,4},{4,6},{7,1},{1,3},{3,5},{5,7},{14,8},{8,10},{10,... | collective-permute-start | bytes 110600 | tf_op jit(solution)/shard_map/ppermute | solution.py:40
  34.8 32.2 %all-to-all-start.1 = ((bf16[16,136,384]{2,1,0:T(8,128)(2,1)}), bf16[16,136,384]{2,1,0:T(8,128)(2,1)S(1)}, u32[]{:S(2)}, u32[]{:S(2)}) async-start(bf16[16,136,384]{2,1,0:T(8,128)(2,1)} %get-tuple-element.32), calls=%async_computation.1 | async-start | bytes 3342336 | tf_op jit(solution)/shard_map/all_to_all | solution.py:32
  45.1 21.8 %collective-permute-start.7 = (bf16[64,1152]{1,0:T(8,128)(2,1)S(1)}, bf16[64,1152]{1,0:T(8,128)(2,1)S(1)}, u32[]{:S(2)}, u32[]{:S(2)}) collective-permute-start(bf16[64,1152]{1,0:T(8,128)(2,1)S(1)} %constant_dynamic-update-slice_fusion.t_own.refs_8_), channel_id=1, source_target_pairs={{0,1},{1,0},{2,3},{3,2},{4,5},{5,4},{6,7},{7,6},{8,9},{9,8},{10,11... | collective-permute-start | bytes 442376 | tf_op jit(solution)/shard_map/ppermute | solution.py:28
  104.3 31.1 %all-to-all-start.3 = ((bf16[16,144,384]{2,1,0:T(8,128)(2,1)}), bf16[16,144,384]{2,1,0:T(8,128)(2,1)S(1)}, u32[]{:S(2)}, u32[]{:S(2)}) async-start(bf16[16,144,384]{2,1,0:T(8,128)(2,1)} %bitcast.32), calls=%async_computation.3 | async-start | bytes 3538944 | tf_op jit(solution)/shard_map/all_to_all | solution.py:32
  110.7 7.3 %collective-permute-start.10 = (bf16[136,384]{1,0:T(8,128)(2,1)S(1)}, bf16[136,384]{1,0:T(8,128)(2,1)S(1)}, u32[]{:S(2)}, u32[]{:S(2)}) collective-permute-start(bf16[136,384]{1,0:T(8,128)(2,1)S(1)} %get-tuple-element.53), channel_id=1, source_target_pairs={{0,4},{2,6},{4,0},{6,2},{1,5},{3,7},{5,1},{7,3},{8,12},{10,14},{12... | collective-permute-start | bytes 313352 | tf_op jit(solution)/shard_map/ppermute | solution.py:44
  112.2 7.2 %collective-permute-start.9 = (bf16[136,384]{1,0:T(8,128)(2,1)S(1)}, bf16[136,384]{1,0:T(8,128)(2,1)S(1)}, u32[]{:S(2)}, u32[]{:S(2)}) collective-permute-start(bf16[136,384]{1,0:T(8,128)(2,1)S(1)} %get-tuple-element.51), channel_id=1, source_target_pairs={{0,2},{2,4},{4,6},{6,0},{1,3},{3,5},{5,7},{7,1},{8,10},{10,12},{12... | collective-permute-start | bytes 313352 | tf_op jit(solution)/shard_map/ppermute | solution.py:44
  119.5 19.5 %collective-permute-start.14 = (bf16[136,384]{1,0:T(8,128)(2,1)S(1)}, bf16[136,384]{1,0:T(8,128)(2,1)S(1)}, u32[]{:S(2)}, u32[]{:S(2)}) collective-permute-start(bf16[136,384]{1,0:T(8,128)(2,1)S(1)} %fusion.6), channel_id=1, source_target_pairs={{6,0},{0,2},{2,4},{4,6},{7,1},{1,3},{3,5},{5,7},{14,8},{8,10},{10,... | collective-permute-start | bytes 313352 | tf_op jit(solution)/shard_map/ppermute | solution.py:40
  119.6 19.4 %collective-permute-start.13 = (bf16[136,384]{1,0:T(8,128)(2,1)S(1)}, bf16[136,384]{1,0:T(8,128)(2,1)S(1)}, u32[]{:S(2)}, u32[]{:S(2)}) collective-permute-start(bf16[136,384]{1,0:T(8,128)(2,1)S(1)} %fusion.6), channel_id=1, source_target_pairs={{4,0},{6,2},{0,4},{2,6},{5,1},{7,3},{1,5},{3,7},{12,8},{14,10},{8,... | collective-permute-start | bytes 313352 | tf_op jit(solution)/shard_map/ppermute | solution.py:40
  121.6 18.2 %collective-permute-start.12 = (bf16[136,384]{1,0:T(8,128)(2,1)S(1)}, bf16[136,384]{1,0:T(8,128)(2,1)}, u32[]{:S(2)}, u32[]{:S(2)}) collective-permute-start(bf16[136,384]{1,0:T(8,128)(2,1)S(1)} %fusion.6), channel_id=1, source_target_pairs={{2,0},{4,2},{6,4},{0,6},{3,1},{5,3},{7,5},{1,7},{10,8},{12,10},{14... | collective-permute-start | bytes 313352 | tf_op jit(solution)/shard_map/ppermute | solution.py:40
  135.7 6.1 %collective-permute-start.18 = (bf16[136,384]{1,0:T(8,128)(2,1)S(1)}, bf16[136,384]{1,0:T(8,128)(2,1)S(1)}, u32[]{:S(2)}, u32[]{:S(2)}) collective-permute-start(bf16[136,384]{1,0:T(8,128)(2,1)S(1)} %slice.85), channel_id=1, source_target_pairs={{6,0},{0,2},{2,4},{4,6},{7,1},{1,3},{3,5},{5,7},{14,8},{8,10},{10,... | collective-permute-start | bytes 313352 | tf_op jit(solution)/shard_map/ppermute | solution.py:40
  136.3 29.3 %collective-permute-start.20 = (bf16[256,768]{1,0:T(8,128)(2,1)}, bf16[256,768]{1,0:T(8,128)(2,1)S(1)}, u32[]{:S(2)}, u32[]{:S(2)}) collective-permute-start(bf16[256,768]{1,0:T(8,128)(2,1)} %get-tuple-element.41.refs_0_), channel_id=1, source_target_pairs={{2,0},{4,2},{6,4},{0,6},{3,1},{5,3},{7,5},{1,7},{10,8},{12,10},{14... | collective-permute-start | bytes 1179656 | tf_op jit(solution)/shard_map/ppermute | solution.py:40
  139.0 27.2 %collective-permute-start.21 = (bf16[256,768]{1,0:T(8,128)(2,1)}, bf16[256,768]{1,0:T(8,128)(2,1)S(1)}, u32[]{:S(2)}, u32[]{:S(2)}) collective-permute-start(bf16[256,768]{1,0:T(8,128)(2,1)} %get-tuple-element.41.refs_0_), channel_id=1, source_target_pairs={{4,0},{6,2},{0,4},{2,6},{5,1},{7,3},{1,5},{3,7},{12,8},{14,10},{8,... | collective-permute-start | bytes 1179656 | tf_op jit(solution)/shard_map/ppermute | solution.py:40
  139.0 27.3 %collective-permute-start.22 = (bf16[256,768]{1,0:T(8,128)(2,1)}, bf16[256,768]{1,0:T(8,128)(2,1)S(1)}, u32[]{:S(2)}, u32[]{:S(2)}) collective-permute-start(bf16[256,768]{1,0:T(8,128)(2,1)} %get-tuple-element.41.refs_0_), channel_id=1, source_target_pairs={{6,0},{0,2},{2,4},{4,6},{7,1},{1,3},{3,5},{5,7},{14,8},{8,10},{10,... | collective-permute-start | bytes 1179656 | tf_op jit(solution)/shard_map/ppermute | solution.py:40
  139.9 26.9 %collective-permute-start.23 = (bf16[256,768]{1,0:T(8,128)(2,1)}, bf16[256,768]{1,0:T(8,128)(2,1)S(1)}, u32[]{:S(2)}, u32[]{:S(2)}) collective-permute-start(bf16[256,768]{1,0:T(8,128)(2,1)} %get-tuple-element.41.refs_0_), channel_id=1, source_target_pairs={{0,1},{1,0},{2,3},{3,2},{4,5},{5,4},{6,7},{7,6},{8,9},{9,8},{10,11... | collective-permute-start | bytes 1179656 | tf_op jit(solution)/shard_map/ppermute | solution.py:28
  141.8 19.1 %collective-permute-start.17 = (bf16[136,384]{1,0:T(8,128)(2,1)S(1)}, bf16[136,384]{1,0:T(8,128)(2,1)S(1)}, u32[]{:S(2)}, u32[]{:S(2)}) collective-permute-start(bf16[136,384]{1,0:T(8,128)(2,1)S(1)} %slice.85), channel_id=1, source_target_pairs={{4,0},{6,2},{0,4},{2,6},{5,1},{7,3},{1,5},{3,7},{12,8},{14,10},{8,... | collective-permute-start | bytes 313352 | tf_op jit(solution)/shard_map/ppermute | solution.py:40
  165.5 10.2 %collective-permute-start.15 = (bf16[544,384]{1,0:T(8,128)(2,1)S(1)}, bf16[544,384]{1,0:T(8,128)(2,1)S(1)}, u32[]{:S(2)}, u32[]{:S(2)}) collective-permute-start(bf16[544,384]{1,0:T(8,128)(2,1)S(1)} %pad_maximum_fusion.refs_0_), channel_id=1, source_target_pairs={{0,1},{1,0},{2,3},{3,2},{4,5},{5,4},{6,7},{7,6},{8,9},{9,8},{10,11... | collective-permute-start | bytes 1253384 | tf_op jit(solution)/shard_map/ppermute | solution.py:28
  165.6 10.1 %collective-permute-start.19 = (bf16[544,384]{1,0:T(8,128)(2,1)S(1)}, bf16[544,384]{1,0:T(8,128)(2,1)}, u32[]{:S(2)}, u32[]{:S(2)}) collective-permute-start(bf16[544,384]{1,0:T(8,128)(2,1)S(1)} %pad_maximum_fusion.1.refs_2_), channel_id=1, source_target_pairs={{0,1},{1,0},{2,3},{3,2},{4,5},{5,4},{6,7},{7,6},{8,9},{9,8},{10,11... | collective-permute-start | bytes 1253384 | tf_op jit(solution)/shard_map/ppermute | solution.py:28
  182.5 16.3 %all-to-all-start.4 = ((bf16[16,8,1792]{2,1,0:T(8,128)(2,1)}), bf16[16,8,1792]{2,1,0:T(8,128)(2,1)S(1)}, u32[]{:S(2)}, u32[]{:S(2)}) async-start(bf16[16,8,1792]{2,1,0:T(8,128)(2,1)} %bitcast.31), calls=%async_computation.4 | async-start | bytes 917504 | tf_op jit(solution)/shard_map/all_to_all | solution.py:32
  (26 other events, 182.2 us)

commit v12 on v11

--- a/solution.py
+++ b/solution.py
@@ -100,12 +100,14 @@
     return (v * grown, slope)
 
 
-def base_kernel(q, p, w_first, w_second, emb, feats):
+def base_kernel(q, p, w_first, w_second, q_out, p_out, feats):
     feats[:LOW] = q[...]
     feats[LOW:] = p[...]
     pre = jnp.dot(feats[...], w_first[...], preferred_element_type=F32)
     hidden = gelu_parts(pre)[0].astype(BF16)
-    emb[...] = jnp.dot(hidden, w_second[...], preferred_element_type=F32).astype(BF16)
+    emb = jnp.dot(hidden, w_second[...], preferred_element_type=F32).astype(BF16)
+    q_out[...] = emb[:LOW]
+    p_out[...] = emb[LOW:]
 
 
 def tail_kernel(heavy_at, arrived, base_p, pos, w_first, w_second, p_out, q_out):
@@ -345,7 +347,7 @@
     def whole(shape):
         return pl.BlockSpec(shape, lambda i: (0, 0))
 
-    shapes = [(2 * LOW, emb_width), (2 * LOW, width)]
+    shapes = [(LOW, emb_width), (LOW, emb_width), (2 * LOW, width)]
     return pl.pallas_call(
         base_kernel,
         grid=(1,),
@@ -460,17 +462,22 @@
     over = over.reshape(16 * UNIT, -1)
     arrived = plane_exchange(over)
 
-    base, feats = base_rows(query_features, passage_features, w_first, w_second)
-    qs = gathered(base[:LOW])
+    q_base, p_base, feats = base_rows(query_features, passage_features, w_first, w_second)
+    q_parts = along_line(q_base)
 
     feats = along_line(feats)
     feats = feats + [swap_core(x) for x in feats]
 
     p_send, q_tail = tail_rows(
-        heavy_at, arrived.reshape(16, UNIT, -1), base[LOW:], pos, w_first, w_second
+        heavy_at, arrived.reshape(16, UNIT, -1), p_base, pos, w_first, w_second
     )
     p_all = plane_exchange(p_send.reshape(16 * BLOCK, emb_width))
-    ts = gathered(q_tail)
+    t_parts = along_line(q_tail)
+    t_own = jnp.concatenate(t_parts, axis=0)
+    ts = (t_own, swap_core(t_own))
+    q_parts, _ = lax.optimization_barrier((q_parts, t_parts[1]))
+    q_own = jnp.concatenate(q_parts, axis=0)
+    qs = (q_own, swap_core(q_own))
 
     late_counts, group, _ = lax.optimization_barrier((counts, group, q_tail))
     heavy = (late_counts > LOW).astype(jnp.int32)

time: 202 us -> 195 us (0.965)
  waiting for transfers between devices: 74.1 us -> 70.5 us
  starting transfers between devices: 47.1 us -> 44.2 us
    all_to_all x4, waiting for transfers between devices: 38.8 us -> 33 us  [plane_exchange(): return lax.all_to_all(x, PLANE, 0, 0, tiled=True)]
    ppermute x15, waiting for transfers between devices: 27.1 us -> 29.5 us  [from_line(): return lax.ppermute(x, LINE, [((i + k) % 4, i) for i in range(4)])]
    ppermute x15, starting transfers between devices: 18.8 us -> 16.6 us  [from_line(): return lax.ppermute(x, LINE, [((i + k) % 4, i) for i in range(4)])]
    unnamed x41 -> x46, local copies, waits for them, and re-layouts: 4.6 us -> 5.33 us
  transfers between devices with their start and end apart: 31 -> 31, of which waited for: 14 -> 13; matrix products, arithmetic and copies ran while one was open for 6% -> 6% of each run, Pallas kernels for 7% -> 7%
where the time goes in v12:
time: 195 us; the launch traced here: 194 us
  waiting for transfers between devices  70.5 us (36%)
  Pallas kernels  45.6 us (23%)
  starting transfers between devices  44.2 us (23%)
  blocking collectives  11.9 us (6%)
  local copies, waits for them, and re-layouts  8.32 us (4%)
  between operations  4.7 us (2%)
  matrix products  4.51 us (2%)
  other arithmetic  4.15 us (2%)
    all_to_all x4, waiting for transfers between devices, plane_exchange(): return lax.all_to_all(x, PLANE, 0, 0, tiled=True)  33 us
    ppermute x15, waiting for transfers between devices, from_line(): return lax.ppermute(x, LINE, [((i + k) % 4, i) for i in range(4)])  29.5 us
    all_to_all x4, starting transfers between devices, plane_exchange(): return lax.all_to_all(x, PLANE, 0, 0, tiled=True)  23.5 us
    ppermute x15, starting transfers between devices, from_line(): return lax.ppermute(x, LINE, [((i + k) % 4, i) for i in range(4)])  16.6 us
    all_to_all x1, blocking collectives, stats_exchange(): return lax.all_to_all(x, (LINE, CORE), 0, 0, tiled=True)  11.9 us
    pallas_call x1, Pallas kernels, score_grads(): pl.pallas_call(functools.partial(grads_kernel, scale=scale), in_specs=[VM...  8.84 us
    pallas_call x1, Pallas kernels, query_grads(): pl.pallas_call(functools.partial(query_kernel, scale=scale), in_specs=[SM...  7.74 us
    ppermute x3, waiting for transfers between devices, to_line(): return lax.ppermute(x, LINE, [(i, (i + k) % 4) for i in range(4)])  7.04 us
  transfers between devices with their start and end apart: 31, of which 13 were waited for; matrix products, arithmetic and copies ran while one was open for 6% of the time, Pallas kernels for 7%

profile of v12, /device:TPU:0, one launch (start us, length us, event | category | flops | bytes accessed | tf_op | source)
XLA Modules:
  0.0 193.9 jit_solution(13617678512947927884)
XLA Ops:
  2.5 8.0 %all-to-all-start = ((bf16[16,8,1664]{2,1,0:T(8,128)(2,1)}), bf16[16,8,1664]{2,1,0:T(8,128)(2,1)S(1)}, u32[]{:S(2)}, u32[]{:S(2)}) async-start(bf16[16,8,1664]{2,1,0:T(8,128)(2,1)} %get-tuple-element.32), calls=%async_computation | async-start | bytes 851968 | tf_op jit(solution)/shard_map/all_to_all | solution.py:32
  10.6 4.2 %base_rows.1 = (bf16[128,384]{1,0:T(8,128)(2,1)}, bf16[128,384]{1,0:T(8,128)(2,1)}, bf16[256,768]{1,0:T(8,128)(2,1)}) custom-call(bf16[256,768]{1,0:T(8,128)(2,1)} %q.3, bf16[256,768]{1,0:T(8,128)(2,1)} %p.3, bf16[768,1536]{1,0:T(8,128)(2,1)} %w_first.3, bf16[1536,384]{1,0:T(8,128)(2,1)} %w_second.3), custom_call_target="tpu_custom_call" | custom-call | tf_op jit(solution)/shard_map/base_rows/pallas_call | solution.py:351
  14.8 3.0 %collective-permute-start = (bf16[128,384]{1,0:T(8,128)(2,1)}, bf16[128,384]{1,0:T(8,128)(2,1)S(1)}, u32[]{:S(2)}, u32[]{:S(2)}) collective-permute-start(bf16[128,384]{1,0:T(8,128)(2,1)} %get-tuple-element.38), channel_id=1, source_target_pairs={{2,0},{4,2},{6,4},{0,6},{3,1},{5,3},{7,5},{1,7},{10,8},{12,10},{14... | collective-permute-start | bytes 294920 | tf_op jit(solution)/shard_map/ppermute | solution.py:40
  21.5 4.6 %tail_rows.1 = (bf16[16,136,384]{2,1,0:T(8,128)(2,1)}, bf16[16,1152]{1,0:T(8,128)(2,1)}) custom-call(s32[1]{0:T(128)} %get-tuple-element.31.heavy_at, bf16[16,8,1664]{2,1,0:T(8,128)(2,1)} %copy-done.2, bf16[128,384]{1,0:T(8,128)(2,1)} %get-tuple-element.33.base_p, s32[2,128]{1,0:T(2,128)} %bitcast.37, bf16[768,1536]{1,0:T(8,128)(2,1)} %w_first.3, ...), custom_call_target="tpu_custom_call" | custom-call | tf_op jit(solution)/shard_map/tail_rows/pallas_call | solution.py:363
  26.1 3.0 %collective-permute-start.3 = (bf16[16,1152]{1,0:T(8,128)(2,1)}, bf16[16,1152]{1,0:T(8,128)(2,1)S(1)}, u32[]{:S(2)}, u32[]{:S(2)}) collective-permute-start(bf16[16,1152]{1,0:T(8,128)(2,1)} %get-tuple-element.34), channel_id=1, source_target_pairs={{2,0},{4,2},{6,4},{0,6},{3,1},{5,3},{7,5},{1,7},{10,8},{12,10},{14... | collective-permute-start | bytes 110600 | tf_op jit(solution)/shard_map/ppermute | solution.py:40
  31.0 6.4 %all-to-all-start.1 = ((bf16[16,136,384]{2,1,0:T(8,128)(2,1)}), bf16[16,136,384]{2,1,0:T(8,128)(2,1)S(1)}, u32[]{:S(2)}, u32[]{:S(2)}) async-start(bf16[16,136,384]{2,1,0:T(8,128)(2,1)} %get-tuple-element.42), calls=%async_computation.1 | async-start | bytes 3342336 | tf_op jit(solution)/shard_map/all_to_all | solution.py:32
  40.5 4.9 %collective-permute-done.6 = bf16[16,1152]{1,0:T(8,128)(2,1)S(1)} collective-permute-done((bf16[16,1152]{1,0:T(8,128)(2,1)S(1)}, bf16[16,1152]{1,0:T(8,128)(2,1)S(1)}, u32[]{:S(2)}, u32[]{:S(2)}) %collective-permute-start.6) | collective-permute-done | bytes 36896 | tf_op jit(solution)/shard_map/ppermute | solution.py:40
  45.5 3.3 %convolution_convert_fusion.refs_10_ = bf16[192,768]{1,0:T(8,128)(2,1)} fusion(bf16[768,1536]{1,0:T(8,128)(2,1)} %w_first.3, s32[192]{0:T(256)S(1)} %fusion.17), kind=kOutput, calls=%fused_computation.1 | convolution fusion | flops 453427200 | bytes 2654976 | tf_op jit(solution)/shard_map/dot_general | solution.py:502
  48.8 11.1 %all-to-all-done.1 = bf16[16,136,384]{2,1,0:T(8,128)(2,1)S(1)} async-done(((bf16[16,136,384]{2,1,0:T(8,128)(2,1)}), bf16[16,136,384]{2,1,0:T(8,128)(2,1)S(1)}, u32[]{:S(2)}, u32[]{:S(2)}) %all-to-all-start.1) | async-done | bytes 1671200 | tf_op jit(solution)/shard_map/all_to_all | solution.py:32
  61.9 6.8 %score_stats.1 = (bf16[1088,384]{1,0:T(8,128)(2,1)}, s32[1,1088]{1,0:T(1,128)}, f32[64,1088]{1,0:T(8,128)}) custom-call(s32[29]{0:T(128)} %concatenate.21.sc, bf16[512,384]{1,0:T(8,128)(2,1)} %copy-done.7, bf16[512,384]{1,0:T(8,128)(2,1)} %copy-done.16, bf16[64,1152]{1,0:T(8,128)(2,1)} %copy-done.6, bf16[64,1152]{1,0:T(8,128)(2,1)} %copy-done.8, ...), custom_call_target="tpu_custom_call" | custom-call | tf_op jit(solution)/shard_map/score_stats/pallas_call | solution.py:392
  68.7 11.9 %all_to_all.44 = f32[8,8,1088]{2,1,0:T(8,128)} all-to-all(f32[8,8,1088]{2,1,0:T(8,128)} %bitcast.34), channel_id=1, replica_groups=mesh['dp_0'=4,'dp_1'=4,'dp_2'=4,'dp_3'=2] {'dp_2','dp_3'}, dimensions={0} | all-to-all | bytes 557056 | tf_op jit(solution)/shard_map/all_to_all | solution.py:36
  80.6 8.8 %score_grads.1 = (bf16[2304,384]{1,0:T(8,128)(2,1)}, bf16[2176,1088]{1,0:T(8,128)(2,1)}) custom-call(f32[64,1088]{1,0:T(8,128)} %bitcast.33, bf16[1088,384]{1,0:T(8,128)(2,1)} %get-tuple-element.45.q, bf16[2176,384]{1,0:T(8,128)(2,1)} %bitcast.29, s32[1,1088]{1,0:T(1,128)} %get-tuple-element.46.place), custom_call_target="tpu_custom_call" | custom-call | tf_op jit(solution)/shard_map/score_grads/pallas_call | solution.py:410
  89.4 7.7 %query_grads.1 = (f32[4,136,384]{2,1,0:T(8,128)}, f32[4,136,384]{2,1,0:T(8,128)}) custom-call(s32[29]{0:T(128)} %concatenate.21.sc, bf16[2176,384]{1,0:T(8,128)(2,1)} %bitcast.30, bf16[2176,1088]{1,0:T(8,128)(2,1)} %get-tuple-element.48.g), custom_call_target="tpu_custom_call" | custom-call | tf_op jit(solution)/shard_map/query_grads/pallas_call | solution.py:429
  97.2 4.4 %all-to-all-start.3 = ((bf16[16,144,384]{2,1,0:T(8,128)(2,1)}), bf16[16,144,384]{2,1,0:T(8,128)(2,1)S(1)}, u32[]{:S(2)}, u32[]{:S(2)}) async-start(bf16[16,144,384]{2,1,0:T(8,128)(2,1)} %bitcast.32), calls=%async_computation.3 | async-start | bytes 3538944 | tf_op jit(solution)/shard_map/all_to_all | solution.py:32
  105.6 3.2 %collective-permute-done.11 = bf16[136,384]{1,0:T(8,128)(2,1)S(1)} collective-permute-done((bf16[136,384]{1,0:T(8,128)(2,1)S(1)}, bf16[136,384]{1,0:T(8,128)(2,1)S(1)}, u32[]{:S(2)}, u32[]{:S(2)}) %collective-permute-start.11) | collective-permute-done | bytes 104480 | tf_op jit(solution)/shard_map/ppermute | solution.py:44
  108.8 2.7 %collective-permute-done.10 = bf16[136,384]{1,0:T(8,128)(2,1)S(1)} collective-permute-done((bf16[136,384]{1,0:T(8,128)(2,1)S(1)}, bf16[136,384]{1,0:T(8,128)(2,1)S(1)}, u32[]{:S(2)}, u32[]{:S(2)}) %collective-permute-start.10) | collective-permute-done | bytes 104480 | tf_op jit(solution)/shard_map/ppermute | solution.py:44
  116.9 11.9 %all-to-all-done.3 = bf16[16,144,384]{2,1,0:T(8,128)(2,1)S(1)} async-done(((bf16[16,144,384]{2,1,0:T(8,128)(2,1)}), bf16[16,144,384]{2,1,0:T(8,128)(2,1)S(1)}, u32[]{:S(2)}, u32[]{:S(2)}) %all-to-all-start.3) | async-done | bytes 1769504 | tf_op jit(solution)/shard_map/all_to_all | solution.py:32
  133.3 8.4 %collective-permute-done.18 = bf16[136,384]{1,0:T(8,128)(2,1)S(1)} collective-permute-done((bf16[136,384]{1,0:T(8,128)(2,1)S(1)}, bf16[136,384]{1,0:T(8,128)(2,1)S(1)}, u32[]{:S(2)}, u32[]{:S(2)}) %collective-permute-start.18) | collective-permute-done | bytes 104480 | tf_op jit(solution)/shard_map/ppermute | solution.py:40
  141.7 12.4 %collective-permute-done.17 = bf16[136,384]{1,0:T(8,128)(2,1)S(1)} collective-permute-done((bf16[136,384]{1,0:T(8,128)(2,1)S(1)}, bf16[136,384]{1,0:T(8,128)(2,1)S(1)}, u32[]{:S(2)}, u32[]{:S(2)}) %collective-permute-start.17) | collective-permute-done | bytes 104480 | tf_op jit(solution)/shard_map/ppermute | solution.py:40
  155.1 3.7 %collective-permute-done.16 = bf16[136,384]{1,0:T(8,128)(2,1)S(1)} collective-permute-done((bf16[136,384]{1,0:T(8,128)(2,1)S(1)}, bf16[136,384]{1,0:T(8,128)(2,1)S(1)}, u32[]{:S(2)}, u32[]{:S(2)}) %collective-permute-start.16) | collective-permute-done | bytes 104480 | tf_op jit(solution)/shard_map/ppermute | solution.py:40
  163.2 5.6 %hidden_units.1 = (bf16[1088,768]{1,0:T(8,128)(2,1)}, bf16[1088,768]{1,0:T(8,128)(2,1)}, bf16[192,1088]{1,0:T(8,128)(2,1)}, bf16[192,1088]{1,0:T(8,128)(2,1)}, f32[192,1088]{1,0:T(8,128)}, /*index=5*/f32[192,1088]{1,0:T(8,128)}) custom-call(bf16[256,768]{1,0:T(8,128)(2,1)} %get-tuple-element.51.refs_0_, bf16[256,768]{1,0:T(8,128)(2,1)} %copy-done.10, ...), custom_call_target="tpu_custom_call" | custom-call | tf_op jit(solution)/shard_map/hidden_units/pallas_call | solution.py:379
  169.7 5.9 %weight_grads.1 = bf16[128,1792]{1,0:T(8,128)(2,1)} custom-call(bf16[544,384]{1,0:T(8,128)(2,1)} %copy-done.3, bf16[544,384]{1,0:T(8,128)(2,1)} %copy-done.9, bf16[544,384]{1,0:T(8,128)(2,1)} %copy-done.4, bf16[544,384]{1,0:T(8,128)(2,1)} %collective-permute-done.19.refs_3_, bf16[192,384]{1,0:T(8,128)(2,1)} %fusion.1.refs_4_, ...), custom_call_target="tpu_custom_call" | custom-call | tf_op jit(solution)/shard_map/weight_grads/pallas_call | solution.py:440
  175.6 4.7 %all-to-all-start.4 = ((bf16[16,8,1792]{2,1,0:T(8,128)(2,1)}), bf16[16,8,1792]{2,1,0:T(8,128)(2,1)S(1)}, u32[]{:S(2)}, u32[]{:S(2)}) async-start(bf16[16,8,1792]{2,1,0:T(8,128)(2,1)} %bitcast.31), calls=%async_computation.4 | async-start | bytes 917504 | tf_op jit(solution)/shard_map/all_to_all | solution.py:32
  182.8 8.6 %all-to-all-done.4 = bf16[16,8,1792]{2,1,0:T(8,128)(2,1)S(1)} async-done(((bf16[16,8,1792]{2,1,0:T(8,128)(2,1)}), bf16[16,8,1792]{2,1,0:T(8,128)(2,1)S(1)}, u32[]{:S(2)}, u32[]{:S(2)}) %all-to-all-start.4) | async-done | bytes 458784 | tf_op jit(solution)/shard_map/all_to_all | solution.py:32
  (123 shorter events, 33.8 us)
Async XLA Ops:
  2.5 18.2 %all-to-all-start = ((bf16[16,8,1664]{2,1,0:T(8,128)(2,1)}), bf16[16,8,1664]{2,1,0:T(8,128)(2,1)S(1)}, u32[]{:S(2)}, u32[]{:S(2)}) async-start(bf16[16,8,1664]{2,1,0:T(8,128)(2,1)} %get-tuple-element.32), calls=%async_computation | async-start | bytes 851968 | tf_op jit(solution)/shard_map/all_to_all | solution.py:32
  14.8 25.5 %collective-permute-start = (bf16[128,384]{1,0:T(8,128)(2,1)}, bf16[128,384]{1,0:T(8,128)(2,1)S(1)}, u32[]{:S(2)}, u32[]{:S(2)}) collective-permute-start(bf16[128,384]{1,0:T(8,128)(2,1)} %get-tuple-element.38), channel_id=1, source_target_pairs={{2,0},{4,2},{6,4},{0,6},{3,1},{5,3},{7,5},{1,7},{10,8},{12,10},{14... | collective-permute-start | bytes 294920 | tf_op jit(solution)/shard_map/ppermute | solution.py:40
  17.8 22.5 %collective-permute-start.1 = (bf16[128,384]{1,0:T(8,128)(2,1)}, bf16[128,384]{1,0:T(8,128)(2,1)S(1)}, u32[]{:S(2)}, u32[]{:S(2)}) collective-permute-start(bf16[128,384]{1,0:T(8,128)(2,1)} %get-tuple-element.38), channel_id=1, source_target_pairs={{4,0},{6,2},{0,4},{2,6},{5,1},{7,3},{1,5},{3,7},{12,8},{14,10},{8,... | collective-permute-start | bytes 294920 | tf_op jit(solution)/shard_map/ppermute | solution.py:40
  18.4 21.8 %collective-permute-start.2 = (bf16[128,384]{1,0:T(8,128)(2,1)}, bf16[128,384]{1,0:T(8,128)(2,1)S(1)}, u32[]{:S(2)}, u32[]{:S(2)}) collective-permute-start(bf16[128,384]{1,0:T(8,128)(2,1)} %get-tuple-element.38), channel_id=1, source_target_pairs={{6,0},{0,2},{2,4},{4,6},{7,1},{1,3},{3,5},{5,7},{14,8},{8,10},{10,... | collective-permute-start | bytes 294920 | tf_op jit(solution)/shard_map/ppermute | solution.py:40
  26.1 14.2 %collective-permute-start.3 = (bf16[16,1152]{1,0:T(8,128)(2,1)}, bf16[16,1152]{1,0:T(8,128)(2,1)S(1)}, u32[]{:S(2)}, u32[]{:S(2)}) collective-permute-start(bf16[16,1152]{1,0:T(8,128)(2,1)} %get-tuple-element.34), channel_id=1, source_target_pairs={{2,0},{4,2},{6,4},{0,6},{3,1},{5,3},{7,5},{1,7},{10,8},{12,10},{14... | collective-permute-start | bytes 110600 | tf_op jit(solution)/shard_map/ppermute | solution.py:40
  29.9 10.6 %collective-permute-start.5 = (bf16[16,1152]{1,0:T(8,128)(2,1)}, bf16[16,1152]{1,0:T(8,128)(2,1)S(1)}, u32[]{:S(2)}, u32[]{:S(2)}) collective-permute-start(bf16[16,1152]{1,0:T(8,128)(2,1)} %get-tuple-element.34), channel_id=1, source_target_pairs={{4,0},{6,2},{0,4},{2,6},{5,1},{7,3},{1,5},{3,7},{12,8},{14,10},{8,... | collective-permute-start | bytes 110600 | tf_op jit(solution)/shard_map/ppermute | solution.py:40
  31.0 28.9 %all-to-all-start.1 = ((bf16[16,136,384]{2,1,0:T(8,128)(2,1)}), bf16[16,136,384]{2,1,0:T(8,128)(2,1)S(1)}, u32[]{:S(2)}, u32[]{:S(2)}) async-start(bf16[16,136,384]{2,1,0:T(8,128)(2,1)} %get-tuple-element.42), calls=%async_computation.1 | async-start | bytes 3342336 | tf_op jit(solution)/shard_map/all_to_all | solution.py:32
  40.4 19.6 %collective-permute-start.4 = (bf16[512,384]{1,0:T(8,128)(2,1)S(1)}, bf16[512,384]{1,0:T(8,128)(2,1)S(1)}, u32[]{:S(2)}, u32[]{:S(2)}) collective-permute-start(bf16[512,384]{1,0:T(8,128)(2,1)S(1)} %constant_dynamic-update-slice_fusion.q_own), channel_id=1, source_target_pairs={{0,1},{1,0},{2,3},{3,2},{4,5},{5,4},{6,7},{7,6},{8,9},{9,8},{10,11... | collective-permute-start | bytes 1179656 | tf_op jit(solution)/shard_map/ppermute | solution.py:28
  45.4 14.6 %collective-permute-start.7 = (bf16[64,1152]{1,0:T(8,128)(2,1)S(1)}, bf16[64,1152]{1,0:T(8,128)(2,1)S(1)}, u32[]{:S(2)}, u32[]{:S(2)}) collective-permute-start(bf16[64,1152]{1,0:T(8,128)(2,1)S(1)} %constant_dynamic-update-slice_fusion.4.t_own.refs_8_), channel_id=1, source_target_pairs={{0,1},{1,0},{2,3},{3,2},{4,5},{5,4},{6,7},{7,6},{8,9},{9,8},{10,11... | collective-permute-start | bytes 442376 | tf_op jit(solution)/shard_map/ppermute | solution.py:28
  97.2 31.7 %all-to-all-start.3 = ((bf16[16,144,384]{2,1,0:T(8,128)(2,1)}), bf16[16,144,384]{2,1,0:T(8,128)(2,1)S(1)}, u32[]{:S(2)}, u32[]{:S(2)}) async-start(bf16[16,144,384]{2,1,0:T(8,128)(2,1)} %bitcast.32), calls=%async_computation.3 | async-start | bytes 3538944 | tf_op jit(solution)/shard_map/all_to_all | solution.py:32
  104.1 7.3 %collective-permute-start.10 = (bf16[136,384]{1,0:T(8,128)(2,1)S(1)}, bf16[136,384]{1,0:T(8,128)(2,1)S(1)}, u32[]{:S(2)}, u32[]{:S(2)}) collective-permute-start(bf16[136,384]{1,0:T(8,128)(2,1)S(1)} %get-tuple-element.63), channel_id=1, source_target_pairs={{0,4},{2,6},{4,0},{6,2},{1,5},{3,7},{5,1},{7,3},{8,12},{10,14},{12... | collective-permute-start | bytes 313352 | tf_op jit(solution)/shard_map/ppermute | solution.py:44
  105.6 7.0 %collective-permute-start.9 = (bf16[136,384]{1,0:T(8,128)(2,1)S(1)}, bf16[136,384]{1,0:T(8,128)(2,1)S(1)}, u32[]{:S(2)}, u32[]{:S(2)}) collective-permute-start(bf16[136,384]{1,0:T(8,128)(2,1)S(1)} %get-tuple-element.61), channel_id=1, source_target_pairs={{0,2},{2,4},{4,6},{6,0},{1,3},{3,5},{5,7},{7,1},{8,10},{10,12},{12... | collective-permute-start | bytes 313352 | tf_op jit(solution)/shard_map/ppermute | solution.py:44
  112.7 19.7 %collective-permute-start.14 = (bf16[136,384]{1,0:T(8,128)(2,1)S(1)}, bf16[136,384]{1,0:T(8,128)(2,1)S(1)}, u32[]{:S(2)}, u32[]{:S(2)}) collective-permute-start(bf16[136,384]{1,0:T(8,128)(2,1)S(1)} %fusion.6), channel_id=1, source_target_pairs={{6,0},{0,2},{2,4},{4,6},{7,1},{1,3},{3,5},{5,7},{14,8},{8,10},{10,... | collective-permute-start | bytes 313352 | tf_op jit(solution)/shard_map/ppermute | solution.py:40
  112.8 19.6 %collective-permute-start.13 = (bf16[136,384]{1,0:T(8,128)(2,1)S(1)}, bf16[136,384]{1,0:T(8,128)(2,1)S(1)}, u32[]{:S(2)}, u32[]{:S(2)}) collective-permute-start(bf16[136,384]{1,0:T(8,128)(2,1)S(1)} %fusion.6), channel_id=1, source_target_pairs={{4,0},{6,2},{0,4},{2,6},{5,1},{7,3},{1,5},{3,7},{12,8},{14,10},{8,... | collective-permute-start | bytes 313352 | tf_op jit(solution)/shard_map/ppermute | solution.py:40
  114.8 18.5 %collective-permute-start.12 = (bf16[136,384]{1,0:T(8,128)(2,1)S(1)}, bf16[136,384]{1,0:T(8,128)(2,1)}, u32[]{:S(2)}, u32[]{:S(2)}) collective-permute-start(bf16[136,384]{1,0:T(8,128)(2,1)S(1)} %fusion.6), channel_id=1, source_target_pairs={{2,0},{4,2},{6,4},{0,6},{3,1},{5,3},{7,5},{1,7},{10,8},{12,10},{14... | collective-permute-start | bytes 313352 | tf_op jit(solution)/shard_map/ppermute | solution.py:40
  129.1 12.6 %collective-permute-start.18 = (bf16[136,384]{1,0:T(8,128)(2,1)S(1)}, bf16[136,384]{1,0:T(8,128)(2,1)S(1)}, u32[]{:S(2)}, u32[]{:S(2)}) collective-permute-start(bf16[136,384]{1,0:T(8,128)(2,1)S(1)} %slice.77), channel_id=1, source_target_pairs={{6,0},{0,2},{2,4},{4,6},{7,1},{1,3},{3,5},{5,7},{14,8},{8,10},{10,... | collective-permute-start | bytes 313352 | tf_op jit(solution)/shard_map/ppermute | solution.py:40
  129.7 29.1 %collective-permute-start.20 = (bf16[256,768]{1,0:T(8,128)(2,1)}, bf16[256,768]{1,0:T(8,128)(2,1)S(1)}, u32[]{:S(2)}, u32[]{:S(2)}) collective-permute-start(bf16[256,768]{1,0:T(8,128)(2,1)} %get-tuple-element.51.refs_0_), channel_id=1, source_target_pairs={{2,0},{4,2},{6,4},{0,6},{3,1},{5,3},{7,5},{1,7},{10,8},{12,10},{14... | collective-permute-start | bytes 1179656 | tf_op jit(solution)/shard_map/ppermute | solution.py:40
  132.4 27.1 %collective-permute-start.21 = (bf16[256,768]{1,0:T(8,128)(2,1)}, bf16[256,768]{1,0:T(8,128)(2,1)S(1)}, u32[]{:S(2)}, u32[]{:S(2)}) collective-permute-start(bf16[256,768]{1,0:T(8,128)(2,1)} %get-tuple-element.51.refs_0_), channel_id=1, source_target_pairs={{4,0},{6,2},{0,4},{2,6},{5,1},{7,3},{1,5},{3,7},{12,8},{14,10},{8,... | collective-permute-start | bytes 1179656 | tf_op jit(solution)/shard_map/ppermute | solution.py:40
  132.4 27.2 %collective-permute-start.22 = (bf16[256,768]{1,0:T(8,128)(2,1)}, bf16[256,768]{1,0:T(8,128)(2,1)S(1)}, u32[]{:S(2)}, u32[]{:S(2)}) collective-permute-start(bf16[256,768]{1,0:T(8,128)(2,1)} %get-tuple-element.51.refs_0_), channel_id=1, source_target_pairs={{6,0},{0,2},{2,4},{4,6},{7,1},{1,3},{3,5},{5,7},{14,8},{8,10},{10,... | collective-permute-start | bytes 1179656 | tf_op jit(solution)/shard_map/ppermute | solution.py:40
  133.3 26.7 %collective-permute-start.23 = (bf16[256,768]{1,0:T(8,128)(2,1)}, bf16[256,768]{1,0:T(8,128)(2,1)S(1)}, u32[]{:S(2)}, u32[]{:S(2)}) collective-permute-start(bf16[256,768]{1,0:T(8,128)(2,1)} %get-tuple-element.51.refs_0_), channel_id=1, source_target_pairs={{0,1},{1,0},{2,3},{3,2},{4,5},{5,4},{6,7},{7,6},{8,9},{9,8},{10,11... | collective-permute-start | bytes 1179656 | tf_op jit(solution)/shard_map/ppermute | solution.py:28
  141.7 12.4 %collective-permute-start.17 = (bf16[136,384]{1,0:T(8,128)(2,1)S(1)}, bf16[136,384]{1,0:T(8,128)(2,1)S(1)}, u32[]{:S(2)}, u32[]{:S(2)}) collective-permute-start(bf16[136,384]{1,0:T(8,128)(2,1)S(1)} %slice.77), channel_id=1, source_target_pairs={{4,0},{6,2},{0,4},{2,6},{5,1},{7,3},{1,5},{3,7},{12,8},{14,10},{8,... | collective-permute-start | bytes 313352 | tf_op jit(solution)/shard_map/ppermute | solution.py:40
  158.8 10.1 %collective-permute-start.15 = (bf16[544,384]{1,0:T(8,128)(2,1)S(1)}, bf16[544,384]{1,0:T(8,128)(2,1)S(1)}, u32[]{:S(2)}, u32[]{:S(2)}) collective-permute-start(bf16[544,384]{1,0:T(8,128)(2,1)S(1)} %pad_maximum_fusion.refs_0_), channel_id=1, source_target_pairs={{0,1},{1,0},{2,3},{3,2},{4,5},{5,4},{6,7},{7,6},{8,9},{9,8},{10,11... | collective-permute-start | bytes 1253384 | tf_op jit(solution)/shard_map/ppermute | solution.py:28
  158.9 10.0 %collective-permute-start.19 = (bf16[544,384]{1,0:T(8,128)(2,1)S(1)}, bf16[544,384]{1,0:T(8,128)(2,1)}, u32[]{:S(2)}, u32[]{:S(2)}) collective-permute-start(bf16[544,384]{1,0:T(8,128)(2,1)S(1)} %pad_maximum_fusion.1.refs_2_), channel_id=1, source_target_pairs={{0,1},{1,0},{2,3},{3,2},{4,5},{5,4},{6,7},{7,6},{8,9},{9,8},{10,11... | collective-permute-start | bytes 1253384 | tf_op jit(solution)/shard_map/ppermute | solution.py:28
  175.6 15.8 %all-to-all-start.4 = ((bf16[16,8,1792]{2,1,0:T(8,128)(2,1)}), bf16[16,8,1792]{2,1,0:T(8,128)(2,1)S(1)}, u32[]{:S(2)}, u32[]{:S(2)}) async-start(bf16[16,8,1792]{2,1,0:T(8,128)(2,1)} %bitcast.31), calls=%async_computation.4 | async-start | bytes 917504 | tf_op jit(solution)/shard_map/all_to_all | solution.py:32
  (27 other events, 183.5 us)
